TPU v7x, 128 devices: a whole 4x4x4 slice. The times are simulated.
128 devices in a mesh: pipe: 2 (over x_lo), tensor: 4 (over x_hi, core), dp: 16 (over z, y).
Axes of the slice: x: 4 (x_hi: 2, x_lo: 2; x = x_hi * 2 + x_lo), y: 4, z: 4, core: 2. Of those that a mesh axis runs over, the one named last changes fastest.
Arguments:
- inputs: bfloat16 [2, 2048, 16384], P(None, 'dp', 'tensor'), may hold values from -6 to 6
- w_in: bfloat16 [2, 16384, 1024], P('pipe', ('tensor', 'dp')), may hold values from -0.046875 to 0.046875
- w_out: bfloat16 [2, 1024, 16384], P('pipe', None, ('tensor', 'dp')), may hold values from -0.1875 to 0.1875
- cotangent: bfloat16 [2, 2048, 16384], P(None, 'dp', 'tensor'), may hold values from -6 to 6
Outputs:
- update_in: float32 [2, 16384, 1024], P('pipe', ('tensor', 'dp'))
- update_out: float32 [2, 1024, 16384], P('pipe', None, ('tensor', 'dp'))
- grad_norm: float32 [], replicated
All inputs are finite; a program needn't handle non-finite values.
Results may differ from a plain program's by a relative error of at most 0.008.
Values may be sent and summed in bfloat16 or wider, within the bound.
No kernel may reach another device: no remote copies, remote signals or barrier semaphores. Data moves between devices by JAX's collectives and lax.ppermute only.
A program may use at most 192 MiB of HBM per device.

v0:
```python
import jax
import jax.numpy as jnp
from jax import lax
from jax.experimental import pallas as pl
from jax.experimental.pallas import tpu as pltpu
from jax.sharding import Mesh
from jax.sharding import PartitionSpec as P


CLIP_NORM = 16384
AXES = ("p", "h", "c", "z", "y")
BF = jnp.bfloat16
F32 = jnp.float32


def dot(a, b):
    return jnp.dot(a, b, preferred_element_type=F32)


def dot_t0(a, b):
    return lax.dot_general(a, b, (((0,), (0,)), ((), ())), preferred_element_type=F32)


def dot_t1(a, b):
    return lax.dot_general(a, b, (((1,), (1,)), ((), ())), preferred_element_type=F32)


def a2a(value, axes):
    return lax.all_to_all(value, axes, 0, 0, tiled=True)


def shift(value, axis, by):
    count = lax.axis_size(axis)
    return lax.ppermute(value, axis, [(i, (i + by) % count) for i in range(count)])


def shift_x(value, by):
    pairs = []
    for p in range(2):
        for h in range(2):
            to = (h * 2 + p + by) % 4
            pairs.append((p * 2 + h, (to % 2) * 2 + to // 2))
    return lax.ppermute(value, ("p", "h"), pairs)


def silu_bf(pre):
    return jax.nn.silu(pre).astype(BF)


def slope_bf(up, pre):
    s = jax.nn.sigmoid(pre)
    return (up * s * (1.0 + pre * (1.0 - s))).astype(BF)


def cut_kernel(at_ref, x_ref, ct_ref, *outs):
    p, x, c, z, y = (at_ref[i] for i in range(5))
    tok = x_ref.shape[0]
    own = x_ref.shape[1] // 16
    half, part = tok // 2, tok // 8

    def copy(v_ref, u_ref):
        def group(i, carry):
            rc, q = i // 4, lax.rem(i, 4)
            source = lax.rem(c + rc, 2) * half + lax.rem(x + 4 - q, 4) * part
            rows = pl.ds(pl.multiple_of(source, part), part)
            to = pl.ds(pl.multiple_of(i * part, part), part)
            for k in range(4):
                for j in range(4):
                    at_v = lax.rem(z + k, 4) * 4 + lax.rem(y + 4 - j, 4)
                    at_u = lax.rem(z + 4 - j, 4) * 4 + lax.rem(y + k, 4)
                    for out, ref, at in ((outs[k], v_ref, at_v), (outs[4 + k], u_ref, at_u)):
                        cols = pl.ds(pl.multiple_of(at * own, own), own)
                        out[to, j * own : (j + 1) * own] = ref[rows, cols]
            return carry

        lax.fori_loop(0, 8, group, 0)

    @pl.when(p == 0)
    def _():
        copy(x_ref, ct_ref)

    @pl.when(p != 0)
    def _():
        copy(ct_ref, x_ref)


def cut(at, x, ct):
    tok, width = x.shape
    vmem = pl.BlockSpec(memory_space=pltpu.VMEM)
    outs = pl.pallas_call(
        cut_kernel,
        out_shape=[jax.ShapeDtypeStruct((tok, width // 4), BF)] * 8,
        in_specs=[pl.BlockSpec(memory_space=pltpu.SMEM), vmem, vmem],
        out_specs=[vmem] * 8,
        name="cut",
    )(at, x, ct)
    return list(outs[:4]), list(outs[4:])


def project_kernel(*refs):
    blocks, weights, sent, kept, left = refs[:4], refs[4:8], refs[8], refs[9], refs[10]
    tok = blocks[0].shape[0]
    half = tok // 2

    @pl.when(pl.program_id(0) == 0)
    def _():
        for k in range(4):
            left[k * half : (k + 1) * half, :] = blocks[k][half:, :]
            left[2 * tok + k * half : 2 * tok + (k + 1) * half, :] = blocks[k][:half, :]

    right = jnp.concatenate([w[...] for w in weights])
    total = dot(left[...], right)
    sent[...] = total[: 2 * tok].astype(BF)
    kept[...] = total[2 * tok :]


def project(blocks, weights):
    tok, wide = blocks[0].shape
    own, hidden = weights[0].shape
    tile = hidden // 4
    return pl.pallas_call(
        project_kernel,
        out_shape=[
            jax.ShapeDtypeStruct((2 * tok, hidden), BF),
            jax.ShapeDtypeStruct((2 * tok, hidden), F32),
        ],
        grid=(4,),
        in_specs=[pl.BlockSpec((tok, wide), lambda n: (0, 0))] * 4
        + [pl.BlockSpec((own, tile), lambda n: (0, n))] * 4,
        out_specs=[pl.BlockSpec((2 * tok, tile), lambda n: (0, n))] * 2,
        scratch_shapes=[pltpu.VMEM((4 * tok, wide), BF)],
        cost_estimate=pl.CostEstimate(
            flops=8 * tok * wide * hidden, bytes_accessed=8 * tok * wide * 2, transcendentals=0
        ),
    )(*blocks, *weights)


def turn_kernel(*refs):
    blocks, out = refs[:4], refs[4]
    tok = blocks[0].shape[0]
    for k in range(4):
        out[:, k * tok : (k + 1) * tok] = blocks[k][...].T


def turn(blocks):
    tok, wide = blocks[0].shape
    return pl.pallas_call(
        turn_kernel,
        out_shape=jax.ShapeDtypeStruct((wide, 4 * tok), BF),
        grid=(4,),
        in_specs=[pl.BlockSpec((tok, wide // 4), lambda j: (0, j))] * 4,
        out_specs=pl.BlockSpec((wide // 4, 4 * tok), lambda j: (j, 0)),
        cost_estimate=pl.CostEstimate(
            flops=2 * tok * wide * wide, bytes_accessed=16 * tok * wide, transcendentals=0
        ),
    )(*blocks)


def interleave(near, far):
    return jnp.concatenate([piece for pair in zip(near, far) for piece in pair])


def split_rows(outs, total):
    own = outs[0].shape[0]
    for j in range(4):
        outs[j][...] = total[j * own : (j + 1) * own].astype(outs[j].dtype)


def grad_v_kernel(*refs):
    turned, near, far, outs = refs[0], refs[1:5], refs[5:9], refs[9:]
    right = interleave([a[...] for a in near], [a[...] for a in far])
    split_rows(outs, dot(turned[...], right))


def grad_v_call(turned, near, far):
    wide, tok = turned.shape
    half, hidden = near[0].shape
    own, tile = wide // 4, hidden // 4
    return pl.pallas_call(
        grad_v_kernel,
        out_shape=[jax.ShapeDtypeStruct((own, hidden), t) for t in (F32, BF, BF, BF)],
        grid=(4,),
        in_specs=[pl.BlockSpec((wide, tok), lambda n: (0, 0))]
        + [pl.BlockSpec((half, tile), lambda n: (0, n))] * 8,
        out_specs=[pl.BlockSpec((own, tile), lambda n: (0, n))] * 4,
        cost_estimate=pl.CostEstimate(
            flops=2 * tok * wide * hidden, bytes_accessed=8 * tok * wide, transcendentals=0
        ),
        name="grad_v",
    )(turned, *near, *far)


def grad_u_kernel(*refs):
    turned, w_refs, q_refs, p_refs = refs[0], refs[1:5], refs[5:13], refs[13:21]
    outs, fold, factor, left = refs[21:25], refs[25], refs[26], refs[27]
    s = pl.program_id(0)
    own = w_refs[0].shape[0]
    half = q_refs[0].shape[1]
    tile = turned.shape[1]

    @pl.when(s == 0)
    def _():
        for j in range(4):
            fold[j * own : (j + 1) * own, :] = w_refs[j][...]
            for i in range(2):
                to = (2 * j + i) * half
                factor[to : to + half, :] = q_refs[4 * i + j][0]

    @pl.when(s < 4)
    def _():
        at = pl.ds(pl.multiple_of(s * tile, tile), tile)
        total = turned[...].astype(F32) + dot_t1(fold[...], factor[at, :])
        left[:, at] = total.astype(BF)

    @pl.when(s >= 4)
    def _():
        right = interleave([a[0] for a in p_refs[:4]], [a[0] for a in p_refs[4:]])
        split_rows(outs, dot(left[...], right))


def grad_u_call(turned, near, far, weights):
    wide, tok = turned.shape
    half, hidden = near[0].shape[1:]
    own, tile = wide // 4, hidden // 4

    def late(s):
        return jnp.maximum(s - 4, 0)

    return pl.pallas_call(
        grad_u_kernel,
        out_shape=[jax.ShapeDtypeStruct((own, hidden), t) for t in (F32, BF, BF, BF)],
        grid=(8,),
        in_specs=[pl.BlockSpec((wide, tok // 4), lambda s: (0, jnp.minimum(s, 3)))]
        + [pl.BlockSpec((own, hidden), lambda s: (0, 0))] * 4
        + [pl.BlockSpec((1, half, hidden), lambda s: (1, 0, 0))] * 8
        + [pl.BlockSpec((1, half, tile), lambda s: (0, 0, late(s)))] * 8,
        out_specs=[pl.BlockSpec((own, tile), lambda s: (0, late(s)))] * 4,
        scratch_shapes=[
            pltpu.VMEM((wide, hidden), BF),
            pltpu.VMEM((tok, hidden), BF),
            pltpu.VMEM((wide, tok), BF),
        ],
        cost_estimate=pl.CostEstimate(
            flops=4 * tok * wide * hidden, bytes_accessed=16 * tok * wide, transcendentals=0
        ),
        name="grad_u",
    )(turned, *weights, *near, *far, *near, *far)


def gather(value, axis):
    return [value] + [shift(value, axis, k) for k in (1, 2, 3)]


def exchange(pieces, axis, sign):
    return [pieces[0]] + [shift(pieces[k], axis, sign * k) for k in (1, 2, 3)]


def sum_back(blocks, axis):
    parts = exchange([blocks[0]] + [b.astype(BF) for b in blocks[1:]], axis, -1)
    return sum((part.astype(F32) for part in parts[1:]), parts[0])


def on_device(inputs, w_in, w_out, cotangent):
    p, h, c, z, y = (lax.axis_index(a) for a in AXES)
    first = p == 0
    n_micro, rows, cols = inputs.shape
    tok = n_micro * rows
    hidden = w_in.shape[2]
    half = tok // 2
    mine = half // 4

    w_i = w_in[0]
    w_o = w_out[0].T
    w_u = jnp.where(first, w_o, w_i)
    w_v = jnp.where(first, w_i, w_o)
    w_3 = lax.ppermute(w_u, "p", [(0, 1), (1, 0)])
    w_vs = gather(w_v, "y")
    at = jnp.stack([p, h * 2 + p, c, z, y])
    vs, us = cut(at, inputs.reshape(tok, cols), cotangent.reshape(tok, cols))
    vs = exchange(vs, "z", 1)
    us = exchange(us, "y", 1)
    w_us = gather(w_u, "z")

    m = 0.0
    far_u, far_3 = shift(w_u, "c", 1), shift(w_3, "c", 1)
    for mine_u, mine_3 in ((w_u, w_3), (far_u, far_3)):
        m += dot_t0(jnp.where(first, mine_u, mine_3), jnp.where(first, mine_3, mine_u))
    m = lax.dynamic_slice(
        m.reshape(2, 16, 2, -1, hidden), (c, 0, p, 0, 0), (1, 16, 1, hidden // 64, hidden)
    )
    m = a2a(m.reshape(hidden // 4, hidden).astype(BF), ("z", "y", "h"))
    m = m.reshape(32, -1, hidden).astype(F32).sum(0).astype(BF)
    m = a2a(jnp.broadcast_to(m[None], (4,) + m.shape), ("p", "h")).reshape(-1, hidden)
    w_us[0], w_vs[0], m = lax.optimization_barrier((w_us[0], w_vs[0], m))
    m_near = lax.all_gather(m, ("z", "y"), axis=0, tiled=True)
    m_far = shift(m_near, "c", 1)

    def reduced(blocks, weights, axis):
        sent, kept = project(blocks, weights)
        sent = shift(sent, "c", 1)
        kept = kept + sent.astype(F32)
        return sum_back([kept[k * half : (k + 1) * half] for k in range(4)], axis)

    a_v = reduced(vs, w_vs, "z")
    a_u = reduced(us, w_us, "y")
    w_3s = gather(w_3, "z")

    both = jnp.concatenate([a_u, a_v], 1)
    pieces = [both[(4 - k) % 4 * mine :][:mine] for k in range(4)]
    got = [pieces[0]] + [shift_x(pieces[k].astype(BF), k).astype(F32) for k in (1, 2, 3)]
    same = got[0] + got[2]
    other = got[1] + got[3]
    layer0 = jnp.where(first, same, other)
    layer1 = jnp.where(first, other, same)
    up0, pre0 = layer0[:, :hidden], layer0[:, hidden:]
    pre1, up1 = layer1[:, :hidden], layer1[:, hidden:]
    side = hidden // 2
    act0 = silu_bf(pre0)
    low, high = act0[:, :side], act0[:, side:]
    near, far = jnp.where(c == 0, low, high), jnp.where(c == 0, high, low)
    pre1 = pre1 + dot(near, m_near) + dot(far, m_far)
    act1 = silu_bf(pre1)
    slope1 = slope_bf(up1, pre1)
    near, far = dot_t1(slope1, m_near), dot_t1(slope1, m_far)
    low, high = jnp.where(c == 0, near, far), jnp.where(c == 0, far, near)
    slope0 = slope_bf(up0 + jnp.concatenate([low, high], 1), pre0)

    to_first = jnp.stack([slope0, act0, slope1])
    to_last = jnp.stack([act1, slope1, act0])
    same = jnp.where(first, to_first, to_last)
    other = jnp.where(first, to_last, to_first)
    got = [same, shift_x(other, 1), shift_x(same, 2), shift_x(other, 3)]
    rpq = jnp.concatenate(got, 1)
    r_near = gather(rpq[0], "z")
    pq_near = gather(rpq[1:], "y")
    r_far = [shift(a, "c", 1) for a in r_near]
    pq_far = [shift(a, "c", 1) for a in pq_near]

    g_v = sum_back(grad_v_call(turn(vs), r_near, r_far), "y")
    g_u = sum_back(grad_u_call(turn(us), pq_near, pq_far, w_3s), "z")

    squares = jnp.sum(g_u * g_u) + jnp.sum(g_v * g_v)
    for axes, count in ((("z", "y"), 16), (("p", "h", "c"), 8)):
        row = jnp.broadcast_to(squares, (count, 8, 128))
        squares = a2a(row, axes)[:, 0, 0].sum()
    grad_norm = jnp.sqrt(squares)
    factor = jnp.minimum(1.0, CLIP_NORM / grad_norm)
    g_in = jnp.where(first, g_v, g_u) * factor
    g_out = jnp.where(first, g_u, g_v) * factor
    return (g_in[None], g_out.T[None], grad_norm)


def solution(mesh):
    split = Mesh(mesh.devices.reshape(mesh.shape["pipe"], 2, 2, 4, 4), AXES)
    tensor, dp, all_model = ("h", "c"), ("z", "y"), ("h", "c", "z", "y")
    placed = (
        P(None, dp, tensor),
        P("p", all_model, None),
        P("p", None, all_model),
        P(None, dp, tensor),
    )
    return jax.shard_map(
        on_device,
        mesh=split,
        in_specs=placed,
        out_specs=(P("p", all_model, None), P("p", None, all_model), P()),
        check_vma=False,
    )
```

profile of v0, /device:TPU:0, one launch (start us, length us, event | category | flops | bytes accessed | tf_op | source)
XLA Modules:
  0.0 311.1 jit_solution(10938023753739601173)
XLA Ops:
  11.3 11.9 %collective-permute-done.6.refs_1_ = bf16[256,1024]{1,0:T(8,128)(2,1)S(1)} collective-permute-done((bf16[256,1024]{1,0:T(8,128)(2,1)S(1)}, bf16[256,1024]{1,0:T(8,128)(2,1)S(1)}, u32[]{:S(2)}, u32[]{:S(2)}) %collective-permute-start.6) | collective-permute-done | bytes 524320 | tf_op jit(solution)/shard_map/ppermute | solution.py:276
  23.9 5.0 %cut.1 = (bf16[256,1024]{1,0:T(8,128)(2,1)}, bf16[256,1024]{1,0:T(8,128)(2,1)}, bf16[256,1024]{1,0:T(8,128)(2,1)}, bf16[256,1024]{1,0:T(8,128)(2,1)}, bf16[256,1...) custom-call(s32[5]{0:T(128)} %stack.43.at_ref, ...), custom_call_target="tpu_custom_call" | custom-call | tf_op jit(solution)/shard_map/cut/pallas_call | solution.py:90
  30.8 2.9 collective-permute-start.4
  37.5 8.3 %all-to-all-start = ((bf16[32,8,1024]{2,1,0:T(8,128)(2,1)}), bf16[32,8,1024]{2,1,0:T(8,128)(2,1)S(1)}, u32[]{:S(2)}, u32[]{:S(2)}) async-start(bf16[32,8,1024]{2,1,0:T(8,128)(2,1)} %bitcast.12), calls=%async_computation | async-start | bytes 1048576 | tf_op jit(solution)/shard_map/all_to_all | solution.py:29
  45.8 3.4 %collective-permute-start.10 = (bf16[256,1024]{1,0:T(8,128)(2,1)S(1)}, bf16[256,1024]{1,0:T(8,128)(2,1)}, u32[]{:S(2)}, u32[]{:S(2)}) collective-permute-start(bf16[256,1024]{1,0:T(8,128)(2,1)S(1)} %get-tuple-element.34.refs_4_), channel_id=1, source_target_pairs={{0,8},{4,12},{8,0},{12,4},{1,9},{5,13},{9,1},{13,5},{2,10},{6,14},... | collective-permute-start | bytes 1572872 | tf_op jit(solution)/shard_map/ppermute | solution.py:34
  51.3 9.6 %collective-permute-done.4.refs_2_ = bf16[256,1024]{1,0:T(8,128)(2,1)} collective-permute-done((bf16[256,1024]{1,0:T(8,128)(2,1)}, bf16[256,1024]{1,0:T(8,128)(2,1)}, u32[]{:S(2)}, u32[]{:S(2)}) %collective-permute-start.4) | collective-permute-done | bytes 524320 | tf_op jit(solution)/shard_map/ppermute | solution.py:34
  60.9 1.9 collective-permute-start
  62.8 3.6 %collective-permute-start.1 = (bf16[256,1024]{1,0:T(8,128)(2,1)}, bf16[256,1024]{1,0:T(8,128)(2,1)}, u32[]{:S(2)}, u32[]{:S(2)}) collective-permute-start(bf16[256,1024]{1,0:T(8,128)(2,1)} %get-tuple-element.28), channel_id=1, source_target_pairs={{0,8},{4,12},{8,0},{12,4},{1,9},{5,13},{9,1},{13,5},{2,10},{6,14},... | collective-permute-start | bytes 1572872 | tf_op jit(solution)/shard_map/ppermute | solution.py:34
  66.5 9.6 %all_to_all.21 = bf16[4,8,1024]{2,1,0:T(8,128)(2,1)} all-to-all(bf16[4,8,1024]{2,1,0:T(8,128)(2,1)S(1)} %broadcast_in_dim.18), channel_id=1, replica_groups=mesh['p'=2,'h'=2,'c'=2,'z'=4,'y'=4] {'p','h'}, dimensions={0} | all-to-all | bytes 131072 | tf_op jit(solution)/shard_map/all_to_all | solution.py:29
  79.0 2.4 collective-permute-start.17
  81.4 1.9 collective-permute-start.18
  83.3 6.7 %collective-permute-done.refs_1_ = bf16[256,1024]{1,0:T(8,128)(2,1)S(1)} collective-permute-done((bf16[256,1024]{1,0:T(8,128)(2,1)}, bf16[256,1024]{1,0:T(8,128)(2,1)S(1)}, u32[]{:S(2)}, u32[]{:S(2)}) %collective-permute-start) | collective-permute-done | bytes 524320 | tf_op jit(solution)/shard_map/ppermute | solution.py:34
  90.7 6.3 %shard_map.68 = (bf16[512,1024]{1,0:T(8,128)(2,1)}, f32[512,1024]{1,0:T(8,128)}) custom-call(bf16[256,1024]{1,0:T(8,128)(2,1)} %get-tuple-element.30.refs_0_, bf16[256,1024]{1,0:T(8,128)(2,1)} %copy-done.9, bf16[256,1024]{1,0:T(8,128)(2,1)} %collective-permute-done.4.refs_2_, bf16[256,1024]{1,0:T(8,128)(2,1)} %collective-permute-done.5.refs_3_, ...), custom_call_target="tpu_custom_call" | custom-call | flops 2147483648 | bytes 4194304 | tf_op jit(solution)/shard_map/pallas_call | solution.py:121
  97.0 2.8 collective-permute-done.1.refs_2_
  99.7 4.5 %collective-permute-done.2.refs_3_ = bf16[256,1024]{1,0:T(8,128)(2,1)S(1)} collective-permute-done((bf16[256,1024]{1,0:T(8,128)(2,1)}, bf16[256,1024]{1,0:T(8,128)(2,1)S(1)}, u32[]{:S(2)}, u32[]{:S(2)}) %collective-permute-start.2) | collective-permute-done | bytes 524320 | tf_op jit(solution)/shard_map/ppermute | solution.py:34
  105.2 6.4 %shard_map.69 = (bf16[512,1024]{1,0:T(8,128)(2,1)}, f32[512,1024]{1,0:T(8,128)}) custom-call(bf16[256,1024]{1,0:T(8,128)(2,1)} %get-tuple-element.26.refs_0_, bf16[256,1024]{1,0:T(8,128)(2,1)} %copy-done.10, bf16[256,1024]{1,0:T(8,128)(2,1)} %collective-permute-done.1.refs_2_, bf16[256,1024]{1,0:T(8,128)(2,1)} %copy-done.11, bf16[256,1024]{1,0:T(8,128)(2,1)} %copy-done.7, ...), custom_call_target="tpu_custom_call" | custom-call | flops 2147483648 | bytes 4194304 | tf_op jit(solution)/shard_map/pallas_call | solution.py:121
  113.6 2.9 collective-permute-start.13
  119.7 2.1 collective-permute-start.20
  122.6 6.4 %collective-permute-done.13 = bf16[128,1024]{1,0:T(8,128)(2,1)S(1)} collective-permute-done((bf16[128,1024]{1,0:T(8,128)(2,1)S(1)}, bf16[128,1024]{1,0:T(8,128)(2,1)S(1)}, u32[]{:S(2)}, u32[]{:S(2)}) %collective-permute-start.13) | collective-permute-done | bytes 262176 | tf_op jit(solution)/shard_map/ppermute | solution.py:34
  130.1 2.7 collective-permute-done.15
  133.7 4.5 %collective-permute-done.22 = bf16[128,1024]{1,0:T(8,128)(2,1)S(1)} collective-permute-done((bf16[128,1024]{1,0:T(8,128)(2,1)S(1)}, bf16[128,1024]{1,0:T(8,128)(2,1)S(1)}, u32[]{:S(2)}, u32[]{:S(2)}) %collective-permute-start.22) | collective-permute-done | bytes 262176 | tf_op jit(solution)/shard_map/ppermute | solution.py:34
  140.5 2.6 collective-permute-start.25
  143.1 15.1 %all-gather.2.cloned.1.call-done = bf16[512,1024]{1,0:T(8,128)(2,1)} async-done(((bf16[32,1024]{1,0:T(8,128)(2,1)}), bf16[512,1024]{1,0:T(8,128)(2,1)}) %all-gather.2.cloned.1.call-update) | async-done | bytes 1048592 | tf_op jit(solution)/shard_map/all_gather | solution.py:295
  163.9 2.7 collective-permute-start.28
  169.3 2.6 collective-permute-start.41
  171.9 3.8 %collective-permute-done.28 = bf16[3,32,1024]{2,1,0:T(8,128)(2,1)S(1)} collective-permute-done((bf16[3,32,1024]{2,1,0:T(8,128)(2,1)S(1)}, bf16[3,32,1024]{2,1,0:T(8,128)(2,1)S(1)}, u32[]{:S(2)}, u32[]{:S(2)}) %collective-permute-start.28) | collective-permute-done | bytes 196640 | tf_op jit(solution)/shard_map/ppermute | solution.py:43
  177.1 2.7 collective-permute-start.31
  180.1 14.6 %collective-permute-done.40.refs_2_ = bf16[256,1024]{1,0:T(8,128)(2,1)S(1)} collective-permute-done((bf16[256,1024]{1,0:T(8,128)(2,1)S(1)}, bf16[256,1024]{1,0:T(8,128)(2,1)S(1)}, u32[]{:S(2)}, u32[]{:S(2)}) %collective-permute-start.40) | collective-permute-done | bytes 524320 | tf_op jit(solution)/shard_map/ppermute | solution.py:34
  194.6 3.1 collective-permute-start.44
  200.3 1.9 collective-permute-start.32
  202.2 3.4 %collective-permute-done.31.refs_3_ = bf16[128,1024]{1,0:T(8,128)(2,1)S(1)} collective-permute-done((bf16[128,1024]{1,0:T(8,128)(2,1)S(1)}, bf16[128,1024]{1,0:T(8,128)(2,1)S(1)}, u32[]{:S(2)}, u32[]{:S(2)}) %collective-permute-start.31) | collective-permute-done | bytes 262176 | tf_op jit(solution)/shard_map/ppermute | solution.py:34
  207.8 2.7 collective-permute-start.42
  210.5 1.9 collective-permute-done.45.refs_8_.refs_16_
  214.4 4.2 %shard_map.67.refs_0_ = bf16[1024,1024]{1,0:T(8,128)(2,1)} custom-call(bf16[256,1024]{1,0:T(8,128)(2,1)} %get-tuple-element.26.refs_0_, bf16[256,1024]{1,0:T(8,128)(2,1)} %copy-done.10, bf16[256,1024]{1,0:T(8,128)(2,1)} %collective-permute-done.1.refs_2_, bf16[256,1024]{1,0:T(8,128)(2,1)} %copy-done.11), custom_call_target="tpu_custom_call" | custom-call | flops 536870912 | bytes 4194304 | tf_op jit(solution)/shard_map/pallas_call | solution.py:147
  218.6 6.1 %grad_v.1 = (f32[256,1024]{1,0:T(8,128)}, bf16[256,1024]{1,0:T(8,128)(2,1)}, bf16[256,1024]{1,0:T(8,128)(2,1)}, bf16[256,1024]{1,0:T(8,128)(2,1)}) custom-call(bf16[1024,1024]{1,0:T(8,128)(2,1)} %shard_map.67.refs_0_, bf16[128,1024]{1,0:T(8,128)(2,1)} %copy-done.12, bf16[128,1024]{1,0:T(8,128)(2,1)} %copy-done.19, bf16[128,1024]{1,0:T(8,128)(2,1)} %copy-done.20, ...), custom_call_target="tpu_custom_call" | custom-call | flops 2147483648 | bytes 8388608 | tf_op jit(solution)/shard_map/grad_v/pallas_call | solution.py:179
  225.5 4.0 %collective-permute-start.37 = (bf16[256,1024]{1,0:T(8,128)(2,1)}, bf16[256,1024]{1,0:T(8,128)(2,1)S(1)}, u32[]{:S(2)}, u32[]{:S(2)}) collective-permute-start(bf16[256,1024]{1,0:T(8,128)(2,1)} %get-tuple-element.42), channel_id=1, source_target_pairs={{0,3},{1,0},{2,1},{3,2},{4,7},{5,4},{6,5},{7,6},{8,11},{9,8},{10,9... | collective-permute-start | bytes 1572872 | tf_op jit(solution)/shard_map/ppermute | solution.py:34
  229.5 4.2 %shard_map.70.refs_0_ = bf16[1024,1024]{1,0:T(8,128)(2,1)} custom-call(bf16[256,1024]{1,0:T(8,128)(2,1)} %get-tuple-element.30.refs_0_, bf16[256,1024]{1,0:T(8,128)(2,1)} %copy-done.9, bf16[256,1024]{1,0:T(8,128)(2,1)} %collective-permute-done.4.refs_2_, bf16[256,1024]{1,0:T(8,128)(2,1)} %collective-permute-done.5.refs_3_), custom_call_target="tpu_custom_call" | custom-call | flops 536870912 | bytes 4194304 | tf_op jit(solution)/shard_map/pallas_call | solution.py:147
  235.4 11.0 %grad_u.1 = (f32[256,1024]{1,0:T(8,128)}, bf16[256,1024]{1,0:T(8,128)(2,1)}, bf16[256,1024]{1,0:T(8,128)(2,1)}, bf16[256,1024]{1,0:T(8,128)(2,1)}) custom-call(bf16[1024,1024]{1,0:T(8,128)(2,1)} %shard_map.70.refs_0_, bf16[256,1024]{1,0:T(8,128)(2,1)} %copy-done.2, bf16[256,1024]{1,0:T(8,128)(2,1)} %copy-done.13, bf16[256,1024]{1,0:T(8,128)(2,1)} %copy-done.14, ...), custom_call_target="tpu_custom_call" | custom-call | flops 4294967296 | bytes 16777216 | tf_op jit(solution)/shard_map/grad_u/pallas_call | solution.py:229
  246.4 2.5 collective-permute-start.50
  248.9 3.2 %collective-permute-done.37 = bf16[256,1024]{1,0:T(8,128)(2,1)S(1)} collective-permute-done((bf16[256,1024]{1,0:T(8,128)(2,1)}, bf16[256,1024]{1,0:T(8,128)(2,1)S(1)}, u32[]{:S(2)}, u32[]{:S(2)}) %collective-permute-start.37) | collective-permute-done | bytes 524320 | tf_op jit(solution)/shard_map/ppermute | solution.py:34
  252.9 7.1 %collective-permute-done.39 = bf16[256,1024]{1,0:T(8,128)(2,1)} collective-permute-done((bf16[256,1024]{1,0:T(8,128)(2,1)S(1)}, bf16[256,1024]{1,0:T(8,128)(2,1)}, u32[]{:S(2)}, u32[]{:S(2)}) %collective-permute-start.39) | collective-permute-done | bytes 524320 | tf_op jit(solution)/shard_map/ppermute | solution.py:34
  260.0 1.9 multiply_reduce_fusion
  261.9 8.7 %collective-permute-done.50 = bf16[256,1024]{1,0:T(8,128)(2,1)S(1)} collective-permute-done((bf16[256,1024]{1,0:T(8,128)(2,1)}, bf16[256,1024]{1,0:T(8,128)(2,1)S(1)}, u32[]{:S(2)}, u32[]{:S(2)}) %collective-permute-start.50) | collective-permute-done | bytes 524320 | tf_op jit(solution)/shard_map/ppermute | solution.py:34
  270.6 3.5 %collective-permute-done.52 = bf16[256,1024]{1,0:T(8,128)(2,1)S(1)} collective-permute-done((bf16[256,1024]{1,0:T(8,128)(2,1)}, bf16[256,1024]{1,0:T(8,128)(2,1)S(1)}, u32[]{:S(2)}, u32[]{:S(2)}) %collective-permute-start.52) | collective-permute-done | bytes 524320 | tf_op jit(solution)/shard_map/ppermute | solution.py:34
  274.1 1.9 multiply_reduce_fusion.1
  277.3 11.7 %all_to_all.22 = f32[16,8,128]{2,1,0:T(8,128)S(1)} all-to-all(f32[16,8,128]{2,1,0:T(8,128)S(1)} %broadcast_in_dim.19), channel_id=1, replica_groups=mesh['p'=2,'h'=2,'c'=2,'z'=4,'y'=4] {'z','y'}, dimensions={0} | all-to-all | bytes 131072 | tf_op jit(solution)/shard_map/all_to_all | solution.py:29
  290.2 7.7 %all_to_all.23 = f32[8,8,128]{2,1,0:T(8,128)S(1)} all-to-all(f32[8,8,128]{2,1,0:T(8,128)S(1)} %broadcast_in_dim.20), channel_id=1, replica_groups=mesh['p'=2,'h'=2,'c'=2,'z'=4,'y'=4] {'p','h','c'}, dimensions={0} | all-to-all | bytes 65536 | tf_op jit(solution)/shard_map/all_to_all | solution.py:29
  299.3 2.5 multiply_bitcast_fusion
  (160 shorter events, 50.4 us)
Async XLA Ops:
  9.6 13.6 %collective-permute-start.6 = (bf16[256,1024]{1,0:T(8,128)(2,1)S(1)}, bf16[256,1024]{1,0:T(8,128)(2,1)S(1)}, u32[]{:S(2)}, u32[]{:S(2)}) collective-permute-start(bf16[256,1024]{1,0:T(8,128)(2,1)S(1)} %get-tuple-element.34.refs_4_), channel_id=1, source_target_pairs={{0,64},{64,0},{1,65},{65,1},{2,66},{66,2},{3,67},{67,3},{4,68},{68... | collective-permute-start | bytes 1572872 | tf_op jit(solution)/shard_map/ppermute | solution.py:276
  11.2 24.5 %collective-permute-start.7 = (bf16[256,1024]{1,0:T(8,128)(2,1)S(1)}, bf16[256,1024]{1,0:T(8,128)(2,1)S(1)}, u32[]{:S(2)}, u32[]{:S(2)}) collective-permute-start(bf16[256,1024]{1,0:T(8,128)(2,1)S(1)} %get-tuple-element.34.refs_4_), channel_id=1, source_target_pairs={{0,16},{16,0},{1,17},{17,1},{2,18},{18,2},{3,19},{19,3},{4,20},{20... | collective-permute-start | bytes 1572872 | tf_op jit(solution)/shard_map/ppermute | solution.py:34
  23.2 12.6 %collective-permute-start.8 = (bf16[256,1024]{1,0:T(8,128)(2,1)S(1)}, bf16[256,1024]{1,0:T(8,128)(2,1)S(1)}, u32[]{:S(2)}, u32[]{:S(2)}) collective-permute-start(bf16[256,1024]{1,0:T(8,128)(2,1)S(1)} %collective-permute-done.6.refs_1_), channel_id=1, source_target_pairs={{0,16},{16,0},{1,17},{17,1},{2,18},{18,2},{3,19},{19,3},{4,20},{20... | collective-permute-start | bytes 1572872 | tf_op jit(solution)/shard_map/ppermute | solution.py:34
  28.9 21.4 %collective-permute-start.3 = (bf16[256,1024]{1,0:T(8,128)(2,1)}, bf16[256,1024]{1,0:T(8,128)(2,1)S(1)}, u32[]{:S(2)}, u32[]{:S(2)}) collective-permute-start(bf16[256,1024]{1,0:T(8,128)(2,1)} %get-tuple-element.31), channel_id=1, source_target_pairs={{0,1},{1,2},{2,3},{3,0},{4,5},{5,6},{6,7},{7,4},{8,9},{9,10},{10,1... | collective-permute-start | bytes 1572872 | tf_op jit(solution)/shard_map/ppermute | solution.py:34
  30.8 30.1 %collective-permute-start.4 = (bf16[256,1024]{1,0:T(8,128)(2,1)}, bf16[256,1024]{1,0:T(8,128)(2,1)}, u32[]{:S(2)}, u32[]{:S(2)}) collective-permute-start(bf16[256,1024]{1,0:T(8,128)(2,1)} %get-tuple-element.32), channel_id=1, source_target_pairs={{0,2},{1,3},{2,0},{3,1},{4,6},{5,7},{6,4},{7,5},{8,10},{9,11},{10,... | collective-permute-start | bytes 1572872 | tf_op jit(solution)/shard_map/ppermute | solution.py:34
  33.7 29.1 %collective-permute-start.5 = (bf16[256,1024]{1,0:T(8,128)(2,1)}, bf16[256,1024]{1,0:T(8,128)(2,1)}, u32[]{:S(2)}, u32[]{:S(2)}) collective-permute-start(bf16[256,1024]{1,0:T(8,128)(2,1)} %get-tuple-element.33), channel_id=1, source_target_pairs={{0,3},{1,0},{2,1},{3,2},{4,7},{5,4},{6,5},{7,6},{8,11},{9,8},{10,9... | collective-permute-start | bytes 1572872 | tf_op jit(solution)/shard_map/ppermute | solution.py:34
  37.5 28.9 %all-to-all-start = ((bf16[32,8,1024]{2,1,0:T(8,128)(2,1)}), bf16[32,8,1024]{2,1,0:T(8,128)(2,1)S(1)}, u32[]{:S(2)}, u32[]{:S(2)}) async-start(bf16[32,8,1024]{2,1,0:T(8,128)(2,1)} %bitcast.12), calls=%async_computation | async-start | bytes 1048576 | tf_op jit(solution)/shard_map/all_to_all | solution.py:29
  45.7 112.5 %all-gather.2.cloned.1.call-start = ((), (), s32[]{:S(2)}) async-start(), calls=%async_computation.4 | async-start | bytes 1114112 | tf_op jit(solution)/shard_map/all_gather | solution.py:295
  45.8 30.3 %collective-permute-start.10 = (bf16[256,1024]{1,0:T(8,128)(2,1)S(1)}, bf16[256,1024]{1,0:T(8,128)(2,1)}, u32[]{:S(2)}, u32[]{:S(2)}) collective-permute-start(bf16[256,1024]{1,0:T(8,128)(2,1)S(1)} %get-tuple-element.34.refs_4_), channel_id=1, source_target_pairs={{0,8},{4,12},{8,0},{12,4},{1,9},{5,13},{9,1},{13,5},{2,10},{6,14},... | collective-permute-start | bytes 1572872 | tf_op jit(solution)/shard_map/ppermute | solution.py:34
  49.2 29.8 %collective-permute-start.11 = (bf16[256,1024]{1,0:T(8,128)(2,1)S(1)}, bf16[256,1024]{1,0:T(8,128)(2,1)}, u32[]{:S(2)}, u32[]{:S(2)}) collective-permute-start(bf16[256,1024]{1,0:T(8,128)(2,1)S(1)} %get-tuple-element.34.refs_4_), channel_id=1, source_target_pairs={{0,12},{4,0},{8,4},{12,8},{1,13},{5,1},{9,5},{13,9},{2,14},{6,2},{... | collective-permute-start | bytes 1572872 | tf_op jit(solution)/shard_map/ppermute | solution.py:34
  50.3 31.1 %collective-permute-start.9 = (bf16[256,1024]{1,0:T(8,128)(2,1)S(1)}, bf16[256,1024]{1,0:T(8,128)(2,1)}, u32[]{:S(2)}, u32[]{:S(2)}) collective-permute-start(bf16[256,1024]{1,0:T(8,128)(2,1)S(1)} %get-tuple-element.34.refs_4_), channel_id=1, source_target_pairs={{0,4},{4,8},{8,12},{12,0},{1,5},{5,9},{9,13},{13,1},{2,6},{6,10},{... | collective-permute-start | bytes 1572872 | tf_op jit(solution)/shard_map/ppermute | solution.py:34
  60.9 29.2 %collective-permute-start = (bf16[256,1024]{1,0:T(8,128)(2,1)}, bf16[256,1024]{1,0:T(8,128)(2,1)S(1)}, u32[]{:S(2)}, u32[]{:S(2)}) collective-permute-start(bf16[256,1024]{1,0:T(8,128)(2,1)} %get-tuple-element.27), channel_id=1, source_target_pairs={{0,4},{4,8},{8,12},{12,0},{1,5},{5,9},{9,13},{13,1},{2,6},{6,10},{... | collective-permute-start | bytes 1572872 | tf_op jit(solution)/shard_map/ppermute | solution.py:34
  62.8 37.0 %collective-permute-start.1 = (bf16[256,1024]{1,0:T(8,128)(2,1)}, bf16[256,1024]{1,0:T(8,128)(2,1)}, u32[]{:S(2)}, u32[]{:S(2)}) collective-permute-start(bf16[256,1024]{1,0:T(8,128)(2,1)} %get-tuple-element.28), channel_id=1, source_target_pairs={{0,8},{4,12},{8,0},{12,4},{1,9},{5,13},{9,1},{13,5},{2,10},{6,14},... | collective-permute-start | bytes 1572872 | tf_op jit(solution)/shard_map/ppermute | solution.py:34
  76.1 28.1 %collective-permute-start.16 = (bf16[256,1024]{1,0:T(8,128)(2,1)S(1)}, bf16[256,1024]{1,0:T(8,128)(2,1)S(1)}, u32[]{:S(2)}, u32[]{:S(2)}) collective-permute-start(bf16[256,1024]{1,0:T(8,128)(2,1)S(1)} %get-tuple-element.37.refs_4_), channel_id=1, source_target_pairs={{0,1},{1,2},{2,3},{3,0},{4,5},{5,6},{6,7},{7,4},{8,9},{9,10},{10,1... | collective-permute-start | bytes 1572872 | tf_op jit(solution)/shard_map/ppermute | solution.py:34
  79.0 25.2 %collective-permute-start.17 = (bf16[256,1024]{1,0:T(8,128)(2,1)S(1)}, bf16[256,1024]{1,0:T(8,128)(2,1)}, u32[]{:S(2)}, u32[]{:S(2)}) collective-permute-start(bf16[256,1024]{1,0:T(8,128)(2,1)S(1)} %get-tuple-element.37.refs_4_), channel_id=1, source_target_pairs={{0,2},{1,3},{2,0},{3,1},{4,6},{5,7},{6,4},{7,5},{8,10},{9,11},{10,... | collective-permute-start | bytes 1572872 | tf_op jit(solution)/shard_map/ppermute | solution.py:34
  81.4 22.8 %collective-permute-start.18 = (bf16[256,1024]{1,0:T(8,128)(2,1)S(1)}, bf16[256,1024]{1,0:T(8,128)(2,1)}, u32[]{:S(2)}, u32[]{:S(2)}) collective-permute-start(bf16[256,1024]{1,0:T(8,128)(2,1)S(1)} %get-tuple-element.37.refs_4_), channel_id=1, source_target_pairs={{0,3},{1,0},{2,1},{3,2},{4,7},{5,4},{6,5},{7,6},{8,11},{9,8},{10,9... | collective-permute-start | bytes 1572872 | tf_op jit(solution)/shard_map/ppermute | solution.py:34
  90.1 14.1 %collective-permute-start.2 = (bf16[256,1024]{1,0:T(8,128)(2,1)}, bf16[256,1024]{1,0:T(8,128)(2,1)S(1)}, u32[]{:S(2)}, u32[]{:S(2)}) collective-permute-start(bf16[256,1024]{1,0:T(8,128)(2,1)} %get-tuple-element.29), channel_id=1, source_target_pairs={{0,12},{4,0},{8,4},{12,8},{1,13},{5,1},{9,5},{13,9},{2,14},{6,2},{... | collective-permute-start | bytes 1572872 | tf_op jit(solution)/shard_map/ppermute | solution.py:34
  99.7 12.0 %collective-permute-start.12 = (bf16[512,1024]{1,0:T(8,128)(2,1)}, bf16[512,1024]{1,0:T(8,128)(2,1)}, u32[]{:S(2)}, u32[]{:S(2)}) collective-permute-start(bf16[512,1024]{1,0:T(8,128)(2,1)} %get-tuple-element.36), channel_id=1, source_target_pairs={{0,16},{16,0},{1,17},{17,1},{2,18},{18,2},{3,19},{19,3},{4,20},{20... | collective-permute-start | bytes 3145736 | tf_op jit(solution)/shard_map/ppermute | solution.py:34
  113.6 15.5 %collective-permute-start.13 = (bf16[128,1024]{1,0:T(8,128)(2,1)S(1)}, bf16[128,1024]{1,0:T(8,128)(2,1)S(1)}, u32[]{:S(2)}, u32[]{:S(2)}) collective-permute-start(bf16[128,1024]{1,0:T(8,128)(2,1)S(1)} %get-tuple-element.70), channel_id=1, source_target_pairs={{0,3},{1,0},{2,1},{3,2},{4,7},{5,4},{6,5},{7,6},{8,11},{9,8},{10,9... | collective-permute-start | bytes 786440 | tf_op jit(solution)/shard_map/ppermute | solution.py:34
  116.5 13.7 %collective-permute-start.14 = (bf16[128,1024]{1,0:T(8,128)(2,1)S(1)}, bf16[128,1024]{1,0:T(8,128)(2,1)S(1)}, u32[]{:S(2)}, u32[]{:S(2)}) collective-permute-start(bf16[128,1024]{1,0:T(8,128)(2,1)S(1)} %get-tuple-element.72), channel_id=1, source_target_pairs={{0,2},{1,3},{2,0},{3,1},{4,6},{5,7},{6,4},{7,5},{8,10},{9,11},{10,... | collective-permute-start | bytes 786440 | tf_op jit(solution)/shard_map/ppermute | solution.py:34
  117.2 15.7 %collective-permute-start.15 = (bf16[128,1024]{1,0:T(8,128)(2,1)S(1)}, bf16[128,1024]{1,0:T(8,128)(2,1)S(1)}, u32[]{:S(2)}, u32[]{:S(2)}) collective-permute-start(bf16[128,1024]{1,0:T(8,128)(2,1)S(1)} %get-tuple-element.71), channel_id=1, source_target_pairs={{0,1},{1,2},{2,3},{3,0},{4,5},{5,6},{6,7},{7,4},{8,9},{9,10},{10,1... | collective-permute-start | bytes 786440 | tf_op jit(solution)/shard_map/ppermute | solution.py:34
  119.7 14.0 %collective-permute-start.20 = (bf16[128,1024]{1,0:T(8,128)(2,1)S(1)}, bf16[128,1024]{1,0:T(8,128)(2,1)S(1)}, u32[]{:S(2)}, u32[]{:S(2)}) collective-permute-start(bf16[128,1024]{1,0:T(8,128)(2,1)S(1)} %get-tuple-element.73), channel_id=1, source_target_pairs={{0,12},{4,0},{8,4},{12,8},{1,13},{5,1},{9,5},{13,9},{2,14},{6,2},{... | collective-permute-start | bytes 786440 | tf_op jit(solution)/shard_map/ppermute | solution.py:34
  121.8 11.9 %collective-permute-start.21 = (bf16[128,1024]{1,0:T(8,128)(2,1)S(1)}, bf16[128,1024]{1,0:T(8,128)(2,1)S(1)}, u32[]{:S(2)}, u32[]{:S(2)}) collective-permute-start(bf16[128,1024]{1,0:T(8,128)(2,1)S(1)} %get-tuple-element.75), channel_id=1, source_target_pairs={{0,8},{4,12},{8,0},{12,4},{1,9},{5,13},{9,1},{13,5},{2,10},{6,14},... | collective-permute-start | bytes 786440 | tf_op jit(solution)/shard_map/ppermute | solution.py:34
  129.1 9.1 %collective-permute-start.22 = (bf16[128,1024]{1,0:T(8,128)(2,1)S(1)}, bf16[128,1024]{1,0:T(8,128)(2,1)S(1)}, u32[]{:S(2)}, u32[]{:S(2)}) collective-permute-start(bf16[128,1024]{1,0:T(8,128)(2,1)S(1)} %get-tuple-element.74), channel_id=1, source_target_pairs={{0,4},{4,8},{8,12},{12,0},{1,5},{5,9},{9,13},{13,1},{2,6},{6,10},{... | collective-permute-start | bytes 786440 | tf_op jit(solution)/shard_map/ppermute | solution.py:34
  138.4 19.8 %collective-permute-start.23 = (bf16[32,2048]{1,0:T(8,128)(2,1)S(1)}, bf16[32,2048]{1,0:T(8,128)(2,1)S(1)}, u32[]{:S(2)}, u32[]{:S(2)}) collective-permute-start(bf16[32,2048]{1,0:T(8,128)(2,1)S(1)} %get-tuple-element.78), channel_id=1, source_target_pairs={{0,32},{32,0},{64,96},{96,64},{1,33},{33,1},{65,97},{97,65},{2,34}... | collective-permute-start | bytes 393224 | tf_op jit(solution)/shard_map/ppermute | solution.py:43
  139.9 18.3 %collective-permute-start.24 = (bf16[32,2048]{1,0:T(8,128)(2,1)S(1)}, bf16[32,2048]{1,0:T(8,128)(2,1)S(1)}, u32[]{:S(2)}, u32[]{:S(2)}) collective-permute-start(bf16[32,2048]{1,0:T(8,128)(2,1)S(1)} %get-tuple-element.80), channel_id=1, source_target_pairs={{0,64},{32,96},{64,32},{96,0},{1,65},{33,97},{65,33},{97,1},{2,66}... | collective-permute-start | bytes 393224 | tf_op jit(solution)/shard_map/ppermute | solution.py:43
  140.5 17.8 %collective-permute-start.25 = (bf16[32,2048]{1,0:T(8,128)(2,1)S(1)}, bf16[32,2048]{1,0:T(8,128)(2,1)S(1)}, u32[]{:S(2)}, u32[]{:S(2)}) collective-permute-start(bf16[32,2048]{1,0:T(8,128)(2,1)S(1)} %get-tuple-element.79), channel_id=1, source_target_pairs={{0,96},{32,64},{64,0},{96,32},{1,97},{33,65},{65,1},{97,33},{2,98}... | collective-permute-start | bytes 393224 | tf_op jit(solution)/shard_map/ppermute | solution.py:43
  162.4 9.5 %collective-permute-start.27 = (bf16[3,32,1024]{2,1,0:T(8,128)(2,1)S(1)}, bf16[3,32,1024]{2,1,0:T(8,128)(2,1)S(1)}, u32[]{:S(2)}, u32[]{:S(2)}) collective-permute-start(bf16[3,32,1024]{2,1,0:T(8,128)(2,1)S(1)} %get-tuple-element.82), channel_id=1, source_target_pairs={{0,64},{32,96},{64,32},{96,0},{1,65},{33,97},{65,33},{97,1},{2,66}... | collective-permute-start | bytes 589832 | tf_op jit(solution)/shard_map/ppermute | solution.py:43
  163.9 11.8 %collective-permute-start.28 = (bf16[3,32,1024]{2,1,0:T(8,128)(2,1)S(1)}, bf16[3,32,1024]{2,1,0:T(8,128)(2,1)S(1)}, u32[]{:S(2)}, u32[]{:S(2)}) collective-permute-start(bf16[3,32,1024]{2,1,0:T(8,128)(2,1)S(1)} %get-tuple-element.81), channel_id=1, source_target_pairs={{0,32},{32,0},{64,96},{96,64},{1,33},{33,1},{65,97},{97,65},{2,34}... | collective-permute-start | bytes 589832 | tf_op jit(solution)/shard_map/ppermute | solution.py:43
  166.6 9.1 %collective-permute-start.29 = (bf16[3,32,1024]{2,1,0:T(8,128)(2,1)S(1)}, bf16[3,32,1024]{2,1,0:T(8,128)(2,1)S(1)}, u32[]{:S(2)}, u32[]{:S(2)}) collective-permute-start(bf16[3,32,1024]{2,1,0:T(8,128)(2,1)S(1)} %get-tuple-element.82), channel_id=1, source_target_pairs={{0,96},{32,64},{64,0},{96,32},{1,97},{33,65},{65,1},{97,33},{2,98}... | collective-permute-start | bytes 589832 | tf_op jit(solution)/shard_map/ppermute | solution.py:43
  168.1 26.6 %collective-permute-start.40 = (bf16[256,1024]{1,0:T(8,128)(2,1)S(1)}, bf16[256,1024]{1,0:T(8,128)(2,1)S(1)}, u32[]{:S(2)}, u32[]{:S(2)}) collective-permute-start(bf16[256,1024]{1,0:T(8,128)(2,1)S(1)} %collective-permute-done.6.refs_1_), channel_id=1, source_target_pairs={{0,4},{4,8},{8,12},{12,0},{1,5},{5,9},{9,13},{13,1},{2,6},{6,10},{... | collective-permute-start | bytes 1572872 | tf_op jit(solution)/shard_map/ppermute | solution.py:34
  169.3 28.4 %collective-permute-start.41 = (bf16[256,1024]{1,0:T(8,128)(2,1)S(1)}, bf16[256,1024]{1,0:T(8,128)(2,1)S(1)}, u32[]{:S(2)}, u32[]{:S(2)}) collective-permute-start(bf16[256,1024]{1,0:T(8,128)(2,1)S(1)} %collective-permute-done.6.refs_1_), channel_id=1, source_target_pairs={{0,8},{4,12},{8,0},{12,4},{1,9},{5,13},{9,1},{13,5},{2,10},{6,14},... | collective-permute-start | bytes 1572872 | tf_op jit(solution)/shard_map/ppermute | solution.py:34
  175.8 24.5 %collective-permute-start.30 = (bf16[128,1024]{1,0:T(8,128)(2,1)S(1)}, bf16[128,1024]{1,0:T(8,128)(2,1)S(1)}, u32[]{:S(2)}, u32[]{:S(2)}) collective-permute-start(bf16[128,1024]{1,0:T(8,128)(2,1)S(1)} %maximum_bitcast_fusion.refs_1_), channel_id=1, source_target_pairs={{0,4},{4,8},{8,12},{12,0},{1,5},{5,9},{9,13},{13,1},{2,6},{6,10},{... | collective-permute-start | bytes 786440 | tf_op jit(solution)/shard_map/ppermute | solution.py:34
  177.1 28.5 %collective-permute-start.31 = (bf16[128,1024]{1,0:T(8,128)(2,1)S(1)}, bf16[128,1024]{1,0:T(8,128)(2,1)S(1)}, u32[]{:S(2)}, u32[]{:S(2)}) collective-permute-start(bf16[128,1024]{1,0:T(8,128)(2,1)S(1)} %maximum_bitcast_fusion.refs_1_), channel_id=1, source_target_pairs={{0,8},{4,12},{8,0},{12,4},{1,9},{5,13},{9,1},{13,5},{2,10},{6,14},... | collective-permute-start | bytes 786440 | tf_op jit(solution)/shard_map/ppermute | solution.py:34
  179.8 27.5 %collective-permute-start.43 = (bf16[2,128,1024]{2,1,0:T(8,128)(2,1)S(1)}, bf16[2,128,1024]{2,1,0:T(8,128)(2,1)S(1)}, u32[]{:S(2)}, u32[]{:S(2)}) collective-permute-start(bf16[2,128,1024]{2,1,0:T(8,128)(2,1)S(1)} %pad_maximum_fusion.1.refs_5_.refs_13_), channel_id=1, source_target_pairs={{0,1},{1,2},{2,3},{3,0},{4,5},{5,6},{6,7},{7,4},{8,9},{9,10},{10,1... | collective-permute-start | bytes 1572872 | tf_op jit(solution)/shard_map/ppermute | solution.py:34
  194.6 13.1 %collective-permute-start.44 = (bf16[2,128,1024]{2,1,0:T(8,128)(2,1)S(1)}, bf16[2,128,1024]{2,1,0:T(8,128)(2,1)}, u32[]{:S(2)}, u32[]{:S(2)}) collective-permute-start(bf16[2,128,1024]{2,1,0:T(8,128)(2,1)S(1)} %pad_maximum_fusion.1.refs_5_.refs_13_), channel_id=1, source_target_pairs={{0,2},{1,3},{2,0},{3,1},{4,6},{5,7},{6,4},{7,5},{8,10},{9,11},{10,... | collective-permute-start | bytes 1572872 | tf_op jit(solution)/shard_map/ppermute | solution.py:34
  197.7 14.6 %collective-permute-start.45 = (bf16[2,128,1024]{2,1,0:T(8,128)(2,1)S(1)}, bf16[2,128,1024]{2,1,0:T(8,128)(2,1)}, u32[]{:S(2)}, u32[]{:S(2)}) collective-permute-start(bf16[2,128,1024]{2,1,0:T(8,128)(2,1)S(1)} %pad_maximum_fusion.1.refs_5_.refs_13_), channel_id=1, source_target_pairs={{0,3},{1,0},{2,1},{3,2},{4,7},{5,4},{6,5},{7,6},{8,11},{9,8},{10,9... | collective-permute-start | bytes 1572872 | tf_op jit(solution)/shard_map/ppermute | solution.py:34
  207.8 16.9 %collective-permute-start.42 = (bf16[256,1024]{1,0:T(8,128)(2,1)S(1)}, bf16[256,1024]{1,0:T(8,128)(2,1)S(1)}, u32[]{:S(2)}, u32[]{:S(2)}) collective-permute-start(bf16[256,1024]{1,0:T(8,128)(2,1)S(1)} %collective-permute-done.6.refs_1_), channel_id=1, source_target_pairs={{0,12},{4,0},{8,4},{12,8},{1,13},{5,1},{9,5},{13,9},{2,14},{6,2},{... | collective-permute-start | bytes 1572872 | tf_op jit(solution)/shard_map/ppermute | solution.py:34
  212.4 21.3 %collective-permute-start.46 = (bf16[2,128,1024]{2,1,0:T(8,128)(2,1)S(1)}, bf16[2,128,1024]{2,1,0:T(8,128)(2,1)}, u32[]{:S(2)}, u32[]{:S(2)}) collective-permute-start(bf16[2,128,1024]{2,1,0:T(8,128)(2,1)S(1)} %pad_maximum_fusion.1.refs_5_.refs_13_), channel_id=1, source_target_pairs={{0,16},{16,0},{1,17},{17,1},{2,18},{18,2},{3,19},{19,3},{4,20},{20... | collective-permute-start | bytes 1572872 | tf_op jit(solution)/shard_map/ppermute | solution.py:34
  212.4 22.2 %collective-permute-start.47 = (bf16[2,128,1024]{2,1,0:T(8,128)(2,1)S(1)}, bf16[2,128,1024]{2,1,0:T(8,128)(2,1)}, u32[]{:S(2)}, u32[]{:S(2)}) collective-permute-start(bf16[2,128,1024]{2,1,0:T(8,128)(2,1)S(1)} %collective-permute-done.43.refs_6_.refs_14_), channel_id=1, source_target_pairs={{0,16},{16,0},{1,17},{17,1},{2,18},{18,2},{3,19},{19,3},{4,20},{20... | collective-permute-start | bytes 1572872 | tf_op jit(solution)/shard_map/ppermute | solution.py:34
  212.9 22.5 %collective-permute-start.48 = (bf16[2,128,1024]{2,1,0:T(8,128)(2,1)}, bf16[2,128,1024]{2,1,0:T(8,128)(2,1)}, u32[]{:S(2)}, u32[]{:S(2)}) collective-permute-start(bf16[2,128,1024]{2,1,0:T(8,128)(2,1)} %collective-permute-done.44.refs_7_.refs_15_), channel_id=1, source_target_pairs={{0,16},{16,0},{1,17},{17,1},{2,18},{18,2},{3,19},{19,3},{4,20},{20... | collective-permute-start | bytes 1572872 | tf_op jit(solution)/shard_map/ppermute | solution.py:34
  214.3 21.1 %collective-permute-start.49 = (bf16[2,128,1024]{2,1,0:T(8,128)(2,1)}, bf16[2,128,1024]{2,1,0:T(8,128)(2,1)}, u32[]{:S(2)}, u32[]{:S(2)}) collective-permute-start(bf16[2,128,1024]{2,1,0:T(8,128)(2,1)} %collective-permute-done.45.refs_8_.refs_16_), channel_id=1, source_target_pairs={{0,16},{16,0},{1,17},{17,1},{2,18},{18,2},{3,19},{19,3},{4,20},{20... | collective-permute-start | bytes 1572872 | tf_op jit(solution)/shard_map/ppermute | solution.py:34
  225.5 26.6 %collective-permute-start.37 = (bf16[256,1024]{1,0:T(8,128)(2,1)}, bf16[256,1024]{1,0:T(8,128)(2,1)S(1)}, u32[]{:S(2)}, u32[]{:S(2)}) collective-permute-start(bf16[256,1024]{1,0:T(8,128)(2,1)} %get-tuple-element.42), channel_id=1, source_target_pairs={{0,3},{1,0},{2,1},{3,2},{4,7},{5,4},{6,5},{7,6},{8,11},{9,8},{10,9... | collective-permute-start | bytes 1572872 | tf_op jit(solution)/shard_map/ppermute | solution.py:34
  233.7 19.2 %collective-permute-start.38 = (bf16[256,1024]{1,0:T(8,128)(2,1)}, bf16[256,1024]{1,0:T(8,128)(2,1)S(1)}, u32[]{:S(2)}, u32[]{:S(2)}) collective-permute-start(bf16[256,1024]{1,0:T(8,128)(2,1)} %get-tuple-element.43), channel_id=1, source_target_pairs={{0,2},{1,3},{2,0},{3,1},{4,6},{5,7},{6,4},{7,5},{8,10},{9,11},{10,... | collective-permute-start | bytes 1572872 | tf_op jit(solution)/shard_map/ppermute | solution.py:34
  234.6 25.4 %collective-permute-start.39 = (bf16[256,1024]{1,0:T(8,128)(2,1)S(1)}, bf16[256,1024]{1,0:T(8,128)(2,1)}, u32[]{:S(2)}, u32[]{:S(2)}) collective-permute-start(bf16[256,1024]{1,0:T(8,128)(2,1)S(1)} %copy-done.17), channel_id=1, source_target_pairs={{0,1},{1,2},{2,3},{3,0},{4,5},{5,6},{6,7},{7,4},{8,9},{9,10},{10,1... | collective-permute-start | bytes 1572872 | tf_op jit(solution)/shard_map/ppermute | solution.py:34
  246.4 24.2 %collective-permute-start.50 = (bf16[256,1024]{1,0:T(8,128)(2,1)}, bf16[256,1024]{1,0:T(8,128)(2,1)S(1)}, u32[]{:S(2)}, u32[]{:S(2)}) collective-permute-start(bf16[256,1024]{1,0:T(8,128)(2,1)} %get-tuple-element.46), channel_id=1, source_target_pairs={{0,12},{4,0},{8,4},{12,8},{1,13},{5,1},{9,5},{13,9},{2,14},{6,2},{... | collective-permute-start | bytes 1572872 | tf_op jit(solution)/shard_map/ppermute | solution.py:34
  248.9 21.7 %collective-permute-start.51 = (bf16[256,1024]{1,0:T(8,128)(2,1)}, bf16[256,1024]{1,0:T(8,128)(2,1)S(1)}, u32[]{:S(2)}, u32[]{:S(2)}) collective-permute-start(bf16[256,1024]{1,0:T(8,128)(2,1)} %get-tuple-element.47), channel_id=1, source_target_pairs={{0,8},{4,12},{8,0},{12,4},{1,9},{5,13},{9,1},{13,5},{2,10},{6,14},... | collective-permute-start | bytes 1572872 | tf_op jit(solution)/shard_map/ppermute | solution.py:34
  252.1 22.0 %collective-permute-start.52 = (bf16[256,1024]{1,0:T(8,128)(2,1)}, bf16[256,1024]{1,0:T(8,128)(2,1)S(1)}, u32[]{:S(2)}, u32[]{:S(2)}) collective-permute-start(bf16[256,1024]{1,0:T(8,128)(2,1)} %get-tuple-element.48), channel_id=1, source_target_pairs={{0,4},{4,8},{8,12},{12,0},{1,5},{5,9},{9,13},{13,1},{2,6},{6,10},{... | collective-permute-start | bytes 1572872 | tf_op jit(solution)/shard_map/ppermute | solution.py:34
  (33 other events, 629.2 us)
Sparse Core Ops, SparseCore 0:
  111.8 46.3 all-gather.1
where the time goes:
time: 313 us; the launch traced here: 311 us
  waiting for transfers between devices  116 us (37%)
  starting transfers between devices  79.6 us (25%)
  Pallas kernels  43.2 us (14%)
  blocking collectives  29 us (9%)
  between operations  17.6 us (6%)
  other arithmetic  13 us (4%)
  local copies, waits for them, and re-layouts  9.2 us (3%)
    ppermute x46, waiting for transfers between devices, shift(): lax.ppermute(value, axis, [(i, (i + by) % count) for i in range(count)])  85.6 us
    ppermute x46, starting transfers between devices, shift(): lax.ppermute(value, axis, [(i, (i + by) % count) for i in range(count)])  59.2 us
    all_to_all x3, blocking collectives, a2a(): return lax.all_to_all(value, axes, 0, 0, tiled=True)  29 us
    all_gather x1, waiting for transfers between devices, on_device(): m_near = lax.all_gather(m, ('z', 'y'), axis=0, tiled=True)  15.1 us
    pallas_call x2, Pallas kernels, project(): pl.pallas_call(project_kernel, out_shape=[jax.ShapeDtypeStruct((2 * tok,...  12.7 us
    ppermute x1, waiting for transfers between devices, on_device(): w_3 = lax.ppermute(w_u, 'p', [(0, 1), (1, 0)])  11.9 us
    pallas_call x1, Pallas kernels, grad_u_call(): pl.pallas_call(grad_u_kernel, out_shape=[jax.ShapeDtypeStruct((own, hidde...  11 us
    ppermute x6, starting transfers between devices, shift_x(): return lax.ppermute(value, ('p', 'h'), pairs)  10.4 us
  transfers between devices with their start and end apart: 55, of which 23 were waited for; matrix products, arithmetic and copies ran while one was open for 3% of the time, Pallas kernels for 14%

commit v1 on v0

--- a/solution.py
+++ b/solution.py
@@ -138,8 +138,11 @@
 def turn_kernel(*refs):
     blocks, out = refs[:4], refs[4]
     tok = blocks[0].shape[0]
-    for k in range(4):
-        out[:, k * tok : (k + 1) * tok] = blocks[k][...].T
+    half = tok // 2
+    for rc in range(2):
+        for k in range(4):
+            to = (rc * 4 + k) * half
+            out[:, to : to + half] = blocks[k][rc * half : (rc + 1) * half, :].T
 
 
 def turn(blocks):
@@ -156,25 +159,20 @@
     )(*blocks)
 
 
-def interleave(near, far):
-    return jnp.concatenate([piece for pair in zip(near, far) for piece in pair])
-
-
 def split_rows(outs, total):
     own = outs[0].shape[0]
     for j in range(4):
         outs[j][...] = total[j * own : (j + 1) * own].astype(outs[j].dtype)
 
 
-def grad_v_kernel(*refs):
-    turned, near, far, outs = refs[0], refs[1:5], refs[5:9], refs[9:]
-    right = interleave([a[...] for a in near], [a[...] for a in far])
-    split_rows(outs, dot(turned[...], right))
-
-
-def grad_v_call(turned, near, far):
+def grad_v_kernel(turned, *refs):
+    right = jnp.concatenate([piece[...] for piece in refs[:8]])
+    split_rows(refs[8:], dot(turned[...], right))
+
+
+def grad_v_call(turned, pieces):
     wide, tok = turned.shape
-    half, hidden = near[0].shape
+    half, hidden = pieces[0].shape
     own, tile = wide // 4, hidden // 4
     return pl.pallas_call(
         grad_v_kernel,
@@ -187,24 +185,26 @@
             flops=2 * tok * wide * hidden, bytes_accessed=8 * tok * wide, transcendentals=0
         ),
         name="grad_v",
-    )(turned, *near, *far)
-
-
-def grad_u_kernel(*refs):
-    turned, w_refs, q_refs, p_refs = refs[0], refs[1:5], refs[5:13], refs[13:21]
-    outs, fold, factor, left = refs[21:25], refs[25], refs[26], refs[27]
+    )(turned, *pieces)
+
+
+def grad_u_kernel(at_ref, turned, *refs):
+    w_refs, acts, slopes, outs = refs[:4], refs[4:12], refs[12:20], refs[20:24]
+    fold, factor, right, left = refs[24:]
     s = pl.program_id(0)
     own = w_refs[0].shape[0]
-    half = q_refs[0].shape[1]
+    half = acts[0].shape[0]
     tile = turned.shape[1]
+    first = at_ref[0] == 0
 
     @pl.when(s == 0)
     def _():
         for j in range(4):
             fold[j * own : (j + 1) * own, :] = w_refs[j][...]
-            for i in range(2):
-                to = (2 * j + i) * half
-                factor[to : to + half, :] = q_refs[4 * i + j][0]
+        for i in range(8):
+            act, slope = acts[i][...], slopes[i][...]
+            right[i * half : (i + 1) * half, :] = jnp.where(first, act, slope)
+            factor[i * half : (i + 1) * half, :] = jnp.where(first, slope, act)
 
     @pl.when(s < 4)
     def _():
@@ -214,13 +214,14 @@
 
     @pl.when(s >= 4)
     def _():
-        right = interleave([a[0] for a in p_refs[:4]], [a[0] for a in p_refs[4:]])
-        split_rows(outs, dot(left[...], right))
-
-
-def grad_u_call(turned, near, far, weights):
+        width = outs[0].shape[1]
+        at = pl.ds(pl.multiple_of((s - 4) * width, width), width)
+        split_rows(outs, dot(left[...], right[:, at]))
+
+
+def grad_u_call(at, turned, act, slope, weights):
     wide, tok = turned.shape
-    half, hidden = near[0].shape[1:]
+    hidden = act[0].shape[1]
     own, tile = wide // 4, hidden // 4
 
     def late(s):
@@ -230,13 +231,14 @@
         grad_u_kernel,
         out_shape=[jax.ShapeDtypeStruct((own, hidden), t) for t in (F32, BF, BF, BF)],
         grid=(8,),
-        in_specs=[pl.BlockSpec((wide, tok // 4), lambda s: (0, jnp.minimum(s, 3)))]
+        in_specs=[pl.BlockSpec(memory_space=pltpu.SMEM)]
+        + [pl.BlockSpec((wide, tok // 4), lambda s: (0, jnp.minimum(s, 3)))]
         + [pl.BlockSpec((own, hidden), lambda s: (0, 0))] * 4
-        + [pl.BlockSpec((1, half, hidden), lambda s: (1, 0, 0))] * 8
-        + [pl.BlockSpec((1, half, tile), lambda s: (0, 0, late(s)))] * 8,
+        + [pl.BlockSpec((tok // 8, hidden), lambda s: (0, 0))] * 16,
         out_specs=[pl.BlockSpec((own, tile), lambda s: (0, late(s)))] * 4,
         scratch_shapes=[
             pltpu.VMEM((wide, hidden), BF),
+            pltpu.VMEM((tok, hidden), BF),
             pltpu.VMEM((tok, hidden), BF),
             pltpu.VMEM((wide, tok), BF),
         ],
@@ -244,7 +246,7 @@
             flops=4 * tok * wide * hidden, bytes_accessed=16 * tok * wide, transcendentals=0
         ),
         name="grad_u",
-    )(turned, *weights, *near, *far, *near, *far)
+    )(at, turned, *weights, *act, *slope)
 
 
 def gather(value, axis):
@@ -316,6 +318,9 @@
     pre1, up1 = layer1[:, :hidden], layer1[:, hidden:]
     side = hidden // 2
     act0 = silu_bf(pre0)
+    act_near = jnp.concatenate([act0] + [shift_x(act0, k) for k in (1, 2, 3)])
+    act_near = gather(act_near, "y")
+    act_near += [shift(a, "c", 1) for a in act_near]
     low, high = act0[:, :side], act0[:, side:]
     near, far = jnp.where(c == 0, low, high), jnp.where(c == 0, high, low)
     pre1 = pre1 + dot(near, m_near) + dot(far, m_far)
@@ -325,19 +330,18 @@
     low, high = jnp.where(c == 0, near, far), jnp.where(c == 0, far, near)
     slope0 = slope_bf(up0 + jnp.concatenate([low, high], 1), pre0)
 
-    to_first = jnp.stack([slope0, act0, slope1])
-    to_last = jnp.stack([act1, slope1, act0])
-    same = jnp.where(first, to_first, to_last)
-    other = jnp.where(first, to_last, to_first)
+    same = jnp.stack([jnp.where(first, slope0, act1), slope1])
+    other = jnp.stack([jnp.where(first, act1, slope0), slope1])
     got = [same, shift_x(other, 1), shift_x(same, 2), shift_x(other, 3)]
-    rpq = jnp.concatenate(got, 1)
-    r_near = gather(rpq[0], "z")
-    pq_near = gather(rpq[1:], "y")
-    r_far = [shift(a, "c", 1) for a in r_near]
-    pq_far = [shift(a, "c", 1) for a in pq_near]
-
-    g_v = sum_back(grad_v_call(turn(vs), r_near, r_far), "y")
-    g_u = sum_back(grad_u_call(turn(us), pq_near, pq_far, w_3s), "z")
+    r_near = jnp.concatenate([g[0] for g in got])
+    s_near = jnp.concatenate([g[1] for g in got])
+    r_near = gather(r_near, "z")
+    s_near = gather(s_near, "y")
+    r_near += [shift(a, "c", 1) for a in r_near]
+    s_near += [shift(a, "c", 1) for a in s_near]
+
+    g_v = sum_back(grad_v_call(turn(vs), r_near), "y")
+    g_u = sum_back(grad_u_call(at, turn(us), act_near, s_near, w_3s), "z")
 
     squares = jnp.sum(g_u * g_u) + jnp.sum(g_v * g_v)
     for axes, count in ((("z", "y"), 16), (("p", "h", "c"), 8)):

time: 313 us -> 315 us (level)
  starting transfers between devices: 79.6 us -> 95.7 us
  waiting for transfers between devices: 116 us -> 104 us
  blocking collectives: 29 us -> 32.8 us
  other arithmetic: 13 us -> 9.59 us
    ppermute x46 -> x53, starting transfers between devices: 59.2 us -> 72.9 us  [shift(): lax.ppermute(value, axis, [(i, (i + by) % count) for i in range(count)])]
    ppermute x46 -> x53, waiting for transfers between devices: 85.6 us -> 73.8 us  [shift(): lax.ppermute(value, axis, [(i, (i + by) % count) for i in range(count)])]
    all_to_all x3, blocking collectives: 29 us -> 32.8 us  [a2a(): return lax.all_to_all(value, axes, 0, 0, tiled=True)]
    unnamed x54 -> x72, local copies, waits for them, and re-layouts: 6.83 us -> 4.33 us
    ppermute x6 -> x9, starting transfers between devices: 10.4 us -> 12.8 us  [shift_x(): return lax.ppermute(value, ('p', 'h'), pairs)]
  transfers between devices with their start and end apart: 55 -> 65, of which waited for: 23 -> 22; matrix products, arithmetic and copies ran while one was open for 3% -> 3% of each run, Pallas kernels for 14% -> 14%
where the time goes in v1:
time: 315 us; the launch traced here: 314 us
  waiting for transfers between devices  104 us (33%)
  starting transfers between devices  95.7 us (30%)
  Pallas kernels  43.4 us (14%)
  blocking collectives  32.8 us (10%)
  between operations  17.8 us (6%)
  other arithmetic  9.59 us (3%)
  local copies, waits for them, and re-layouts  7.39 us (2%)
    ppermute x53, waiting for transfers between devices, shift(): lax.ppermute(value, axis, [(i, (i + by) % count) for i in range(count)])  73.8 us
    ppermute x53, starting transfers between devices, shift(): lax.ppermute(value, axis, [(i, (i + by) % count) for i in range(count)])  72.9 us
    all_to_all x3, blocking collectives, a2a(): return lax.all_to_all(value, axes, 0, 0, tiled=True)  32.8 us
    all_gather x1, waiting for transfers between devices, on_device(): m_near = lax.all_gather(m, ('z', 'y'), axis=0, tiled=True)  14.3 us
    ppermute x9, starting transfers between devices, shift_x(): return lax.ppermute(value, ('p', 'h'), pairs)  12.8 us
    pallas_call x2, Pallas kernels, project(): pl.pallas_call(project_kernel, out_shape=[jax.ShapeDtypeStruct((2 * tok,...  12.8 us
    ppermute x1, waiting for transfers between devices, on_device(): w_3 = lax.ppermute(w_u, 'p', [(0, 1), (1, 0)])  11.9 us
    pallas_call x1, Pallas kernels, grad_u_call(): pl.pallas_call(grad_u_kernel, out_shape=[jax.ShapeDtypeStruct((own, hidde...  11.1 us
  transfers between devices with their start and end apart: 65, of which 22 were waited for; matrix products, arithmetic and copies ran while one was open for 3% of the time, Pallas kernels for 14%

profile of v1, /device:TPU:0, one launch (start us, length us, event | category | flops | bytes accessed | tf_op | source)
XLA Modules:
  0.0 313.8 jit_solution(15038414043770042671)
XLA Ops:
  11.3 11.9 %collective-permute-done.6.refs_0_ = bf16[256,1024]{1,0:T(8,128)(2,1)S(1)} collective-permute-done((bf16[256,1024]{1,0:T(8,128)(2,1)S(1)}, bf16[256,1024]{1,0:T(8,128)(2,1)S(1)}, u32[]{:S(2)}, u32[]{:S(2)}) %collective-permute-start.6) | collective-permute-done | bytes 524320 | tf_op jit(solution)/shard_map/ppermute | solution.py:278
  23.9 5.0 %cut.1 = (bf16[256,1024]{1,0:T(8,128)(2,1)}, bf16[256,1024]{1,0:T(8,128)(2,1)}, bf16[256,1024]{1,0:T(8,128)(2,1)}, bf16[256,1024]{1,0:T(8,128)(2,1)}, bf16[256,1...) custom-call(s32[5]{0:T(128)} %stack.39.at_ref, ...), custom_call_target="tpu_custom_call" | custom-call | tf_op jit(solution)/shard_map/cut/pallas_call | solution.py:90
  28.9 1.8 collective-permute-start.3
  30.7 2.9 collective-permute-start.4
  37.4 8.3 %all-to-all-start = ((bf16[32,8,1024]{2,1,0:T(8,128)(2,1)}), bf16[32,8,1024]{2,1,0:T(8,128)(2,1)S(1)}, u32[]{:S(2)}, u32[]{:S(2)}) async-start(bf16[32,8,1024]{2,1,0:T(8,128)(2,1)} %bitcast.12), calls=%async_computation | async-start | bytes 1048576 | tf_op jit(solution)/shard_map/all_to_all | solution.py:29
  45.7 3.4 %collective-permute-start.10 = (bf16[256,1024]{1,0:T(8,128)(2,1)S(1)}, bf16[256,1024]{1,0:T(8,128)(2,1)}, u32[]{:S(2)}, u32[]{:S(2)}) collective-permute-start(bf16[256,1024]{1,0:T(8,128)(2,1)S(1)} %get-tuple-element.34.refs_4_), channel_id=1, source_target_pairs={{0,8},{4,12},{8,0},{12,4},{1,9},{5,13},{9,1},{13,5},{2,10},{6,14},... | collective-permute-start | bytes 1572872 | tf_op jit(solution)/shard_map/ppermute | solution.py:34
  51.2 9.6 %collective-permute-done.4.refs_2_ = bf16[256,1024]{1,0:T(8,128)(2,1)} collective-permute-done((bf16[256,1024]{1,0:T(8,128)(2,1)}, bf16[256,1024]{1,0:T(8,128)(2,1)}, u32[]{:S(2)}, u32[]{:S(2)}) %collective-permute-start.4) | collective-permute-done | bytes 524320 | tf_op jit(solution)/shard_map/ppermute | solution.py:34
  60.8 1.9 collective-permute-start
  62.8 3.6 %collective-permute-start.1 = (bf16[256,1024]{1,0:T(8,128)(2,1)}, bf16[256,1024]{1,0:T(8,128)(2,1)S(1)}, u32[]{:S(2)}, u32[]{:S(2)}) collective-permute-start(bf16[256,1024]{1,0:T(8,128)(2,1)} %get-tuple-element.28), channel_id=1, source_target_pairs={{0,8},{4,12},{8,0},{12,4},{1,9},{5,13},{9,1},{13,5},{2,10},{6,14},... | collective-permute-start | bytes 1572872 | tf_op jit(solution)/shard_map/ppermute | solution.py:34
  66.4 9.6 %all_to_all.21 = bf16[4,8,1024]{2,1,0:T(8,128)(2,1)} all-to-all(bf16[4,8,1024]{2,1,0:T(8,128)(2,1)S(1)} %broadcast_in_dim.18), channel_id=1, replica_groups=mesh['p'=2,'h'=2,'c'=2,'z'=4,'y'=4] {'p','h'}, dimensions={0} | all-to-all | bytes 131072 | tf_op jit(solution)/shard_map/all_to_all | solution.py:29
  79.0 2.4 collective-permute-start.17
  81.4 1.9 collective-permute-start.18
  83.3 6.7 %collective-permute-done.refs_1_ = bf16[256,1024]{1,0:T(8,128)(2,1)S(1)} collective-permute-done((bf16[256,1024]{1,0:T(8,128)(2,1)}, bf16[256,1024]{1,0:T(8,128)(2,1)S(1)}, u32[]{:S(2)}, u32[]{:S(2)}) %collective-permute-start) | collective-permute-done | bytes 524320 | tf_op jit(solution)/shard_map/ppermute | solution.py:34
  90.6 6.3 %shard_map.68 = (bf16[512,1024]{1,0:T(8,128)(2,1)}, f32[512,1024]{1,0:T(8,128)}) custom-call(bf16[256,1024]{1,0:T(8,128)(2,1)} %get-tuple-element.30.refs_0_, bf16[256,1024]{1,0:T(8,128)(2,1)} %copy-done.9, bf16[256,1024]{1,0:T(8,128)(2,1)} %collective-permute-done.4.refs_2_, bf16[256,1024]{1,0:T(8,128)(2,1)} %collective-permute-done.5.refs_3_, ...), custom_call_target="tpu_custom_call" | custom-call | flops 2147483648 | bytes 4194304 | tf_op jit(solution)/shard_map/pallas_call | solution.py:121
  96.9 2.7 collective-permute-done.1.refs_2_
  99.6 4.6 %collective-permute-done.2.refs_3_ = bf16[256,1024]{1,0:T(8,128)(2,1)S(1)} collective-permute-done((bf16[256,1024]{1,0:T(8,128)(2,1)}, bf16[256,1024]{1,0:T(8,128)(2,1)S(1)}, u32[]{:S(2)}, u32[]{:S(2)}) %collective-permute-start.2) | collective-permute-done | bytes 524320 | tf_op jit(solution)/shard_map/ppermute | solution.py:34
  105.1 6.5 %shard_map.69 = (bf16[512,1024]{1,0:T(8,128)(2,1)}, f32[512,1024]{1,0:T(8,128)}) custom-call(bf16[256,1024]{1,0:T(8,128)(2,1)} %get-tuple-element.26.refs_0_, bf16[256,1024]{1,0:T(8,128)(2,1)} %copy-done.10, bf16[256,1024]{1,0:T(8,128)(2,1)} %copy-done.11, bf16[256,1024]{1,0:T(8,128)(2,1)} %copy-done.12, bf16[256,1024]{1,0:T(8,128)(2,1)} %copy-done.8, ...), custom_call_target="tpu_custom_call" | custom-call | flops 2147483648 | bytes 4194304 | tf_op jit(solution)/shard_map/pallas_call | solution.py:121
  113.5 2.9 collective-permute-start.13
  118.4 2.1 collective-permute-start.20
  121.3 7.7 %collective-permute-done.13 = bf16[128,1024]{1,0:T(8,128)(2,1)S(1)} collective-permute-done((bf16[128,1024]{1,0:T(8,128)(2,1)S(1)}, bf16[128,1024]{1,0:T(8,128)(2,1)S(1)}, u32[]{:S(2)}, u32[]{:S(2)}) %collective-permute-start.13) | collective-permute-done | bytes 262176 | tf_op jit(solution)/shard_map/ppermute | solution.py:34
  130.0 2.8 collective-permute-done.15
  133.0 5.1 %collective-permute-done.22 = bf16[128,1024]{1,0:T(8,128)(2,1)S(1)} collective-permute-done((bf16[128,1024]{1,0:T(8,128)(2,1)S(1)}, bf16[128,1024]{1,0:T(8,128)(2,1)S(1)}, u32[]{:S(2)}, u32[]{:S(2)}) %collective-permute-start.22) | collective-permute-done | bytes 262176 | tf_op jit(solution)/shard_map/ppermute | solution.py:34
  140.4 2.6 collective-permute-start.25
  143.1 14.3 %all-gather.2.cloned.1.call-done = bf16[512,1024]{1,0:T(8,128)(2,1)} async-done(((bf16[32,1024]{1,0:T(8,128)(2,1)}), bf16[512,1024]{1,0:T(8,128)(2,1)}) %all-gather.2.cloned.1.call-update) | async-done | bytes 1048592 | tf_op jit(solution)/shard_map/all_gather | solution.py:297
  160.3 2.7 collective-permute-start.44
  166.8 2.7 collective-permute-start.41
  169.8 2.1 collective-permute-start.47
  173.2 2.2 collective-permute-start.42
  175.4 3.5 %collective-permute-done.28 = bf16[2,32,1024]{2,1,0:T(8,128)(2,1)S(1)} collective-permute-done((bf16[2,32,1024]{2,1,0:T(8,128)(2,1)S(1)}, bf16[2,32,1024]{2,1,0:T(8,128)(2,1)S(1)}, u32[]{:S(2)}, u32[]{:S(2)}) %collective-permute-start.28) | collective-permute-done | bytes 131104 | tf_op jit(solution)/shard_map/ppermute | solution.py:43
  178.8 2.1 collective-permute-start.29
  181.0 4.1 %collective-permute-done.41.refs_2_ = bf16[256,1024]{1,0:T(8,128)(2,1)S(1)} collective-permute-done((bf16[256,1024]{1,0:T(8,128)(2,1)S(1)}, bf16[256,1024]{1,0:T(8,128)(2,1)S(1)}, u32[]{:S(2)}, u32[]{:S(2)}) %collective-permute-start.41) | collective-permute-done | bytes 524320 | tf_op jit(solution)/shard_map/ppermute | solution.py:34
  185.0 4.7 %collective-permute-start.48 = (bf16[128,1024]{1,0:T(8,128)(2,1)S(1)}, bf16[128,1024]{1,0:T(8,128)(2,1)S(1)}, u32[]{:S(2)}, u32[]{:S(2)}) collective-permute-start(bf16[128,1024]{1,0:T(8,128)(2,1)S(1)} %pad_maximum_fusion.2.refs_4_), channel_id=1, source_target_pairs={{0,3},{1,0},{2,1},{3,2},{4,7},{5,4},{6,5},{7,6},{8,11},{9,8},{10,9... | collective-permute-start | bytes 786440 | tf_op jit(solution)/shard_map/ppermute | solution.py:34
  196.1 3.1 collective-permute-start.32
  201.0 7.1 %collective-permute-start.54 = (bf16[128,1024]{1,0:T(8,128)(2,1)S(1)}, bf16[128,1024]{1,0:T(8,128)(2,1)}, u32[]{:S(2)}, u32[]{:S(2)}) collective-permute-start(bf16[128,1024]{1,0:T(8,128)(2,1)S(1)} %pad_maximum_fusion.3.refs_12_), channel_id=1, source_target_pairs={{0,2},{1,3},{2,0},{3,1},{4,6},{5,7},{6,4},{7,5},{8,10},{9,11},{10,... | collective-permute-start | bytes 786440 | tf_op jit(solution)/shard_map/ppermute | solution.py:34
  208.1 6.0 %collective-permute-start.55 = (bf16[128,1024]{1,0:T(8,128)(2,1)S(1)}, bf16[128,1024]{1,0:T(8,128)(2,1)}, u32[]{:S(2)}, u32[]{:S(2)}) collective-permute-start(bf16[128,1024]{1,0:T(8,128)(2,1)S(1)} %pad_maximum_fusion.3.refs_12_), channel_id=1, source_target_pairs={{0,3},{1,0},{2,1},{3,2},{4,7},{5,4},{6,5},{7,6},{8,11},{9,8},{10,9... | collective-permute-start | bytes 786440 | tf_op jit(solution)/shard_map/ppermute | solution.py:34
  215.0 2.7 collective-permute-done.54.refs_14_
  217.8 4.2 %shard_map.67.turned = bf16[1024,1024]{1,0:T(8,128)(2,1)} custom-call(bf16[256,1024]{1,0:T(8,128)(2,1)} %get-tuple-element.26.refs_0_, bf16[256,1024]{1,0:T(8,128)(2,1)} %copy-done.10, bf16[256,1024]{1,0:T(8,128)(2,1)} %copy-done.11, bf16[256,1024]{1,0:T(8,128)(2,1)} %copy-done.12), custom_call_target="tpu_custom_call" | custom-call | flops 536870912 | bytes 4194304 | tf_op jit(solution)/shard_map/pallas_call | solution.py:150
  223.3 6.1 %grad_v.1 = (f32[256,1024]{1,0:T(8,128)}, bf16[256,1024]{1,0:T(8,128)(2,1)}, bf16[256,1024]{1,0:T(8,128)(2,1)}, bf16[256,1024]{1,0:T(8,128)(2,1)}) custom-call(bf16[1024,1024]{1,0:T(8,128)(2,1)} %shard_map.67.turned, bf16[128,1024]{1,0:T(8,128)(2,1)} %copy-done.15, bf16[128,1024]{1,0:T(8,128)(2,1)} %copy-done.28, bf16[128,1024]{1,0:T(8,128)(2,1)} %copy-done.29, ...), custom_call_target="tpu_custom_call" | custom-call | flops 2147483648 | bytes 8388608 | tf_op jit(solution)/shard_map/grad_v/pallas_call | solution.py:177
  230.1 2.1 collective-permute-start.37
  232.2 4.2 %shard_map.70.turned = bf16[1024,1024]{1,0:T(8,128)(2,1)} custom-call(bf16[256,1024]{1,0:T(8,128)(2,1)} %get-tuple-element.30.refs_0_, bf16[256,1024]{1,0:T(8,128)(2,1)} %copy-done.9, bf16[256,1024]{1,0:T(8,128)(2,1)} %collective-permute-done.4.refs_2_, bf16[256,1024]{1,0:T(8,128)(2,1)} %collective-permute-done.5.refs_3_), custom_call_target="tpu_custom_call" | custom-call | flops 536870912 | bytes 4194304 | tf_op jit(solution)/shard_map/pallas_call | solution.py:150
  237.5 11.1 %grad_u.1 = (f32[256,1024]{1,0:T(8,128)}, bf16[256,1024]{1,0:T(8,128)(2,1)}, bf16[256,1024]{1,0:T(8,128)(2,1)}, bf16[256,1024]{1,0:T(8,128)(2,1)}) custom-call(s32[5]{0:T(128)} %stack.39.at_ref, bf16[1024,1024]{1,0:T(8,128)(2,1)} %shard_map.70.turned, bf16[256,1024]{1,0:T(8,128)(2,1)} %copy-done.2, bf16[256,1024]{1,0:T(8,128)(2,1)} %copy-done.16, ...), custom_call_target="tpu_custom_call" | custom-call | flops 4294967296 | bytes 16777216 | tf_op jit(solution)/shard_map/grad_u/pallas_call | solution.py:230
  249.0 2.5 collective-permute-start.61
  251.5 3.7 %collective-permute-done.37 = bf16[256,1024]{1,0:T(8,128)(2,1)S(1)} collective-permute-done((bf16[256,1024]{1,0:T(8,128)(2,1)}, bf16[256,1024]{1,0:T(8,128)(2,1)S(1)}, u32[]{:S(2)}, u32[]{:S(2)}) %collective-permute-start.37) | collective-permute-done | bytes 524320 | tf_op jit(solution)/shard_map/ppermute | solution.py:34
  255.2 7.6 %collective-permute-done.39 = bf16[256,1024]{1,0:T(8,128)(2,1)} collective-permute-done((bf16[256,1024]{1,0:T(8,128)(2,1)S(1)}, bf16[256,1024]{1,0:T(8,128)(2,1)}, u32[]{:S(2)}, u32[]{:S(2)}) %collective-permute-start.39) | collective-permute-done | bytes 524320 | tf_op jit(solution)/shard_map/ppermute | solution.py:34
  262.8 2.0 multiply_reduce_fusion
  265.5 9.8 %collective-permute-done.62 = bf16[256,1024]{1,0:T(8,128)(2,1)S(1)} collective-permute-done((bf16[256,1024]{1,0:T(8,128)(2,1)}, bf16[256,1024]{1,0:T(8,128)(2,1)S(1)}, u32[]{:S(2)}, u32[]{:S(2)}) %collective-permute-start.62) | collective-permute-done | bytes 524320 | tf_op jit(solution)/shard_map/ppermute | solution.py:34
  277.6 13.7 %all_to_all.22 = f32[16,8,128]{2,1,0:T(8,128)S(1)} all-to-all(f32[16,8,128]{2,1,0:T(8,128)S(1)} %broadcast_in_dim.19), channel_id=1, replica_groups=mesh['p'=2,'h'=2,'c'=2,'z'=4,'y'=4] {'z','y'}, dimensions={0} | all-to-all | bytes 131072 | tf_op jit(solution)/shard_map/all_to_all | solution.py:29
  292.5 9.4 %all_to_all.23 = f32[8,8,128]{2,1,0:T(8,128)S(1)} all-to-all(f32[8,8,128]{2,1,0:T(8,128)S(1)} %broadcast_in_dim.20), channel_id=1, replica_groups=mesh['p'=2,'h'=2,'c'=2,'z'=4,'y'=4] {'p','h','c'}, dimensions={0} | all-to-all | bytes 65536 | tf_op jit(solution)/shard_map/all_to_all | solution.py:29
  (202 shorter events, 50.0 us)
Async XLA Ops:
  9.6 13.6 %collective-permute-start.6 = (bf16[256,1024]{1,0:T(8,128)(2,1)S(1)}, bf16[256,1024]{1,0:T(8,128)(2,1)S(1)}, u32[]{:S(2)}, u32[]{:S(2)}) collective-permute-start(bf16[256,1024]{1,0:T(8,128)(2,1)S(1)} %get-tuple-element.34.refs_4_), channel_id=1, source_target_pairs={{0,64},{64,0},{1,65},{65,1},{2,66},{66,2},{3,67},{67,3},{4,68},{68... | collective-permute-start | bytes 1572872 | tf_op jit(solution)/shard_map/ppermute | solution.py:278
  11.2 24.5 %collective-permute-start.7 = (bf16[256,1024]{1,0:T(8,128)(2,1)S(1)}, bf16[256,1024]{1,0:T(8,128)(2,1)S(1)}, u32[]{:S(2)}, u32[]{:S(2)}) collective-permute-start(bf16[256,1024]{1,0:T(8,128)(2,1)S(1)} %get-tuple-element.34.refs_4_), channel_id=1, source_target_pairs={{0,16},{16,0},{1,17},{17,1},{2,18},{18,2},{3,19},{19,3},{4,20},{20... | collective-permute-start | bytes 1572872 | tf_op jit(solution)/shard_map/ppermute | solution.py:34
  23.2 12.6 %collective-permute-start.8 = (bf16[256,1024]{1,0:T(8,128)(2,1)S(1)}, bf16[256,1024]{1,0:T(8,128)(2,1)S(1)}, u32[]{:S(2)}, u32[]{:S(2)}) collective-permute-start(bf16[256,1024]{1,0:T(8,128)(2,1)S(1)} %collective-permute-done.6.refs_0_), channel_id=1, source_target_pairs={{0,16},{16,0},{1,17},{17,1},{2,18},{18,2},{3,19},{19,3},{4,20},{20... | collective-permute-start | bytes 1572872 | tf_op jit(solution)/shard_map/ppermute | solution.py:34
  28.9 21.4 %collective-permute-start.3 = (bf16[256,1024]{1,0:T(8,128)(2,1)}, bf16[256,1024]{1,0:T(8,128)(2,1)S(1)}, u32[]{:S(2)}, u32[]{:S(2)}) collective-permute-start(bf16[256,1024]{1,0:T(8,128)(2,1)} %get-tuple-element.31), channel_id=1, source_target_pairs={{0,1},{1,2},{2,3},{3,0},{4,5},{5,6},{6,7},{7,4},{8,9},{9,10},{10,1... | collective-permute-start | bytes 1572872 | tf_op jit(solution)/shard_map/ppermute | solution.py:34
  30.7 30.1 %collective-permute-start.4 = (bf16[256,1024]{1,0:T(8,128)(2,1)}, bf16[256,1024]{1,0:T(8,128)(2,1)}, u32[]{:S(2)}, u32[]{:S(2)}) collective-permute-start(bf16[256,1024]{1,0:T(8,128)(2,1)} %get-tuple-element.32), channel_id=1, source_target_pairs={{0,2},{1,3},{2,0},{3,1},{4,6},{5,7},{6,4},{7,5},{8,10},{9,11},{10,... | collective-permute-start | bytes 1572872 | tf_op jit(solution)/shard_map/ppermute | solution.py:34
  33.6 29.1 %collective-permute-start.5 = (bf16[256,1024]{1,0:T(8,128)(2,1)}, bf16[256,1024]{1,0:T(8,128)(2,1)}, u32[]{:S(2)}, u32[]{:S(2)}) collective-permute-start(bf16[256,1024]{1,0:T(8,128)(2,1)} %get-tuple-element.33), channel_id=1, source_target_pairs={{0,3},{1,0},{2,1},{3,2},{4,7},{5,4},{6,5},{7,6},{8,11},{9,8},{10,9... | collective-permute-start | bytes 1572872 | tf_op jit(solution)/shard_map/ppermute | solution.py:34
  37.4 28.9 %all-to-all-start = ((bf16[32,8,1024]{2,1,0:T(8,128)(2,1)}), bf16[32,8,1024]{2,1,0:T(8,128)(2,1)S(1)}, u32[]{:S(2)}, u32[]{:S(2)}) async-start(bf16[32,8,1024]{2,1,0:T(8,128)(2,1)} %bitcast.12), calls=%async_computation | async-start | bytes 1048576 | tf_op jit(solution)/shard_map/all_to_all | solution.py:29
  45.7 111.7 %all-gather.2.cloned.1.call-start = ((), (), s32[]{:S(2)}) async-start(), calls=%async_computation.4 | async-start | bytes 1114112 | tf_op jit(solution)/shard_map/all_gather | solution.py:297
  45.7 30.4 %collective-permute-start.10 = (bf16[256,1024]{1,0:T(8,128)(2,1)S(1)}, bf16[256,1024]{1,0:T(8,128)(2,1)}, u32[]{:S(2)}, u32[]{:S(2)}) collective-permute-start(bf16[256,1024]{1,0:T(8,128)(2,1)S(1)} %get-tuple-element.34.refs_4_), channel_id=1, source_target_pairs={{0,8},{4,12},{8,0},{12,4},{1,9},{5,13},{9,1},{13,5},{2,10},{6,14},... | collective-permute-start | bytes 1572872 | tf_op jit(solution)/shard_map/ppermute | solution.py:34
  49.1 29.8 %collective-permute-start.11 = (bf16[256,1024]{1,0:T(8,128)(2,1)S(1)}, bf16[256,1024]{1,0:T(8,128)(2,1)}, u32[]{:S(2)}, u32[]{:S(2)}) collective-permute-start(bf16[256,1024]{1,0:T(8,128)(2,1)S(1)} %get-tuple-element.34.refs_4_), channel_id=1, source_target_pairs={{0,12},{4,0},{8,4},{12,8},{1,13},{5,1},{9,5},{13,9},{2,14},{6,2},{... | collective-permute-start | bytes 1572872 | tf_op jit(solution)/shard_map/ppermute | solution.py:34
  50.3 31.1 %collective-permute-start.9 = (bf16[256,1024]{1,0:T(8,128)(2,1)S(1)}, bf16[256,1024]{1,0:T(8,128)(2,1)}, u32[]{:S(2)}, u32[]{:S(2)}) collective-permute-start(bf16[256,1024]{1,0:T(8,128)(2,1)S(1)} %get-tuple-element.34.refs_4_), channel_id=1, source_target_pairs={{0,4},{4,8},{8,12},{12,0},{1,5},{5,9},{9,13},{13,1},{2,6},{6,10},{... | collective-permute-start | bytes 1572872 | tf_op jit(solution)/shard_map/ppermute | solution.py:34
  60.8 29.2 %collective-permute-start = (bf16[256,1024]{1,0:T(8,128)(2,1)}, bf16[256,1024]{1,0:T(8,128)(2,1)S(1)}, u32[]{:S(2)}, u32[]{:S(2)}) collective-permute-start(bf16[256,1024]{1,0:T(8,128)(2,1)} %get-tuple-element.27), channel_id=1, source_target_pairs={{0,4},{4,8},{8,12},{12,0},{1,5},{5,9},{9,13},{13,1},{2,6},{6,10},{... | collective-permute-start | bytes 1572872 | tf_op jit(solution)/shard_map/ppermute | solution.py:34
  62.8 36.8 %collective-permute-start.1 = (bf16[256,1024]{1,0:T(8,128)(2,1)}, bf16[256,1024]{1,0:T(8,128)(2,1)S(1)}, u32[]{:S(2)}, u32[]{:S(2)}) collective-permute-start(bf16[256,1024]{1,0:T(8,128)(2,1)} %get-tuple-element.28), channel_id=1, source_target_pairs={{0,8},{4,12},{8,0},{12,4},{1,9},{5,13},{9,1},{13,5},{2,10},{6,14},... | collective-permute-start | bytes 1572872 | tf_op jit(solution)/shard_map/ppermute | solution.py:34
  76.1 28.1 %collective-permute-start.16 = (bf16[256,1024]{1,0:T(8,128)(2,1)S(1)}, bf16[256,1024]{1,0:T(8,128)(2,1)S(1)}, u32[]{:S(2)}, u32[]{:S(2)}) collective-permute-start(bf16[256,1024]{1,0:T(8,128)(2,1)S(1)} %get-tuple-element.37.refs_4_), channel_id=1, source_target_pairs={{0,1},{1,2},{2,3},{3,0},{4,5},{5,6},{6,7},{7,4},{8,9},{9,10},{10,1... | collective-permute-start | bytes 1572872 | tf_op jit(solution)/shard_map/ppermute | solution.py:34
  79.0 25.2 %collective-permute-start.17 = (bf16[256,1024]{1,0:T(8,128)(2,1)S(1)}, bf16[256,1024]{1,0:T(8,128)(2,1)}, u32[]{:S(2)}, u32[]{:S(2)}) collective-permute-start(bf16[256,1024]{1,0:T(8,128)(2,1)S(1)} %get-tuple-element.37.refs_4_), channel_id=1, source_target_pairs={{0,2},{1,3},{2,0},{3,1},{4,6},{5,7},{6,4},{7,5},{8,10},{9,11},{10,... | collective-permute-start | bytes 1572872 | tf_op jit(solution)/shard_map/ppermute | solution.py:34
  81.4 22.8 %collective-permute-start.18 = (bf16[256,1024]{1,0:T(8,128)(2,1)S(1)}, bf16[256,1024]{1,0:T(8,128)(2,1)}, u32[]{:S(2)}, u32[]{:S(2)}) collective-permute-start(bf16[256,1024]{1,0:T(8,128)(2,1)S(1)} %get-tuple-element.37.refs_4_), channel_id=1, source_target_pairs={{0,3},{1,0},{2,1},{3,2},{4,7},{5,4},{6,5},{7,6},{8,11},{9,8},{10,9... | collective-permute-start | bytes 1572872 | tf_op jit(solution)/shard_map/ppermute | solution.py:34
  90.0 14.1 %collective-permute-start.2 = (bf16[256,1024]{1,0:T(8,128)(2,1)}, bf16[256,1024]{1,0:T(8,128)(2,1)S(1)}, u32[]{:S(2)}, u32[]{:S(2)}) collective-permute-start(bf16[256,1024]{1,0:T(8,128)(2,1)} %get-tuple-element.29), channel_id=1, source_target_pairs={{0,12},{4,0},{8,4},{12,8},{1,13},{5,1},{9,5},{13,9},{2,14},{6,2},{... | collective-permute-start | bytes 1572872 | tf_op jit(solution)/shard_map/ppermute | solution.py:34
  99.6 12.0 %collective-permute-start.12 = (bf16[512,1024]{1,0:T(8,128)(2,1)}, bf16[512,1024]{1,0:T(8,128)(2,1)}, u32[]{:S(2)}, u32[]{:S(2)}) collective-permute-start(bf16[512,1024]{1,0:T(8,128)(2,1)} %get-tuple-element.36), channel_id=1, source_target_pairs={{0,16},{16,0},{1,17},{17,1},{2,18},{18,2},{3,19},{19,3},{4,20},{20... | collective-permute-start | bytes 3145736 | tf_op jit(solution)/shard_map/ppermute | solution.py:34
  113.5 15.5 %collective-permute-start.13 = (bf16[128,1024]{1,0:T(8,128)(2,1)S(1)}, bf16[128,1024]{1,0:T(8,128)(2,1)S(1)}, u32[]{:S(2)}, u32[]{:S(2)}) collective-permute-start(bf16[128,1024]{1,0:T(8,128)(2,1)S(1)} %get-tuple-element.72), channel_id=1, source_target_pairs={{0,3},{1,0},{2,1},{3,2},{4,7},{5,4},{6,5},{7,6},{8,11},{9,8},{10,9... | collective-permute-start | bytes 786440 | tf_op jit(solution)/shard_map/ppermute | solution.py:34
  116.4 13.6 %collective-permute-start.14 = (bf16[128,1024]{1,0:T(8,128)(2,1)S(1)}, bf16[128,1024]{1,0:T(8,128)(2,1)S(1)}, u32[]{:S(2)}, u32[]{:S(2)}) collective-permute-start(bf16[128,1024]{1,0:T(8,128)(2,1)S(1)} %get-tuple-element.74), channel_id=1, source_target_pairs={{0,2},{1,3},{2,0},{3,1},{4,6},{5,7},{6,4},{7,5},{8,10},{9,11},{10,... | collective-permute-start | bytes 786440 | tf_op jit(solution)/shard_map/ppermute | solution.py:34
  117.1 15.7 %collective-permute-start.15 = (bf16[128,1024]{1,0:T(8,128)(2,1)S(1)}, bf16[128,1024]{1,0:T(8,128)(2,1)S(1)}, u32[]{:S(2)}, u32[]{:S(2)}) collective-permute-start(bf16[128,1024]{1,0:T(8,128)(2,1)S(1)} %get-tuple-element.73), channel_id=1, source_target_pairs={{0,1},{1,2},{2,3},{3,0},{4,5},{5,6},{6,7},{7,4},{8,9},{9,10},{10,1... | collective-permute-start | bytes 786440 | tf_op jit(solution)/shard_map/ppermute | solution.py:34
  118.4 14.5 %collective-permute-start.20 = (bf16[128,1024]{1,0:T(8,128)(2,1)S(1)}, bf16[128,1024]{1,0:T(8,128)(2,1)S(1)}, u32[]{:S(2)}, u32[]{:S(2)}) collective-permute-start(bf16[128,1024]{1,0:T(8,128)(2,1)S(1)} %get-tuple-element.75), channel_id=1, source_target_pairs={{0,12},{4,0},{8,4},{12,8},{1,13},{5,1},{9,5},{13,9},{2,14},{6,2},{... | collective-permute-start | bytes 786440 | tf_op jit(solution)/shard_map/ppermute | solution.py:34
  120.5 12.5 %collective-permute-start.21 = (bf16[128,1024]{1,0:T(8,128)(2,1)S(1)}, bf16[128,1024]{1,0:T(8,128)(2,1)S(1)}, u32[]{:S(2)}, u32[]{:S(2)}) collective-permute-start(bf16[128,1024]{1,0:T(8,128)(2,1)S(1)} %get-tuple-element.77), channel_id=1, source_target_pairs={{0,8},{4,12},{8,0},{12,4},{1,9},{5,13},{9,1},{13,5},{2,10},{6,14},... | collective-permute-start | bytes 786440 | tf_op jit(solution)/shard_map/ppermute | solution.py:34
  139.1 19.6 %collective-permute-start.23 = (bf16[32,2048]{1,0:T(8,128)(2,1)}, bf16[32,2048]{1,0:T(8,128)(2,1)S(1)}, u32[]{:S(2)}, u32[]{:S(2)}) collective-permute-start(bf16[32,2048]{1,0:T(8,128)(2,1)} %get-tuple-element.80), channel_id=1, source_target_pairs={{0,32},{32,0},{64,96},{96,64},{1,33},{33,1},{65,97},{97,65},{2,34}... | collective-permute-start | bytes 393224 | tf_op jit(solution)/shard_map/ppermute | solution.py:43
  139.8 18.8 %collective-permute-start.24 = (bf16[32,2048]{1,0:T(8,128)(2,1)}, bf16[32,2048]{1,0:T(8,128)(2,1)S(1)}, u32[]{:S(2)}, u32[]{:S(2)}) collective-permute-start(bf16[32,2048]{1,0:T(8,128)(2,1)} %get-tuple-element.82), channel_id=1, source_target_pairs={{0,64},{32,96},{64,32},{96,0},{1,65},{33,97},{65,33},{97,1},{2,66}... | collective-permute-start | bytes 393224 | tf_op jit(solution)/shard_map/ppermute | solution.py:43
  140.4 18.2 %collective-permute-start.25 = (bf16[32,2048]{1,0:T(8,128)(2,1)}, bf16[32,2048]{1,0:T(8,128)(2,1)S(1)}, u32[]{:S(2)}, u32[]{:S(2)}) collective-permute-start(bf16[32,2048]{1,0:T(8,128)(2,1)} %get-tuple-element.81), channel_id=1, source_target_pairs={{0,96},{32,64},{64,0},{96,32},{1,97},{33,65},{65,1},{97,33},{2,98}... | collective-permute-start | bytes 393224 | tf_op jit(solution)/shard_map/ppermute | solution.py:43
  157.4 15.8 %collective-permute-start.40 = (bf16[256,1024]{1,0:T(8,128)(2,1)}, bf16[256,1024]{1,0:T(8,128)(2,1)S(1)}, u32[]{:S(2)}, u32[]{:S(2)}) collective-permute-start(bf16[256,1024]{1,0:T(8,128)(2,1)} %copy-done.2), channel_id=1, source_target_pairs={{0,4},{4,8},{8,12},{12,0},{1,5},{5,9},{9,13},{13,1},{2,6},{6,10},{... | collective-permute-start | bytes 1572872 | tf_op jit(solution)/shard_map/ppermute | solution.py:34
  166.8 18.3 %collective-permute-start.41 = (bf16[256,1024]{1,0:T(8,128)(2,1)S(1)}, bf16[256,1024]{1,0:T(8,128)(2,1)S(1)}, u32[]{:S(2)}, u32[]{:S(2)}) collective-permute-start(bf16[256,1024]{1,0:T(8,128)(2,1)S(1)} %copy-done.3), channel_id=1, source_target_pairs={{0,8},{4,12},{8,0},{12,4},{1,9},{5,13},{9,1},{13,5},{2,10},{6,14},... | collective-permute-start | bytes 1572872 | tf_op jit(solution)/shard_map/ppermute | solution.py:34
  169.5 20.3 %collective-permute-start.46 = (bf16[128,1024]{1,0:T(8,128)(2,1)S(1)}, bf16[128,1024]{1,0:T(8,128)(2,1)S(1)}, u32[]{:S(2)}, u32[]{:S(2)}) collective-permute-start(bf16[128,1024]{1,0:T(8,128)(2,1)S(1)} %pad_maximum_fusion.2.refs_4_), channel_id=1, source_target_pairs={{0,1},{1,2},{2,3},{3,0},{4,5},{5,6},{6,7},{7,4},{8,9},{9,10},{10,1... | collective-permute-start | bytes 786440 | tf_op jit(solution)/shard_map/ppermute | solution.py:34
  169.8 20.0 %collective-permute-start.47 = (bf16[128,1024]{1,0:T(8,128)(2,1)S(1)}, bf16[128,1024]{1,0:T(8,128)(2,1)S(1)}, u32[]{:S(2)}, u32[]{:S(2)}) collective-permute-start(bf16[128,1024]{1,0:T(8,128)(2,1)S(1)} %pad_maximum_fusion.2.refs_4_), channel_id=1, source_target_pairs={{0,2},{1,3},{2,0},{3,1},{4,6},{5,7},{6,4},{7,5},{8,10},{9,11},{10,... | collective-permute-start | bytes 786440 | tf_op jit(solution)/shard_map/ppermute | solution.py:34
  173.2 18.7 %collective-permute-start.42 = (bf16[256,1024]{1,0:T(8,128)(2,1)S(1)}, bf16[256,1024]{1,0:T(8,128)(2,1)S(1)}, u32[]{:S(2)}, u32[]{:S(2)}) collective-permute-start(bf16[256,1024]{1,0:T(8,128)(2,1)S(1)} %copy-done.3), channel_id=1, source_target_pairs={{0,12},{4,0},{8,4},{12,8},{1,13},{5,1},{9,5},{13,9},{2,14},{6,2},{... | collective-permute-start | bytes 1572872 | tf_op jit(solution)/shard_map/ppermute | solution.py:34
  194.8 13.3 %collective-permute-start.31 = (bf16[128,1024]{1,0:T(8,128)(2,1)S(1)}, bf16[128,1024]{1,0:T(8,128)(2,1)S(1)}, u32[]{:S(2)}, u32[]{:S(2)}) collective-permute-start(bf16[128,1024]{1,0:T(8,128)(2,1)S(1)} %pad_maximum_fusion.1.refs_0_), channel_id=1, source_target_pairs={{0,8},{4,12},{8,0},{12,4},{1,9},{5,13},{9,1},{13,5},{2,10},{6,14},... | collective-permute-start | bytes 786440 | tf_op jit(solution)/shard_map/ppermute | solution.py:34
  196.1 18.1 %collective-permute-start.32 = (bf16[128,1024]{1,0:T(8,128)(2,1)S(1)}, bf16[128,1024]{1,0:T(8,128)(2,1)S(1)}, u32[]{:S(2)}, u32[]{:S(2)}) collective-permute-start(bf16[128,1024]{1,0:T(8,128)(2,1)S(1)} %pad_maximum_fusion.1.refs_0_), channel_id=1, source_target_pairs={{0,12},{4,0},{8,4},{12,8},{1,13},{5,1},{9,5},{13,9},{2,14},{6,2},{... | collective-permute-start | bytes 786440 | tf_op jit(solution)/shard_map/ppermute | solution.py:34
  199.2 15.0 %collective-permute-start.33 = (bf16[128,1024]{1,0:T(8,128)(2,1)S(1)}, bf16[128,1024]{1,0:T(8,128)(2,1)S(1)}, u32[]{:S(2)}, u32[]{:S(2)}) collective-permute-start(bf16[128,1024]{1,0:T(8,128)(2,1)S(1)} %pad_maximum_fusion.1.refs_0_), channel_id=1, source_target_pairs={{0,16},{16,0},{1,17},{17,1},{2,18},{18,2},{3,19},{19,3},{4,20},{20... | collective-permute-start | bytes 786440 | tf_op jit(solution)/shard_map/ppermute | solution.py:34
  199.2 15.5 %collective-permute-start.53 = (bf16[128,1024]{1,0:T(8,128)(2,1)S(1)}, bf16[128,1024]{1,0:T(8,128)(2,1)S(1)}, u32[]{:S(2)}, u32[]{:S(2)}) collective-permute-start(bf16[128,1024]{1,0:T(8,128)(2,1)S(1)} %pad_maximum_fusion.3.refs_12_), channel_id=1, source_target_pairs={{0,1},{1,2},{2,3},{3,0},{4,5},{5,6},{6,7},{7,4},{8,9},{9,10},{10,1... | collective-permute-start | bytes 786440 | tf_op jit(solution)/shard_map/ppermute | solution.py:34
  201.0 16.7 %collective-permute-start.54 = (bf16[128,1024]{1,0:T(8,128)(2,1)S(1)}, bf16[128,1024]{1,0:T(8,128)(2,1)}, u32[]{:S(2)}, u32[]{:S(2)}) collective-permute-start(bf16[128,1024]{1,0:T(8,128)(2,1)S(1)} %pad_maximum_fusion.3.refs_12_), channel_id=1, source_target_pairs={{0,2},{1,3},{2,0},{3,1},{4,6},{5,7},{6,4},{7,5},{8,10},{9,11},{10,... | collective-permute-start | bytes 786440 | tf_op jit(solution)/shard_map/ppermute | solution.py:34
  208.1 14.0 %collective-permute-start.55 = (bf16[128,1024]{1,0:T(8,128)(2,1)S(1)}, bf16[128,1024]{1,0:T(8,128)(2,1)}, u32[]{:S(2)}, u32[]{:S(2)}) collective-permute-start(bf16[128,1024]{1,0:T(8,128)(2,1)S(1)} %pad_maximum_fusion.3.refs_12_), channel_id=1, source_target_pairs={{0,3},{1,0},{2,1},{3,2},{4,7},{5,4},{6,5},{7,6},{8,11},{9,8},{10,9... | collective-permute-start | bytes 786440 | tf_op jit(solution)/shard_map/ppermute | solution.py:34
  217.7 11.7 %collective-permute-start.52 = (bf16[128,1024]{1,0:T(8,128)(2,1)S(1)}, bf16[128,1024]{1,0:T(8,128)(2,1)S(1)}, u32[]{:S(2)}, u32[]{:S(2)}) collective-permute-start(bf16[128,1024]{1,0:T(8,128)(2,1)S(1)} %collective-permute-done.48.refs_7_), channel_id=1, source_target_pairs={{0,16},{16,0},{1,17},{17,1},{2,18},{18,2},{3,19},{19,3},{4,20},{20... | collective-permute-start | bytes 786440 | tf_op jit(solution)/shard_map/ppermute | solution.py:34
  222.2 14.3 %collective-permute-start.56 = (bf16[128,1024]{1,0:T(8,128)(2,1)S(1)}, bf16[128,1024]{1,0:T(8,128)(2,1)S(1)}, u32[]{:S(2)}, u32[]{:S(2)}) collective-permute-start(bf16[128,1024]{1,0:T(8,128)(2,1)S(1)} %pad_maximum_fusion.3.refs_12_), channel_id=1, source_target_pairs={{0,16},{16,0},{1,17},{17,1},{2,18},{18,2},{3,19},{19,3},{4,20},{20... | collective-permute-start | bytes 786440 | tf_op jit(solution)/shard_map/ppermute | solution.py:34
  222.7 13.8 %collective-permute-start.57 = (bf16[128,1024]{1,0:T(8,128)(2,1)S(1)}, bf16[128,1024]{1,0:T(8,128)(2,1)S(1)}, u32[]{:S(2)}, u32[]{:S(2)}) collective-permute-start(bf16[128,1024]{1,0:T(8,128)(2,1)S(1)} %collective-permute-done.53.refs_13_), channel_id=1, source_target_pairs={{0,16},{16,0},{1,17},{17,1},{2,18},{18,2},{3,19},{19,3},{4,20},{20... | collective-permute-start | bytes 786440 | tf_op jit(solution)/shard_map/ppermute | solution.py:34
  222.8 14.7 %collective-permute-start.58 = (bf16[128,1024]{1,0:T(8,128)(2,1)}, bf16[128,1024]{1,0:T(8,128)(2,1)}, u32[]{:S(2)}, u32[]{:S(2)}) collective-permute-start(bf16[128,1024]{1,0:T(8,128)(2,1)} %collective-permute-done.54.refs_14_), channel_id=1, source_target_pairs={{0,16},{16,0},{1,17},{17,1},{2,18},{18,2},{3,19},{19,3},{4,20},{20... | collective-permute-start | bytes 786440 | tf_op jit(solution)/shard_map/ppermute | solution.py:34
  223.2 14.3 %collective-permute-start.59 = (bf16[128,1024]{1,0:T(8,128)(2,1)}, bf16[128,1024]{1,0:T(8,128)(2,1)}, u32[]{:S(2)}, u32[]{:S(2)}) collective-permute-start(bf16[128,1024]{1,0:T(8,128)(2,1)} %collective-permute-done.55.refs_15_), channel_id=1, source_target_pairs={{0,16},{16,0},{1,17},{17,1},{2,18},{18,2},{3,19},{19,3},{4,20},{20... | collective-permute-start | bytes 786440 | tf_op jit(solution)/shard_map/ppermute | solution.py:34
  230.1 25.1 %collective-permute-start.37 = (bf16[256,1024]{1,0:T(8,128)(2,1)}, bf16[256,1024]{1,0:T(8,128)(2,1)S(1)}, u32[]{:S(2)}, u32[]{:S(2)}) collective-permute-start(bf16[256,1024]{1,0:T(8,128)(2,1)} %get-tuple-element.42), channel_id=1, source_target_pairs={{0,3},{1,0},{2,1},{3,2},{4,7},{5,4},{6,5},{7,6},{8,11},{9,8},{10,9... | collective-permute-start | bytes 1572872 | tf_op jit(solution)/shard_map/ppermute | solution.py:34
  236.4 18.8 %collective-permute-start.38 = (bf16[256,1024]{1,0:T(8,128)(2,1)}, bf16[256,1024]{1,0:T(8,128)(2,1)S(1)}, u32[]{:S(2)}, u32[]{:S(2)}) collective-permute-start(bf16[256,1024]{1,0:T(8,128)(2,1)} %get-tuple-element.43), channel_id=1, source_target_pairs={{0,2},{1,3},{2,0},{3,1},{4,6},{5,7},{6,4},{7,5},{8,10},{9,11},{10,... | collective-permute-start | bytes 1572872 | tf_op jit(solution)/shard_map/ppermute | solution.py:34
  236.6 26.3 %collective-permute-start.39 = (bf16[256,1024]{1,0:T(8,128)(2,1)S(1)}, bf16[256,1024]{1,0:T(8,128)(2,1)}, u32[]{:S(2)}, u32[]{:S(2)}) collective-permute-start(bf16[256,1024]{1,0:T(8,128)(2,1)S(1)} %copy-done.19), channel_id=1, source_target_pairs={{0,1},{1,2},{2,3},{3,0},{4,5},{5,6},{6,7},{7,4},{8,9},{9,10},{10,1... | collective-permute-start | bytes 1572872 | tf_op jit(solution)/shard_map/ppermute | solution.py:34
  248.6 16.1 %collective-permute-start.60 = (bf16[256,1024]{1,0:T(8,128)(2,1)}, bf16[256,1024]{1,0:T(8,128)(2,1)S(1)}, u32[]{:S(2)}, u32[]{:S(2)}) collective-permute-start(bf16[256,1024]{1,0:T(8,128)(2,1)} %get-tuple-element.46), channel_id=1, source_target_pairs={{0,12},{4,0},{8,4},{12,8},{1,13},{5,1},{9,5},{13,9},{2,14},{6,2},{... | collective-permute-start | bytes 1572872 | tf_op jit(solution)/shard_map/ppermute | solution.py:34
  249.0 16.6 %collective-permute-start.61 = (bf16[256,1024]{1,0:T(8,128)(2,1)}, bf16[256,1024]{1,0:T(8,128)(2,1)S(1)}, u32[]{:S(2)}, u32[]{:S(2)}) collective-permute-start(bf16[256,1024]{1,0:T(8,128)(2,1)} %get-tuple-element.47), channel_id=1, source_target_pairs={{0,8},{4,12},{8,0},{12,4},{1,9},{5,13},{9,1},{13,5},{2,10},{6,14},... | collective-permute-start | bytes 1572872 | tf_op jit(solution)/shard_map/ppermute | solution.py:34
  255.2 20.1 %collective-permute-start.62 = (bf16[256,1024]{1,0:T(8,128)(2,1)}, bf16[256,1024]{1,0:T(8,128)(2,1)S(1)}, u32[]{:S(2)}, u32[]{:S(2)}) collective-permute-start(bf16[256,1024]{1,0:T(8,128)(2,1)} %get-tuple-element.48), channel_id=1, source_target_pairs={{0,4},{4,8},{8,12},{12,0},{1,5},{5,9},{9,13},{13,1},{2,6},{6,10},{... | collective-permute-start | bytes 1572872 | tf_op jit(solution)/shard_map/ppermute | solution.py:34
  (52 other events, 830.9 us)
Sparse Core Ops, SparseCore 0:
  111.8 45.6 all-gather.1

commit v2 on v1

--- a/solution.py
+++ b/solution.py
@@ -249,6 +249,29 @@
     )(at, turned, *weights, *act, *slope)
 
 
+def join_kernel(at_ref, *refs):
+    blocks, out = refs[:4], refs[4]
+    z, y = at_ref[3], at_ref[4]
+    part = blocks[0].shape[0] // 4
+    for kz in range(4):
+        for ky in range(4):
+            to = (lax.rem(z + 4 - kz, 4) * 4 + lax.rem(y + 4 - ky, 4)) * part
+            rows = pl.ds(pl.multiple_of(to, part), part)
+            out[rows, :] = blocks[kz][ky * part : (ky + 1) * part, :]
+
+
+def join(at, blocks):
+    rows, hidden = blocks[0].shape
+    vmem = pl.BlockSpec(memory_space=pltpu.VMEM)
+    return pl.pallas_call(
+        join_kernel,
+        out_shape=jax.ShapeDtypeStruct((4 * rows, hidden), BF),
+        in_specs=[pl.BlockSpec(memory_space=pltpu.SMEM)] + [vmem] * 4,
+        out_specs=vmem,
+        name="join",
+    )(at, *blocks)
+
+
 def gather(value, axis):
     return [value] + [shift(value, axis, k) for k in (1, 2, 3)]
 
@@ -294,7 +317,9 @@
     m = m.reshape(32, -1, hidden).astype(F32).sum(0).astype(BF)
     m = a2a(jnp.broadcast_to(m[None], (4,) + m.shape), ("p", "h")).reshape(-1, hidden)
     w_us[0], w_vs[0], m = lax.optimization_barrier((w_us[0], w_vs[0], m))
-    m_near = lax.all_gather(m, ("z", "y"), axis=0, tiled=True)
+    m = jnp.concatenate(gather(m, "y"))
+    m = gather(m, "z")
+    m_near = join(at, m)
     m_far = shift(m_near, "c", 1)
 
     def reduced(blocks, weights, axis):

time: 315 us -> 305 us (0.968)
  between operations: 17.8 us -> 4.47 us
    all_gather x1 -> x0, waiting for transfers between devices: 14.3 us -> none  [on_device(): m_near = lax.all_gather(m, ('z', 'y'), axis=0, tiled=True)]
    ppermute x53 -> x59, waiting for transfers between devices: 73.8 us -> 86.4 us  [shift(): lax.ppermute(value, axis, [(i, (i + by) % count) for i in range(count)])]
    ppermute x53 -> x59, starting transfers between devices: 72.9 us -> 71 us  [shift(): lax.ppermute(value, axis, [(i, (i + by) % count) for i in range(count)])]
  transfers between devices with their start and end apart: 65 -> 70, of which waited for: 22 -> 21; matrix products, arithmetic and copies ran while one was open for 3% -> 4% of each run, Pallas kernels for 14% -> 15%
where the time goes in v2:
time: 305 us; the launch traced here: 303 us
  waiting for transfers between devices  105 us (34%)
  starting transfers between devices  95 us (31%)
  Pallas kernels  45.7 us (15%)
  blocking collectives  30.8 us (10%)
  other arithmetic  9.97 us (3%)
  local copies, waits for them, and re-layouts  9.63 us (3%)
  between operations  4.47 us (1%)
    ppermute x59, waiting for transfers between devices, shift(): lax.ppermute(value, axis, [(i, (i + by) % count) for i in range(count)])  86.4 us
    ppermute x59, starting transfers between devices, shift(): lax.ppermute(value, axis, [(i, (i + by) % count) for i in range(count)])  71 us
    all_to_all x3, blocking collectives, a2a(): return lax.all_to_all(value, axes, 0, 0, tiled=True)  30.8 us
    ppermute x9, starting transfers between devices, shift_x(): return lax.ppermute(value, ('p', 'h'), pairs)  14.1 us
    pallas_call x2, Pallas kernels, project(): pl.pallas_call(project_kernel, out_shape=[jax.ShapeDtypeStruct((2 * tok,...  12.7 us
    ppermute x1, waiting for transfers between devices, on_device(): w_3 = lax.ppermute(w_u, 'p', [(0, 1), (1, 0)])  11.9 us
    pallas_call x1, Pallas kernels, grad_u_call(): pl.pallas_call(grad_u_kernel, out_shape=[jax.ShapeDtypeStruct((own, hidde...  11.1 us
    pallas_call x2, Pallas kernels, turn(): pl.pallas_call(turn_kernel, out_shape=jax.ShapeDtypeStruct((wide, 4 * tok...  8.48 us
  transfers between devices with their start and end apart: 70, of which 21 were waited for; matrix products, arithmetic and copies ran while one was open for 4% of the time, Pallas kernels for 15%

profile of v2, /device:TPU:0, one launch (start us, length us, event | category | flops | bytes accessed | tf_op | source)
XLA Modules:
  0.0 303.1 jit_solution(16719637693141130178)
XLA Ops:
  1.9 1.9 bitcast_select_fusion
  5.4 11.9 %collective-permute-done.6.refs_0_ = bf16[256,1024]{1,0:T(8,128)(2,1)S(1)} collective-permute-done((bf16[256,1024]{1,0:T(8,128)(2,1)S(1)}, bf16[256,1024]{1,0:T(8,128)(2,1)S(1)}, u32[]{:S(2)}, u32[]{:S(2)}) %collective-permute-start.6) | collective-permute-done | bytes 524320 | tf_op jit(solution)/shard_map/ppermute | solution.py:301
  18.1 5.0 %cut.1 = (bf16[256,1024]{1,0:T(8,128)(2,1)}, bf16[256,1024]{1,0:T(8,128)(2,1)}, bf16[256,1024]{1,0:T(8,128)(2,1)}, bf16[256,1024]{1,0:T(8,128)(2,1)}, bf16[256,1...) custom-call(s32[5]{0:T(128)} %stack.39.at_ref, ...), custom_call_target="tpu_custom_call" | custom-call | tf_op jit(solution)/shard_map/cut/pallas_call | solution.py:90
  23.1 1.8 collective-permute-start.3
  24.9 2.9 collective-permute-start.4
  31.6 8.3 %all-to-all-start = ((bf16[32,8,1024]{2,1,0:T(8,128)(2,1)}), bf16[32,8,1024]{2,1,0:T(8,128)(2,1)S(1)}, u32[]{:S(2)}, u32[]{:S(2)}) async-start(bf16[32,8,1024]{2,1,0:T(8,128)(2,1)} %bitcast.12), calls=%async_computation | async-start | bytes 1048576 | tf_op jit(solution)/shard_map/all_to_all | solution.py:29
  39.9 3.4 %collective-permute-start.10 = (bf16[256,1024]{1,0:T(8,128)(2,1)S(1)}, bf16[256,1024]{1,0:T(8,128)(2,1)}, u32[]{:S(2)}, u32[]{:S(2)}) collective-permute-start(bf16[256,1024]{1,0:T(8,128)(2,1)S(1)} %get-tuple-element.34.refs_4_), channel_id=1, source_target_pairs={{0,8},{4,12},{8,0},{12,4},{1,9},{5,13},{9,1},{13,5},{2,10},{6,14},... | collective-permute-start | bytes 1572872 | tf_op jit(solution)/shard_map/ppermute | solution.py:34
  45.4 9.6 %collective-permute-done.4.refs_2_ = bf16[256,1024]{1,0:T(8,128)(2,1)S(1)} collective-permute-done((bf16[256,1024]{1,0:T(8,128)(2,1)}, bf16[256,1024]{1,0:T(8,128)(2,1)S(1)}, u32[]{:S(2)}, u32[]{:S(2)}) %collective-permute-start.4) | collective-permute-done | bytes 524320 | tf_op jit(solution)/shard_map/ppermute | solution.py:34
  55.0 1.9 collective-permute-start
  56.9 3.6 %collective-permute-start.1 = (bf16[256,1024]{1,0:T(8,128)(2,1)}, bf16[256,1024]{1,0:T(8,128)(2,1)S(1)}, u32[]{:S(2)}, u32[]{:S(2)}) collective-permute-start(bf16[256,1024]{1,0:T(8,128)(2,1)} %get-tuple-element.28), channel_id=1, source_target_pairs={{0,8},{4,12},{8,0},{12,4},{1,9},{5,13},{9,1},{13,5},{2,10},{6,14},... | collective-permute-start | bytes 1572872 | tf_op jit(solution)/shard_map/ppermute | solution.py:34
  60.6 9.5 %all_to_all.21 = bf16[4,8,1024]{2,1,0:T(8,128)(2,1)S(1)} all-to-all(bf16[4,8,1024]{2,1,0:T(8,128)(2,1)S(1)} %broadcast_in_dim.18), channel_id=1, replica_groups=mesh['p'=2,'h'=2,'c'=2,'z'=4,'y'=4] {'p','h'}, dimensions={0} | all-to-all | bytes 131072 | tf_op jit(solution)/shard_map/all_to_all | solution.py:29
  73.1 2.5 collective-permute-start.17
  75.6 1.9 collective-permute-start.18
  77.5 6.7 %collective-permute-done.refs_1_ = bf16[256,1024]{1,0:T(8,128)(2,1)S(1)} collective-permute-done((bf16[256,1024]{1,0:T(8,128)(2,1)}, bf16[256,1024]{1,0:T(8,128)(2,1)S(1)}, u32[]{:S(2)}, u32[]{:S(2)}) %collective-permute-start) | collective-permute-done | bytes 524320 | tf_op jit(solution)/shard_map/ppermute | solution.py:34
  84.8 6.3 %shard_map.68 = (bf16[512,1024]{1,0:T(8,128)(2,1)}, f32[512,1024]{1,0:T(8,128)}) custom-call(bf16[256,1024]{1,0:T(8,128)(2,1)} %get-tuple-element.30.refs_0_, bf16[256,1024]{1,0:T(8,128)(2,1)} %copy-done.8, bf16[256,1024]{1,0:T(8,128)(2,1)} %copy-done.9, bf16[256,1024]{1,0:T(8,128)(2,1)} %collective-permute-done.5.refs_3_, bf16[256,1024]{1,0:T(8,128)(2,1)} %copy-done.1, ...), custom_call_target="tpu_custom_call" | custom-call | flops 2147483648 | bytes 4194304 | tf_op jit(solution)/shard_map/pallas_call | solution.py:121
  91.1 2.7 collective-permute-done.1.refs_2_
  93.8 4.6 %collective-permute-done.2.refs_3_ = bf16[256,1024]{1,0:T(8,128)(2,1)S(1)} collective-permute-done((bf16[256,1024]{1,0:T(8,128)(2,1)}, bf16[256,1024]{1,0:T(8,128)(2,1)S(1)}, u32[]{:S(2)}, u32[]{:S(2)}) %collective-permute-start.2) | collective-permute-done | bytes 524320 | tf_op jit(solution)/shard_map/ppermute | solution.py:34
  99.9 2.8 collective-permute-start.27
  103.9 6.4 %shard_map.69 = (bf16[512,1024]{1,0:T(8,128)(2,1)}, f32[512,1024]{1,0:T(8,128)}) custom-call(bf16[256,1024]{1,0:T(8,128)(2,1)} %get-tuple-element.26.refs_0_, bf16[256,1024]{1,0:T(8,128)(2,1)} %copy-done.10, bf16[256,1024]{1,0:T(8,128)(2,1)} %copy-done.11, bf16[256,1024]{1,0:T(8,128)(2,1)} %copy-done.12, bf16[256,1024]{1,0:T(8,128)(2,1)} %get-tuple-element.37.refs_4_, ...), custom_call_target="tpu_custom_call" | custom-call | flops 2147483648 | bytes 4194304 | tf_op jit(solution)/shard_map/pallas_call | solution.py:121
  112.1 2.9 collective-permute-start.30
  115.7 2.8 collective-permute-start.14
  119.1 5.6 %collective-permute-done.13 = bf16[128,1024]{1,0:T(8,128)(2,1)S(1)} collective-permute-done((bf16[128,1024]{1,0:T(8,128)(2,1)S(1)}, bf16[128,1024]{1,0:T(8,128)(2,1)S(1)}, u32[]{:S(2)}, u32[]{:S(2)}) %collective-permute-start.13) | collective-permute-done | bytes 262176 | tf_op jit(solution)/shard_map/ppermute | solution.py:34
  128.0 3.0 collective-permute-done.15
  135.0 5.3 %collective-permute-done.22 = bf16[128,1024]{1,0:T(8,128)(2,1)S(1)} collective-permute-done((bf16[128,1024]{1,0:T(8,128)(2,1)S(1)}, bf16[128,1024]{1,0:T(8,128)(2,1)S(1)}, u32[]{:S(2)}, u32[]{:S(2)}) %collective-permute-start.22) | collective-permute-done | bytes 262176 | tf_op jit(solution)/shard_map/ppermute | solution.py:34
  141.3 2.4 collective-permute-start.23
  144.3 2.7 collective-permute-start.25
  148.3 2.2 join.1
  152.7 3.4 %collective-permute-start.50 = (bf16[32,1024]{1,0:T(8,128)(2,1)S(1)}, bf16[32,1024]{1,0:T(8,128)(2,1)S(1)}, u32[]{:S(2)}, u32[]{:S(2)}) collective-permute-start(bf16[32,1024]{1,0:T(8,128)(2,1)S(1)} %multiply_convert_fusion.1), channel_id=1, source_target_pairs={{0,32},{32,0},{64,96},{96,64},{1,33},{33,1},{65,97},{97,65},{2,34}... | collective-permute-start | bytes 196616 | tf_op jit(solution)/shard_map/ppermute | solution.py:43
  157.8 2.1 collective-permute-start.33
  159.9 2.2 collective-permute-start.47
  166.4 5.9 %collective-permute-done.34 = bf16[2,32,1024]{2,1,0:T(8,128)(2,1)S(1)} collective-permute-done((bf16[2,32,1024]{2,1,0:T(8,128)(2,1)S(1)}, bf16[2,32,1024]{2,1,0:T(8,128)(2,1)S(1)}, u32[]{:S(2)}, u32[]{:S(2)}) %collective-permute-start.34) | collective-permute-done | bytes 131104 | tf_op jit(solution)/shard_map/ppermute | solution.py:43
  172.3 5.3 %collective-permute-start.52 = (bf16[128,1024]{1,0:T(8,128)(2,1)S(1)}, bf16[128,1024]{1,0:T(8,128)(2,1)S(1)}, u32[]{:S(2)}, u32[]{:S(2)}) collective-permute-start(bf16[128,1024]{1,0:T(8,128)(2,1)S(1)} %pad_maximum_fusion.2.refs_4_), channel_id=1, source_target_pairs={{0,1},{1,2},{2,3},{3,0},{4,5},{5,6},{6,7},{7,4},{8,9},{9,10},{10,1... | collective-permute-start | bytes 786440 | tf_op jit(solution)/shard_map/ppermute | solution.py:34
  177.6 2.6 collective-permute-start.53
  180.2 3.6 %collective-permute-done.46.refs_1_ = bf16[256,1024]{1,0:T(8,128)(2,1)S(1)} collective-permute-done((bf16[256,1024]{1,0:T(8,128)(2,1)S(1)}, bf16[256,1024]{1,0:T(8,128)(2,1)S(1)}, u32[]{:S(2)}, u32[]{:S(2)}) %collective-permute-start.46) | collective-permute-done | bytes 524320 | tf_op jit(solution)/shard_map/ppermute | solution.py:34
  183.8 6.8 %collective-permute-start.54 = (bf16[128,1024]{1,0:T(8,128)(2,1)S(1)}, bf16[128,1024]{1,0:T(8,128)(2,1)S(1)}, u32[]{:S(2)}, u32[]{:S(2)}) collective-permute-start(bf16[128,1024]{1,0:T(8,128)(2,1)S(1)} %pad_maximum_fusion.2.refs_4_), channel_id=1, source_target_pairs={{0,3},{1,0},{2,1},{3,2},{4,7},{5,4},{6,5},{7,6},{8,11},{9,8},{10,9... | collective-permute-start | bytes 786440 | tf_op jit(solution)/shard_map/ppermute | solution.py:34
  191.7 2.3 collective-permute-start.38
  194.6 11.5 %collective-permute-done.36.refs_1_ = bf16[128,1024]{1,0:T(8,128)(2,1)S(1)} collective-permute-done((bf16[128,1024]{1,0:T(8,128)(2,1)S(1)}, bf16[128,1024]{1,0:T(8,128)(2,1)S(1)}, u32[]{:S(2)}, u32[]{:S(2)}) %collective-permute-start.36) | collective-permute-done | bytes 262176 | tf_op jit(solution)/shard_map/ppermute | solution.py:34
  207.7 7.8 %collective-permute-done.60.refs_14_ = bf16[128,1024]{1,0:T(8,128)(2,1)} collective-permute-done((bf16[128,1024]{1,0:T(8,128)(2,1)S(1)}, bf16[128,1024]{1,0:T(8,128)(2,1)}, u32[]{:S(2)}, u32[]{:S(2)}) %collective-permute-start.60) | collective-permute-done | bytes 262176 | tf_op jit(solution)/shard_map/ppermute | solution.py:34
  216.1 4.3 %shard_map.67.turned = bf16[1024,1024]{1,0:T(8,128)(2,1)} custom-call(bf16[256,1024]{1,0:T(8,128)(2,1)} %get-tuple-element.26.refs_0_, bf16[256,1024]{1,0:T(8,128)(2,1)} %copy-done.10, bf16[256,1024]{1,0:T(8,128)(2,1)} %copy-done.11, bf16[256,1024]{1,0:T(8,128)(2,1)} %copy-done.12), custom_call_target="tpu_custom_call" | custom-call | flops 536870912 | bytes 4194304 | tf_op jit(solution)/shard_map/pallas_call | solution.py:150
  221.7 6.1 %grad_v.1 = (f32[256,1024]{1,0:T(8,128)}, bf16[256,1024]{1,0:T(8,128)(2,1)}, bf16[256,1024]{1,0:T(8,128)(2,1)}, bf16[256,1024]{1,0:T(8,128)(2,1)}) custom-call(bf16[1024,1024]{1,0:T(8,128)(2,1)} %shard_map.67.turned, bf16[128,1024]{1,0:T(8,128)(2,1)} %copy-done.19, bf16[128,1024]{1,0:T(8,128)(2,1)} %copy-done.31, bf16[128,1024]{1,0:T(8,128)(2,1)} %copy-done.33, ...), custom_call_target="tpu_custom_call" | custom-call | flops 2147483648 | bytes 8388608 | tf_op jit(solution)/shard_map/grad_v/pallas_call | solution.py:177
  228.2 4.2 %shard_map.70.turned = bf16[1024,1024]{1,0:T(8,128)(2,1)} custom-call(bf16[256,1024]{1,0:T(8,128)(2,1)} %get-tuple-element.30.refs_0_, bf16[256,1024]{1,0:T(8,128)(2,1)} %copy-done.8, bf16[256,1024]{1,0:T(8,128)(2,1)} %copy-done.9, bf16[256,1024]{1,0:T(8,128)(2,1)} %collective-permute-done.5.refs_3_), custom_call_target="tpu_custom_call" | custom-call | flops 536870912 | bytes 4194304 | tf_op jit(solution)/shard_map/pallas_call | solution.py:150
  236.0 11.1 %grad_u.1 = (f32[256,1024]{1,0:T(8,128)}, bf16[256,1024]{1,0:T(8,128)(2,1)}, bf16[256,1024]{1,0:T(8,128)(2,1)}, bf16[256,1024]{1,0:T(8,128)(2,1)}) custom-call(s32[5]{0:T(128)} %stack.39.at_ref, bf16[1024,1024]{1,0:T(8,128)(2,1)} %shard_map.70.turned, bf16[256,1024]{1,0:T(8,128)(2,1)} %copy-done.2, bf16[256,1024]{1,0:T(8,128)(2,1)} %copy-done.20, ...), custom_call_target="tpu_custom_call" | custom-call | flops 4294967296 | bytes 16777216 | tf_op jit(solution)/shard_map/grad_u/pallas_call | solution.py:230
  247.3 2.8 collective-permute-start.68
  250.1 9.3 %collective-permute-done.45 = bf16[256,1024]{1,0:T(8,128)(2,1)} collective-permute-done((bf16[256,1024]{1,0:T(8,128)(2,1)S(1)}, bf16[256,1024]{1,0:T(8,128)(2,1)}, u32[]{:S(2)}, u32[]{:S(2)}) %collective-permute-start.45) | collective-permute-done | bytes 524320 | tf_op jit(solution)/shard_map/ppermute | solution.py:34
  259.4 2.0 multiply_reduce_fusion
  263.9 9.5 %collective-permute-done.68 = bf16[256,1024]{1,0:T(8,128)(2,1)S(1)} collective-permute-done((bf16[256,1024]{1,0:T(8,128)(2,1)}, bf16[256,1024]{1,0:T(8,128)(2,1)S(1)}, u32[]{:S(2)}, u32[]{:S(2)}) %collective-permute-start.68) | collective-permute-done | bytes 524320 | tf_op jit(solution)/shard_map/ppermute | solution.py:34
  275.6 12.8 %all_to_all.22 = f32[16,8,128]{2,1,0:T(8,128)S(1)} all-to-all(f32[16,8,128]{2,1,0:T(8,128)S(1)} %broadcast_in_dim.19), channel_id=1, replica_groups=mesh['p'=2,'h'=2,'c'=2,'z'=4,'y'=4] {'z','y'}, dimensions={0} | all-to-all | bytes 131072 | tf_op jit(solution)/shard_map/all_to_all | solution.py:29
  289.6 8.4 %all_to_all.23 = f32[8,8,128]{2,1,0:T(8,128)S(1)} all-to-all(f32[8,8,128]{2,1,0:T(8,128)S(1)} %broadcast_in_dim.20), channel_id=1, replica_groups=mesh['p'=2,'h'=2,'c'=2,'z'=4,'y'=4] {'p','h','c'}, dimensions={0} | all-to-all | bytes 65536 | tf_op jit(solution)/shard_map/all_to_all | solution.py:29
  (220 shorter events, 54.0 us)
Async XLA Ops:
  3.8 13.5 %collective-permute-start.6 = (bf16[256,1024]{1,0:T(8,128)(2,1)S(1)}, bf16[256,1024]{1,0:T(8,128)(2,1)S(1)}, u32[]{:S(2)}, u32[]{:S(2)}) collective-permute-start(bf16[256,1024]{1,0:T(8,128)(2,1)S(1)} %get-tuple-element.34.refs_4_), channel_id=1, source_target_pairs={{0,64},{64,0},{1,65},{65,1},{2,66},{66,2},{3,67},{67,3},{4,68},{68... | collective-permute-start | bytes 1572872 | tf_op jit(solution)/shard_map/ppermute | solution.py:301
  5.4 24.6 %collective-permute-start.7 = (bf16[256,1024]{1,0:T(8,128)(2,1)S(1)}, bf16[256,1024]{1,0:T(8,128)(2,1)S(1)}, u32[]{:S(2)}, u32[]{:S(2)}) collective-permute-start(bf16[256,1024]{1,0:T(8,128)(2,1)S(1)} %get-tuple-element.34.refs_4_), channel_id=1, source_target_pairs={{0,16},{16,0},{1,17},{17,1},{2,18},{18,2},{3,19},{19,3},{4,20},{20... | collective-permute-start | bytes 1572872 | tf_op jit(solution)/shard_map/ppermute | solution.py:34
  17.3 12.6 %collective-permute-start.8 = (bf16[256,1024]{1,0:T(8,128)(2,1)S(1)}, bf16[256,1024]{1,0:T(8,128)(2,1)S(1)}, u32[]{:S(2)}, u32[]{:S(2)}) collective-permute-start(bf16[256,1024]{1,0:T(8,128)(2,1)S(1)} %collective-permute-done.6.refs_0_), channel_id=1, source_target_pairs={{0,16},{16,0},{1,17},{17,1},{2,18},{18,2},{3,19},{19,3},{4,20},{20... | collective-permute-start | bytes 1572872 | tf_op jit(solution)/shard_map/ppermute | solution.py:34
  23.1 21.4 %collective-permute-start.3 = (bf16[256,1024]{1,0:T(8,128)(2,1)}, bf16[256,1024]{1,0:T(8,128)(2,1)S(1)}, u32[]{:S(2)}, u32[]{:S(2)}) collective-permute-start(bf16[256,1024]{1,0:T(8,128)(2,1)} %get-tuple-element.31), channel_id=1, source_target_pairs={{0,1},{1,2},{2,3},{3,0},{4,5},{5,6},{6,7},{7,4},{8,9},{9,10},{10,1... | collective-permute-start | bytes 1572872 | tf_op jit(solution)/shard_map/ppermute | solution.py:34
  24.9 30.0 %collective-permute-start.4 = (bf16[256,1024]{1,0:T(8,128)(2,1)}, bf16[256,1024]{1,0:T(8,128)(2,1)S(1)}, u32[]{:S(2)}, u32[]{:S(2)}) collective-permute-start(bf16[256,1024]{1,0:T(8,128)(2,1)} %get-tuple-element.32), channel_id=1, source_target_pairs={{0,2},{1,3},{2,0},{3,1},{4,6},{5,7},{6,4},{7,5},{8,10},{9,11},{10,... | collective-permute-start | bytes 1572872 | tf_op jit(solution)/shard_map/ppermute | solution.py:34
  27.8 29.0 %collective-permute-start.5 = (bf16[256,1024]{1,0:T(8,128)(2,1)}, bf16[256,1024]{1,0:T(8,128)(2,1)}, u32[]{:S(2)}, u32[]{:S(2)}) collective-permute-start(bf16[256,1024]{1,0:T(8,128)(2,1)} %get-tuple-element.33), channel_id=1, source_target_pairs={{0,3},{1,0},{2,1},{3,2},{4,7},{5,4},{6,5},{7,6},{8,11},{9,8},{10,9... | collective-permute-start | bytes 1572872 | tf_op jit(solution)/shard_map/ppermute | solution.py:34
  31.6 28.8 %all-to-all-start = ((bf16[32,8,1024]{2,1,0:T(8,128)(2,1)}), bf16[32,8,1024]{2,1,0:T(8,128)(2,1)S(1)}, u32[]{:S(2)}, u32[]{:S(2)}) async-start(bf16[32,8,1024]{2,1,0:T(8,128)(2,1)} %bitcast.12), calls=%async_computation | async-start | bytes 1048576 | tf_op jit(solution)/shard_map/all_to_all | solution.py:29
  39.9 30.2 %collective-permute-start.10 = (bf16[256,1024]{1,0:T(8,128)(2,1)S(1)}, bf16[256,1024]{1,0:T(8,128)(2,1)}, u32[]{:S(2)}, u32[]{:S(2)}) collective-permute-start(bf16[256,1024]{1,0:T(8,128)(2,1)S(1)} %get-tuple-element.34.refs_4_), channel_id=1, source_target_pairs={{0,8},{4,12},{8,0},{12,4},{1,9},{5,13},{9,1},{13,5},{2,10},{6,14},... | collective-permute-start | bytes 1572872 | tf_op jit(solution)/shard_map/ppermute | solution.py:34
  43.3 29.8 %collective-permute-start.11 = (bf16[256,1024]{1,0:T(8,128)(2,1)S(1)}, bf16[256,1024]{1,0:T(8,128)(2,1)}, u32[]{:S(2)}, u32[]{:S(2)}) collective-permute-start(bf16[256,1024]{1,0:T(8,128)(2,1)S(1)} %get-tuple-element.34.refs_4_), channel_id=1, source_target_pairs={{0,12},{4,0},{8,4},{12,8},{1,13},{5,1},{9,5},{13,9},{2,14},{6,2},{... | collective-permute-start | bytes 1572872 | tf_op jit(solution)/shard_map/ppermute | solution.py:34
  44.5 31.1 %collective-permute-start.9 = (bf16[256,1024]{1,0:T(8,128)(2,1)S(1)}, bf16[256,1024]{1,0:T(8,128)(2,1)}, u32[]{:S(2)}, u32[]{:S(2)}) collective-permute-start(bf16[256,1024]{1,0:T(8,128)(2,1)S(1)} %get-tuple-element.34.refs_4_), channel_id=1, source_target_pairs={{0,4},{4,8},{8,12},{12,0},{1,5},{5,9},{9,13},{13,1},{2,6},{6,10},{... | collective-permute-start | bytes 1572872 | tf_op jit(solution)/shard_map/ppermute | solution.py:34
  55.0 29.3 %collective-permute-start = (bf16[256,1024]{1,0:T(8,128)(2,1)}, bf16[256,1024]{1,0:T(8,128)(2,1)S(1)}, u32[]{:S(2)}, u32[]{:S(2)}) collective-permute-start(bf16[256,1024]{1,0:T(8,128)(2,1)} %get-tuple-element.27), channel_id=1, source_target_pairs={{0,4},{4,8},{8,12},{12,0},{1,5},{5,9},{9,13},{13,1},{2,6},{6,10},{... | collective-permute-start | bytes 1572872 | tf_op jit(solution)/shard_map/ppermute | solution.py:34
  56.9 37.0 %collective-permute-start.1 = (bf16[256,1024]{1,0:T(8,128)(2,1)}, bf16[256,1024]{1,0:T(8,128)(2,1)S(1)}, u32[]{:S(2)}, u32[]{:S(2)}) collective-permute-start(bf16[256,1024]{1,0:T(8,128)(2,1)} %get-tuple-element.28), channel_id=1, source_target_pairs={{0,8},{4,12},{8,0},{12,4},{1,9},{5,13},{9,1},{13,5},{2,10},{6,14},... | collective-permute-start | bytes 1572872 | tf_op jit(solution)/shard_map/ppermute | solution.py:34
  70.1 29.8 %collective-permute-start.16 = (bf16[256,1024]{1,0:T(8,128)(2,1)}, bf16[256,1024]{1,0:T(8,128)(2,1)S(1)}, u32[]{:S(2)}, u32[]{:S(2)}) collective-permute-start(bf16[256,1024]{1,0:T(8,128)(2,1)} %get-tuple-element.37.refs_4_), channel_id=1, source_target_pairs={{0,1},{1,2},{2,3},{3,0},{4,5},{5,6},{6,7},{7,4},{8,9},{9,10},{10,1... | collective-permute-start | bytes 1572872 | tf_op jit(solution)/shard_map/ppermute | solution.py:34
  73.1 29.5 %collective-permute-start.17 = (bf16[256,1024]{1,0:T(8,128)(2,1)}, bf16[256,1024]{1,0:T(8,128)(2,1)}, u32[]{:S(2)}, u32[]{:S(2)}) collective-permute-start(bf16[256,1024]{1,0:T(8,128)(2,1)} %get-tuple-element.37.refs_4_), channel_id=1, source_target_pairs={{0,2},{1,3},{2,0},{3,1},{4,6},{5,7},{6,4},{7,5},{8,10},{9,11},{10,... | collective-permute-start | bytes 1572872 | tf_op jit(solution)/shard_map/ppermute | solution.py:34
  75.6 28.2 %collective-permute-start.18 = (bf16[256,1024]{1,0:T(8,128)(2,1)}, bf16[256,1024]{1,0:T(8,128)(2,1)}, u32[]{:S(2)}, u32[]{:S(2)}) collective-permute-start(bf16[256,1024]{1,0:T(8,128)(2,1)} %get-tuple-element.37.refs_4_), channel_id=1, source_target_pairs={{0,3},{1,0},{2,1},{3,2},{4,7},{5,4},{6,5},{7,6},{8,11},{9,8},{10,9... | collective-permute-start | bytes 1572872 | tf_op jit(solution)/shard_map/ppermute | solution.py:34
  84.3 14.1 %collective-permute-start.2 = (bf16[256,1024]{1,0:T(8,128)(2,1)}, bf16[256,1024]{1,0:T(8,128)(2,1)S(1)}, u32[]{:S(2)}, u32[]{:S(2)}) collective-permute-start(bf16[256,1024]{1,0:T(8,128)(2,1)} %get-tuple-element.29), channel_id=1, source_target_pairs={{0,12},{4,0},{8,4},{12,8},{1,13},{5,1},{9,5},{13,9},{2,14},{6,2},{... | collective-permute-start | bytes 1572872 | tf_op jit(solution)/shard_map/ppermute | solution.py:34
  93.8 21.2 %collective-permute-start.12 = (bf16[512,1024]{1,0:T(8,128)(2,1)}, bf16[512,1024]{1,0:T(8,128)(2,1)S(1)}, u32[]{:S(2)}, u32[]{:S(2)}) collective-permute-start(bf16[512,1024]{1,0:T(8,128)(2,1)} %get-tuple-element.36), channel_id=1, source_target_pairs={{0,16},{16,0},{1,17},{17,1},{2,18},{18,2},{3,19},{19,3},{4,20},{20... | collective-permute-start | bytes 3145736 | tf_op jit(solution)/shard_map/ppermute | solution.py:34
  98.4 11.9 %collective-permute-start.26 = (bf16[32,1024]{1,0:T(8,128)(2,1)S(1)}, bf16[32,1024]{1,0:T(8,128)(2,1)S(1)}, u32[]{:S(2)}, u32[]{:S(2)}) collective-permute-start(bf16[32,1024]{1,0:T(8,128)(2,1)S(1)} %bitcast.51), channel_id=1, source_target_pairs={{0,1},{1,2},{2,3},{3,0},{4,5},{5,6},{6,7},{7,4},{8,9},{9,10},{10,1... | collective-permute-start | bytes 196616 | tf_op jit(solution)/shard_map/ppermute | solution.py:34
  112.1 32.2 %collective-permute-start.29 = (bf16[128,1024]{1,0:T(8,128)(2,1)S(1)}, bf16[128,1024]{1,0:T(8,128)(2,1)S(1)}, u32[]{:S(2)}, u32[]{:S(2)}) collective-permute-start(bf16[128,1024]{1,0:T(8,128)(2,1)S(1)} %constant_dynamic-update-slice_fusion.refs_0_), channel_id=1, source_target_pairs={{0,4},{4,8},{8,12},{12,0},{1,5},{5,9},{9,13},{13,1},{2,6},{6,10},{... | collective-permute-start | bytes 786440 | tf_op jit(solution)/shard_map/ppermute | solution.py:34
  112.1 34.9 %collective-permute-start.30 = (bf16[128,1024]{1,0:T(8,128)(2,1)S(1)}, bf16[128,1024]{1,0:T(8,128)(2,1)S(1)}, u32[]{:S(2)}, u32[]{:S(2)}) collective-permute-start(bf16[128,1024]{1,0:T(8,128)(2,1)S(1)} %constant_dynamic-update-slice_fusion.refs_0_), channel_id=1, source_target_pairs={{0,8},{4,12},{8,0},{12,4},{1,9},{5,13},{9,1},{13,5},{2,10},{6,14},... | collective-permute-start | bytes 786440 | tf_op jit(solution)/shard_map/ppermute | solution.py:34
  115.7 10.7 %collective-permute-start.14 = (bf16[128,1024]{1,0:T(8,128)(2,1)S(1)}, bf16[128,1024]{1,0:T(8,128)(2,1)S(1)}, u32[]{:S(2)}, u32[]{:S(2)}) collective-permute-start(bf16[128,1024]{1,0:T(8,128)(2,1)S(1)} %get-tuple-element.74), channel_id=1, source_target_pairs={{0,2},{1,3},{2,0},{3,1},{4,6},{5,7},{6,4},{7,5},{8,10},{9,11},{10,... | collective-permute-start | bytes 786440 | tf_op jit(solution)/shard_map/ppermute | solution.py:34
  118.5 12.4 %collective-permute-start.15 = (bf16[128,1024]{1,0:T(8,128)(2,1)S(1)}, bf16[128,1024]{1,0:T(8,128)(2,1)S(1)}, u32[]{:S(2)}, u32[]{:S(2)}) collective-permute-start(bf16[128,1024]{1,0:T(8,128)(2,1)S(1)} %get-tuple-element.73), channel_id=1, source_target_pairs={{0,1},{1,2},{2,3},{3,0},{4,5},{5,6},{6,7},{7,4},{8,9},{9,10},{10,1... | collective-permute-start | bytes 786440 | tf_op jit(solution)/shard_map/ppermute | solution.py:34
  133.8 13.8 %collective-permute-start.31 = (bf16[128,1024]{1,0:T(8,128)(2,1)S(1)}, bf16[128,1024]{1,0:T(8,128)(2,1)S(1)}, u32[]{:S(2)}, u32[]{:S(2)}) collective-permute-start(bf16[128,1024]{1,0:T(8,128)(2,1)S(1)} %constant_dynamic-update-slice_fusion.refs_0_), channel_id=1, source_target_pairs={{0,12},{4,0},{8,4},{12,8},{1,13},{5,1},{9,5},{13,9},{2,14},{6,2},{... | collective-permute-start | bytes 786440 | tf_op jit(solution)/shard_map/ppermute | solution.py:34
  159.9 23.9 %collective-permute-start.46 = (bf16[256,1024]{1,0:T(8,128)(2,1)S(1)}, bf16[256,1024]{1,0:T(8,128)(2,1)S(1)}, u32[]{:S(2)}, u32[]{:S(2)}) collective-permute-start(bf16[256,1024]{1,0:T(8,128)(2,1)S(1)} %copy-done.3), channel_id=1, source_target_pairs={{0,4},{4,8},{8,12},{12,0},{1,5},{5,9},{9,13},{13,1},{2,6},{6,10},{... | collective-permute-start | bytes 1572872 | tf_op jit(solution)/shard_map/ppermute | solution.py:34
  159.9 30.7 %collective-permute-start.47 = (bf16[256,1024]{1,0:T(8,128)(2,1)S(1)}, bf16[256,1024]{1,0:T(8,128)(2,1)S(1)}, u32[]{:S(2)}, u32[]{:S(2)}) collective-permute-start(bf16[256,1024]{1,0:T(8,128)(2,1)S(1)} %copy-done.3), channel_id=1, source_target_pairs={{0,8},{4,12},{8,0},{12,4},{1,9},{5,13},{9,1},{13,5},{2,10},{6,14},... | collective-permute-start | bytes 1572872 | tf_op jit(solution)/shard_map/ppermute | solution.py:34
  162.1 28.4 %collective-permute-start.48 = (bf16[256,1024]{1,0:T(8,128)(2,1)S(1)}, bf16[256,1024]{1,0:T(8,128)(2,1)S(1)}, u32[]{:S(2)}, u32[]{:S(2)}) collective-permute-start(bf16[256,1024]{1,0:T(8,128)(2,1)S(1)} %copy-done.3), channel_id=1, source_target_pairs={{0,12},{4,0},{8,4},{12,8},{1,13},{5,1},{9,5},{13,9},{2,14},{6,2},{... | collective-permute-start | bytes 1572872 | tf_op jit(solution)/shard_map/ppermute | solution.py:34
  164.0 13.7 %collective-permute-start.35 = (bf16[2,32,1024]{2,1,0:T(8,128)(2,1)S(1)}, bf16[2,32,1024]{2,1,0:T(8,128)(2,1)S(1)}, u32[]{:S(2)}, u32[]{:S(2)}) collective-permute-start(bf16[2,32,1024]{2,1,0:T(8,128)(2,1)S(1)} %get-tuple-element.92), channel_id=1, source_target_pairs={{0,96},{32,64},{64,0},{96,32},{1,97},{33,65},{65,1},{97,33},{2,98}... | collective-permute-start | bytes 393224 | tf_op jit(solution)/shard_map/ppermute | solution.py:43
  172.3 18.4 %collective-permute-start.52 = (bf16[128,1024]{1,0:T(8,128)(2,1)S(1)}, bf16[128,1024]{1,0:T(8,128)(2,1)S(1)}, u32[]{:S(2)}, u32[]{:S(2)}) collective-permute-start(bf16[128,1024]{1,0:T(8,128)(2,1)S(1)} %pad_maximum_fusion.2.refs_4_), channel_id=1, source_target_pairs={{0,1},{1,2},{2,3},{3,0},{4,5},{5,6},{6,7},{7,4},{8,9},{9,10},{10,1... | collective-permute-start | bytes 786440 | tf_op jit(solution)/shard_map/ppermute | solution.py:34
  177.6 14.1 %collective-permute-start.53 = (bf16[128,1024]{1,0:T(8,128)(2,1)S(1)}, bf16[128,1024]{1,0:T(8,128)(2,1)S(1)}, u32[]{:S(2)}, u32[]{:S(2)}) collective-permute-start(bf16[128,1024]{1,0:T(8,128)(2,1)S(1)} %pad_maximum_fusion.2.refs_4_), channel_id=1, source_target_pairs={{0,2},{1,3},{2,0},{3,1},{4,6},{5,7},{6,4},{7,5},{8,10},{9,11},{10,... | collective-permute-start | bytes 786440 | tf_op jit(solution)/shard_map/ppermute | solution.py:34
  183.8 10.7 %collective-permute-start.54 = (bf16[128,1024]{1,0:T(8,128)(2,1)S(1)}, bf16[128,1024]{1,0:T(8,128)(2,1)S(1)}, u32[]{:S(2)}, u32[]{:S(2)}) collective-permute-start(bf16[128,1024]{1,0:T(8,128)(2,1)S(1)} %pad_maximum_fusion.2.refs_4_), channel_id=1, source_target_pairs={{0,3},{1,0},{2,1},{3,2},{4,7},{5,4},{6,5},{7,6},{8,11},{9,8},{10,9... | collective-permute-start | bytes 786440 | tf_op jit(solution)/shard_map/ppermute | solution.py:34
  190.6 15.5 %collective-permute-start.36 = (bf16[128,1024]{1,0:T(8,128)(2,1)S(1)}, bf16[128,1024]{1,0:T(8,128)(2,1)S(1)}, u32[]{:S(2)}, u32[]{:S(2)}) collective-permute-start(bf16[128,1024]{1,0:T(8,128)(2,1)S(1)} %pad_maximum_fusion.1.refs_0_), channel_id=1, source_target_pairs={{0,4},{4,8},{8,12},{12,0},{1,5},{5,9},{9,13},{13,1},{2,6},{6,10},{... | collective-permute-start | bytes 786440 | tf_op jit(solution)/shard_map/ppermute | solution.py:34
  190.7 15.4 %collective-permute-start.37 = (bf16[128,1024]{1,0:T(8,128)(2,1)S(1)}, bf16[128,1024]{1,0:T(8,128)(2,1)S(1)}, u32[]{:S(2)}, u32[]{:S(2)}) collective-permute-start(bf16[128,1024]{1,0:T(8,128)(2,1)S(1)} %pad_maximum_fusion.1.refs_0_), channel_id=1, source_target_pairs={{0,8},{4,12},{8,0},{12,4},{1,9},{5,13},{9,1},{13,5},{2,10},{6,14},... | collective-permute-start | bytes 786440 | tf_op jit(solution)/shard_map/ppermute | solution.py:34
  191.7 15.4 %collective-permute-start.38 = (bf16[128,1024]{1,0:T(8,128)(2,1)S(1)}, bf16[128,1024]{1,0:T(8,128)(2,1)S(1)}, u32[]{:S(2)}, u32[]{:S(2)}) collective-permute-start(bf16[128,1024]{1,0:T(8,128)(2,1)S(1)} %pad_maximum_fusion.1.refs_0_), channel_id=1, source_target_pairs={{0,12},{4,0},{8,4},{12,8},{1,13},{5,1},{9,5},{13,9},{2,14},{6,2},{... | collective-permute-start | bytes 786440 | tf_op jit(solution)/shard_map/ppermute | solution.py:34
  194.5 12.7 %collective-permute-start.39 = (bf16[128,1024]{1,0:T(8,128)(2,1)S(1)}, bf16[128,1024]{1,0:T(8,128)(2,1)}, u32[]{:S(2)}, u32[]{:S(2)}) collective-permute-start(bf16[128,1024]{1,0:T(8,128)(2,1)S(1)} %pad_maximum_fusion.1.refs_0_), channel_id=1, source_target_pairs={{0,16},{16,0},{1,17},{17,1},{2,18},{18,2},{3,19},{19,3},{4,20},{20... | collective-permute-start | bytes 786440 | tf_op jit(solution)/shard_map/ppermute | solution.py:34
  194.5 13.1 %collective-permute-start.59 = (bf16[128,1024]{1,0:T(8,128)(2,1)S(1)}, bf16[128,1024]{1,0:T(8,128)(2,1)}, u32[]{:S(2)}, u32[]{:S(2)}) collective-permute-start(bf16[128,1024]{1,0:T(8,128)(2,1)S(1)} %pad_maximum_fusion.3.refs_12_), channel_id=1, source_target_pairs={{0,1},{1,2},{2,3},{3,0},{4,5},{5,6},{6,7},{7,4},{8,9},{9,10},{10,1... | collective-permute-start | bytes 786440 | tf_op jit(solution)/shard_map/ppermute | solution.py:34
  207.1 13.4 %collective-permute-start.56 = (bf16[128,1024]{1,0:T(8,128)(2,1)S(1)}, bf16[128,1024]{1,0:T(8,128)(2,1)S(1)}, u32[]{:S(2)}, u32[]{:S(2)}) collective-permute-start(bf16[128,1024]{1,0:T(8,128)(2,1)S(1)} %collective-permute-done.52.refs_5_), channel_id=1, source_target_pairs={{0,16},{16,0},{1,17},{17,1},{2,18},{18,2},{3,19},{19,3},{4,20},{20... | collective-permute-start | bytes 786440 | tf_op jit(solution)/shard_map/ppermute | solution.py:34
  207.6 13.5 %collective-permute-start.40 = (bf16[128,1024]{1,0:T(8,128)(2,1)S(1)}, bf16[128,1024]{1,0:T(8,128)(2,1)}, u32[]{:S(2)}, u32[]{:S(2)}) collective-permute-start(bf16[128,1024]{1,0:T(8,128)(2,1)S(1)} %collective-permute-done.36.refs_1_), channel_id=1, source_target_pairs={{0,16},{16,0},{1,17},{17,1},{2,18},{18,2},{3,19},{19,3},{4,20},{20... | collective-permute-start | bytes 786440 | tf_op jit(solution)/shard_map/ppermute | solution.py:34
  216.1 11.8 %collective-permute-start.57 = (bf16[128,1024]{1,0:T(8,128)(2,1)S(1)}, bf16[128,1024]{1,0:T(8,128)(2,1)}, u32[]{:S(2)}, u32[]{:S(2)}) collective-permute-start(bf16[128,1024]{1,0:T(8,128)(2,1)S(1)} %collective-permute-done.53.refs_6_), channel_id=1, source_target_pairs={{0,16},{16,0},{1,17},{17,1},{2,18},{18,2},{3,19},{19,3},{4,20},{20... | collective-permute-start | bytes 786440 | tf_op jit(solution)/shard_map/ppermute | solution.py:34
  220.5 11.9 %collective-permute-start.58 = (bf16[128,1024]{1,0:T(8,128)(2,1)S(1)}, bf16[128,1024]{1,0:T(8,128)(2,1)S(1)}, u32[]{:S(2)}, u32[]{:S(2)}) collective-permute-start(bf16[128,1024]{1,0:T(8,128)(2,1)S(1)} %collective-permute-done.54.refs_7_), channel_id=1, source_target_pairs={{0,16},{16,0},{1,17},{17,1},{2,18},{18,2},{3,19},{19,3},{4,20},{20... | collective-permute-start | bytes 786440 | tf_op jit(solution)/shard_map/ppermute | solution.py:34
  221.1 13.1 %collective-permute-start.63 = (bf16[128,1024]{1,0:T(8,128)(2,1)}, bf16[128,1024]{1,0:T(8,128)(2,1)S(1)}, u32[]{:S(2)}, u32[]{:S(2)}) collective-permute-start(bf16[128,1024]{1,0:T(8,128)(2,1)} %collective-permute-done.59.refs_13_), channel_id=1, source_target_pairs={{0,16},{16,0},{1,17},{17,1},{2,18},{18,2},{3,19},{19,3},{4,20},{20... | collective-permute-start | bytes 786440 | tf_op jit(solution)/shard_map/ppermute | solution.py:34
  221.2 14.8 %collective-permute-start.64 = (bf16[128,1024]{1,0:T(8,128)(2,1)}, bf16[128,1024]{1,0:T(8,128)(2,1)}, u32[]{:S(2)}, u32[]{:S(2)}) collective-permute-start(bf16[128,1024]{1,0:T(8,128)(2,1)} %collective-permute-done.60.refs_14_), channel_id=1, source_target_pairs={{0,16},{16,0},{1,17},{17,1},{2,18},{18,2},{3,19},{19,3},{4,20},{20... | collective-permute-start | bytes 786440 | tf_op jit(solution)/shard_map/ppermute | solution.py:34
  221.6 14.4 %collective-permute-start.65 = (bf16[128,1024]{1,0:T(8,128)(2,1)}, bf16[128,1024]{1,0:T(8,128)(2,1)}, u32[]{:S(2)}, u32[]{:S(2)}) collective-permute-start(bf16[128,1024]{1,0:T(8,128)(2,1)} %collective-permute-done.61.refs_15_), channel_id=1, source_target_pairs={{0,16},{16,0},{1,17},{17,1},{2,18},{18,2},{3,19},{19,3},{4,20},{20... | collective-permute-start | bytes 786440 | tf_op jit(solution)/shard_map/ppermute | solution.py:34
  227.8 19.5 %collective-permute-start.43 = (bf16[256,1024]{1,0:T(8,128)(2,1)}, bf16[256,1024]{1,0:T(8,128)(2,1)S(1)}, u32[]{:S(2)}, u32[]{:S(2)}) collective-permute-start(bf16[256,1024]{1,0:T(8,128)(2,1)} %get-tuple-element.42), channel_id=1, source_target_pairs={{0,3},{1,0},{2,1},{3,2},{4,7},{5,4},{6,5},{7,6},{8,11},{9,8},{10,9... | collective-permute-start | bytes 1572872 | tf_op jit(solution)/shard_map/ppermute | solution.py:34
  232.4 17.7 %collective-permute-start.44 = (bf16[256,1024]{1,0:T(8,128)(2,1)S(1)}, bf16[256,1024]{1,0:T(8,128)(2,1)S(1)}, u32[]{:S(2)}, u32[]{:S(2)}) collective-permute-start(bf16[256,1024]{1,0:T(8,128)(2,1)S(1)} %copy-done.24), channel_id=1, source_target_pairs={{0,2},{1,3},{2,0},{3,1},{4,6},{5,7},{6,4},{7,5},{8,10},{9,11},{10,... | collective-permute-start | bytes 1572872 | tf_op jit(solution)/shard_map/ppermute | solution.py:34
  234.9 24.5 %collective-permute-start.45 = (bf16[256,1024]{1,0:T(8,128)(2,1)S(1)}, bf16[256,1024]{1,0:T(8,128)(2,1)}, u32[]{:S(2)}, u32[]{:S(2)}) collective-permute-start(bf16[256,1024]{1,0:T(8,128)(2,1)S(1)} %copy-done.23), channel_id=1, source_target_pairs={{0,1},{1,2},{2,3},{3,0},{4,5},{5,6},{6,7},{7,4},{8,9},{9,10},{10,1... | collective-permute-start | bytes 1572872 | tf_op jit(solution)/shard_map/ppermute | solution.py:34
  247.1 15.1 %collective-permute-start.66 = (bf16[256,1024]{1,0:T(8,128)(2,1)}, bf16[256,1024]{1,0:T(8,128)(2,1)S(1)}, u32[]{:S(2)}, u32[]{:S(2)}) collective-permute-start(bf16[256,1024]{1,0:T(8,128)(2,1)} %get-tuple-element.46), channel_id=1, source_target_pairs={{0,12},{4,0},{8,4},{12,8},{1,13},{5,1},{9,5},{13,9},{2,14},{6,2},{... | collective-permute-start | bytes 1572872 | tf_op jit(solution)/shard_map/ppermute | solution.py:34
  247.2 16.6 %collective-permute-start.67 = (bf16[256,1024]{1,0:T(8,128)(2,1)}, bf16[256,1024]{1,0:T(8,128)(2,1)S(1)}, u32[]{:S(2)}, u32[]{:S(2)}) collective-permute-start(bf16[256,1024]{1,0:T(8,128)(2,1)} %get-tuple-element.47), channel_id=1, source_target_pairs={{0,8},{4,12},{8,0},{12,4},{1,9},{5,13},{9,1},{13,5},{2,10},{6,14},... | collective-permute-start | bytes 1572872 | tf_op jit(solution)/shard_map/ppermute | solution.py:34
  247.3 26.0 %collective-permute-start.68 = (bf16[256,1024]{1,0:T(8,128)(2,1)}, bf16[256,1024]{1,0:T(8,128)(2,1)S(1)}, u32[]{:S(2)}, u32[]{:S(2)}) collective-permute-start(bf16[256,1024]{1,0:T(8,128)(2,1)} %get-tuple-element.48), channel_id=1, source_target_pairs={{0,4},{4,8},{8,12},{12,0},{1,5},{5,9},{9,13},{13,1},{2,6},{6,10},{... | collective-permute-start | bytes 1572872 | tf_op jit(solution)/shard_map/ppermute | solution.py:34
  (59 other events, 809.2 us)

commit v3 on v2

--- a/solution.py
+++ b/solution.py
@@ -117,14 +117,14 @@
 def project(blocks, weights):
     tok, wide = blocks[0].shape
     own, hidden = weights[0].shape
-    tile = hidden // 4
+    tile = hidden // 2
     return pl.pallas_call(
         project_kernel,
         out_shape=[
             jax.ShapeDtypeStruct((2 * tok, hidden), BF),
             jax.ShapeDtypeStruct((2 * tok, hidden), F32),
         ],
-        grid=(4,),
+        grid=(2,),
         in_specs=[pl.BlockSpec((tok, wide), lambda n: (0, 0))] * 4
         + [pl.BlockSpec((own, tile), lambda n: (0, n))] * 4,
         out_specs=[pl.BlockSpec((2 * tok, tile), lambda n: (0, n))] * 2,
@@ -150,9 +150,9 @@
     return pl.pallas_call(
         turn_kernel,
         out_shape=jax.ShapeDtypeStruct((wide, 4 * tok), BF),
-        grid=(4,),
-        in_specs=[pl.BlockSpec((tok, wide // 4), lambda j: (0, j))] * 4,
-        out_specs=pl.BlockSpec((wide // 4, 4 * tok), lambda j: (j, 0)),
+        grid=(2,),
+        in_specs=[pl.BlockSpec((tok, wide // 2), lambda j: (0, j))] * 4,
+        out_specs=pl.BlockSpec((wide // 2, 4 * tok), lambda j: (j, 0)),
         cost_estimate=pl.CostEstimate(
             flops=2 * tok * wide * wide, bytes_accessed=16 * tok * wide, transcendentals=0
         ),
@@ -173,11 +173,11 @@
 def grad_v_call(turned, pieces):
     wide, tok = turned.shape
     half, hidden = pieces[0].shape
-    own, tile = wide // 4, hidden // 4
+    own, tile = wide // 4, hidden // 2
     return pl.pallas_call(
         grad_v_kernel,
         out_shape=[jax.ShapeDtypeStruct((own, hidden), t) for t in (F32, BF, BF, BF)],
-        grid=(4,),
+        grid=(2,),
         in_specs=[pl.BlockSpec((wide, tok), lambda n: (0, 0))]
         + [pl.BlockSpec((half, tile), lambda n: (0, n))] * 8,
         out_specs=[pl.BlockSpec((own, tile), lambda n: (0, n))] * 4,
@@ -189,11 +189,11 @@
 
 
 def grad_u_kernel(at_ref, turned, *refs):
-    w_refs, acts, slopes, outs = refs[:4], refs[4:12], refs[12:20], refs[20:24]
-    fold, factor, right, left = refs[24:]
+    w_refs, pairs, outs = refs[:4], refs[4:12], refs[12:16]
+    fold, factor, right, left = refs[16:]
     s = pl.program_id(0)
     own = w_refs[0].shape[0]
-    half = acts[0].shape[0]
+    half = pairs[0].shape[1]
     tile = turned.shape[1]
     first = at_ref[0] == 0
 
@@ -202,39 +202,39 @@
         for j in range(4):
             fold[j * own : (j + 1) * own, :] = w_refs[j][...]
         for i in range(8):
-            act, slope = acts[i][...], slopes[i][...]
+            act, slope = pairs[i][0], pairs[i][1]
             right[i * half : (i + 1) * half, :] = jnp.where(first, act, slope)
             factor[i * half : (i + 1) * half, :] = jnp.where(first, slope, act)
 
-    @pl.when(s < 4)
+    @pl.when(s < 2)
     def _():
         at = pl.ds(pl.multiple_of(s * tile, tile), tile)
         total = turned[...].astype(F32) + dot_t1(fold[...], factor[at, :])
         left[:, at] = total.astype(BF)
 
-    @pl.when(s >= 4)
+    @pl.when(s >= 2)
     def _():
         width = outs[0].shape[1]
-        at = pl.ds(pl.multiple_of((s - 4) * width, width), width)
+        at = pl.ds(pl.multiple_of((s - 2) * width, width), width)
         split_rows(outs, dot(left[...], right[:, at]))
 
 
-def grad_u_call(at, turned, act, slope, weights):
+def grad_u_call(at, turned, pairs, weights):
     wide, tok = turned.shape
-    hidden = act[0].shape[1]
-    own, tile = wide // 4, hidden // 4
+    hidden = pairs[0].shape[2]
+    own, tile = wide // 4, hidden // 2
 
     def late(s):
-        return jnp.maximum(s - 4, 0)
+        return jnp.maximum(s - 2, 0)
 
     return pl.pallas_call(
         grad_u_kernel,
         out_shape=[jax.ShapeDtypeStruct((own, hidden), t) for t in (F32, BF, BF, BF)],
-        grid=(8,),
+        grid=(4,),
         in_specs=[pl.BlockSpec(memory_space=pltpu.SMEM)]
-        + [pl.BlockSpec((wide, tok // 4), lambda s: (0, jnp.minimum(s, 3)))]
+        + [pl.BlockSpec((wide, tok // 2), lambda s: (0, jnp.minimum(s, 1)))]
         + [pl.BlockSpec((own, hidden), lambda s: (0, 0))] * 4
-        + [pl.BlockSpec((tok // 8, hidden), lambda s: (0, 0))] * 16,
+        + [pl.BlockSpec((2, tok // 8, hidden), lambda s: (0, 0, 0))] * 8,
         out_specs=[pl.BlockSpec((own, tile), lambda s: (0, late(s)))] * 4,
         scratch_shapes=[
             pltpu.VMEM((wide, hidden), BF),
@@ -246,7 +246,7 @@
             flops=4 * tok * wide * hidden, bytes_accessed=16 * tok * wide, transcendentals=0
         ),
         name="grad_u",
-    )(at, turned, *weights, *act, *slope)
+    )(at, turned, *weights, *pairs)
 
 
 def join_kernel(at_ref, *refs):
@@ -343,9 +343,6 @@
     pre1, up1 = layer1[:, :hidden], layer1[:, hidden:]
     side = hidden // 2
     act0 = silu_bf(pre0)
-    act_near = jnp.concatenate([act0] + [shift_x(act0, k) for k in (1, 2, 3)])
-    act_near = gather(act_near, "y")
-    act_near += [shift(a, "c", 1) for a in act_near]
     low, high = act0[:, :side], act0[:, side:]
     near, far = jnp.where(c == 0, low, high), jnp.where(c == 0, high, low)
     pre1 = pre1 + dot(near, m_near) + dot(far, m_far)
@@ -355,18 +352,20 @@
     low, high = jnp.where(c == 0, near, far), jnp.where(c == 0, far, near)
     slope0 = slope_bf(up0 + jnp.concatenate([low, high], 1), pre0)
 
-    same = jnp.stack([jnp.where(first, slope0, act1), slope1])
-    other = jnp.stack([jnp.where(first, act1, slope0), slope1])
+    same = jnp.stack([jnp.where(first, slope0, act1), act0, slope1])
+    other = jnp.stack([jnp.where(first, act1, slope0), act0, slope1])
     got = [same, shift_x(other, 1), shift_x(same, 2), shift_x(other, 3)]
-    r_near = jnp.concatenate([g[0] for g in got])
-    s_near = jnp.concatenate([g[1] for g in got])
-    r_near = gather(r_near, "z")
-    s_near = gather(s_near, "y")
-    r_near += [shift(a, "c", 1) for a in r_near]
-    s_near += [shift(a, "c", 1) for a in s_near]
-
-    g_v = sum_back(grad_v_call(turn(vs), r_near), "y")
-    g_u = sum_back(grad_u_call(at, turn(us), act_near, s_near, w_3s), "z")
+    back = jnp.concatenate(got, 1)
+    rs = gather(back[0], "z")
+    pairs = gather(back[1:], "y")
+    rs += [shift(a, "c", 1) for a in rs]
+    pair_own = shift(pairs[0], "c", 1)
+    pairs += [pair_own] + [shift(a, "c", 1) for a in pairs[1:]]
+
+    g_v = grad_v_call(turn(vs), rs)
+    g_v = sum_back(g_v, "y")
+    g_u = grad_u_call(at, turn(us), pairs, w_3s)
+    g_u = sum_back(g_u, "z")
 
     squares = jnp.sum(g_u * g_u) + jnp.sum(g_v * g_v)
     for axes, count in ((("z", "y"), 16), (("p", "h", "c"), 8)):

time: 305 us -> 295 us (0.967)
  starting transfers between devices: 95 us -> 87.5 us
  Pallas kernels: 45.7 us -> 40.1 us
    ppermute x9 -> x6, starting transfers between devices: 14.1 us -> 8.99 us  [shift_x(): return lax.ppermute(value, ('p', 'h'), pairs)]
    ppermute x59 -> x52, starting transfers between devices: 71 us -> 68.5 us  [shift(): lax.ppermute(value, axis, [(i, (i + by) % count) for i in range(count)])]
    unnamed x79 -> x59, local copies, waits for them, and re-layouts: 5.63 us -> 8.1 us
    ppermute x59 -> x52, waiting for transfers between devices: 86.4 us -> 88.6 us  [shift(): lax.ppermute(value, axis, [(i, (i + by) % count) for i in range(count)])]
    ppermute x9 -> x6, waiting for transfers between devices: 6.27 us -> 7.45 us  [shift_x(): return lax.ppermute(value, ('p', 'h'), pairs)]
  transfers between devices with their start and end apart: 70 -> 60, of which waited for: 21 -> 23; matrix products, arithmetic and copies ran while one was open for 4% -> 3% of each run, Pallas kernels for 15% -> 14%
where the time goes in v3:
time: 295 us; the launch traced here: 294 us
  waiting for transfers between devices  108 us (37%)
  starting transfers between devices  87.5 us (30%)
  Pallas kernels  40.1 us (14%)
  blocking collectives  30.2 us (10%)
  local copies, waits for them, and re-layouts  10.5 us (4%)
  other arithmetic  9.99 us (3%)
  between operations  4.32 us (1%)
  matrix products  2.99 us (1%)
    ppermute x52, waiting for transfers between devices, shift(): lax.ppermute(value, axis, [(i, (i + by) % count) for i in range(count)])  88.6 us
    ppermute x52, starting transfers between devices, shift(): lax.ppermute(value, axis, [(i, (i + by) % count) for i in range(count)])  68.5 us
    all_to_all x3, blocking collectives, a2a(): return lax.all_to_all(value, axes, 0, 0, tiled=True)  30.2 us
    ppermute x1, waiting for transfers between devices, on_device(): w_3 = lax.ppermute(w_u, 'p', [(0, 1), (1, 0)])  11.9 us
    pallas_call x2, Pallas kernels, project(): pl.pallas_call(project_kernel, out_shape=[jax.ShapeDtypeStruct((2 * tok,...  11.3 us
    pallas_call x1, Pallas kernels, grad_u_call(): pl.pallas_call(grad_u_kernel, out_shape=[jax.ShapeDtypeStruct((own, hidde...  9.96 us
    ppermute x6, starting transfers between devices, shift_x(): return lax.ppermute(value, ('p', 'h'), pairs)  8.99 us
    all_to_all x1, starting transfers between devices, a2a(): return lax.all_to_all(value, axes, 0, 0, tiled=True)  8.28 us
  transfers between devices with their start and end apart: 60, of which 23 were waited for; matrix products, arithmetic and copies ran while one was open for 3% of the time, Pallas kernels for 14%

profile of v3, /device:TPU:0, one launch (start us, length us, event | category | flops | bytes accessed | tf_op | source)
XLA Modules:
  0.0 293.6 jit_solution(1494485073140949076)
XLA Ops:
  4.7 11.9 %collective-permute-done.6.refs_0_ = bf16[256,1024]{1,0:T(8,128)(2,1)S(1)} collective-permute-done((bf16[256,1024]{1,0:T(8,128)(2,1)S(1)}, bf16[256,1024]{1,0:T(8,128)(2,1)S(1)}, u32[]{:S(2)}, u32[]{:S(2)}) %collective-permute-start.6) | collective-permute-done | bytes 524320 | tf_op jit(solution)/shard_map/ppermute | solution.py:301
  17.4 5.0 %cut.1 = (bf16[256,1024]{1,0:T(8,128)(2,1)}, bf16[256,1024]{1,0:T(8,128)(2,1)}, bf16[256,1024]{1,0:T(8,128)(2,1)}, bf16[256,1024]{1,0:T(8,128)(2,1)}, bf16[256,1...) custom-call(s32[5]{0:T(128)} %stack.43.at_ref, ...), custom_call_target="tpu_custom_call" | custom-call | tf_op jit(solution)/shard_map/cut/pallas_call | solution.py:90
  24.2 2.9 collective-permute-start.4
  30.9 8.3 %all-to-all-start = ((bf16[32,8,1024]{2,1,0:T(8,128)(2,1)}), bf16[32,8,1024]{2,1,0:T(8,128)(2,1)S(1)}, u32[]{:S(2)}, u32[]{:S(2)}) async-start(bf16[32,8,1024]{2,1,0:T(8,128)(2,1)} %bitcast.12), calls=%async_computation | async-start | bytes 1048576 | tf_op jit(solution)/shard_map/all_to_all | solution.py:29
  39.2 3.4 %collective-permute-start.10 = (bf16[256,1024]{1,0:T(8,128)(2,1)S(1)}, bf16[256,1024]{1,0:T(8,128)(2,1)}, u32[]{:S(2)}, u32[]{:S(2)}) collective-permute-start(bf16[256,1024]{1,0:T(8,128)(2,1)S(1)} %get-tuple-element.34.refs_4_), channel_id=1, source_target_pairs={{0,8},{4,12},{8,0},{12,4},{1,9},{5,13},{9,1},{13,5},{2,10},{6,14},... | collective-permute-start | bytes 1572872 | tf_op jit(solution)/shard_map/ppermute | solution.py:34
  44.7 9.7 %collective-permute-done.4.refs_2_ = bf16[256,1024]{1,0:T(8,128)(2,1)} collective-permute-done((bf16[256,1024]{1,0:T(8,128)(2,1)}, bf16[256,1024]{1,0:T(8,128)(2,1)}, u32[]{:S(2)}, u32[]{:S(2)}) %collective-permute-start.4) | collective-permute-done | bytes 524320 | tf_op jit(solution)/shard_map/ppermute | solution.py:34
  54.4 1.9 collective-permute-start
  56.3 3.6 %collective-permute-start.1 = (bf16[256,1024]{1,0:T(8,128)(2,1)}, bf16[256,1024]{1,0:T(8,128)(2,1)}, u32[]{:S(2)}, u32[]{:S(2)}) collective-permute-start(bf16[256,1024]{1,0:T(8,128)(2,1)} %get-tuple-element.28), channel_id=1, source_target_pairs={{0,8},{4,12},{8,0},{12,4},{1,9},{5,13},{9,1},{13,5},{2,10},{6,14},... | collective-permute-start | bytes 1572872 | tf_op jit(solution)/shard_map/ppermute | solution.py:34
  60.0 9.5 %all_to_all.21 = bf16[4,8,1024]{2,1,0:T(8,128)(2,1)S(1)} all-to-all(bf16[4,8,1024]{2,1,0:T(8,128)(2,1)S(1)} %broadcast_in_dim.18), channel_id=1, replica_groups=mesh['p'=2,'h'=2,'c'=2,'z'=4,'y'=4] {'p','h'}, dimensions={0} | all-to-all | bytes 131072 | tf_op jit(solution)/shard_map/all_to_all | solution.py:29
  72.4 2.5 collective-permute-start.17
  74.9 1.9 collective-permute-start.18
  76.8 6.7 %collective-permute-done.refs_1_ = bf16[256,1024]{1,0:T(8,128)(2,1)S(1)} collective-permute-done((bf16[256,1024]{1,0:T(8,128)(2,1)}, bf16[256,1024]{1,0:T(8,128)(2,1)S(1)}, u32[]{:S(2)}, u32[]{:S(2)}) %collective-permute-start) | collective-permute-done | bytes 524320 | tf_op jit(solution)/shard_map/ppermute | solution.py:34
  84.1 5.6 %shard_map.68 = (bf16[512,1024]{1,0:T(8,128)(2,1)}, f32[512,1024]{1,0:T(8,128)}) custom-call(bf16[256,1024]{1,0:T(8,128)(2,1)} %get-tuple-element.30.refs_0_, bf16[256,1024]{1,0:T(8,128)(2,1)} %copy-done.8, bf16[256,1024]{1,0:T(8,128)(2,1)} %collective-permute-done.4.refs_2_, bf16[256,1024]{1,0:T(8,128)(2,1)} %collective-permute-done.5.refs_3_, ...), custom_call_target="tpu_custom_call" | custom-call | flops 2147483648 | bytes 4194304 | tf_op jit(solution)/shard_map/pallas_call | solution.py:121
  89.8 3.5 %collective-permute-done.1.refs_2_ = bf16[256,1024]{1,0:T(8,128)(2,1)} collective-permute-done((bf16[256,1024]{1,0:T(8,128)(2,1)}, bf16[256,1024]{1,0:T(8,128)(2,1)}, u32[]{:S(2)}, u32[]{:S(2)}) %collective-permute-start.1) | collective-permute-done | bytes 524320 | tf_op jit(solution)/shard_map/ppermute | solution.py:34
  93.2 4.7 %collective-permute-done.2.refs_3_ = bf16[256,1024]{1,0:T(8,128)(2,1)} collective-permute-done((bf16[256,1024]{1,0:T(8,128)(2,1)}, bf16[256,1024]{1,0:T(8,128)(2,1)}, u32[]{:S(2)}, u32[]{:S(2)}) %collective-permute-start.2) | collective-permute-done | bytes 524320 | tf_op jit(solution)/shard_map/ppermute | solution.py:34
  99.3 2.8 collective-permute-start.27
  103.2 5.7 %shard_map.69 = (bf16[512,1024]{1,0:T(8,128)(2,1)}, f32[512,1024]{1,0:T(8,128)}) custom-call(bf16[256,1024]{1,0:T(8,128)(2,1)} %get-tuple-element.26.refs_0_, bf16[256,1024]{1,0:T(8,128)(2,1)} %copy-done.9, bf16[256,1024]{1,0:T(8,128)(2,1)} %collective-permute-done.1.refs_2_, bf16[256,1024]{1,0:T(8,128)(2,1)} %collective-permute-done.2.refs_3_, ...), custom_call_target="tpu_custom_call" | custom-call | flops 2147483648 | bytes 4194304 | tf_op jit(solution)/shard_map/pallas_call | solution.py:121
  109.0 2.9 %collective-permute-start.30 = (bf16[128,1024]{1,0:T(8,128)(2,1)S(1)}, bf16[128,1024]{1,0:T(8,128)(2,1)S(1)}, u32[]{:S(2)}, u32[]{:S(2)}) collective-permute-start(bf16[128,1024]{1,0:T(8,128)(2,1)S(1)} %constant_dynamic-update-slice_fusion.refs_0_), channel_id=1, source_target_pairs={{0,8},{4,12},{8,0},{12,4},{1,9},{5,13},{9,1},{13,5},{2,10},{6,14},... | collective-permute-start | bytes 786440 | tf_op jit(solution)/shard_map/ppermute | solution.py:34
  112.0 2.2 fusion.35
  114.5 2.8 collective-permute-start.14
  117.9 5.6 %collective-permute-done.13 = bf16[128,1024]{1,0:T(8,128)(2,1)S(1)} collective-permute-done((bf16[128,1024]{1,0:T(8,128)(2,1)S(1)}, bf16[128,1024]{1,0:T(8,128)(2,1)S(1)}, u32[]{:S(2)}, u32[]{:S(2)}) %collective-permute-start.13) | collective-permute-done | bytes 262176 | tf_op jit(solution)/shard_map/ppermute | solution.py:34
  126.7 3.0 %collective-permute-done.15 = bf16[128,1024]{1,0:T(8,128)(2,1)S(1)} collective-permute-done((bf16[128,1024]{1,0:T(8,128)(2,1)S(1)}, bf16[128,1024]{1,0:T(8,128)(2,1)S(1)}, u32[]{:S(2)}, u32[]{:S(2)}) %collective-permute-start.15) | collective-permute-done | bytes 262176 | tf_op jit(solution)/shard_map/ppermute | solution.py:34
  133.7 5.4 %collective-permute-done.22 = bf16[128,1024]{1,0:T(8,128)(2,1)S(1)} collective-permute-done((bf16[128,1024]{1,0:T(8,128)(2,1)S(1)}, bf16[128,1024]{1,0:T(8,128)(2,1)S(1)}, u32[]{:S(2)}, u32[]{:S(2)}) %collective-permute-start.22) | collective-permute-done | bytes 262176 | tf_op jit(solution)/shard_map/ppermute | solution.py:34
  139.3 2.5 collective-permute-start.23
  142.4 2.6 collective-permute-start.25
  146.5 2.2 join.1
  156.3 2.3 collective-permute-start.47
  158.6 6.8 %collective-permute-done.33 = bf16[3,32,1024]{2,1,0:T(8,128)(2,1)S(1)} collective-permute-done((bf16[3,32,1024]{2,1,0:T(8,128)(2,1)S(1)}, bf16[3,32,1024]{2,1,0:T(8,128)(2,1)S(1)}, u32[]{:S(2)}, u32[]{:S(2)}) %collective-permute-start.33) | collective-permute-done | bytes 196640 | tf_op jit(solution)/shard_map/ppermute | solution.py:43
  166.2 2.3 collective-permute-start.37
  168.5 5.2 %collective-permute-start.49 = (bf16[2,128,1024]{2,1,0:T(8,128)(2,1)S(1)}, bf16[2,128,1024]{2,1,0:T(8,128)(2,1)}, u32[]{:S(2)}, u32[]{:S(2)}) collective-permute-start(bf16[2,128,1024]{2,1,0:T(8,128)(2,1)S(1)} %pad_maximum_fusion.1.refs_4_), channel_id=1, source_target_pairs={{0,1},{1,2},{2,3},{3,0},{4,5},{5,6},{6,7},{7,4},{8,9},{9,10},{10,1... | collective-permute-start | bytes 1572872 | tf_op jit(solution)/shard_map/ppermute | solution.py:34
  173.7 9.8 %collective-permute-done.46.refs_1_ = bf16[256,1024]{1,0:T(8,128)(2,1)S(1)} collective-permute-done((bf16[256,1024]{1,0:T(8,128)(2,1)S(1)}, bf16[256,1024]{1,0:T(8,128)(2,1)S(1)}, u32[]{:S(2)}, u32[]{:S(2)}) %collective-permute-start.46) | collective-permute-done | bytes 524320 | tf_op jit(solution)/shard_map/ppermute | solution.py:34
  183.5 2.7 collective-permute-start.50
  186.2 4.7 %collective-permute-start.51 = (bf16[2,128,1024]{2,1,0:T(8,128)(2,1)S(1)}, bf16[2,128,1024]{2,1,0:T(8,128)(2,1)}, u32[]{:S(2)}, u32[]{:S(2)}) collective-permute-start(bf16[2,128,1024]{2,1,0:T(8,128)(2,1)S(1)} %pad_maximum_fusion.1.refs_4_), channel_id=1, source_target_pairs={{0,3},{1,0},{2,1},{3,2},{4,7},{5,4},{6,5},{7,6},{8,11},{9,8},{10,9... | collective-permute-start | bytes 1572872 | tf_op jit(solution)/shard_map/ppermute | solution.py:34
  191.0 2.4 collective-permute-done.36.refs_1_
  193.5 6.3 %collective-permute-done.38.refs_3_ = bf16[128,1024]{1,0:T(8,128)(2,1)S(1)} collective-permute-done((bf16[128,1024]{1,0:T(8,128)(2,1)S(1)}, bf16[128,1024]{1,0:T(8,128)(2,1)S(1)}, u32[]{:S(2)}, u32[]{:S(2)}) %collective-permute-start.38) | collective-permute-done | bytes 262176 | tf_op jit(solution)/shard_map/ppermute | solution.py:34
  205.5 2.9 shard_map.67.turned
  208.5 5.7 %grad_v.1 = (f32[256,1024]{1,0:T(8,128)}, bf16[256,1024]{1,0:T(8,128)(2,1)}, bf16[256,1024]{1,0:T(8,128)(2,1)}, bf16[256,1024]{1,0:T(8,128)(2,1)}) custom-call(bf16[1024,1024]{1,0:T(8,128)(2,1)} %shard_map.67.turned, bf16[128,1024]{1,0:T(8,128)(2,1)} %copy-done.14, bf16[128,1024]{1,0:T(8,128)(2,1)} %copy-done.20, bf16[128,1024]{1,0:T(8,128)(2,1)} %copy-done.21, ...), custom_call_target="tpu_custom_call" | custom-call | flops 2147483648 | bytes 8388608 | tf_op jit(solution)/shard_map/grad_v/pallas_call | solution.py:177
  215.6 6.0 %collective-permute-start.43 = (bf16[256,1024]{1,0:T(8,128)(2,1)}, bf16[256,1024]{1,0:T(8,128)(2,1)S(1)}, u32[]{:S(2)}, u32[]{:S(2)}) collective-permute-start(bf16[256,1024]{1,0:T(8,128)(2,1)} %get-tuple-element.42), channel_id=1, source_target_pairs={{0,3},{1,0},{2,1},{3,2},{4,7},{5,4},{6,5},{7,6},{8,11},{9,8},{10,9... | collective-permute-start | bytes 1572872 | tf_op jit(solution)/shard_map/ppermute | solution.py:34
  221.6 2.9 shard_map.70.turned
  226.4 10.0 %grad_u.1 = (f32[256,1024]{1,0:T(8,128)}, bf16[256,1024]{1,0:T(8,128)(2,1)}, bf16[256,1024]{1,0:T(8,128)(2,1)}, bf16[256,1024]{1,0:T(8,128)(2,1)}) custom-call(s32[5]{0:T(128)} %stack.43.at_ref, bf16[1024,1024]{1,0:T(8,128)(2,1)} %shard_map.70.turned, bf16[256,1024]{1,0:T(8,128)(2,1)} %copy-done.2, bf16[256,1024]{1,0:T(8,128)(2,1)} %copy-done.15, ...), custom_call_target="tpu_custom_call" | custom-call | flops 4294967296 | bytes 16777216 | tf_op jit(solution)/shard_map/grad_u/pallas_call | solution.py:230
  236.3 2.5 collective-permute-start.56
  238.8 5.3 %collective-permute-done.43 = bf16[256,1024]{1,0:T(8,128)(2,1)S(1)} collective-permute-done((bf16[256,1024]{1,0:T(8,128)(2,1)}, bf16[256,1024]{1,0:T(8,128)(2,1)S(1)}, u32[]{:S(2)}, u32[]{:S(2)}) %collective-permute-start.43) | collective-permute-done | bytes 524320 | tf_op jit(solution)/shard_map/ppermute | solution.py:34
  244.1 7.0 %collective-permute-done.45 = bf16[256,1024]{1,0:T(8,128)(2,1)} collective-permute-done((bf16[256,1024]{1,0:T(8,128)(2,1)S(1)}, bf16[256,1024]{1,0:T(8,128)(2,1)}, u32[]{:S(2)}, u32[]{:S(2)}) %collective-permute-start.45) | collective-permute-done | bytes 524320 | tf_op jit(solution)/shard_map/ppermute | solution.py:34
  251.1 2.0 multiply_reduce_fusion
  253.1 7.7 %collective-permute-done.56 = bf16[256,1024]{1,0:T(8,128)(2,1)S(1)} collective-permute-done((bf16[256,1024]{1,0:T(8,128)(2,1)}, bf16[256,1024]{1,0:T(8,128)(2,1)S(1)}, u32[]{:S(2)}, u32[]{:S(2)}) %collective-permute-start.56) | collective-permute-done | bytes 524320 | tf_op jit(solution)/shard_map/ppermute | solution.py:34
  260.8 3.6 %collective-permute-done.58 = bf16[256,1024]{1,0:T(8,128)(2,1)S(1)} collective-permute-done((bf16[256,1024]{1,0:T(8,128)(2,1)}, bf16[256,1024]{1,0:T(8,128)(2,1)S(1)}, u32[]{:S(2)}, u32[]{:S(2)}) %collective-permute-start.58) | collective-permute-done | bytes 524320 | tf_op jit(solution)/shard_map/ppermute | solution.py:34
  266.6 11.6 %all_to_all.22 = f32[16,8,128]{2,1,0:T(8,128)S(1)} all-to-all(f32[16,8,128]{2,1,0:T(8,128)S(1)} %broadcast_in_dim.19), channel_id=1, replica_groups=mesh['p'=2,'h'=2,'c'=2,'z'=4,'y'=4] {'z','y'}, dimensions={0} | all-to-all | bytes 131072 | tf_op jit(solution)/shard_map/all_to_all | solution.py:29
  279.5 9.1 %all_to_all.23 = f32[8,8,128]{2,1,0:T(8,128)S(1)} all-to-all(f32[8,8,128]{2,1,0:T(8,128)S(1)} %broadcast_in_dim.20), channel_id=1, replica_groups=mesh['p'=2,'h'=2,'c'=2,'z'=4,'y'=4] {'p','h','c'}, dimensions={0} | all-to-all | bytes 65536 | tf_op jit(solution)/shard_map/all_to_all | solution.py:29
  (177 shorter events, 51.7 us)
Async XLA Ops:
  3.0 13.6 %collective-permute-start.6 = (bf16[256,1024]{1,0:T(8,128)(2,1)S(1)}, bf16[256,1024]{1,0:T(8,128)(2,1)S(1)}, u32[]{:S(2)}, u32[]{:S(2)}) collective-permute-start(bf16[256,1024]{1,0:T(8,128)(2,1)S(1)} %get-tuple-element.34.refs_4_), channel_id=1, source_target_pairs={{0,64},{64,0},{1,65},{65,1},{2,66},{66,2},{3,67},{67,3},{4,68},{68... | collective-permute-start | bytes 1572872 | tf_op jit(solution)/shard_map/ppermute | solution.py:301
  4.7 24.5 %collective-permute-start.7 = (bf16[256,1024]{1,0:T(8,128)(2,1)S(1)}, bf16[256,1024]{1,0:T(8,128)(2,1)S(1)}, u32[]{:S(2)}, u32[]{:S(2)}) collective-permute-start(bf16[256,1024]{1,0:T(8,128)(2,1)S(1)} %get-tuple-element.34.refs_4_), channel_id=1, source_target_pairs={{0,16},{16,0},{1,17},{17,1},{2,18},{18,2},{3,19},{19,3},{4,20},{20... | collective-permute-start | bytes 1572872 | tf_op jit(solution)/shard_map/ppermute | solution.py:34
  16.6 12.6 %collective-permute-start.8 = (bf16[256,1024]{1,0:T(8,128)(2,1)S(1)}, bf16[256,1024]{1,0:T(8,128)(2,1)S(1)}, u32[]{:S(2)}, u32[]{:S(2)}) collective-permute-start(bf16[256,1024]{1,0:T(8,128)(2,1)S(1)} %collective-permute-done.6.refs_0_), channel_id=1, source_target_pairs={{0,16},{16,0},{1,17},{17,1},{2,18},{18,2},{3,19},{19,3},{4,20},{20... | collective-permute-start | bytes 1572872 | tf_op jit(solution)/shard_map/ppermute | solution.py:34
  22.4 21.3 %collective-permute-start.3 = (bf16[256,1024]{1,0:T(8,128)(2,1)}, bf16[256,1024]{1,0:T(8,128)(2,1)S(1)}, u32[]{:S(2)}, u32[]{:S(2)}) collective-permute-start(bf16[256,1024]{1,0:T(8,128)(2,1)} %get-tuple-element.31), channel_id=1, source_target_pairs={{0,1},{1,2},{2,3},{3,0},{4,5},{5,6},{6,7},{7,4},{8,9},{9,10},{10,1... | collective-permute-start | bytes 1572872 | tf_op jit(solution)/shard_map/ppermute | solution.py:34
  24.2 30.1 %collective-permute-start.4 = (bf16[256,1024]{1,0:T(8,128)(2,1)}, bf16[256,1024]{1,0:T(8,128)(2,1)}, u32[]{:S(2)}, u32[]{:S(2)}) collective-permute-start(bf16[256,1024]{1,0:T(8,128)(2,1)} %get-tuple-element.32), channel_id=1, source_target_pairs={{0,2},{1,3},{2,0},{3,1},{4,6},{5,7},{6,4},{7,5},{8,10},{9,11},{10,... | collective-permute-start | bytes 1572872 | tf_op jit(solution)/shard_map/ppermute | solution.py:34
  27.1 29.1 %collective-permute-start.5 = (bf16[256,1024]{1,0:T(8,128)(2,1)}, bf16[256,1024]{1,0:T(8,128)(2,1)}, u32[]{:S(2)}, u32[]{:S(2)}) collective-permute-start(bf16[256,1024]{1,0:T(8,128)(2,1)} %get-tuple-element.33), channel_id=1, source_target_pairs={{0,3},{1,0},{2,1},{3,2},{4,7},{5,4},{6,5},{7,6},{8,11},{9,8},{10,9... | collective-permute-start | bytes 1572872 | tf_op jit(solution)/shard_map/ppermute | solution.py:34
  30.9 29.0 %all-to-all-start = ((bf16[32,8,1024]{2,1,0:T(8,128)(2,1)}), bf16[32,8,1024]{2,1,0:T(8,128)(2,1)S(1)}, u32[]{:S(2)}, u32[]{:S(2)}) async-start(bf16[32,8,1024]{2,1,0:T(8,128)(2,1)} %bitcast.12), calls=%async_computation | async-start | bytes 1048576 | tf_op jit(solution)/shard_map/all_to_all | solution.py:29
  39.2 30.3 %collective-permute-start.10 = (bf16[256,1024]{1,0:T(8,128)(2,1)S(1)}, bf16[256,1024]{1,0:T(8,128)(2,1)}, u32[]{:S(2)}, u32[]{:S(2)}) collective-permute-start(bf16[256,1024]{1,0:T(8,128)(2,1)S(1)} %get-tuple-element.34.refs_4_), channel_id=1, source_target_pairs={{0,8},{4,12},{8,0},{12,4},{1,9},{5,13},{9,1},{13,5},{2,10},{6,14},... | collective-permute-start | bytes 1572872 | tf_op jit(solution)/shard_map/ppermute | solution.py:34
  42.6 29.8 %collective-permute-start.11 = (bf16[256,1024]{1,0:T(8,128)(2,1)S(1)}, bf16[256,1024]{1,0:T(8,128)(2,1)}, u32[]{:S(2)}, u32[]{:S(2)}) collective-permute-start(bf16[256,1024]{1,0:T(8,128)(2,1)S(1)} %get-tuple-element.34.refs_4_), channel_id=1, source_target_pairs={{0,12},{4,0},{8,4},{12,8},{1,13},{5,1},{9,5},{13,9},{2,14},{6,2},{... | collective-permute-start | bytes 1572872 | tf_op jit(solution)/shard_map/ppermute | solution.py:34
  43.8 31.1 %collective-permute-start.9 = (bf16[256,1024]{1,0:T(8,128)(2,1)S(1)}, bf16[256,1024]{1,0:T(8,128)(2,1)}, u32[]{:S(2)}, u32[]{:S(2)}) collective-permute-start(bf16[256,1024]{1,0:T(8,128)(2,1)S(1)} %get-tuple-element.34.refs_4_), channel_id=1, source_target_pairs={{0,4},{4,8},{8,12},{12,0},{1,5},{5,9},{9,13},{13,1},{2,6},{6,10},{... | collective-permute-start | bytes 1572872 | tf_op jit(solution)/shard_map/ppermute | solution.py:34
  54.4 29.2 %collective-permute-start = (bf16[256,1024]{1,0:T(8,128)(2,1)}, bf16[256,1024]{1,0:T(8,128)(2,1)S(1)}, u32[]{:S(2)}, u32[]{:S(2)}) collective-permute-start(bf16[256,1024]{1,0:T(8,128)(2,1)} %get-tuple-element.27), channel_id=1, source_target_pairs={{0,4},{4,8},{8,12},{12,0},{1,5},{5,9},{9,13},{13,1},{2,6},{6,10},{... | collective-permute-start | bytes 1572872 | tf_op jit(solution)/shard_map/ppermute | solution.py:34
  56.3 36.9 %collective-permute-start.1 = (bf16[256,1024]{1,0:T(8,128)(2,1)}, bf16[256,1024]{1,0:T(8,128)(2,1)}, u32[]{:S(2)}, u32[]{:S(2)}) collective-permute-start(bf16[256,1024]{1,0:T(8,128)(2,1)} %get-tuple-element.28), channel_id=1, source_target_pairs={{0,8},{4,12},{8,0},{12,4},{1,9},{5,13},{9,1},{13,5},{2,10},{6,14},... | collective-permute-start | bytes 1572872 | tf_op jit(solution)/shard_map/ppermute | solution.py:34
  69.5 29.7 %collective-permute-start.16 = (bf16[256,1024]{1,0:T(8,128)(2,1)S(1)}, bf16[256,1024]{1,0:T(8,128)(2,1)}, u32[]{:S(2)}, u32[]{:S(2)}) collective-permute-start(bf16[256,1024]{1,0:T(8,128)(2,1)S(1)} %get-tuple-element.37.refs_4_), channel_id=1, source_target_pairs={{0,1},{1,2},{2,3},{3,0},{4,5},{5,6},{6,7},{7,4},{8,9},{9,10},{10,1... | collective-permute-start | bytes 1572872 | tf_op jit(solution)/shard_map/ppermute | solution.py:34
  72.4 29.6 %collective-permute-start.17 = (bf16[256,1024]{1,0:T(8,128)(2,1)S(1)}, bf16[256,1024]{1,0:T(8,128)(2,1)}, u32[]{:S(2)}, u32[]{:S(2)}) collective-permute-start(bf16[256,1024]{1,0:T(8,128)(2,1)S(1)} %get-tuple-element.37.refs_4_), channel_id=1, source_target_pairs={{0,2},{1,3},{2,0},{3,1},{4,6},{5,7},{6,4},{7,5},{8,10},{9,11},{10,... | collective-permute-start | bytes 1572872 | tf_op jit(solution)/shard_map/ppermute | solution.py:34
  74.9 28.3 %collective-permute-start.18 = (bf16[256,1024]{1,0:T(8,128)(2,1)S(1)}, bf16[256,1024]{1,0:T(8,128)(2,1)}, u32[]{:S(2)}, u32[]{:S(2)}) collective-permute-start(bf16[256,1024]{1,0:T(8,128)(2,1)S(1)} %get-tuple-element.37.refs_4_), channel_id=1, source_target_pairs={{0,3},{1,0},{2,1},{3,2},{4,7},{5,4},{6,5},{7,6},{8,11},{9,8},{10,9... | collective-permute-start | bytes 1572872 | tf_op jit(solution)/shard_map/ppermute | solution.py:34
  83.5 14.4 %collective-permute-start.2 = (bf16[256,1024]{1,0:T(8,128)(2,1)}, bf16[256,1024]{1,0:T(8,128)(2,1)}, u32[]{:S(2)}, u32[]{:S(2)}) collective-permute-start(bf16[256,1024]{1,0:T(8,128)(2,1)} %get-tuple-element.29), channel_id=1, source_target_pairs={{0,12},{4,0},{8,4},{12,8},{1,13},{5,1},{9,5},{13,9},{2,14},{6,2},{... | collective-permute-start | bytes 1572872 | tf_op jit(solution)/shard_map/ppermute | solution.py:34
  93.2 18.8 %collective-permute-start.12 = (bf16[512,1024]{1,0:T(8,128)(2,1)}, bf16[512,1024]{1,0:T(8,128)(2,1)S(1)}, u32[]{:S(2)}, u32[]{:S(2)}) collective-permute-start(bf16[512,1024]{1,0:T(8,128)(2,1)} %get-tuple-element.36), channel_id=1, source_target_pairs={{0,16},{16,0},{1,17},{17,1},{2,18},{18,2},{3,19},{19,3},{4,20},{20... | collective-permute-start | bytes 3145736 | tf_op jit(solution)/shard_map/ppermute | solution.py:34
  97.9 11.0 %collective-permute-start.26 = (bf16[32,1024]{1,0:T(8,128)(2,1)S(1)}, bf16[32,1024]{1,0:T(8,128)(2,1)S(1)}, u32[]{:S(2)}, u32[]{:S(2)}) collective-permute-start(bf16[32,1024]{1,0:T(8,128)(2,1)S(1)} %bitcast.45), channel_id=1, source_target_pairs={{0,1},{1,2},{2,3},{3,0},{4,5},{5,6},{6,7},{7,4},{8,9},{9,10},{10,1... | collective-permute-start | bytes 196616 | tf_op jit(solution)/shard_map/ppermute | solution.py:34
  99.3 9.6 %collective-permute-start.27 = (bf16[32,1024]{1,0:T(8,128)(2,1)S(1)}, bf16[32,1024]{1,0:T(8,128)(2,1)S(1)}, u32[]{:S(2)}, u32[]{:S(2)}) collective-permute-start(bf16[32,1024]{1,0:T(8,128)(2,1)S(1)} %bitcast.46), channel_id=1, source_target_pairs={{0,2},{1,3},{2,0},{3,1},{4,6},{5,7},{6,4},{7,5},{8,10},{9,11},{10,... | collective-permute-start | bytes 196616 | tf_op jit(solution)/shard_map/ppermute | solution.py:34
  109.0 33.4 %collective-permute-start.29 = (bf16[128,1024]{1,0:T(8,128)(2,1)S(1)}, bf16[128,1024]{1,0:T(8,128)(2,1)S(1)}, u32[]{:S(2)}, u32[]{:S(2)}) collective-permute-start(bf16[128,1024]{1,0:T(8,128)(2,1)S(1)} %constant_dynamic-update-slice_fusion.refs_0_), channel_id=1, source_target_pairs={{0,4},{4,8},{8,12},{12,0},{1,5},{5,9},{9,13},{13,1},{2,6},{6,10},{... | collective-permute-start | bytes 786440 | tf_op jit(solution)/shard_map/ppermute | solution.py:34
  109.0 36.0 %collective-permute-start.30 = (bf16[128,1024]{1,0:T(8,128)(2,1)S(1)}, bf16[128,1024]{1,0:T(8,128)(2,1)S(1)}, u32[]{:S(2)}, u32[]{:S(2)}) collective-permute-start(bf16[128,1024]{1,0:T(8,128)(2,1)S(1)} %constant_dynamic-update-slice_fusion.refs_0_), channel_id=1, source_target_pairs={{0,8},{4,12},{8,0},{12,4},{1,9},{5,13},{9,1},{13,5},{2,10},{6,14},... | collective-permute-start | bytes 786440 | tf_op jit(solution)/shard_map/ppermute | solution.py:34
  114.2 9.2 %collective-permute-start.13 = (bf16[128,1024]{1,0:T(8,128)(2,1)S(1)}, bf16[128,1024]{1,0:T(8,128)(2,1)S(1)}, u32[]{:S(2)}, u32[]{:S(2)}) collective-permute-start(bf16[128,1024]{1,0:T(8,128)(2,1)S(1)} %get-tuple-element.72), channel_id=1, source_target_pairs={{0,3},{1,0},{2,1},{3,2},{4,7},{5,4},{6,5},{7,6},{8,11},{9,8},{10,9... | collective-permute-start | bytes 786440 | tf_op jit(solution)/shard_map/ppermute | solution.py:34
  114.5 10.7 %collective-permute-start.14 = (bf16[128,1024]{1,0:T(8,128)(2,1)S(1)}, bf16[128,1024]{1,0:T(8,128)(2,1)S(1)}, u32[]{:S(2)}, u32[]{:S(2)}) collective-permute-start(bf16[128,1024]{1,0:T(8,128)(2,1)S(1)} %get-tuple-element.74), channel_id=1, source_target_pairs={{0,2},{1,3},{2,0},{3,1},{4,6},{5,7},{6,4},{7,5},{8,10},{9,11},{10,... | collective-permute-start | bytes 786440 | tf_op jit(solution)/shard_map/ppermute | solution.py:34
  117.3 12.4 %collective-permute-start.15 = (bf16[128,1024]{1,0:T(8,128)(2,1)S(1)}, bf16[128,1024]{1,0:T(8,128)(2,1)S(1)}, u32[]{:S(2)}, u32[]{:S(2)}) collective-permute-start(bf16[128,1024]{1,0:T(8,128)(2,1)S(1)} %get-tuple-element.73), channel_id=1, source_target_pairs={{0,1},{1,2},{2,3},{3,0},{4,5},{5,6},{6,7},{7,4},{8,9},{9,10},{10,1... | collective-permute-start | bytes 786440 | tf_op jit(solution)/shard_map/ppermute | solution.py:34
  129.6 9.5 %collective-permute-start.22 = (bf16[128,1024]{1,0:T(8,128)(2,1)S(1)}, bf16[128,1024]{1,0:T(8,128)(2,1)S(1)}, u32[]{:S(2)}, u32[]{:S(2)}) collective-permute-start(bf16[128,1024]{1,0:T(8,128)(2,1)S(1)} %get-tuple-element.76), channel_id=1, source_target_pairs={{0,4},{4,8},{8,12},{12,0},{1,5},{5,9},{9,13},{13,1},{2,6},{6,10},{... | collective-permute-start | bytes 786440 | tf_op jit(solution)/shard_map/ppermute | solution.py:34
  132.5 12.5 %collective-permute-start.31 = (bf16[128,1024]{1,0:T(8,128)(2,1)S(1)}, bf16[128,1024]{1,0:T(8,128)(2,1)S(1)}, u32[]{:S(2)}, u32[]{:S(2)}) collective-permute-start(bf16[128,1024]{1,0:T(8,128)(2,1)S(1)} %constant_dynamic-update-slice_fusion.refs_0_), channel_id=1, source_target_pairs={{0,12},{4,0},{8,4},{12,8},{1,13},{5,1},{9,5},{13,9},{2,14},{6,2},{... | collective-permute-start | bytes 786440 | tf_op jit(solution)/shard_map/ppermute | solution.py:34
  139.3 9.4 %collective-permute-start.23 = (bf16[32,2048]{1,0:T(8,128)(2,1)S(1)}, bf16[32,2048]{1,0:T(8,128)(2,1)S(1)}, u32[]{:S(2)}, u32[]{:S(2)}) collective-permute-start(bf16[32,2048]{1,0:T(8,128)(2,1)S(1)} %get-tuple-element.80), channel_id=1, source_target_pairs={{0,32},{32,0},{64,96},{96,64},{1,33},{33,1},{65,97},{97,65},{2,34}... | collective-permute-start | bytes 393224 | tf_op jit(solution)/shard_map/ppermute | solution.py:43
  153.0 12.4 %collective-permute-start.33 = (bf16[3,32,1024]{2,1,0:T(8,128)(2,1)S(1)}, bf16[3,32,1024]{2,1,0:T(8,128)(2,1)S(1)}, u32[]{:S(2)}, u32[]{:S(2)}) collective-permute-start(bf16[3,32,1024]{2,1,0:T(8,128)(2,1)S(1)} %get-tuple-element.84), channel_id=1, source_target_pairs={{0,64},{32,96},{64,32},{96,0},{1,65},{33,97},{65,33},{97,1},{2,66}... | collective-permute-start | bytes 589832 | tf_op jit(solution)/shard_map/ppermute | solution.py:43
  153.1 12.4 %collective-permute-start.34 = (bf16[3,32,1024]{2,1,0:T(8,128)(2,1)S(1)}, bf16[3,32,1024]{2,1,0:T(8,128)(2,1)S(1)}, u32[]{:S(2)}, u32[]{:S(2)}) collective-permute-start(bf16[3,32,1024]{2,1,0:T(8,128)(2,1)S(1)} %get-tuple-element.83), channel_id=1, source_target_pairs={{0,32},{32,0},{64,96},{96,64},{1,33},{33,1},{65,97},{97,65},{2,34}... | collective-permute-start | bytes 589832 | tf_op jit(solution)/shard_map/ppermute | solution.py:43
  154.7 11.4 %collective-permute-start.35 = (bf16[3,32,1024]{2,1,0:T(8,128)(2,1)S(1)}, bf16[3,32,1024]{2,1,0:T(8,128)(2,1)S(1)}, u32[]{:S(2)}, u32[]{:S(2)}) collective-permute-start(bf16[3,32,1024]{2,1,0:T(8,128)(2,1)S(1)} %get-tuple-element.84), channel_id=1, source_target_pairs={{0,96},{32,64},{64,0},{96,32},{1,97},{33,65},{65,1},{97,33},{2,98}... | collective-permute-start | bytes 589832 | tf_op jit(solution)/shard_map/ppermute | solution.py:43
  156.3 27.2 %collective-permute-start.46 = (bf16[256,1024]{1,0:T(8,128)(2,1)S(1)}, bf16[256,1024]{1,0:T(8,128)(2,1)S(1)}, u32[]{:S(2)}, u32[]{:S(2)}) collective-permute-start(bf16[256,1024]{1,0:T(8,128)(2,1)S(1)} %collective-permute-done.6.refs_0_), channel_id=1, source_target_pairs={{0,4},{4,8},{8,12},{12,0},{1,5},{5,9},{9,13},{13,1},{2,6},{6,10},{... | collective-permute-start | bytes 1572872 | tf_op jit(solution)/shard_map/ppermute | solution.py:34
  156.3 29.9 %collective-permute-start.47 = (bf16[256,1024]{1,0:T(8,128)(2,1)S(1)}, bf16[256,1024]{1,0:T(8,128)(2,1)S(1)}, u32[]{:S(2)}, u32[]{:S(2)}) collective-permute-start(bf16[256,1024]{1,0:T(8,128)(2,1)S(1)} %collective-permute-done.6.refs_0_), channel_id=1, source_target_pairs={{0,8},{4,12},{8,0},{12,4},{1,9},{5,13},{9,1},{13,5},{2,10},{6,14},... | collective-permute-start | bytes 1572872 | tf_op jit(solution)/shard_map/ppermute | solution.py:34
  166.1 27.3 %collective-permute-start.36 = (bf16[128,1024]{1,0:T(8,128)(2,1)S(1)}, bf16[128,1024]{1,0:T(8,128)(2,1)S(1)}, u32[]{:S(2)}, u32[]{:S(2)}) collective-permute-start(bf16[128,1024]{1,0:T(8,128)(2,1)S(1)} %maximum_bitcast_fusion.refs_0_), channel_id=1, source_target_pairs={{0,4},{4,8},{8,12},{12,0},{1,5},{5,9},{9,13},{13,1},{2,6},{6,10},{... | collective-permute-start | bytes 786440 | tf_op jit(solution)/shard_map/ppermute | solution.py:34
  166.2 27.2 %collective-permute-start.37 = (bf16[128,1024]{1,0:T(8,128)(2,1)S(1)}, bf16[128,1024]{1,0:T(8,128)(2,1)S(1)}, u32[]{:S(2)}, u32[]{:S(2)}) collective-permute-start(bf16[128,1024]{1,0:T(8,128)(2,1)S(1)} %maximum_bitcast_fusion.refs_0_), channel_id=1, source_target_pairs={{0,8},{4,12},{8,0},{12,4},{1,9},{5,13},{9,1},{13,5},{2,10},{6,14},... | collective-permute-start | bytes 786440 | tf_op jit(solution)/shard_map/ppermute | solution.py:34
  168.5 31.8 %collective-permute-start.49 = (bf16[2,128,1024]{2,1,0:T(8,128)(2,1)S(1)}, bf16[2,128,1024]{2,1,0:T(8,128)(2,1)}, u32[]{:S(2)}, u32[]{:S(2)}) collective-permute-start(bf16[2,128,1024]{2,1,0:T(8,128)(2,1)S(1)} %pad_maximum_fusion.1.refs_4_), channel_id=1, source_target_pairs={{0,1},{1,2},{2,3},{3,0},{4,5},{5,6},{6,7},{7,4},{8,9},{9,10},{10,1... | collective-permute-start | bytes 1572872 | tf_op jit(solution)/shard_map/ppermute | solution.py:34
  183.5 17.0 %collective-permute-start.50 = (bf16[2,128,1024]{2,1,0:T(8,128)(2,1)S(1)}, bf16[2,128,1024]{2,1,0:T(8,128)(2,1)}, u32[]{:S(2)}, u32[]{:S(2)}) collective-permute-start(bf16[2,128,1024]{2,1,0:T(8,128)(2,1)S(1)} %pad_maximum_fusion.1.refs_4_), channel_id=1, source_target_pairs={{0,2},{1,3},{2,0},{3,1},{4,6},{5,7},{6,4},{7,5},{8,10},{9,11},{10,... | collective-permute-start | bytes 1572872 | tf_op jit(solution)/shard_map/ppermute | solution.py:34
  186.2 17.2 %collective-permute-start.51 = (bf16[2,128,1024]{2,1,0:T(8,128)(2,1)S(1)}, bf16[2,128,1024]{2,1,0:T(8,128)(2,1)}, u32[]{:S(2)}, u32[]{:S(2)}) collective-permute-start(bf16[2,128,1024]{2,1,0:T(8,128)(2,1)S(1)} %pad_maximum_fusion.1.refs_4_), channel_id=1, source_target_pairs={{0,3},{1,0},{2,1},{3,2},{4,7},{5,4},{6,5},{7,6},{8,11},{9,8},{10,9... | collective-permute-start | bytes 1572872 | tf_op jit(solution)/shard_map/ppermute | solution.py:34
  200.5 14.3 %collective-permute-start.48 = (bf16[256,1024]{1,0:T(8,128)(2,1)S(1)}, bf16[256,1024]{1,0:T(8,128)(2,1)S(1)}, u32[]{:S(2)}, u32[]{:S(2)}) collective-permute-start(bf16[256,1024]{1,0:T(8,128)(2,1)S(1)} %collective-permute-done.6.refs_0_), channel_id=1, source_target_pairs={{0,12},{4,0},{8,4},{12,8},{1,13},{5,1},{9,5},{13,9},{2,14},{6,2},{... | collective-permute-start | bytes 1572872 | tf_op jit(solution)/shard_map/ppermute | solution.py:34
  203.4 21.1 %collective-permute-start.52 = (bf16[2,128,1024]{2,1,0:T(8,128)(2,1)S(1)}, bf16[2,128,1024]{2,1,0:T(8,128)(2,1)S(1)}, u32[]{:S(2)}, u32[]{:S(2)}) collective-permute-start(bf16[2,128,1024]{2,1,0:T(8,128)(2,1)S(1)} %pad_maximum_fusion.1.refs_4_), channel_id=1, source_target_pairs={{0,16},{16,0},{1,17},{17,1},{2,18},{18,2},{3,19},{19,3},{4,20},{20... | collective-permute-start | bytes 1572872 | tf_op jit(solution)/shard_map/ppermute | solution.py:34
  203.5 21.9 %collective-permute-start.53 = (bf16[2,128,1024]{2,1,0:T(8,128)(2,1)}, bf16[2,128,1024]{2,1,0:T(8,128)(2,1)}, u32[]{:S(2)}, u32[]{:S(2)}) collective-permute-start(bf16[2,128,1024]{2,1,0:T(8,128)(2,1)} %collective-permute-done.49.refs_5_), channel_id=1, source_target_pairs={{0,16},{16,0},{1,17},{17,1},{2,18},{18,2},{3,19},{19,3},{4,20},{20... | collective-permute-start | bytes 1572872 | tf_op jit(solution)/shard_map/ppermute | solution.py:34
  204.0 22.4 %collective-permute-start.54 = (bf16[2,128,1024]{2,1,0:T(8,128)(2,1)}, bf16[2,128,1024]{2,1,0:T(8,128)(2,1)}, u32[]{:S(2)}, u32[]{:S(2)}) collective-permute-start(bf16[2,128,1024]{2,1,0:T(8,128)(2,1)} %collective-permute-done.50.refs_6_), channel_id=1, source_target_pairs={{0,16},{16,0},{1,17},{17,1},{2,18},{18,2},{3,19},{19,3},{4,20},{20... | collective-permute-start | bytes 1572872 | tf_op jit(solution)/shard_map/ppermute | solution.py:34
  205.4 21.0 %collective-permute-start.55 = (bf16[2,128,1024]{2,1,0:T(8,128)(2,1)}, bf16[2,128,1024]{2,1,0:T(8,128)(2,1)}, u32[]{:S(2)}, u32[]{:S(2)}) collective-permute-start(bf16[2,128,1024]{2,1,0:T(8,128)(2,1)} %collective-permute-done.51.refs_7_), channel_id=1, source_target_pairs={{0,16},{16,0},{1,17},{17,1},{2,18},{18,2},{3,19},{19,3},{4,20},{20... | collective-permute-start | bytes 1572872 | tf_op jit(solution)/shard_map/ppermute | solution.py:34
  215.6 28.5 %collective-permute-start.43 = (bf16[256,1024]{1,0:T(8,128)(2,1)}, bf16[256,1024]{1,0:T(8,128)(2,1)S(1)}, u32[]{:S(2)}, u32[]{:S(2)}) collective-permute-start(bf16[256,1024]{1,0:T(8,128)(2,1)} %get-tuple-element.42), channel_id=1, source_target_pairs={{0,3},{1,0},{2,1},{3,2},{4,7},{5,4},{6,5},{7,6},{8,11},{9,8},{10,9... | collective-permute-start | bytes 1572872 | tf_op jit(solution)/shard_map/ppermute | solution.py:34
  225.4 18.7 %collective-permute-start.44 = (bf16[256,1024]{1,0:T(8,128)(2,1)}, bf16[256,1024]{1,0:T(8,128)(2,1)S(1)}, u32[]{:S(2)}, u32[]{:S(2)}) collective-permute-start(bf16[256,1024]{1,0:T(8,128)(2,1)} %get-tuple-element.43), channel_id=1, source_target_pairs={{0,2},{1,3},{2,0},{3,1},{4,6},{5,7},{6,4},{7,5},{8,10},{9,11},{10,... | collective-permute-start | bytes 1572872 | tf_op jit(solution)/shard_map/ppermute | solution.py:34
  225.4 25.8 %collective-permute-start.45 = (bf16[256,1024]{1,0:T(8,128)(2,1)S(1)}, bf16[256,1024]{1,0:T(8,128)(2,1)}, u32[]{:S(2)}, u32[]{:S(2)}) collective-permute-start(bf16[256,1024]{1,0:T(8,128)(2,1)S(1)} %copy-done.19), channel_id=1, source_target_pairs={{0,1},{1,2},{2,3},{3,0},{4,5},{5,6},{6,7},{7,4},{8,9},{9,10},{10,1... | collective-permute-start | bytes 1572872 | tf_op jit(solution)/shard_map/ppermute | solution.py:34
  236.3 24.5 %collective-permute-start.56 = (bf16[256,1024]{1,0:T(8,128)(2,1)}, bf16[256,1024]{1,0:T(8,128)(2,1)S(1)}, u32[]{:S(2)}, u32[]{:S(2)}) collective-permute-start(bf16[256,1024]{1,0:T(8,128)(2,1)} %get-tuple-element.46), channel_id=1, source_target_pairs={{0,12},{4,0},{8,4},{12,8},{1,13},{5,1},{9,5},{13,9},{2,14},{6,2},{... | collective-permute-start | bytes 1572872 | tf_op jit(solution)/shard_map/ppermute | solution.py:34
  238.8 22.0 %collective-permute-start.57 = (bf16[256,1024]{1,0:T(8,128)(2,1)}, bf16[256,1024]{1,0:T(8,128)(2,1)S(1)}, u32[]{:S(2)}, u32[]{:S(2)}) collective-permute-start(bf16[256,1024]{1,0:T(8,128)(2,1)} %get-tuple-element.47), channel_id=1, source_target_pairs={{0,8},{4,12},{8,0},{12,4},{1,9},{5,13},{9,1},{13,5},{2,10},{6,14},... | collective-permute-start | bytes 1572872 | tf_op jit(solution)/shard_map/ppermute | solution.py:34
  244.1 20.3 %collective-permute-start.58 = (bf16[256,1024]{1,0:T(8,128)(2,1)}, bf16[256,1024]{1,0:T(8,128)(2,1)S(1)}, u32[]{:S(2)}, u32[]{:S(2)}) collective-permute-start(bf16[256,1024]{1,0:T(8,128)(2,1)} %get-tuple-element.48), channel_id=1, source_target_pairs={{0,4},{4,8},{8,12},{12,0},{1,5},{5,9},{9,13},{13,1},{2,6},{6,10},{... | collective-permute-start | bytes 1572872 | tf_op jit(solution)/shard_map/ppermute | solution.py:34
  (39 other events, 677.4 us)

commit v4 on v3

--- a/solution.py
+++ b/solution.py
@@ -53,27 +53,17 @@
 
 
 def cut_kernel(at_ref, x_ref, ct_ref, *outs):
-    p, x, c, z, y = (at_ref[i] for i in range(5))
-    tok = x_ref.shape[0]
+    p, z, y = at_ref[0], at_ref[3], at_ref[4]
     own = x_ref.shape[1] // 16
-    half, part = tok // 2, tok // 8
 
     def copy(v_ref, u_ref):
-        def group(i, carry):
-            rc, q = i // 4, lax.rem(i, 4)
-            source = lax.rem(c + rc, 2) * half + lax.rem(x + 4 - q, 4) * part
-            rows = pl.ds(pl.multiple_of(source, part), part)
-            to = pl.ds(pl.multiple_of(i * part, part), part)
-            for k in range(4):
-                for j in range(4):
-                    at_v = lax.rem(z + k, 4) * 4 + lax.rem(y + 4 - j, 4)
-                    at_u = lax.rem(z + 4 - j, 4) * 4 + lax.rem(y + k, 4)
-                    for out, ref, at in ((outs[k], v_ref, at_v), (outs[4 + k], u_ref, at_u)):
-                        cols = pl.ds(pl.multiple_of(at * own, own), own)
-                        out[to, j * own : (j + 1) * own] = ref[rows, cols]
-            return carry
-
-        lax.fori_loop(0, 8, group, 0)
+        for k in range(4):
+            for j in range(4):
+                at_v = lax.rem(z + k, 4) * 4 + lax.rem(y + 4 - j, 4)
+                at_u = lax.rem(z + 4 - j, 4) * 4 + lax.rem(y + k, 4)
+                for out, ref, at in ((outs[k], v_ref, at_v), (outs[4 + k], u_ref, at_u)):
+                    cols = pl.ds(pl.multiple_of(at * own, own), own)
+                    out[:, j * own : (j + 1) * own] = ref[:, cols]
 
     @pl.when(p == 0)
     def _():
@@ -86,12 +76,20 @@
 
 def cut(at, x, ct):
     tok, width = x.shape
-    vmem = pl.BlockSpec(memory_space=pltpu.VMEM)
+    part = tok // 8
+
+    def source(i, at_ref):
+        return (lax.rem(at_ref[2] + i // 4, 2) * 4 + lax.rem(at_ref[1] + 4 - lax.rem(i, 4), 4), 0)
+
     outs = pl.pallas_call(
         cut_kernel,
         out_shape=[jax.ShapeDtypeStruct((tok, width // 4), BF)] * 8,
-        in_specs=[pl.BlockSpec(memory_space=pltpu.SMEM), vmem, vmem],
-        out_specs=[vmem] * 8,
+        grid_spec=pltpu.PrefetchScalarGridSpec(
+            num_scalar_prefetch=1,
+            grid=(8,),
+            in_specs=[pl.BlockSpec((part, width), source)] * 2,
+            out_specs=[pl.BlockSpec((part, width // 4), lambda i, at_ref: (i, 0))] * 8,
+        ),
         name="cut",
     )(at, x, ct)
     return list(outs[:4]), list(outs[4:])
@@ -368,9 +366,8 @@
     g_u = sum_back(g_u, "z")
 
     squares = jnp.sum(g_u * g_u) + jnp.sum(g_v * g_v)
-    for axes, count in ((("z", "y"), 16), (("p", "h", "c"), 8)):
-        row = jnp.broadcast_to(squares, (count, 8, 128))
-        squares = a2a(row, axes)[:, 0, 0].sum()
+    row = jnp.broadcast_to(squares, (lax.axis_size(AXES), 1, 128))
+    squares = a2a(row, AXES)[:, 0, 0].sum()
     grad_norm = jnp.sqrt(squares)
     factor = jnp.minimum(1.0, CLIP_NORM / grad_norm)
     g_in = jnp.where(first, g_v, g_u) * factor

time: 295 us -> 291 us (0.986)
  blocking collectives: 30.2 us -> 25.2 us
    all_to_all x3 -> x2, blocking collectives: 30.2 us -> 25.2 us  [a2a(): return lax.all_to_all(value, axes, 0, 0, tiled=True)]
  transfers between devices with their start and end apart: 60 -> 60, of which waited for: 23 -> 23; matrix products, arithmetic and copies ran while one was open for 3% -> 3% of each run, Pallas kernels for 14% -> 15%
where the time goes in v4:
time: 291 us; the launch traced here: 290 us
  waiting for transfers between devices  108 us (37%)
  starting transfers between devices  87.5 us (30%)
  Pallas kernels  42.5 us (15%)
  blocking collectives  25.2 us (9%)
  local copies, waits for them, and re-layouts  9.89 us (3%)
  other arithmetic  9.5 us (3%)
  between operations  4.32 us (1%)
  matrix products  2.99 us (1%)
    ppermute x52, waiting for transfers between devices, shift(): lax.ppermute(value, axis, [(i, (i + by) % count) for i in range(count)])  88.5 us
    ppermute x52, starting transfers between devices, shift(): lax.ppermute(value, axis, [(i, (i + by) % count) for i in range(count)])  68.6 us
    all_to_all x2, blocking collectives, a2a(): return lax.all_to_all(value, axes, 0, 0, tiled=True)  25.2 us
    ppermute x1, waiting for transfers between devices, on_device(): w_3 = lax.ppermute(w_u, 'p', [(0, 1), (1, 0)])  11.9 us
    pallas_call x2, Pallas kernels, project(): pl.pallas_call(project_kernel, out_shape=[jax.ShapeDtypeStruct((2 * tok,...  11.3 us
    pallas_call x1, Pallas kernels, grad_u_call(): pl.pallas_call(grad_u_kernel, out_shape=[jax.ShapeDtypeStruct((own, hidde...  9.96 us
    ppermute x6, starting transfers between devices, shift_x(): return lax.ppermute(value, ('p', 'h'), pairs)  9 us
    all_to_all x1, starting transfers between devices, a2a(): return lax.all_to_all(value, axes, 0, 0, tiled=True)  8.28 us
  transfers between devices with their start and end apart: 60, of which 23 were waited for; matrix products, arithmetic and copies ran while one was open for 3% of the time, Pallas kernels for 15%

profile of v4, /device:TPU:0, one launch (start us, length us, event | category | flops | bytes accessed | tf_op | source)
XLA Modules:
  0.0 289.8 jit_solution(7596702977006766410)
XLA Ops:
  4.7 11.9 %collective-permute-done.6.refs_0_ = bf16[256,1024]{1,0:T(8,128)(2,1)S(1)} collective-permute-done((bf16[256,1024]{1,0:T(8,128)(2,1)S(1)}, bf16[256,1024]{1,0:T(8,128)(2,1)S(1)}, u32[]{:S(2)}, u32[]{:S(2)}) %collective-permute-start.6) | collective-permute-done | bytes 524320 | tf_op jit(solution)/shard_map/ppermute | solution.py:299
  17.4 7.3 %cut.1 = (bf16[256,1024]{1,0:T(8,128)(2,1)}, bf16[256,1024]{1,0:T(8,128)(2,1)}, bf16[256,1024]{1,0:T(8,128)(2,1)}, bf16[256,1024]{1,0:T(8,128)(2,1)}, bf16[256,1...) custom-call(s32[5]{0:T(128)} %stack.43.at_ref, ...), custom_call_target="tpu_custom_call" | custom-call | tf_op jit(solution)/shard_map/cut/pallas_call | solution.py:84
  24.7 1.9 collective-permute-start.3
  26.6 2.9 %collective-permute-start.4 = (bf16[256,1024]{1,0:T(8,128)(2,1)}, bf16[256,1024]{1,0:T(8,128)(2,1)}, u32[]{:S(2)}, u32[]{:S(2)}) collective-permute-start(bf16[256,1024]{1,0:T(8,128)(2,1)} %get-tuple-element.32), channel_id=1, source_target_pairs={{0,2},{1,3},{2,0},{3,1},{4,6},{5,7},{6,4},{7,5},{8,10},{9,11},{10,... | collective-permute-start | bytes 1572872 | tf_op jit(solution)/shard_map/ppermute | solution.py:34
  33.3 8.3 %all-to-all-start = ((bf16[32,8,1024]{2,1,0:T(8,128)(2,1)}), bf16[32,8,1024]{2,1,0:T(8,128)(2,1)S(1)}, u32[]{:S(2)}, u32[]{:S(2)}) async-start(bf16[32,8,1024]{2,1,0:T(8,128)(2,1)} %bitcast.12), calls=%async_computation | async-start | bytes 1048576 | tf_op jit(solution)/shard_map/all_to_all | solution.py:29
  41.6 3.4 %collective-permute-start.10 = (bf16[256,1024]{1,0:T(8,128)(2,1)S(1)}, bf16[256,1024]{1,0:T(8,128)(2,1)}, u32[]{:S(2)}, u32[]{:S(2)}) collective-permute-start(bf16[256,1024]{1,0:T(8,128)(2,1)S(1)} %get-tuple-element.34.refs_4_), channel_id=1, source_target_pairs={{0,8},{4,12},{8,0},{12,4},{1,9},{5,13},{9,1},{13,5},{2,10},{6,14},... | collective-permute-start | bytes 1572872 | tf_op jit(solution)/shard_map/ppermute | solution.py:34
  47.1 9.7 %collective-permute-done.4.refs_2_ = bf16[256,1024]{1,0:T(8,128)(2,1)} collective-permute-done((bf16[256,1024]{1,0:T(8,128)(2,1)}, bf16[256,1024]{1,0:T(8,128)(2,1)}, u32[]{:S(2)}, u32[]{:S(2)}) %collective-permute-start.4) | collective-permute-done | bytes 524320 | tf_op jit(solution)/shard_map/ppermute | solution.py:34
  56.7 1.9 collective-permute-start
  58.6 3.6 %collective-permute-start.1 = (bf16[256,1024]{1,0:T(8,128)(2,1)}, bf16[256,1024]{1,0:T(8,128)(2,1)}, u32[]{:S(2)}, u32[]{:S(2)}) collective-permute-start(bf16[256,1024]{1,0:T(8,128)(2,1)} %get-tuple-element.28), channel_id=1, source_target_pairs={{0,8},{4,12},{8,0},{12,4},{1,9},{5,13},{9,1},{13,5},{2,10},{6,14},... | collective-permute-start | bytes 1572872 | tf_op jit(solution)/shard_map/ppermute | solution.py:34
  62.3 9.5 %all_to_all.16 = bf16[4,8,1024]{2,1,0:T(8,128)(2,1)S(1)} all-to-all(bf16[4,8,1024]{2,1,0:T(8,128)(2,1)S(1)} %broadcast_in_dim.15), channel_id=1, replica_groups=mesh['p'=2,'h'=2,'c'=2,'z'=4,'y'=4] {'p','h'}, dimensions={0} | all-to-all | bytes 131072 | tf_op jit(solution)/shard_map/all_to_all | solution.py:29
  74.8 2.5 collective-permute-start.17
  77.3 1.9 collective-permute-start.18
  79.2 6.7 %collective-permute-done.refs_1_ = bf16[256,1024]{1,0:T(8,128)(2,1)S(1)} collective-permute-done((bf16[256,1024]{1,0:T(8,128)(2,1)}, bf16[256,1024]{1,0:T(8,128)(2,1)S(1)}, u32[]{:S(2)}, u32[]{:S(2)}) %collective-permute-start) | collective-permute-done | bytes 524320 | tf_op jit(solution)/shard_map/ppermute | solution.py:34
  86.5 5.7 %shard_map.68 = (bf16[512,1024]{1,0:T(8,128)(2,1)}, f32[512,1024]{1,0:T(8,128)}) custom-call(bf16[256,1024]{1,0:T(8,128)(2,1)} %get-tuple-element.30.refs_0_, bf16[256,1024]{1,0:T(8,128)(2,1)} %copy-done.8, bf16[256,1024]{1,0:T(8,128)(2,1)} %collective-permute-done.4.refs_2_, bf16[256,1024]{1,0:T(8,128)(2,1)} %collective-permute-done.5.refs_3_, ...), custom_call_target="tpu_custom_call" | custom-call | flops 2147483648 | bytes 4194304 | tf_op jit(solution)/shard_map/pallas_call | solution.py:119
  92.2 3.4 %collective-permute-done.1.refs_2_ = bf16[256,1024]{1,0:T(8,128)(2,1)} collective-permute-done((bf16[256,1024]{1,0:T(8,128)(2,1)}, bf16[256,1024]{1,0:T(8,128)(2,1)}, u32[]{:S(2)}, u32[]{:S(2)}) %collective-permute-start.1) | collective-permute-done | bytes 524320 | tf_op jit(solution)/shard_map/ppermute | solution.py:34
  95.6 4.7 %collective-permute-done.2.refs_3_ = bf16[256,1024]{1,0:T(8,128)(2,1)} collective-permute-done((bf16[256,1024]{1,0:T(8,128)(2,1)}, bf16[256,1024]{1,0:T(8,128)(2,1)}, u32[]{:S(2)}, u32[]{:S(2)}) %collective-permute-start.2) | collective-permute-done | bytes 524320 | tf_op jit(solution)/shard_map/ppermute | solution.py:34
  101.6 2.8 collective-permute-start.27
  105.6 5.7 %shard_map.69 = (bf16[512,1024]{1,0:T(8,128)(2,1)}, f32[512,1024]{1,0:T(8,128)}) custom-call(bf16[256,1024]{1,0:T(8,128)(2,1)} %get-tuple-element.26.refs_0_, bf16[256,1024]{1,0:T(8,128)(2,1)} %copy-done.9, bf16[256,1024]{1,0:T(8,128)(2,1)} %collective-permute-done.1.refs_2_, bf16[256,1024]{1,0:T(8,128)(2,1)} %collective-permute-done.2.refs_3_, ...), custom_call_target="tpu_custom_call" | custom-call | flops 2147483648 | bytes 4194304 | tf_op jit(solution)/shard_map/pallas_call | solution.py:119
  111.4 2.9 %collective-permute-start.30 = (bf16[128,1024]{1,0:T(8,128)(2,1)S(1)}, bf16[128,1024]{1,0:T(8,128)(2,1)S(1)}, u32[]{:S(2)}, u32[]{:S(2)}) collective-permute-start(bf16[128,1024]{1,0:T(8,128)(2,1)S(1)} %constant_dynamic-update-slice_fusion.refs_0_), channel_id=1, source_target_pairs={{0,8},{4,12},{8,0},{12,4},{1,9},{5,13},{9,1},{13,5},{2,10},{6,14},... | collective-permute-start | bytes 786440 | tf_op jit(solution)/shard_map/ppermute | solution.py:34
  114.4 2.2 fusion.35
  116.8 2.8 collective-permute-start.14
  120.3 5.6 %collective-permute-done.13 = bf16[128,1024]{1,0:T(8,128)(2,1)S(1)} collective-permute-done((bf16[128,1024]{1,0:T(8,128)(2,1)S(1)}, bf16[128,1024]{1,0:T(8,128)(2,1)S(1)}, u32[]{:S(2)}, u32[]{:S(2)}) %collective-permute-start.13) | collective-permute-done | bytes 262176 | tf_op jit(solution)/shard_map/ppermute | solution.py:34
  129.1 3.0 %collective-permute-done.15 = bf16[128,1024]{1,0:T(8,128)(2,1)S(1)} collective-permute-done((bf16[128,1024]{1,0:T(8,128)(2,1)S(1)}, bf16[128,1024]{1,0:T(8,128)(2,1)S(1)}, u32[]{:S(2)}, u32[]{:S(2)}) %collective-permute-start.15) | collective-permute-done | bytes 262176 | tf_op jit(solution)/shard_map/ppermute | solution.py:34
  136.1 5.4 %collective-permute-done.22 = bf16[128,1024]{1,0:T(8,128)(2,1)S(1)} collective-permute-done((bf16[128,1024]{1,0:T(8,128)(2,1)S(1)}, bf16[128,1024]{1,0:T(8,128)(2,1)S(1)}, u32[]{:S(2)}, u32[]{:S(2)}) %collective-permute-start.22) | collective-permute-done | bytes 262176 | tf_op jit(solution)/shard_map/ppermute | solution.py:34
  141.7 2.5 collective-permute-start.23
  144.8 2.7 collective-permute-start.25
  148.9 2.2 join.1
  158.7 2.3 collective-permute-start.47
  161.0 6.8 %collective-permute-done.33 = bf16[3,32,1024]{2,1,0:T(8,128)(2,1)S(1)} collective-permute-done((bf16[3,32,1024]{2,1,0:T(8,128)(2,1)S(1)}, bf16[3,32,1024]{2,1,0:T(8,128)(2,1)S(1)}, u32[]{:S(2)}, u32[]{:S(2)}) %collective-permute-start.33) | collective-permute-done | bytes 196640 | tf_op jit(solution)/shard_map/ppermute | solution.py:43
  168.5 2.3 collective-permute-start.37
  170.9 5.2 %collective-permute-start.49 = (bf16[2,128,1024]{2,1,0:T(8,128)(2,1)S(1)}, bf16[2,128,1024]{2,1,0:T(8,128)(2,1)}, u32[]{:S(2)}, u32[]{:S(2)}) collective-permute-start(bf16[2,128,1024]{2,1,0:T(8,128)(2,1)S(1)} %pad_maximum_fusion.1.refs_4_), channel_id=1, source_target_pairs={{0,1},{1,2},{2,3},{3,0},{4,5},{5,6},{6,7},{7,4},{8,9},{9,10},{10,1... | collective-permute-start | bytes 1572872 | tf_op jit(solution)/shard_map/ppermute | solution.py:34
  176.1 9.8 %collective-permute-done.46.refs_1_ = bf16[256,1024]{1,0:T(8,128)(2,1)S(1)} collective-permute-done((bf16[256,1024]{1,0:T(8,128)(2,1)S(1)}, bf16[256,1024]{1,0:T(8,128)(2,1)S(1)}, u32[]{:S(2)}, u32[]{:S(2)}) %collective-permute-start.46) | collective-permute-done | bytes 524320 | tf_op jit(solution)/shard_map/ppermute | solution.py:34
  185.9 2.6 collective-permute-start.50
  188.6 4.7 %collective-permute-start.51 = (bf16[2,128,1024]{2,1,0:T(8,128)(2,1)S(1)}, bf16[2,128,1024]{2,1,0:T(8,128)(2,1)}, u32[]{:S(2)}, u32[]{:S(2)}) collective-permute-start(bf16[2,128,1024]{2,1,0:T(8,128)(2,1)S(1)} %pad_maximum_fusion.1.refs_4_), channel_id=1, source_target_pairs={{0,3},{1,0},{2,1},{3,2},{4,7},{5,4},{6,5},{7,6},{8,11},{9,8},{10,9... | collective-permute-start | bytes 1572872 | tf_op jit(solution)/shard_map/ppermute | solution.py:34
  193.3 2.4 collective-permute-done.36.refs_1_
  195.9 6.3 %collective-permute-done.38.refs_3_ = bf16[128,1024]{1,0:T(8,128)(2,1)S(1)} collective-permute-done((bf16[128,1024]{1,0:T(8,128)(2,1)S(1)}, bf16[128,1024]{1,0:T(8,128)(2,1)S(1)}, u32[]{:S(2)}, u32[]{:S(2)}) %collective-permute-start.38) | collective-permute-done | bytes 262176 | tf_op jit(solution)/shard_map/ppermute | solution.py:34
  207.9 2.9 %shard_map.67.turned = bf16[1024,1024]{1,0:T(8,128)(2,1)} custom-call(bf16[256,1024]{1,0:T(8,128)(2,1)} %get-tuple-element.26.refs_0_, bf16[256,1024]{1,0:T(8,128)(2,1)} %copy-done.9, bf16[256,1024]{1,0:T(8,128)(2,1)} %collective-permute-done.1.refs_2_, bf16[256,1024]{1,0:T(8,128)(2,1)} %collective-permute-done.2.refs_3_), custom_call_target="tpu_custom_call" | custom-call | flops 536870912 | bytes 4194304 | tf_op jit(solution)/shard_map/pallas_call | solution.py:148
  210.8 5.7 %grad_v.1 = (f32[256,1024]{1,0:T(8,128)}, bf16[256,1024]{1,0:T(8,128)(2,1)}, bf16[256,1024]{1,0:T(8,128)(2,1)}, bf16[256,1024]{1,0:T(8,128)(2,1)}) custom-call(bf16[1024,1024]{1,0:T(8,128)(2,1)} %shard_map.67.turned, bf16[128,1024]{1,0:T(8,128)(2,1)} %copy-done.14, bf16[128,1024]{1,0:T(8,128)(2,1)} %copy-done.20, bf16[128,1024]{1,0:T(8,128)(2,1)} %copy-done.21, ...), custom_call_target="tpu_custom_call" | custom-call | flops 2147483648 | bytes 8388608 | tf_op jit(solution)/shard_map/grad_v/pallas_call | solution.py:175
  218.0 6.0 %collective-permute-start.43 = (bf16[256,1024]{1,0:T(8,128)(2,1)}, bf16[256,1024]{1,0:T(8,128)(2,1)S(1)}, u32[]{:S(2)}, u32[]{:S(2)}) collective-permute-start(bf16[256,1024]{1,0:T(8,128)(2,1)} %get-tuple-element.42), channel_id=1, source_target_pairs={{0,3},{1,0},{2,1},{3,2},{4,7},{5,4},{6,5},{7,6},{8,11},{9,8},{10,9... | collective-permute-start | bytes 1572872 | tf_op jit(solution)/shard_map/ppermute | solution.py:34
  224.0 2.9 %shard_map.70.turned = bf16[1024,1024]{1,0:T(8,128)(2,1)} custom-call(bf16[256,1024]{1,0:T(8,128)(2,1)} %get-tuple-element.30.refs_0_, bf16[256,1024]{1,0:T(8,128)(2,1)} %copy-done.8, bf16[256,1024]{1,0:T(8,128)(2,1)} %collective-permute-done.4.refs_2_, bf16[256,1024]{1,0:T(8,128)(2,1)} %collective-permute-done.5.refs_3_), custom_call_target="tpu_custom_call" | custom-call | flops 536870912 | bytes 4194304 | tf_op jit(solution)/shard_map/pallas_call | solution.py:148
  228.7 10.0 %grad_u.1 = (f32[256,1024]{1,0:T(8,128)}, bf16[256,1024]{1,0:T(8,128)(2,1)}, bf16[256,1024]{1,0:T(8,128)(2,1)}, bf16[256,1024]{1,0:T(8,128)(2,1)}) custom-call(s32[5]{0:T(128)} %stack.43.at_ref, bf16[1024,1024]{1,0:T(8,128)(2,1)} %shard_map.70.turned, bf16[256,1024]{1,0:T(8,128)(2,1)} %copy-done.2, bf16[256,1024]{1,0:T(8,128)(2,1)} %copy-done.15, ...), custom_call_target="tpu_custom_call" | custom-call | flops 4294967296 | bytes 16777216 | tf_op jit(solution)/shard_map/grad_u/pallas_call | solution.py:228
  238.7 2.5 collective-permute-start.56
  241.2 5.3 %collective-permute-done.43 = bf16[256,1024]{1,0:T(8,128)(2,1)S(1)} collective-permute-done((bf16[256,1024]{1,0:T(8,128)(2,1)}, bf16[256,1024]{1,0:T(8,128)(2,1)S(1)}, u32[]{:S(2)}, u32[]{:S(2)}) %collective-permute-start.43) | collective-permute-done | bytes 524320 | tf_op jit(solution)/shard_map/ppermute | solution.py:34
  246.5 7.0 %collective-permute-done.45 = bf16[256,1024]{1,0:T(8,128)(2,1)} collective-permute-done((bf16[256,1024]{1,0:T(8,128)(2,1)S(1)}, bf16[256,1024]{1,0:T(8,128)(2,1)}, u32[]{:S(2)}, u32[]{:S(2)}) %collective-permute-start.45) | collective-permute-done | bytes 524320 | tf_op jit(solution)/shard_map/ppermute | solution.py:34
  253.5 2.0 multiply_reduce_fusion
  255.5 7.7 %collective-permute-done.56 = bf16[256,1024]{1,0:T(8,128)(2,1)S(1)} collective-permute-done((bf16[256,1024]{1,0:T(8,128)(2,1)}, bf16[256,1024]{1,0:T(8,128)(2,1)S(1)}, u32[]{:S(2)}, u32[]{:S(2)}) %collective-permute-start.56) | collective-permute-done | bytes 524320 | tf_op jit(solution)/shard_map/ppermute | solution.py:34
  263.2 3.6 %collective-permute-done.58 = bf16[256,1024]{1,0:T(8,128)(2,1)S(1)} collective-permute-done((bf16[256,1024]{1,0:T(8,128)(2,1)}, bf16[256,1024]{1,0:T(8,128)(2,1)S(1)}, u32[]{:S(2)}, u32[]{:S(2)}) %collective-permute-start.58) | collective-permute-done | bytes 524320 | tf_op jit(solution)/shard_map/ppermute | solution.py:34
  269.0 15.6 %all_to_all.17 = f32[128,1,128]{2,1,0:T(1,128)S(1)} all-to-all(f32[128,1,128]{2,1,0:T(1,128)S(1)} %broadcast_in_dim.16), channel_id=1, replica_groups=mesh['p'=2,'h'=2,'c'=2,'z'=4,'y'=4] {'p','h','c','z','y'}, dimensions={0} | all-to-all | bytes 131072 | tf_op jit(solution)/shard_map/all_to_all | solution.py:29
  (174 shorter events, 48.8 us)
Async XLA Ops:
  3.0 13.6 %collective-permute-start.6 = (bf16[256,1024]{1,0:T(8,128)(2,1)S(1)}, bf16[256,1024]{1,0:T(8,128)(2,1)S(1)}, u32[]{:S(2)}, u32[]{:S(2)}) collective-permute-start(bf16[256,1024]{1,0:T(8,128)(2,1)S(1)} %get-tuple-element.34.refs_4_), channel_id=1, source_target_pairs={{0,64},{64,0},{1,65},{65,1},{2,66},{66,2},{3,67},{67,3},{4,68},{68... | collective-permute-start | bytes 1572872 | tf_op jit(solution)/shard_map/ppermute | solution.py:299
  4.7 26.9 %collective-permute-start.7 = (bf16[256,1024]{1,0:T(8,128)(2,1)S(1)}, bf16[256,1024]{1,0:T(8,128)(2,1)S(1)}, u32[]{:S(2)}, u32[]{:S(2)}) collective-permute-start(bf16[256,1024]{1,0:T(8,128)(2,1)S(1)} %get-tuple-element.34.refs_4_), channel_id=1, source_target_pairs={{0,16},{16,0},{1,17},{17,1},{2,18},{18,2},{3,19},{19,3},{4,20},{20... | collective-permute-start | bytes 1572872 | tf_op jit(solution)/shard_map/ppermute | solution.py:34
  16.6 15.0 %collective-permute-start.8 = (bf16[256,1024]{1,0:T(8,128)(2,1)S(1)}, bf16[256,1024]{1,0:T(8,128)(2,1)S(1)}, u32[]{:S(2)}, u32[]{:S(2)}) collective-permute-start(bf16[256,1024]{1,0:T(8,128)(2,1)S(1)} %collective-permute-done.6.refs_0_), channel_id=1, source_target_pairs={{0,16},{16,0},{1,17},{17,1},{2,18},{18,2},{3,19},{19,3},{4,20},{20... | collective-permute-start | bytes 1572872 | tf_op jit(solution)/shard_map/ppermute | solution.py:34
  24.7 21.4 %collective-permute-start.3 = (bf16[256,1024]{1,0:T(8,128)(2,1)}, bf16[256,1024]{1,0:T(8,128)(2,1)S(1)}, u32[]{:S(2)}, u32[]{:S(2)}) collective-permute-start(bf16[256,1024]{1,0:T(8,128)(2,1)} %get-tuple-element.31), channel_id=1, source_target_pairs={{0,1},{1,2},{2,3},{3,0},{4,5},{5,6},{6,7},{7,4},{8,9},{9,10},{10,1... | collective-permute-start | bytes 1572872 | tf_op jit(solution)/shard_map/ppermute | solution.py:34
  26.6 30.1 %collective-permute-start.4 = (bf16[256,1024]{1,0:T(8,128)(2,1)}, bf16[256,1024]{1,0:T(8,128)(2,1)}, u32[]{:S(2)}, u32[]{:S(2)}) collective-permute-start(bf16[256,1024]{1,0:T(8,128)(2,1)} %get-tuple-element.32), channel_id=1, source_target_pairs={{0,2},{1,3},{2,0},{3,1},{4,6},{5,7},{6,4},{7,5},{8,10},{9,11},{10,... | collective-permute-start | bytes 1572872 | tf_op jit(solution)/shard_map/ppermute | solution.py:34
  29.5 29.1 %collective-permute-start.5 = (bf16[256,1024]{1,0:T(8,128)(2,1)}, bf16[256,1024]{1,0:T(8,128)(2,1)}, u32[]{:S(2)}, u32[]{:S(2)}) collective-permute-start(bf16[256,1024]{1,0:T(8,128)(2,1)} %get-tuple-element.33), channel_id=1, source_target_pairs={{0,3},{1,0},{2,1},{3,2},{4,7},{5,4},{6,5},{7,6},{8,11},{9,8},{10,9... | collective-permute-start | bytes 1572872 | tf_op jit(solution)/shard_map/ppermute | solution.py:34
  33.3 28.9 %all-to-all-start = ((bf16[32,8,1024]{2,1,0:T(8,128)(2,1)}), bf16[32,8,1024]{2,1,0:T(8,128)(2,1)S(1)}, u32[]{:S(2)}, u32[]{:S(2)}) async-start(bf16[32,8,1024]{2,1,0:T(8,128)(2,1)} %bitcast.12), calls=%async_computation | async-start | bytes 1048576 | tf_op jit(solution)/shard_map/all_to_all | solution.py:29
  41.6 30.3 %collective-permute-start.10 = (bf16[256,1024]{1,0:T(8,128)(2,1)S(1)}, bf16[256,1024]{1,0:T(8,128)(2,1)}, u32[]{:S(2)}, u32[]{:S(2)}) collective-permute-start(bf16[256,1024]{1,0:T(8,128)(2,1)S(1)} %get-tuple-element.34.refs_4_), channel_id=1, source_target_pairs={{0,8},{4,12},{8,0},{12,4},{1,9},{5,13},{9,1},{13,5},{2,10},{6,14},... | collective-permute-start | bytes 1572872 | tf_op jit(solution)/shard_map/ppermute | solution.py:34
  45.0 29.8 %collective-permute-start.11 = (bf16[256,1024]{1,0:T(8,128)(2,1)S(1)}, bf16[256,1024]{1,0:T(8,128)(2,1)}, u32[]{:S(2)}, u32[]{:S(2)}) collective-permute-start(bf16[256,1024]{1,0:T(8,128)(2,1)S(1)} %get-tuple-element.34.refs_4_), channel_id=1, source_target_pairs={{0,12},{4,0},{8,4},{12,8},{1,13},{5,1},{9,5},{13,9},{2,14},{6,2},{... | collective-permute-start | bytes 1572872 | tf_op jit(solution)/shard_map/ppermute | solution.py:34
  46.1 31.1 %collective-permute-start.9 = (bf16[256,1024]{1,0:T(8,128)(2,1)S(1)}, bf16[256,1024]{1,0:T(8,128)(2,1)}, u32[]{:S(2)}, u32[]{:S(2)}) collective-permute-start(bf16[256,1024]{1,0:T(8,128)(2,1)S(1)} %get-tuple-element.34.refs_4_), channel_id=1, source_target_pairs={{0,4},{4,8},{8,12},{12,0},{1,5},{5,9},{9,13},{13,1},{2,6},{6,10},{... | collective-permute-start | bytes 1572872 | tf_op jit(solution)/shard_map/ppermute | solution.py:34
  56.7 29.2 %collective-permute-start = (bf16[256,1024]{1,0:T(8,128)(2,1)}, bf16[256,1024]{1,0:T(8,128)(2,1)S(1)}, u32[]{:S(2)}, u32[]{:S(2)}) collective-permute-start(bf16[256,1024]{1,0:T(8,128)(2,1)} %get-tuple-element.27), channel_id=1, source_target_pairs={{0,4},{4,8},{8,12},{12,0},{1,5},{5,9},{9,13},{13,1},{2,6},{6,10},{... | collective-permute-start | bytes 1572872 | tf_op jit(solution)/shard_map/ppermute | solution.py:34
  58.6 37.0 %collective-permute-start.1 = (bf16[256,1024]{1,0:T(8,128)(2,1)}, bf16[256,1024]{1,0:T(8,128)(2,1)}, u32[]{:S(2)}, u32[]{:S(2)}) collective-permute-start(bf16[256,1024]{1,0:T(8,128)(2,1)} %get-tuple-element.28), channel_id=1, source_target_pairs={{0,8},{4,12},{8,0},{12,4},{1,9},{5,13},{9,1},{13,5},{2,10},{6,14},... | collective-permute-start | bytes 1572872 | tf_op jit(solution)/shard_map/ppermute | solution.py:34
  71.9 29.8 %collective-permute-start.16 = (bf16[256,1024]{1,0:T(8,128)(2,1)S(1)}, bf16[256,1024]{1,0:T(8,128)(2,1)}, u32[]{:S(2)}, u32[]{:S(2)}) collective-permute-start(bf16[256,1024]{1,0:T(8,128)(2,1)S(1)} %get-tuple-element.37.refs_4_), channel_id=1, source_target_pairs={{0,1},{1,2},{2,3},{3,0},{4,5},{5,6},{6,7},{7,4},{8,9},{9,10},{10,1... | collective-permute-start | bytes 1572872 | tf_op jit(solution)/shard_map/ppermute | solution.py:34
  74.8 29.7 %collective-permute-start.17 = (bf16[256,1024]{1,0:T(8,128)(2,1)S(1)}, bf16[256,1024]{1,0:T(8,128)(2,1)}, u32[]{:S(2)}, u32[]{:S(2)}) collective-permute-start(bf16[256,1024]{1,0:T(8,128)(2,1)S(1)} %get-tuple-element.37.refs_4_), channel_id=1, source_target_pairs={{0,2},{1,3},{2,0},{3,1},{4,6},{5,7},{6,4},{7,5},{8,10},{9,11},{10,... | collective-permute-start | bytes 1572872 | tf_op jit(solution)/shard_map/ppermute | solution.py:34
  77.3 28.3 %collective-permute-start.18 = (bf16[256,1024]{1,0:T(8,128)(2,1)S(1)}, bf16[256,1024]{1,0:T(8,128)(2,1)}, u32[]{:S(2)}, u32[]{:S(2)}) collective-permute-start(bf16[256,1024]{1,0:T(8,128)(2,1)S(1)} %get-tuple-element.37.refs_4_), channel_id=1, source_target_pairs={{0,3},{1,0},{2,1},{3,2},{4,7},{5,4},{6,5},{7,6},{8,11},{9,8},{10,9... | collective-permute-start | bytes 1572872 | tf_op jit(solution)/shard_map/ppermute | solution.py:34
  85.9 14.4 %collective-permute-start.2 = (bf16[256,1024]{1,0:T(8,128)(2,1)}, bf16[256,1024]{1,0:T(8,128)(2,1)}, u32[]{:S(2)}, u32[]{:S(2)}) collective-permute-start(bf16[256,1024]{1,0:T(8,128)(2,1)} %get-tuple-element.29), channel_id=1, source_target_pairs={{0,12},{4,0},{8,4},{12,8},{1,13},{5,1},{9,5},{13,9},{2,14},{6,2},{... | collective-permute-start | bytes 1572872 | tf_op jit(solution)/shard_map/ppermute | solution.py:34
  95.6 18.8 %collective-permute-start.12 = (bf16[512,1024]{1,0:T(8,128)(2,1)}, bf16[512,1024]{1,0:T(8,128)(2,1)S(1)}, u32[]{:S(2)}, u32[]{:S(2)}) collective-permute-start(bf16[512,1024]{1,0:T(8,128)(2,1)} %get-tuple-element.36), channel_id=1, source_target_pairs={{0,16},{16,0},{1,17},{17,1},{2,18},{18,2},{3,19},{19,3},{4,20},{20... | collective-permute-start | bytes 3145736 | tf_op jit(solution)/shard_map/ppermute | solution.py:34
  100.3 11.0 %collective-permute-start.26 = (bf16[32,1024]{1,0:T(8,128)(2,1)S(1)}, bf16[32,1024]{1,0:T(8,128)(2,1)S(1)}, u32[]{:S(2)}, u32[]{:S(2)}) collective-permute-start(bf16[32,1024]{1,0:T(8,128)(2,1)S(1)} %bitcast.45), channel_id=1, source_target_pairs={{0,1},{1,2},{2,3},{3,0},{4,5},{5,6},{6,7},{7,4},{8,9},{9,10},{10,1... | collective-permute-start | bytes 196616 | tf_op jit(solution)/shard_map/ppermute | solution.py:34
  101.6 9.6 %collective-permute-start.27 = (bf16[32,1024]{1,0:T(8,128)(2,1)S(1)}, bf16[32,1024]{1,0:T(8,128)(2,1)S(1)}, u32[]{:S(2)}, u32[]{:S(2)}) collective-permute-start(bf16[32,1024]{1,0:T(8,128)(2,1)S(1)} %bitcast.46), channel_id=1, source_target_pairs={{0,2},{1,3},{2,0},{3,1},{4,6},{5,7},{6,4},{7,5},{8,10},{9,11},{10,... | collective-permute-start | bytes 196616 | tf_op jit(solution)/shard_map/ppermute | solution.py:34
  111.3 33.4 %collective-permute-start.29 = (bf16[128,1024]{1,0:T(8,128)(2,1)S(1)}, bf16[128,1024]{1,0:T(8,128)(2,1)S(1)}, u32[]{:S(2)}, u32[]{:S(2)}) collective-permute-start(bf16[128,1024]{1,0:T(8,128)(2,1)S(1)} %constant_dynamic-update-slice_fusion.refs_0_), channel_id=1, source_target_pairs={{0,4},{4,8},{8,12},{12,0},{1,5},{5,9},{9,13},{13,1},{2,6},{6,10},{... | collective-permute-start | bytes 786440 | tf_op jit(solution)/shard_map/ppermute | solution.py:34
  111.4 36.0 %collective-permute-start.30 = (bf16[128,1024]{1,0:T(8,128)(2,1)S(1)}, bf16[128,1024]{1,0:T(8,128)(2,1)S(1)}, u32[]{:S(2)}, u32[]{:S(2)}) collective-permute-start(bf16[128,1024]{1,0:T(8,128)(2,1)S(1)} %constant_dynamic-update-slice_fusion.refs_0_), channel_id=1, source_target_pairs={{0,8},{4,12},{8,0},{12,4},{1,9},{5,13},{9,1},{13,5},{2,10},{6,14},... | collective-permute-start | bytes 786440 | tf_op jit(solution)/shard_map/ppermute | solution.py:34
  116.6 9.2 %collective-permute-start.13 = (bf16[128,1024]{1,0:T(8,128)(2,1)S(1)}, bf16[128,1024]{1,0:T(8,128)(2,1)S(1)}, u32[]{:S(2)}, u32[]{:S(2)}) collective-permute-start(bf16[128,1024]{1,0:T(8,128)(2,1)S(1)} %get-tuple-element.72), channel_id=1, source_target_pairs={{0,3},{1,0},{2,1},{3,2},{4,7},{5,4},{6,5},{7,6},{8,11},{9,8},{10,9... | collective-permute-start | bytes 786440 | tf_op jit(solution)/shard_map/ppermute | solution.py:34
  116.8 10.7 %collective-permute-start.14 = (bf16[128,1024]{1,0:T(8,128)(2,1)S(1)}, bf16[128,1024]{1,0:T(8,128)(2,1)S(1)}, u32[]{:S(2)}, u32[]{:S(2)}) collective-permute-start(bf16[128,1024]{1,0:T(8,128)(2,1)S(1)} %get-tuple-element.74), channel_id=1, source_target_pairs={{0,2},{1,3},{2,0},{3,1},{4,6},{5,7},{6,4},{7,5},{8,10},{9,11},{10,... | collective-permute-start | bytes 786440 | tf_op jit(solution)/shard_map/ppermute | solution.py:34
  119.6 12.4 %collective-permute-start.15 = (bf16[128,1024]{1,0:T(8,128)(2,1)S(1)}, bf16[128,1024]{1,0:T(8,128)(2,1)S(1)}, u32[]{:S(2)}, u32[]{:S(2)}) collective-permute-start(bf16[128,1024]{1,0:T(8,128)(2,1)S(1)} %get-tuple-element.73), channel_id=1, source_target_pairs={{0,1},{1,2},{2,3},{3,0},{4,5},{5,6},{6,7},{7,4},{8,9},{9,10},{10,1... | collective-permute-start | bytes 786440 | tf_op jit(solution)/shard_map/ppermute | solution.py:34
  132.0 9.5 %collective-permute-start.22 = (bf16[128,1024]{1,0:T(8,128)(2,1)S(1)}, bf16[128,1024]{1,0:T(8,128)(2,1)S(1)}, u32[]{:S(2)}, u32[]{:S(2)}) collective-permute-start(bf16[128,1024]{1,0:T(8,128)(2,1)S(1)} %get-tuple-element.76), channel_id=1, source_target_pairs={{0,4},{4,8},{8,12},{12,0},{1,5},{5,9},{9,13},{13,1},{2,6},{6,10},{... | collective-permute-start | bytes 786440 | tf_op jit(solution)/shard_map/ppermute | solution.py:34
  134.9 12.5 %collective-permute-start.31 = (bf16[128,1024]{1,0:T(8,128)(2,1)S(1)}, bf16[128,1024]{1,0:T(8,128)(2,1)S(1)}, u32[]{:S(2)}, u32[]{:S(2)}) collective-permute-start(bf16[128,1024]{1,0:T(8,128)(2,1)S(1)} %constant_dynamic-update-slice_fusion.refs_0_), channel_id=1, source_target_pairs={{0,12},{4,0},{8,4},{12,8},{1,13},{5,1},{9,5},{13,9},{2,14},{6,2},{... | collective-permute-start | bytes 786440 | tf_op jit(solution)/shard_map/ppermute | solution.py:34
  141.7 9.4 %collective-permute-start.23 = (bf16[32,2048]{1,0:T(8,128)(2,1)S(1)}, bf16[32,2048]{1,0:T(8,128)(2,1)S(1)}, u32[]{:S(2)}, u32[]{:S(2)}) collective-permute-start(bf16[32,2048]{1,0:T(8,128)(2,1)S(1)} %get-tuple-element.80), channel_id=1, source_target_pairs={{0,32},{32,0},{64,96},{96,64},{1,33},{33,1},{65,97},{97,65},{2,34}... | collective-permute-start | bytes 393224 | tf_op jit(solution)/shard_map/ppermute | solution.py:43
  155.4 12.4 %collective-permute-start.33 = (bf16[3,32,1024]{2,1,0:T(8,128)(2,1)S(1)}, bf16[3,32,1024]{2,1,0:T(8,128)(2,1)S(1)}, u32[]{:S(2)}, u32[]{:S(2)}) collective-permute-start(bf16[3,32,1024]{2,1,0:T(8,128)(2,1)S(1)} %get-tuple-element.84), channel_id=1, source_target_pairs={{0,64},{32,96},{64,32},{96,0},{1,65},{33,97},{65,33},{97,1},{2,66}... | collective-permute-start | bytes 589832 | tf_op jit(solution)/shard_map/ppermute | solution.py:43
  155.5 12.4 %collective-permute-start.34 = (bf16[3,32,1024]{2,1,0:T(8,128)(2,1)S(1)}, bf16[3,32,1024]{2,1,0:T(8,128)(2,1)S(1)}, u32[]{:S(2)}, u32[]{:S(2)}) collective-permute-start(bf16[3,32,1024]{2,1,0:T(8,128)(2,1)S(1)} %get-tuple-element.83), channel_id=1, source_target_pairs={{0,32},{32,0},{64,96},{96,64},{1,33},{33,1},{65,97},{97,65},{2,34}... | collective-permute-start | bytes 589832 | tf_op jit(solution)/shard_map/ppermute | solution.py:43
  157.1 11.4 %collective-permute-start.35 = (bf16[3,32,1024]{2,1,0:T(8,128)(2,1)S(1)}, bf16[3,32,1024]{2,1,0:T(8,128)(2,1)S(1)}, u32[]{:S(2)}, u32[]{:S(2)}) collective-permute-start(bf16[3,32,1024]{2,1,0:T(8,128)(2,1)S(1)} %get-tuple-element.84), channel_id=1, source_target_pairs={{0,96},{32,64},{64,0},{96,32},{1,97},{33,65},{65,1},{97,33},{2,98}... | collective-permute-start | bytes 589832 | tf_op jit(solution)/shard_map/ppermute | solution.py:43
  158.7 27.2 %collective-permute-start.46 = (bf16[256,1024]{1,0:T(8,128)(2,1)S(1)}, bf16[256,1024]{1,0:T(8,128)(2,1)S(1)}, u32[]{:S(2)}, u32[]{:S(2)}) collective-permute-start(bf16[256,1024]{1,0:T(8,128)(2,1)S(1)} %collective-permute-done.6.refs_0_), channel_id=1, source_target_pairs={{0,4},{4,8},{8,12},{12,0},{1,5},{5,9},{9,13},{13,1},{2,6},{6,10},{... | collective-permute-start | bytes 1572872 | tf_op jit(solution)/shard_map/ppermute | solution.py:34
  158.7 29.9 %collective-permute-start.47 = (bf16[256,1024]{1,0:T(8,128)(2,1)S(1)}, bf16[256,1024]{1,0:T(8,128)(2,1)S(1)}, u32[]{:S(2)}, u32[]{:S(2)}) collective-permute-start(bf16[256,1024]{1,0:T(8,128)(2,1)S(1)} %collective-permute-done.6.refs_0_), channel_id=1, source_target_pairs={{0,8},{4,12},{8,0},{12,4},{1,9},{5,13},{9,1},{13,5},{2,10},{6,14},... | collective-permute-start | bytes 1572872 | tf_op jit(solution)/shard_map/ppermute | solution.py:34
  168.5 27.3 %collective-permute-start.36 = (bf16[128,1024]{1,0:T(8,128)(2,1)S(1)}, bf16[128,1024]{1,0:T(8,128)(2,1)S(1)}, u32[]{:S(2)}, u32[]{:S(2)}) collective-permute-start(bf16[128,1024]{1,0:T(8,128)(2,1)S(1)} %maximum_bitcast_fusion.refs_0_), channel_id=1, source_target_pairs={{0,4},{4,8},{8,12},{12,0},{1,5},{5,9},{9,13},{13,1},{2,6},{6,10},{... | collective-permute-start | bytes 786440 | tf_op jit(solution)/shard_map/ppermute | solution.py:34
  168.5 27.2 %collective-permute-start.37 = (bf16[128,1024]{1,0:T(8,128)(2,1)S(1)}, bf16[128,1024]{1,0:T(8,128)(2,1)S(1)}, u32[]{:S(2)}, u32[]{:S(2)}) collective-permute-start(bf16[128,1024]{1,0:T(8,128)(2,1)S(1)} %maximum_bitcast_fusion.refs_0_), channel_id=1, source_target_pairs={{0,8},{4,12},{8,0},{12,4},{1,9},{5,13},{9,1},{13,5},{2,10},{6,14},... | collective-permute-start | bytes 786440 | tf_op jit(solution)/shard_map/ppermute | solution.py:34
  170.9 31.8 %collective-permute-start.49 = (bf16[2,128,1024]{2,1,0:T(8,128)(2,1)S(1)}, bf16[2,128,1024]{2,1,0:T(8,128)(2,1)}, u32[]{:S(2)}, u32[]{:S(2)}) collective-permute-start(bf16[2,128,1024]{2,1,0:T(8,128)(2,1)S(1)} %pad_maximum_fusion.1.refs_4_), channel_id=1, source_target_pairs={{0,1},{1,2},{2,3},{3,0},{4,5},{5,6},{6,7},{7,4},{8,9},{9,10},{10,1... | collective-permute-start | bytes 1572872 | tf_op jit(solution)/shard_map/ppermute | solution.py:34
  185.9 17.0 %collective-permute-start.50 = (bf16[2,128,1024]{2,1,0:T(8,128)(2,1)S(1)}, bf16[2,128,1024]{2,1,0:T(8,128)(2,1)}, u32[]{:S(2)}, u32[]{:S(2)}) collective-permute-start(bf16[2,128,1024]{2,1,0:T(8,128)(2,1)S(1)} %pad_maximum_fusion.1.refs_4_), channel_id=1, source_target_pairs={{0,2},{1,3},{2,0},{3,1},{4,6},{5,7},{6,4},{7,5},{8,10},{9,11},{10,... | collective-permute-start | bytes 1572872 | tf_op jit(solution)/shard_map/ppermute | solution.py:34
  188.6 17.2 %collective-permute-start.51 = (bf16[2,128,1024]{2,1,0:T(8,128)(2,1)S(1)}, bf16[2,128,1024]{2,1,0:T(8,128)(2,1)}, u32[]{:S(2)}, u32[]{:S(2)}) collective-permute-start(bf16[2,128,1024]{2,1,0:T(8,128)(2,1)S(1)} %pad_maximum_fusion.1.refs_4_), channel_id=1, source_target_pairs={{0,3},{1,0},{2,1},{3,2},{4,7},{5,4},{6,5},{7,6},{8,11},{9,8},{10,9... | collective-permute-start | bytes 1572872 | tf_op jit(solution)/shard_map/ppermute | solution.py:34
  202.9 14.3 %collective-permute-start.48 = (bf16[256,1024]{1,0:T(8,128)(2,1)S(1)}, bf16[256,1024]{1,0:T(8,128)(2,1)S(1)}, u32[]{:S(2)}, u32[]{:S(2)}) collective-permute-start(bf16[256,1024]{1,0:T(8,128)(2,1)S(1)} %collective-permute-done.6.refs_0_), channel_id=1, source_target_pairs={{0,12},{4,0},{8,4},{12,8},{1,13},{5,1},{9,5},{13,9},{2,14},{6,2},{... | collective-permute-start | bytes 1572872 | tf_op jit(solution)/shard_map/ppermute | solution.py:34
  205.8 21.1 %collective-permute-start.52 = (bf16[2,128,1024]{2,1,0:T(8,128)(2,1)S(1)}, bf16[2,128,1024]{2,1,0:T(8,128)(2,1)S(1)}, u32[]{:S(2)}, u32[]{:S(2)}) collective-permute-start(bf16[2,128,1024]{2,1,0:T(8,128)(2,1)S(1)} %pad_maximum_fusion.1.refs_4_), channel_id=1, source_target_pairs={{0,16},{16,0},{1,17},{17,1},{2,18},{18,2},{3,19},{19,3},{4,20},{20... | collective-permute-start | bytes 1572872 | tf_op jit(solution)/shard_map/ppermute | solution.py:34
  205.8 21.9 %collective-permute-start.53 = (bf16[2,128,1024]{2,1,0:T(8,128)(2,1)}, bf16[2,128,1024]{2,1,0:T(8,128)(2,1)}, u32[]{:S(2)}, u32[]{:S(2)}) collective-permute-start(bf16[2,128,1024]{2,1,0:T(8,128)(2,1)} %collective-permute-done.49.refs_5_), channel_id=1, source_target_pairs={{0,16},{16,0},{1,17},{17,1},{2,18},{18,2},{3,19},{19,3},{4,20},{20... | collective-permute-start | bytes 1572872 | tf_op jit(solution)/shard_map/ppermute | solution.py:34
  206.4 22.4 %collective-permute-start.54 = (bf16[2,128,1024]{2,1,0:T(8,128)(2,1)}, bf16[2,128,1024]{2,1,0:T(8,128)(2,1)}, u32[]{:S(2)}, u32[]{:S(2)}) collective-permute-start(bf16[2,128,1024]{2,1,0:T(8,128)(2,1)} %collective-permute-done.50.refs_6_), channel_id=1, source_target_pairs={{0,16},{16,0},{1,17},{17,1},{2,18},{18,2},{3,19},{19,3},{4,20},{20... | collective-permute-start | bytes 1572872 | tf_op jit(solution)/shard_map/ppermute | solution.py:34
  207.8 21.0 %collective-permute-start.55 = (bf16[2,128,1024]{2,1,0:T(8,128)(2,1)}, bf16[2,128,1024]{2,1,0:T(8,128)(2,1)}, u32[]{:S(2)}, u32[]{:S(2)}) collective-permute-start(bf16[2,128,1024]{2,1,0:T(8,128)(2,1)} %collective-permute-done.51.refs_7_), channel_id=1, source_target_pairs={{0,16},{16,0},{1,17},{17,1},{2,18},{18,2},{3,19},{19,3},{4,20},{20... | collective-permute-start | bytes 1572872 | tf_op jit(solution)/shard_map/ppermute | solution.py:34
  218.0 28.5 %collective-permute-start.43 = (bf16[256,1024]{1,0:T(8,128)(2,1)}, bf16[256,1024]{1,0:T(8,128)(2,1)S(1)}, u32[]{:S(2)}, u32[]{:S(2)}) collective-permute-start(bf16[256,1024]{1,0:T(8,128)(2,1)} %get-tuple-element.42), channel_id=1, source_target_pairs={{0,3},{1,0},{2,1},{3,2},{4,7},{5,4},{6,5},{7,6},{8,11},{9,8},{10,9... | collective-permute-start | bytes 1572872 | tf_op jit(solution)/shard_map/ppermute | solution.py:34
  227.7 18.7 %collective-permute-start.44 = (bf16[256,1024]{1,0:T(8,128)(2,1)}, bf16[256,1024]{1,0:T(8,128)(2,1)S(1)}, u32[]{:S(2)}, u32[]{:S(2)}) collective-permute-start(bf16[256,1024]{1,0:T(8,128)(2,1)} %get-tuple-element.43), channel_id=1, source_target_pairs={{0,2},{1,3},{2,0},{3,1},{4,6},{5,7},{6,4},{7,5},{8,10},{9,11},{10,... | collective-permute-start | bytes 1572872 | tf_op jit(solution)/shard_map/ppermute | solution.py:34
  227.8 25.8 %collective-permute-start.45 = (bf16[256,1024]{1,0:T(8,128)(2,1)S(1)}, bf16[256,1024]{1,0:T(8,128)(2,1)}, u32[]{:S(2)}, u32[]{:S(2)}) collective-permute-start(bf16[256,1024]{1,0:T(8,128)(2,1)S(1)} %copy-done.19), channel_id=1, source_target_pairs={{0,1},{1,2},{2,3},{3,0},{4,5},{5,6},{6,7},{7,4},{8,9},{9,10},{10,1... | collective-permute-start | bytes 1572872 | tf_op jit(solution)/shard_map/ppermute | solution.py:34
  238.7 24.5 %collective-permute-start.56 = (bf16[256,1024]{1,0:T(8,128)(2,1)}, bf16[256,1024]{1,0:T(8,128)(2,1)S(1)}, u32[]{:S(2)}, u32[]{:S(2)}) collective-permute-start(bf16[256,1024]{1,0:T(8,128)(2,1)} %get-tuple-element.46), channel_id=1, source_target_pairs={{0,12},{4,0},{8,4},{12,8},{1,13},{5,1},{9,5},{13,9},{2,14},{6,2},{... | collective-permute-start | bytes 1572872 | tf_op jit(solution)/shard_map/ppermute | solution.py:34
  241.2 22.0 %collective-permute-start.57 = (bf16[256,1024]{1,0:T(8,128)(2,1)}, bf16[256,1024]{1,0:T(8,128)(2,1)S(1)}, u32[]{:S(2)}, u32[]{:S(2)}) collective-permute-start(bf16[256,1024]{1,0:T(8,128)(2,1)} %get-tuple-element.47), channel_id=1, source_target_pairs={{0,8},{4,12},{8,0},{12,4},{1,9},{5,13},{9,1},{13,5},{2,10},{6,14},... | collective-permute-start | bytes 1572872 | tf_op jit(solution)/shard_map/ppermute | solution.py:34
  246.5 20.3 %collective-permute-start.58 = (bf16[256,1024]{1,0:T(8,128)(2,1)}, bf16[256,1024]{1,0:T(8,128)(2,1)S(1)}, u32[]{:S(2)}, u32[]{:S(2)}) collective-permute-start(bf16[256,1024]{1,0:T(8,128)(2,1)} %get-tuple-element.48), channel_id=1, source_target_pairs={{0,4},{4,8},{8,12},{12,0},{1,5},{5,9},{9,13},{13,1},{2,6},{6,10},{... | collective-permute-start | bytes 1572872 | tf_op jit(solution)/shard_map/ppermute | solution.py:34
  (39 other events, 684.7 us)

commit v5 on v3

--- a/solution.py
+++ b/solution.py
@@ -160,9 +160,15 @@
 
 
 def split_rows(outs, total):
-    own = outs[0].shape[0]
-    for j in range(4):
-        outs[j][...] = total[j * own : (j + 1) * own].astype(outs[j].dtype)
+    at = 0
+    for out in outs:
+        out[...] = total[at : at + out.shape[0]].astype(out.dtype)
+        at += out.shape[0]
+
+
+def piece_shapes(own, hidden):
+    halves = [jax.ShapeDtypeStruct((own // 2, hidden), BF)] * 6
+    return [jax.ShapeDtypeStruct((own, hidden), F32)] + halves
 
 
 def grad_v_kernel(turned, *refs):
@@ -176,11 +182,12 @@
     own, tile = wide // 4, hidden // 2
     return pl.pallas_call(
         grad_v_kernel,
-        out_shape=[jax.ShapeDtypeStruct((own, hidden), t) for t in (F32, BF, BF, BF)],
+        out_shape=piece_shapes(own, hidden),
         grid=(2,),
         in_specs=[pl.BlockSpec((wide, tok), lambda n: (0, 0))]
         + [pl.BlockSpec((half, tile), lambda n: (0, n))] * 8,
-        out_specs=[pl.BlockSpec((own, tile), lambda n: (0, n))] * 4,
+        out_specs=[pl.BlockSpec((own, tile), lambda n: (0, n))]
+        + [pl.BlockSpec((own // 2, tile), lambda n: (0, n))] * 6,
         cost_estimate=pl.CostEstimate(
             flops=2 * tok * wide * hidden, bytes_accessed=8 * tok * wide, transcendentals=0
         ),
@@ -189,8 +196,8 @@
 
 
 def grad_u_kernel(at_ref, turned, *refs):
-    w_refs, pairs, outs = refs[:4], refs[4:12], refs[12:16]
-    fold, factor, right, left = refs[16:]
+    w_refs, pairs, outs = refs[:4], refs[4:12], refs[12:19]
+    fold, factor, right, left = refs[19:]
     s = pl.program_id(0)
     own = w_refs[0].shape[0]
     half = pairs[0].shape[1]
@@ -229,13 +236,14 @@
 
     return pl.pallas_call(
         grad_u_kernel,
-        out_shape=[jax.ShapeDtypeStruct((own, hidden), t) for t in (F32, BF, BF, BF)],
+        out_shape=piece_shapes(own, hidden),
         grid=(4,),
         in_specs=[pl.BlockSpec(memory_space=pltpu.SMEM)]
         + [pl.BlockSpec((wide, tok // 2), lambda s: (0, jnp.minimum(s, 1)))]
         + [pl.BlockSpec((own, hidden), lambda s: (0, 0))] * 4
         + [pl.BlockSpec((2, tok // 8, hidden), lambda s: (0, 0, 0))] * 8,
-        out_specs=[pl.BlockSpec((own, tile), lambda s: (0, late(s)))] * 4,
+        out_specs=[pl.BlockSpec((own, tile), lambda s: (0, late(s)))]
+        + [pl.BlockSpec((own // 2, tile), lambda s: (0, late(s)))] * 6,
         scratch_shapes=[
             pltpu.VMEM((wide, hidden), BF),
             pltpu.VMEM((tok, hidden), BF),
@@ -283,6 +291,39 @@
 def sum_back(blocks, axis):
     parts = exchange([blocks[0]] + [b.astype(BF) for b in blocks[1:]], axis, -1)
     return sum((part.astype(F32) for part in parts[1:]), parts[0])
+
+
+def finish_kernel(own, low1, low3, high1, high3, out, squares):
+    half = low1.shape[0]
+    low = own[:half, :] + low1[...].astype(F32) + low3[...].astype(F32)
+    high = own[half:, :] + high1[...].astype(F32) + high3[...].astype(F32)
+    out[:half, :] = low
+    out[half:, :] = high
+    squares[0, 0] = jnp.sum(low * low + high * high)
+
+
+def finish(*parts):
+    vmem = pl.BlockSpec(memory_space=pltpu.VMEM)
+    return pl.pallas_call(
+        finish_kernel,
+        out_shape=[
+            jax.ShapeDtypeStruct(parts[0].shape, F32),
+            jax.ShapeDtypeStruct((1, 1), F32),
+        ],
+        in_specs=[vmem] * 5,
+        out_specs=[vmem, pl.BlockSpec(memory_space=pltpu.SMEM)],
+        name="finish",
+    )(*parts)
+
+
+def sum_near(pieces, axis):
+    own, low1, high1, low2, high2, low3, high3 = pieces
+    low2, high2 = shift(low2, axis, -1), shift(high2, axis, 1)
+    high1, low3 = shift(high1, axis, -1), shift(low3, axis, 1)
+    low1 = (low1.astype(F32) + low2.astype(F32)).astype(BF)
+    high3 = (high3.astype(F32) + high2.astype(F32)).astype(BF)
+    low1, high3 = shift(low1, axis, -1), shift(high3, axis, 1)
+    return finish(own, low1, low3, high1, high3)
 
 
 def on_device(inputs, w_in, w_out, cotangent):
@@ -362,15 +403,12 @@
     pair_own = shift(pairs[0], "c", 1)
     pairs += [pair_own] + [shift(a, "c", 1) for a in pairs[1:]]
 
-    g_v = grad_v_call(turn(vs), rs)
-    g_v = sum_back(g_v, "y")
-    g_u = grad_u_call(at, turn(us), pairs, w_3s)
-    g_u = sum_back(g_u, "z")
-
-    squares = jnp.sum(g_u * g_u) + jnp.sum(g_v * g_v)
-    for axes, count in ((("z", "y"), 16), (("p", "h", "c"), 8)):
-        row = jnp.broadcast_to(squares, (count, 8, 128))
-        squares = a2a(row, axes)[:, 0, 0].sum()
+    g_v, squares_v = sum_near(grad_v_call(turn(vs), rs), "y")
+    g_u, squares_u = sum_near(grad_u_call(at, turn(us), pairs, w_3s), "z")
+
+    squares = squares_u[0, 0] + squares_v[0, 0]
+    row = jnp.broadcast_to(squares, (lax.axis_size(AXES), 1, 128))
+    squares = a2a(row, AXES)[:, 0, 0].sum()
     grad_norm = jnp.sqrt(squares)
     factor = jnp.minimum(1.0, CLIP_NORM / grad_norm)
     g_in = jnp.where(first, g_v, g_u) * factor

time: 295 us -> 289 us (0.980)
  waiting for transfers between devices: 108 us -> 92.3 us
  starting transfers between devices: 87.5 us -> 96.4 us
  Pallas kernels: 40.1 us -> 45.8 us
  blocking collectives: 30.2 us -> 26.6 us
    ppermute x52 -> x58, waiting for transfers between devices: 88.6 us -> 72.9 us  [shift(): lax.ppermute(value, axis, [(i, (i + by) % count) for i in range(count)])]
    ppermute x52 -> x58, starting transfers between devices: 68.5 us -> 77.4 us  [shift(): lax.ppermute(value, axis, [(i, (i + by) % count) for i in range(count)])]
    pallas_call x2 -> x4, Pallas kernels: 15.6 us -> 21.1 us  [the longest x1 10 us: grad_u_call(): pl.pallas_call(grad_u_kernel, out_shape=piece_shapes(own, hidden), grid=(...]
    all_to_all x3 -> x2, blocking collectives: 30.2 us -> 26.6 us  [a2a(): return lax.all_to_all(value, axes, 0, 0, tiled=True)]
    reduce_sum x4 -> x1, other arithmetic: 4.09 us -> 0.73 us  [on_device(): squares = a2a(row, AXES)[:, 0, 0].sum()]
    unnamed x59 -> x87, local copies, waits for them, and re-layouts: 8.1 us -> 8.03 us
  transfers between devices with their start and end apart: 60 -> 66, of which waited for: 23 -> 21; matrix products, arithmetic and copies ran while one was open for 3% -> 3% of each run, Pallas kernels for 14% -> 15%
where the time goes in v5:
time: 289 us; the launch traced here: 287 us
  starting transfers between devices  96.4 us (33%)
  waiting for transfers between devices  92.3 us (32%)
  Pallas kernels  45.8 us (16%)
  blocking collectives  26.6 us (9%)
  local copies, waits for them, and re-layouts  9.79 us (3%)
  other arithmetic  8.71 us (3%)
  between operations  4.47 us (2%)
  matrix products  2.99 us (1%)
    ppermute x58, starting transfers between devices, shift(): lax.ppermute(value, axis, [(i, (i + by) % count) for i in range(count)])  77.4 us
    ppermute x58, waiting for transfers between devices, shift(): lax.ppermute(value, axis, [(i, (i + by) % count) for i in range(count)])  72.9 us
    all_to_all x2, blocking collectives, a2a(): return lax.all_to_all(value, axes, 0, 0, tiled=True)  26.6 us
    ppermute x1, waiting for transfers between devices, on_device(): w_3 = lax.ppermute(w_u, 'p', [(0, 1), (1, 0)])  11.9 us
    pallas_call x2, Pallas kernels, project(): pl.pallas_call(project_kernel, out_shape=[jax.ShapeDtypeStruct((2 * tok,...  11.5 us
    pallas_call x1, Pallas kernels, grad_u_call(): pl.pallas_call(grad_u_kernel, out_shape=piece_shapes(own, hidden), grid=(...  10 us
    ppermute x6, starting transfers between devices, shift_x(): return lax.ppermute(value, ('p', 'h'), pairs)  9.02 us
    all_to_all x1, starting transfers between devices, a2a(): return lax.all_to_all(value, axes, 0, 0, tiled=True)  8.27 us
  transfers between devices with their start and end apart: 66, of which 21 were waited for; matrix products, arithmetic and copies ran while one was open for 3% of the time, Pallas kernels for 15%

profile of v5, /device:TPU:0, one launch (start us, length us, event | category | flops | bytes accessed | tf_op | source)
XLA Modules:
  0.0 287.0 jit_solution(11197978180954898699)
XLA Ops:
  4.7 11.9 %collective-permute-done.6.refs_0_ = bf16[256,1024]{1,0:T(8,128)(2,1)S(1)} collective-permute-done((bf16[256,1024]{1,0:T(8,128)(2,1)S(1)}, bf16[256,1024]{1,0:T(8,128)(2,1)S(1)}, u32[]{:S(2)}, u32[]{:S(2)}) %collective-permute-start.6) | collective-permute-done | bytes 524320 | tf_op jit(solution)/shard_map/ppermute | solution.py:342
  17.4 5.0 %cut.1 = (bf16[256,1024]{1,0:T(8,128)(2,1)}, bf16[256,1024]{1,0:T(8,128)(2,1)}, bf16[256,1024]{1,0:T(8,128)(2,1)}, bf16[256,1024]{1,0:T(8,128)(2,1)}, bf16[256,1...) custom-call(s32[5]{0:T(128)} %stack.43.at_ref, ...), custom_call_target="tpu_custom_call" | custom-call | tf_op jit(solution)/shard_map/cut/pallas_call | solution.py:90
  24.2 2.9 %collective-permute-start.4 = (bf16[256,1024]{1,0:T(8,128)(2,1)}, bf16[256,1024]{1,0:T(8,128)(2,1)}, u32[]{:S(2)}, u32[]{:S(2)}) collective-permute-start(bf16[256,1024]{1,0:T(8,128)(2,1)} %get-tuple-element.42), channel_id=1, source_target_pairs={{0,2},{1,3},{2,0},{3,1},{4,6},{5,7},{6,4},{7,5},{8,10},{9,11},{10,... | collective-permute-start | bytes 1572872 | tf_op jit(solution)/shard_map/ppermute | solution.py:34
  30.9 8.3 %all-to-all-start = ((bf16[32,8,1024]{2,1,0:T(8,128)(2,1)}), bf16[32,8,1024]{2,1,0:T(8,128)(2,1)S(1)}, u32[]{:S(2)}, u32[]{:S(2)}) async-start(bf16[32,8,1024]{2,1,0:T(8,128)(2,1)} %bitcast.12), calls=%async_computation | async-start | bytes 1048576 | tf_op jit(solution)/shard_map/all_to_all | solution.py:29
  39.2 3.4 %collective-permute-start.10 = (bf16[256,1024]{1,0:T(8,128)(2,1)S(1)}, bf16[256,1024]{1,0:T(8,128)(2,1)}, u32[]{:S(2)}, u32[]{:S(2)}) collective-permute-start(bf16[256,1024]{1,0:T(8,128)(2,1)S(1)} %get-tuple-element.44.refs_4_), channel_id=1, source_target_pairs={{0,8},{4,12},{8,0},{12,4},{1,9},{5,13},{9,1},{13,5},{2,10},{6,14},... | collective-permute-start | bytes 1572872 | tf_op jit(solution)/shard_map/ppermute | solution.py:34
  44.7 9.7 %collective-permute-done.4.refs_2_ = bf16[256,1024]{1,0:T(8,128)(2,1)} collective-permute-done((bf16[256,1024]{1,0:T(8,128)(2,1)}, bf16[256,1024]{1,0:T(8,128)(2,1)}, u32[]{:S(2)}, u32[]{:S(2)}) %collective-permute-start.4) | collective-permute-done | bytes 524320 | tf_op jit(solution)/shard_map/ppermute | solution.py:34
  56.2 3.6 %collective-permute-start.1 = (bf16[256,1024]{1,0:T(8,128)(2,1)}, bf16[256,1024]{1,0:T(8,128)(2,1)}, u32[]{:S(2)}, u32[]{:S(2)}) collective-permute-start(bf16[256,1024]{1,0:T(8,128)(2,1)} %get-tuple-element.38), channel_id=1, source_target_pairs={{0,8},{4,12},{8,0},{12,4},{1,9},{5,13},{9,1},{13,5},{2,10},{6,14},... | collective-permute-start | bytes 1572872 | tf_op jit(solution)/shard_map/ppermute | solution.py:34
  59.9 9.5 %all_to_all.16 = bf16[4,8,1024]{2,1,0:T(8,128)(2,1)S(1)} all-to-all(bf16[4,8,1024]{2,1,0:T(8,128)(2,1)S(1)} %broadcast_in_dim.15), channel_id=1, replica_groups=mesh['p'=2,'h'=2,'c'=2,'z'=4,'y'=4] {'p','h'}, dimensions={0} | all-to-all | bytes 131072 | tf_op jit(solution)/shard_map/all_to_all | solution.py:29
  72.4 2.4 collective-permute-start.17
  74.8 1.9 collective-permute-start.18
  76.8 6.7 %collective-permute-done.refs_1_ = bf16[256,1024]{1,0:T(8,128)(2,1)S(1)} collective-permute-done((bf16[256,1024]{1,0:T(8,128)(2,1)}, bf16[256,1024]{1,0:T(8,128)(2,1)S(1)}, u32[]{:S(2)}, u32[]{:S(2)}) %collective-permute-start) | collective-permute-done | bytes 524320 | tf_op jit(solution)/shard_map/ppermute | solution.py:34
  84.1 5.6 %shard_map.68 = (bf16[512,1024]{1,0:T(8,128)(2,1)}, f32[512,1024]{1,0:T(8,128)}) custom-call(bf16[256,1024]{1,0:T(8,128)(2,1)} %get-tuple-element.40.refs_0_, bf16[256,1024]{1,0:T(8,128)(2,1)} %copy-done.8, bf16[256,1024]{1,0:T(8,128)(2,1)} %collective-permute-done.4.refs_2_, bf16[256,1024]{1,0:T(8,128)(2,1)} %collective-permute-done.5.refs_3_, ...), custom_call_target="tpu_custom_call" | custom-call | flops 2147483648 | bytes 4194304 | tf_op jit(solution)/shard_map/pallas_call | solution.py:121
  89.7 3.4 %collective-permute-done.1.refs_2_ = bf16[256,1024]{1,0:T(8,128)(2,1)} collective-permute-done((bf16[256,1024]{1,0:T(8,128)(2,1)}, bf16[256,1024]{1,0:T(8,128)(2,1)}, u32[]{:S(2)}, u32[]{:S(2)}) %collective-permute-start.1) | collective-permute-done | bytes 524320 | tf_op jit(solution)/shard_map/ppermute | solution.py:34
  93.2 4.5 %collective-permute-done.2.refs_3_ = bf16[256,1024]{1,0:T(8,128)(2,1)S(1)} collective-permute-done((bf16[256,1024]{1,0:T(8,128)(2,1)}, bf16[256,1024]{1,0:T(8,128)(2,1)S(1)}, u32[]{:S(2)}, u32[]{:S(2)}) %collective-permute-start.2) | collective-permute-done | bytes 524320 | tf_op jit(solution)/shard_map/ppermute | solution.py:34
  99.1 2.8 collective-permute-start.27
  103.1 5.8 %shard_map.69 = (bf16[512,1024]{1,0:T(8,128)(2,1)}, f32[512,1024]{1,0:T(8,128)}) custom-call(bf16[256,1024]{1,0:T(8,128)(2,1)} %get-tuple-element.36.refs_0_, bf16[256,1024]{1,0:T(8,128)(2,1)} %copy-done.9, bf16[256,1024]{1,0:T(8,128)(2,1)} %collective-permute-done.1.refs_2_, bf16[256,1024]{1,0:T(8,128)(2,1)} %copy-done.10, bf16[256,1024]{1,0:T(8,128)(2,1)} %copy-done.6, ...), custom_call_target="tpu_custom_call" | custom-call | flops 2147483648 | bytes 4194304 | tf_op jit(solution)/shard_map/pallas_call | solution.py:121
  109.1 2.9 %collective-permute-start.30 = (bf16[128,1024]{1,0:T(8,128)(2,1)S(1)}, bf16[128,1024]{1,0:T(8,128)(2,1)S(1)}, u32[]{:S(2)}, u32[]{:S(2)}) collective-permute-start(bf16[128,1024]{1,0:T(8,128)(2,1)S(1)} %constant_dynamic-update-slice_fusion.refs_0_), channel_id=1, source_target_pairs={{0,8},{4,12},{8,0},{12,4},{1,9},{5,13},{9,1},{13,5},{2,10},{6,14},... | collective-permute-start | bytes 786440 | tf_op jit(solution)/shard_map/ppermute | solution.py:34
  114.1 2.8 collective-permute-start.14
  117.6 5.6 %collective-permute-done.13 = bf16[128,1024]{1,0:T(8,128)(2,1)S(1)} collective-permute-done((bf16[128,1024]{1,0:T(8,128)(2,1)S(1)}, bf16[128,1024]{1,0:T(8,128)(2,1)S(1)}, u32[]{:S(2)}, u32[]{:S(2)}) %collective-permute-start.13) | collective-permute-done | bytes 262176 | tf_op jit(solution)/shard_map/ppermute | solution.py:34
  126.3 3.0 %collective-permute-done.15 = bf16[128,1024]{1,0:T(8,128)(2,1)S(1)} collective-permute-done((bf16[128,1024]{1,0:T(8,128)(2,1)S(1)}, bf16[128,1024]{1,0:T(8,128)(2,1)S(1)}, u32[]{:S(2)}, u32[]{:S(2)}) %collective-permute-start.15) | collective-permute-done | bytes 262176 | tf_op jit(solution)/shard_map/ppermute | solution.py:34
  133.4 5.4 %collective-permute-done.22 = bf16[128,1024]{1,0:T(8,128)(2,1)S(1)} collective-permute-done((bf16[128,1024]{1,0:T(8,128)(2,1)S(1)}, bf16[128,1024]{1,0:T(8,128)(2,1)S(1)}, u32[]{:S(2)}, u32[]{:S(2)}) %collective-permute-start.22) | collective-permute-done | bytes 262176 | tf_op jit(solution)/shard_map/ppermute | solution.py:34
  139.0 2.5 collective-permute-start.23
  142.1 2.6 collective-permute-start.25
  146.2 2.2 join.1
  156.0 2.3 collective-permute-start.50
  158.3 6.8 %collective-permute-done.33 = bf16[3,32,1024]{2,1,0:T(8,128)(2,1)S(1)} collective-permute-done((bf16[3,32,1024]{2,1,0:T(8,128)(2,1)S(1)}, bf16[3,32,1024]{2,1,0:T(8,128)(2,1)S(1)}, u32[]{:S(2)}, u32[]{:S(2)}) %collective-permute-start.33) | collective-permute-done | bytes 196640 | tf_op jit(solution)/shard_map/ppermute | solution.py:43
  165.9 2.3 collective-permute-start.37
  168.2 5.1 %collective-permute-start.52 = (bf16[2,128,1024]{2,1,0:T(8,128)(2,1)S(1)}, bf16[2,128,1024]{2,1,0:T(8,128)(2,1)S(1)}, u32[]{:S(2)}, u32[]{:S(2)}) collective-permute-start(bf16[2,128,1024]{2,1,0:T(8,128)(2,1)S(1)} %pad_maximum_fusion.1.refs_4_), channel_id=1, source_target_pairs={{0,1},{1,2},{2,3},{3,0},{4,5},{5,6},{6,7},{7,4},{8,9},{9,10},{10,1... | collective-permute-start | bytes 1572872 | tf_op jit(solution)/shard_map/ppermute | solution.py:34
  173.3 9.9 %collective-permute-done.49.refs_1_ = bf16[256,1024]{1,0:T(8,128)(2,1)S(1)} collective-permute-done((bf16[256,1024]{1,0:T(8,128)(2,1)S(1)}, bf16[256,1024]{1,0:T(8,128)(2,1)S(1)}, u32[]{:S(2)}, u32[]{:S(2)}) %collective-permute-start.49) | collective-permute-done | bytes 524320 | tf_op jit(solution)/shard_map/ppermute | solution.py:34
  183.2 2.6 collective-permute-start.53
  185.9 4.7 %collective-permute-start.54 = (bf16[2,128,1024]{2,1,0:T(8,128)(2,1)S(1)}, bf16[2,128,1024]{2,1,0:T(8,128)(2,1)}, u32[]{:S(2)}, u32[]{:S(2)}) collective-permute-start(bf16[2,128,1024]{2,1,0:T(8,128)(2,1)S(1)} %pad_maximum_fusion.1.refs_4_), channel_id=1, source_target_pairs={{0,3},{1,0},{2,1},{3,2},{4,7},{5,4},{6,5},{7,6},{8,11},{9,8},{10,9... | collective-permute-start | bytes 1572872 | tf_op jit(solution)/shard_map/ppermute | solution.py:34
  190.6 2.5 collective-permute-done.36.refs_1_
  193.2 6.3 %collective-permute-done.38.refs_3_ = bf16[128,1024]{1,0:T(8,128)(2,1)S(1)} collective-permute-done((bf16[128,1024]{1,0:T(8,128)(2,1)S(1)}, bf16[128,1024]{1,0:T(8,128)(2,1)S(1)}, u32[]{:S(2)}, u32[]{:S(2)}) %collective-permute-start.38) | collective-permute-done | bytes 262176 | tf_op jit(solution)/shard_map/ppermute | solution.py:34
  205.2 2.9 %shard_map.67.turned = bf16[1024,1024]{1,0:T(8,128)(2,1)} custom-call(bf16[256,1024]{1,0:T(8,128)(2,1)} %get-tuple-element.36.refs_0_, bf16[256,1024]{1,0:T(8,128)(2,1)} %copy-done.9, bf16[256,1024]{1,0:T(8,128)(2,1)} %collective-permute-done.1.refs_2_, bf16[256,1024]{1,0:T(8,128)(2,1)} %copy-done.10), custom_call_target="tpu_custom_call" | custom-call | flops 536870912 | bytes 4194304 | tf_op jit(solution)/shard_map/pallas_call | solution.py:150
  208.1 3.0 %shard_map.70.turned = bf16[1024,1024]{1,0:T(8,128)(2,1)} custom-call(bf16[256,1024]{1,0:T(8,128)(2,1)} %get-tuple-element.40.refs_0_, bf16[256,1024]{1,0:T(8,128)(2,1)} %copy-done.8, bf16[256,1024]{1,0:T(8,128)(2,1)} %collective-permute-done.4.refs_2_, bf16[256,1024]{1,0:T(8,128)(2,1)} %collective-permute-done.5.refs_3_), custom_call_target="tpu_custom_call" | custom-call | flops 536870912 | bytes 4194304 | tf_op jit(solution)/shard_map/pallas_call | solution.py:150
  211.1 5.7 %grad_v.1 = (f32[256,1024]{1,0:T(8,128)}, bf16[128,1024]{1,0:T(8,128)(2,1)}, bf16[128,1024]{1,0:T(8,128)(2,1)}, bf16[128,1024]{1,0:T(8,128)(2,1)}, bf16[128,1024...) custom-call(bf16[1024,1024]{1,0:T(8,128)(2,1)} %shard_map.67.turned, ...), custom_call_target="tpu_custom_call" | custom-call | flops 2147483648 | bytes 8388608 | tf_op jit(solution)/shard_map/grad_v/pallas_call | solution.py:183
  218.6 2.9 %collective-permute-start.43 = (bf16[128,1024]{1,0:T(8,128)(2,1)}, bf16[128,1024]{1,0:T(8,128)(2,1)S(1)}, u32[]{:S(2)}, u32[]{:S(2)}) collective-permute-start(bf16[128,1024]{1,0:T(8,128)(2,1)} %get-tuple-element.53), channel_id=1, source_target_pairs={{0,3},{1,0},{2,1},{3,2},{4,7},{5,4},{6,5},{7,6},{8,11},{9,8},{10,9... | collective-permute-start | bytes 786440 | tf_op jit(solution)/shard_map/ppermute | solution.py:34
  221.5 3.2 %collective-permute-start.46 = (bf16[128,1024]{1,0:T(8,128)(2,1)}, bf16[128,1024]{1,0:T(8,128)(2,1)S(1)}, u32[]{:S(2)}, u32[]{:S(2)}) collective-permute-start(bf16[128,1024]{1,0:T(8,128)(2,1)} %get-tuple-element.55), channel_id=1, source_target_pairs={{0,3},{1,0},{2,1},{3,2},{4,7},{5,4},{6,5},{7,6},{8,11},{9,8},{10,9... | collective-permute-start | bytes 786440 | tf_op jit(solution)/shard_map/ppermute | solution.py:34
  224.7 10.0 %grad_u.1 = (f32[256,1024]{1,0:T(8,128)}, bf16[128,1024]{1,0:T(8,128)(2,1)}, bf16[128,1024]{1,0:T(8,128)(2,1)}, bf16[128,1024]{1,0:T(8,128)(2,1)}, bf16[128,1024...) custom-call(s32[5]{0:T(128)} %stack.43.at_ref, bf16[1024,1024]{1,0:T(8,128)(2,1)} %shard_map.70.turned, ...), custom_call_target="tpu_custom_call" | custom-call | flops 4294967296 | bytes 16777216 | tf_op jit(solution)/shard_map/grad_u/pallas_call | solution.py:237
  235.8 2.5 collective-permute-start.59
  238.4 5.6 %collective-permute-done.63 = bf16[128,1024]{1,0:T(8,128)(2,1)S(1)} collective-permute-done((bf16[128,1024]{1,0:T(8,128)(2,1)}, bf16[128,1024]{1,0:T(8,128)(2,1)S(1)}, u32[]{:S(2)}, u32[]{:S(2)}) %collective-permute-start.63) | collective-permute-done | bytes 262176 | tf_op jit(solution)/shard_map/ppermute | solution.py:34
  245.7 3.3 %collective-permute-start.62 = (bf16[128,1024]{1,0:T(8,128)(2,1)S(1)}, bf16[128,1024]{1,0:T(8,128)(2,1)S(1)}, u32[]{:S(2)}, u32[]{:S(2)}) collective-permute-start(bf16[128,1024]{1,0:T(8,128)(2,1)S(1)} %copy-done.34), channel_id=1, source_target_pairs={{0,12},{4,0},{8,4},{12,8},{1,13},{5,1},{9,5},{13,9},{2,14},{6,2},{... | collective-permute-start | bytes 786440 | tf_op jit(solution)/shard_map/ppermute | solution.py:34
  249.0 3.2 %collective-permute-start.60 = (bf16[128,1024]{1,0:T(8,128)(2,1)S(1)}, bf16[128,1024]{1,0:T(8,128)(2,1)S(1)}, u32[]{:S(2)}, u32[]{:S(2)}) collective-permute-start(bf16[128,1024]{1,0:T(8,128)(2,1)S(1)} %add_convert_fusion.1), channel_id=1, source_target_pairs={{0,12},{4,0},{8,4},{12,8},{1,13},{5,1},{9,5},{13,9},{2,14},{6,2},{... | collective-permute-start | bytes 786440 | tf_op jit(solution)/shard_map/ppermute | solution.py:34
  252.9 2.7 finish.2
  255.9 2.9 collective-permute-done.64.high3
  259.5 2.7 finish.3
  263.5 17.1 %all_to_all.17 = f32[128,1,128]{2,1,0:T(1,128)S(1)} all-to-all(f32[128,1,128]{2,1,0:T(1,128)S(1)} %broadcast_in_dim.16), channel_id=1, replica_groups=mesh['p'=2,'h'=2,'c'=2,'z'=4,'y'=4] {'p','h','c','z','y'}, dimensions={0} | all-to-all | bytes 131072 | tf_op jit(solution)/shard_map/all_to_all | solution.py:29
  282.1 2.5 multiply_bitcast_fusion
  (218 shorter events, 55.3 us)
Async XLA Ops:
  3.0 13.6 %collective-permute-start.6 = (bf16[256,1024]{1,0:T(8,128)(2,1)S(1)}, bf16[256,1024]{1,0:T(8,128)(2,1)S(1)}, u32[]{:S(2)}, u32[]{:S(2)}) collective-permute-start(bf16[256,1024]{1,0:T(8,128)(2,1)S(1)} %get-tuple-element.44.refs_4_), channel_id=1, source_target_pairs={{0,64},{64,0},{1,65},{65,1},{2,66},{66,2},{3,67},{67,3},{4,68},{68... | collective-permute-start | bytes 1572872 | tf_op jit(solution)/shard_map/ppermute | solution.py:342
  4.7 24.5 %collective-permute-start.7 = (bf16[256,1024]{1,0:T(8,128)(2,1)S(1)}, bf16[256,1024]{1,0:T(8,128)(2,1)S(1)}, u32[]{:S(2)}, u32[]{:S(2)}) collective-permute-start(bf16[256,1024]{1,0:T(8,128)(2,1)S(1)} %get-tuple-element.44.refs_4_), channel_id=1, source_target_pairs={{0,16},{16,0},{1,17},{17,1},{2,18},{18,2},{3,19},{19,3},{4,20},{20... | collective-permute-start | bytes 1572872 | tf_op jit(solution)/shard_map/ppermute | solution.py:34
  16.6 12.6 %collective-permute-start.8 = (bf16[256,1024]{1,0:T(8,128)(2,1)S(1)}, bf16[256,1024]{1,0:T(8,128)(2,1)S(1)}, u32[]{:S(2)}, u32[]{:S(2)}) collective-permute-start(bf16[256,1024]{1,0:T(8,128)(2,1)S(1)} %collective-permute-done.6.refs_0_), channel_id=1, source_target_pairs={{0,16},{16,0},{1,17},{17,1},{2,18},{18,2},{3,19},{19,3},{4,20},{20... | collective-permute-start | bytes 1572872 | tf_op jit(solution)/shard_map/ppermute | solution.py:34
  22.4 21.3 %collective-permute-start.3 = (bf16[256,1024]{1,0:T(8,128)(2,1)}, bf16[256,1024]{1,0:T(8,128)(2,1)S(1)}, u32[]{:S(2)}, u32[]{:S(2)}) collective-permute-start(bf16[256,1024]{1,0:T(8,128)(2,1)} %get-tuple-element.41), channel_id=1, source_target_pairs={{0,1},{1,2},{2,3},{3,0},{4,5},{5,6},{6,7},{7,4},{8,9},{9,10},{10,1... | collective-permute-start | bytes 1572872 | tf_op jit(solution)/shard_map/ppermute | solution.py:34
  24.2 30.1 %collective-permute-start.4 = (bf16[256,1024]{1,0:T(8,128)(2,1)}, bf16[256,1024]{1,0:T(8,128)(2,1)}, u32[]{:S(2)}, u32[]{:S(2)}) collective-permute-start(bf16[256,1024]{1,0:T(8,128)(2,1)} %get-tuple-element.42), channel_id=1, source_target_pairs={{0,2},{1,3},{2,0},{3,1},{4,6},{5,7},{6,4},{7,5},{8,10},{9,11},{10,... | collective-permute-start | bytes 1572872 | tf_op jit(solution)/shard_map/ppermute | solution.py:34
  27.1 29.1 %collective-permute-start.5 = (bf16[256,1024]{1,0:T(8,128)(2,1)}, bf16[256,1024]{1,0:T(8,128)(2,1)}, u32[]{:S(2)}, u32[]{:S(2)}) collective-permute-start(bf16[256,1024]{1,0:T(8,128)(2,1)} %get-tuple-element.43), channel_id=1, source_target_pairs={{0,3},{1,0},{2,1},{3,2},{4,7},{5,4},{6,5},{7,6},{8,11},{9,8},{10,9... | collective-permute-start | bytes 1572872 | tf_op jit(solution)/shard_map/ppermute | solution.py:34
  30.9 28.9 %all-to-all-start = ((bf16[32,8,1024]{2,1,0:T(8,128)(2,1)}), bf16[32,8,1024]{2,1,0:T(8,128)(2,1)S(1)}, u32[]{:S(2)}, u32[]{:S(2)}) async-start(bf16[32,8,1024]{2,1,0:T(8,128)(2,1)} %bitcast.12), calls=%async_computation | async-start | bytes 1048576 | tf_op jit(solution)/shard_map/all_to_all | solution.py:29
  39.2 30.3 %collective-permute-start.10 = (bf16[256,1024]{1,0:T(8,128)(2,1)S(1)}, bf16[256,1024]{1,0:T(8,128)(2,1)}, u32[]{:S(2)}, u32[]{:S(2)}) collective-permute-start(bf16[256,1024]{1,0:T(8,128)(2,1)S(1)} %get-tuple-element.44.refs_4_), channel_id=1, source_target_pairs={{0,8},{4,12},{8,0},{12,4},{1,9},{5,13},{9,1},{13,5},{2,10},{6,14},... | collective-permute-start | bytes 1572872 | tf_op jit(solution)/shard_map/ppermute | solution.py:34
  42.6 29.8 %collective-permute-start.11 = (bf16[256,1024]{1,0:T(8,128)(2,1)S(1)}, bf16[256,1024]{1,0:T(8,128)(2,1)}, u32[]{:S(2)}, u32[]{:S(2)}) collective-permute-start(bf16[256,1024]{1,0:T(8,128)(2,1)S(1)} %get-tuple-element.44.refs_4_), channel_id=1, source_target_pairs={{0,12},{4,0},{8,4},{12,8},{1,13},{5,1},{9,5},{13,9},{2,14},{6,2},{... | collective-permute-start | bytes 1572872 | tf_op jit(solution)/shard_map/ppermute | solution.py:34
  43.7 31.1 %collective-permute-start.9 = (bf16[256,1024]{1,0:T(8,128)(2,1)S(1)}, bf16[256,1024]{1,0:T(8,128)(2,1)}, u32[]{:S(2)}, u32[]{:S(2)}) collective-permute-start(bf16[256,1024]{1,0:T(8,128)(2,1)S(1)} %get-tuple-element.44.refs_4_), channel_id=1, source_target_pairs={{0,4},{4,8},{8,12},{12,0},{1,5},{5,9},{9,13},{13,1},{2,6},{6,10},{... | collective-permute-start | bytes 1572872 | tf_op jit(solution)/shard_map/ppermute | solution.py:34
  54.3 29.2 %collective-permute-start = (bf16[256,1024]{1,0:T(8,128)(2,1)}, bf16[256,1024]{1,0:T(8,128)(2,1)S(1)}, u32[]{:S(2)}, u32[]{:S(2)}) collective-permute-start(bf16[256,1024]{1,0:T(8,128)(2,1)} %get-tuple-element.37), channel_id=1, source_target_pairs={{0,4},{4,8},{8,12},{12,0},{1,5},{5,9},{9,13},{13,1},{2,6},{6,10},{... | collective-permute-start | bytes 1572872 | tf_op jit(solution)/shard_map/ppermute | solution.py:34
  56.2 36.9 %collective-permute-start.1 = (bf16[256,1024]{1,0:T(8,128)(2,1)}, bf16[256,1024]{1,0:T(8,128)(2,1)}, u32[]{:S(2)}, u32[]{:S(2)}) collective-permute-start(bf16[256,1024]{1,0:T(8,128)(2,1)} %get-tuple-element.38), channel_id=1, source_target_pairs={{0,8},{4,12},{8,0},{12,4},{1,9},{5,13},{9,1},{13,5},{2,10},{6,14},... | collective-permute-start | bytes 1572872 | tf_op jit(solution)/shard_map/ppermute | solution.py:34
  69.5 29.7 %collective-permute-start.16 = (bf16[256,1024]{1,0:T(8,128)(2,1)S(1)}, bf16[256,1024]{1,0:T(8,128)(2,1)S(1)}, u32[]{:S(2)}, u32[]{:S(2)}) collective-permute-start(bf16[256,1024]{1,0:T(8,128)(2,1)S(1)} %get-tuple-element.47.refs_4_), channel_id=1, source_target_pairs={{0,1},{1,2},{2,3},{3,0},{4,5},{5,6},{6,7},{7,4},{8,9},{9,10},{10,1... | collective-permute-start | bytes 1572872 | tf_op jit(solution)/shard_map/ppermute | solution.py:34
  72.4 29.5 %collective-permute-start.17 = (bf16[256,1024]{1,0:T(8,128)(2,1)S(1)}, bf16[256,1024]{1,0:T(8,128)(2,1)}, u32[]{:S(2)}, u32[]{:S(2)}) collective-permute-start(bf16[256,1024]{1,0:T(8,128)(2,1)S(1)} %get-tuple-element.47.refs_4_), channel_id=1, source_target_pairs={{0,2},{1,3},{2,0},{3,1},{4,6},{5,7},{6,4},{7,5},{8,10},{9,11},{10,... | collective-permute-start | bytes 1572872 | tf_op jit(solution)/shard_map/ppermute | solution.py:34
  74.8 28.2 %collective-permute-start.18 = (bf16[256,1024]{1,0:T(8,128)(2,1)S(1)}, bf16[256,1024]{1,0:T(8,128)(2,1)}, u32[]{:S(2)}, u32[]{:S(2)}) collective-permute-start(bf16[256,1024]{1,0:T(8,128)(2,1)S(1)} %get-tuple-element.47.refs_4_), channel_id=1, source_target_pairs={{0,3},{1,0},{2,1},{3,2},{4,7},{5,4},{6,5},{7,6},{8,11},{9,8},{10,9... | collective-permute-start | bytes 1572872 | tf_op jit(solution)/shard_map/ppermute | solution.py:34
  83.5 14.1 %collective-permute-start.2 = (bf16[256,1024]{1,0:T(8,128)(2,1)}, bf16[256,1024]{1,0:T(8,128)(2,1)S(1)}, u32[]{:S(2)}, u32[]{:S(2)}) collective-permute-start(bf16[256,1024]{1,0:T(8,128)(2,1)} %get-tuple-element.39), channel_id=1, source_target_pairs={{0,12},{4,0},{8,4},{12,8},{1,13},{5,1},{9,5},{13,9},{2,14},{6,2},{... | collective-permute-start | bytes 1572872 | tf_op jit(solution)/shard_map/ppermute | solution.py:34
  93.2 18.8 %collective-permute-start.12 = (bf16[512,1024]{1,0:T(8,128)(2,1)}, bf16[512,1024]{1,0:T(8,128)(2,1)}, u32[]{:S(2)}, u32[]{:S(2)}) collective-permute-start(bf16[512,1024]{1,0:T(8,128)(2,1)} %get-tuple-element.46), channel_id=1, source_target_pairs={{0,16},{16,0},{1,17},{17,1},{2,18},{18,2},{3,19},{19,3},{4,20},{20... | collective-permute-start | bytes 3145736 | tf_op jit(solution)/shard_map/ppermute | solution.py:34
  97.7 11.2 %collective-permute-start.26 = (bf16[32,1024]{1,0:T(8,128)(2,1)S(1)}, bf16[32,1024]{1,0:T(8,128)(2,1)S(1)}, u32[]{:S(2)}, u32[]{:S(2)}) collective-permute-start(bf16[32,1024]{1,0:T(8,128)(2,1)S(1)} %bitcast.46), channel_id=1, source_target_pairs={{0,1},{1,2},{2,3},{3,0},{4,5},{5,6},{6,7},{7,4},{8,9},{9,10},{10,1... | collective-permute-start | bytes 196616 | tf_op jit(solution)/shard_map/ppermute | solution.py:34
  99.1 9.8 %collective-permute-start.27 = (bf16[32,1024]{1,0:T(8,128)(2,1)S(1)}, bf16[32,1024]{1,0:T(8,128)(2,1)S(1)}, u32[]{:S(2)}, u32[]{:S(2)}) collective-permute-start(bf16[32,1024]{1,0:T(8,128)(2,1)S(1)} %bitcast.47), channel_id=1, source_target_pairs={{0,2},{1,3},{2,0},{3,1},{4,6},{5,7},{6,4},{7,5},{8,10},{9,11},{10,... | collective-permute-start | bytes 196616 | tf_op jit(solution)/shard_map/ppermute | solution.py:34
  109.0 33.1 %collective-permute-start.29 = (bf16[128,1024]{1,0:T(8,128)(2,1)S(1)}, bf16[128,1024]{1,0:T(8,128)(2,1)S(1)}, u32[]{:S(2)}, u32[]{:S(2)}) collective-permute-start(bf16[128,1024]{1,0:T(8,128)(2,1)S(1)} %constant_dynamic-update-slice_fusion.refs_0_), channel_id=1, source_target_pairs={{0,4},{4,8},{8,12},{12,0},{1,5},{5,9},{9,13},{13,1},{2,6},{6,10},{... | collective-permute-start | bytes 786440 | tf_op jit(solution)/shard_map/ppermute | solution.py:34
  109.1 35.7 %collective-permute-start.30 = (bf16[128,1024]{1,0:T(8,128)(2,1)S(1)}, bf16[128,1024]{1,0:T(8,128)(2,1)S(1)}, u32[]{:S(2)}, u32[]{:S(2)}) collective-permute-start(bf16[128,1024]{1,0:T(8,128)(2,1)S(1)} %constant_dynamic-update-slice_fusion.refs_0_), channel_id=1, source_target_pairs={{0,8},{4,12},{8,0},{12,4},{1,9},{5,13},{9,1},{13,5},{2,10},{6,14},... | collective-permute-start | bytes 786440 | tf_op jit(solution)/shard_map/ppermute | solution.py:34
  114.1 10.7 %collective-permute-start.14 = (bf16[128,1024]{1,0:T(8,128)(2,1)S(1)}, bf16[128,1024]{1,0:T(8,128)(2,1)S(1)}, u32[]{:S(2)}, u32[]{:S(2)}) collective-permute-start(bf16[128,1024]{1,0:T(8,128)(2,1)S(1)} %get-tuple-element.90), channel_id=1, source_target_pairs={{0,2},{1,3},{2,0},{3,1},{4,6},{5,7},{6,4},{7,5},{8,10},{9,11},{10,... | collective-permute-start | bytes 786440 | tf_op jit(solution)/shard_map/ppermute | solution.py:34
  116.9 12.3 %collective-permute-start.15 = (bf16[128,1024]{1,0:T(8,128)(2,1)S(1)}, bf16[128,1024]{1,0:T(8,128)(2,1)S(1)}, u32[]{:S(2)}, u32[]{:S(2)}) collective-permute-start(bf16[128,1024]{1,0:T(8,128)(2,1)S(1)} %get-tuple-element.89), channel_id=1, source_target_pairs={{0,1},{1,2},{2,3},{3,0},{4,5},{5,6},{6,7},{7,4},{8,9},{9,10},{10,1... | collective-permute-start | bytes 786440 | tf_op jit(solution)/shard_map/ppermute | solution.py:34
  132.2 12.6 %collective-permute-start.31 = (bf16[128,1024]{1,0:T(8,128)(2,1)S(1)}, bf16[128,1024]{1,0:T(8,128)(2,1)S(1)}, u32[]{:S(2)}, u32[]{:S(2)}) collective-permute-start(bf16[128,1024]{1,0:T(8,128)(2,1)S(1)} %constant_dynamic-update-slice_fusion.refs_0_), channel_id=1, source_target_pairs={{0,12},{4,0},{8,4},{12,8},{1,13},{5,1},{9,5},{13,9},{2,14},{6,2},{... | collective-permute-start | bytes 786440 | tf_op jit(solution)/shard_map/ppermute | solution.py:34
  152.7 12.4 %collective-permute-start.33 = (bf16[3,32,1024]{2,1,0:T(8,128)(2,1)S(1)}, bf16[3,32,1024]{2,1,0:T(8,128)(2,1)S(1)}, u32[]{:S(2)}, u32[]{:S(2)}) collective-permute-start(bf16[3,32,1024]{2,1,0:T(8,128)(2,1)S(1)} %get-tuple-element.100), channel_id=1, source_target_pairs={{0,64},{32,96},{64,32},{96,0},{1,65},{33,97},{65,33},{97,1},{2,66}... | collective-permute-start | bytes 589832 | tf_op jit(solution)/shard_map/ppermute | solution.py:43
  152.8 12.4 %collective-permute-start.34 = (bf16[3,32,1024]{2,1,0:T(8,128)(2,1)S(1)}, bf16[3,32,1024]{2,1,0:T(8,128)(2,1)S(1)}, u32[]{:S(2)}, u32[]{:S(2)}) collective-permute-start(bf16[3,32,1024]{2,1,0:T(8,128)(2,1)S(1)} %get-tuple-element.99), channel_id=1, source_target_pairs={{0,32},{32,0},{64,96},{96,64},{1,33},{33,1},{65,97},{97,65},{2,34}... | collective-permute-start | bytes 589832 | tf_op jit(solution)/shard_map/ppermute | solution.py:43
  154.4 11.4 %collective-permute-start.35 = (bf16[3,32,1024]{2,1,0:T(8,128)(2,1)S(1)}, bf16[3,32,1024]{2,1,0:T(8,128)(2,1)S(1)}, u32[]{:S(2)}, u32[]{:S(2)}) collective-permute-start(bf16[3,32,1024]{2,1,0:T(8,128)(2,1)S(1)} %get-tuple-element.100), channel_id=1, source_target_pairs={{0,96},{32,64},{64,0},{96,32},{1,97},{33,65},{65,1},{97,33},{2,98}... | collective-permute-start | bytes 589832 | tf_op jit(solution)/shard_map/ppermute | solution.py:43
  156.0 27.2 %collective-permute-start.49 = (bf16[256,1024]{1,0:T(8,128)(2,1)S(1)}, bf16[256,1024]{1,0:T(8,128)(2,1)S(1)}, u32[]{:S(2)}, u32[]{:S(2)}) collective-permute-start(bf16[256,1024]{1,0:T(8,128)(2,1)S(1)} %collective-permute-done.6.refs_0_), channel_id=1, source_target_pairs={{0,4},{4,8},{8,12},{12,0},{1,5},{5,9},{9,13},{13,1},{2,6},{6,10},{... | collective-permute-start | bytes 1572872 | tf_op jit(solution)/shard_map/ppermute | solution.py:34
  156.0 29.8 %collective-permute-start.50 = (bf16[256,1024]{1,0:T(8,128)(2,1)S(1)}, bf16[256,1024]{1,0:T(8,128)(2,1)S(1)}, u32[]{:S(2)}, u32[]{:S(2)}) collective-permute-start(bf16[256,1024]{1,0:T(8,128)(2,1)S(1)} %collective-permute-done.6.refs_0_), channel_id=1, source_target_pairs={{0,8},{4,12},{8,0},{12,4},{1,9},{5,13},{9,1},{13,5},{2,10},{6,14},... | collective-permute-start | bytes 1572872 | tf_op jit(solution)/shard_map/ppermute | solution.py:34
  165.8 27.3 %collective-permute-start.36 = (bf16[128,1024]{1,0:T(8,128)(2,1)S(1)}, bf16[128,1024]{1,0:T(8,128)(2,1)S(1)}, u32[]{:S(2)}, u32[]{:S(2)}) collective-permute-start(bf16[128,1024]{1,0:T(8,128)(2,1)S(1)} %maximum_bitcast_fusion.refs_0_), channel_id=1, source_target_pairs={{0,4},{4,8},{8,12},{12,0},{1,5},{5,9},{9,13},{13,1},{2,6},{6,10},{... | collective-permute-start | bytes 786440 | tf_op jit(solution)/shard_map/ppermute | solution.py:34
  165.9 27.2 %collective-permute-start.37 = (bf16[128,1024]{1,0:T(8,128)(2,1)S(1)}, bf16[128,1024]{1,0:T(8,128)(2,1)S(1)}, u32[]{:S(2)}, u32[]{:S(2)}) collective-permute-start(bf16[128,1024]{1,0:T(8,128)(2,1)S(1)} %maximum_bitcast_fusion.refs_0_), channel_id=1, source_target_pairs={{0,8},{4,12},{8,0},{12,4},{1,9},{5,13},{9,1},{13,5},{2,10},{6,14},... | collective-permute-start | bytes 786440 | tf_op jit(solution)/shard_map/ppermute | solution.py:34
  168.2 31.8 %collective-permute-start.52 = (bf16[2,128,1024]{2,1,0:T(8,128)(2,1)S(1)}, bf16[2,128,1024]{2,1,0:T(8,128)(2,1)S(1)}, u32[]{:S(2)}, u32[]{:S(2)}) collective-permute-start(bf16[2,128,1024]{2,1,0:T(8,128)(2,1)S(1)} %pad_maximum_fusion.1.refs_4_), channel_id=1, source_target_pairs={{0,1},{1,2},{2,3},{3,0},{4,5},{5,6},{6,7},{7,4},{8,9},{9,10},{10,1... | collective-permute-start | bytes 1572872 | tf_op jit(solution)/shard_map/ppermute | solution.py:34
  183.2 17.0 %collective-permute-start.53 = (bf16[2,128,1024]{2,1,0:T(8,128)(2,1)S(1)}, bf16[2,128,1024]{2,1,0:T(8,128)(2,1)}, u32[]{:S(2)}, u32[]{:S(2)}) collective-permute-start(bf16[2,128,1024]{2,1,0:T(8,128)(2,1)S(1)} %pad_maximum_fusion.1.refs_4_), channel_id=1, source_target_pairs={{0,2},{1,3},{2,0},{3,1},{4,6},{5,7},{6,4},{7,5},{8,10},{9,11},{10,... | collective-permute-start | bytes 1572872 | tf_op jit(solution)/shard_map/ppermute | solution.py:34
  185.9 17.2 %collective-permute-start.54 = (bf16[2,128,1024]{2,1,0:T(8,128)(2,1)S(1)}, bf16[2,128,1024]{2,1,0:T(8,128)(2,1)}, u32[]{:S(2)}, u32[]{:S(2)}) collective-permute-start(bf16[2,128,1024]{2,1,0:T(8,128)(2,1)S(1)} %pad_maximum_fusion.1.refs_4_), channel_id=1, source_target_pairs={{0,3},{1,0},{2,1},{3,2},{4,7},{5,4},{6,5},{7,6},{8,11},{9,8},{10,9... | collective-permute-start | bytes 1572872 | tf_op jit(solution)/shard_map/ppermute | solution.py:34
  200.2 16.6 %collective-permute-start.51 = (bf16[256,1024]{1,0:T(8,128)(2,1)S(1)}, bf16[256,1024]{1,0:T(8,128)(2,1)S(1)}, u32[]{:S(2)}, u32[]{:S(2)}) collective-permute-start(bf16[256,1024]{1,0:T(8,128)(2,1)S(1)} %collective-permute-done.6.refs_0_), channel_id=1, source_target_pairs={{0,12},{4,0},{8,4},{12,8},{1,13},{5,1},{9,5},{13,9},{2,14},{6,2},{... | collective-permute-start | bytes 1572872 | tf_op jit(solution)/shard_map/ppermute | solution.py:34
  203.1 15.5 %collective-permute-start.55 = (bf16[2,128,1024]{2,1,0:T(8,128)(2,1)S(1)}, bf16[2,128,1024]{2,1,0:T(8,128)(2,1)}, u32[]{:S(2)}, u32[]{:S(2)}) collective-permute-start(bf16[2,128,1024]{2,1,0:T(8,128)(2,1)S(1)} %pad_maximum_fusion.1.refs_4_), channel_id=1, source_target_pairs={{0,16},{16,0},{1,17},{17,1},{2,18},{18,2},{3,19},{19,3},{4,20},{20... | collective-permute-start | bytes 1572872 | tf_op jit(solution)/shard_map/ppermute | solution.py:34
  203.1 18.4 %collective-permute-start.56 = (bf16[2,128,1024]{2,1,0:T(8,128)(2,1)S(1)}, bf16[2,128,1024]{2,1,0:T(8,128)(2,1)}, u32[]{:S(2)}, u32[]{:S(2)}) collective-permute-start(bf16[2,128,1024]{2,1,0:T(8,128)(2,1)S(1)} %collective-permute-done.52.refs_5_), channel_id=1, source_target_pairs={{0,16},{16,0},{1,17},{17,1},{2,18},{18,2},{3,19},{19,3},{4,20},{20... | collective-permute-start | bytes 1572872 | tf_op jit(solution)/shard_map/ppermute | solution.py:34
  203.7 17.8 %collective-permute-start.57 = (bf16[2,128,1024]{2,1,0:T(8,128)(2,1)}, bf16[2,128,1024]{2,1,0:T(8,128)(2,1)}, u32[]{:S(2)}, u32[]{:S(2)}) collective-permute-start(bf16[2,128,1024]{2,1,0:T(8,128)(2,1)} %collective-permute-done.53.refs_6_), channel_id=1, source_target_pairs={{0,16},{16,0},{1,17},{17,1},{2,18},{18,2},{3,19},{19,3},{4,20},{20... | collective-permute-start | bytes 1572872 | tf_op jit(solution)/shard_map/ppermute | solution.py:34
  205.1 19.6 %collective-permute-start.58 = (bf16[2,128,1024]{2,1,0:T(8,128)(2,1)}, bf16[2,128,1024]{2,1,0:T(8,128)(2,1)}, u32[]{:S(2)}, u32[]{:S(2)}) collective-permute-start(bf16[2,128,1024]{2,1,0:T(8,128)(2,1)} %collective-permute-done.54.refs_7_), channel_id=1, source_target_pairs={{0,16},{16,0},{1,17},{17,1},{2,18},{18,2},{3,19},{19,3},{4,20},{20... | collective-permute-start | bytes 1572872 | tf_op jit(solution)/shard_map/ppermute | solution.py:34
  216.8 18.8 %collective-permute-start.47 = (bf16[128,1024]{1,0:T(8,128)(2,1)}, bf16[128,1024]{1,0:T(8,128)(2,1)S(1)}, u32[]{:S(2)}, u32[]{:S(2)}) collective-permute-start(bf16[128,1024]{1,0:T(8,128)(2,1)} %get-tuple-element.57), channel_id=1, source_target_pairs={{0,1},{1,2},{2,3},{3,0},{4,5},{5,6},{6,7},{7,4},{8,9},{9,10},{10,1... | collective-permute-start | bytes 786440 | tf_op jit(solution)/shard_map/ppermute | solution.py:34
  218.6 17.2 %collective-permute-start.43 = (bf16[128,1024]{1,0:T(8,128)(2,1)}, bf16[128,1024]{1,0:T(8,128)(2,1)S(1)}, u32[]{:S(2)}, u32[]{:S(2)}) collective-permute-start(bf16[128,1024]{1,0:T(8,128)(2,1)} %get-tuple-element.53), channel_id=1, source_target_pairs={{0,3},{1,0},{2,1},{3,2},{4,7},{5,4},{6,5},{7,6},{8,11},{9,8},{10,9... | collective-permute-start | bytes 786440 | tf_op jit(solution)/shard_map/ppermute | solution.py:34
  221.5 24.1 %collective-permute-start.45 = (bf16[128,1024]{1,0:T(8,128)(2,1)}, bf16[128,1024]{1,0:T(8,128)(2,1)S(1)}, u32[]{:S(2)}, u32[]{:S(2)}) collective-permute-start(bf16[128,1024]{1,0:T(8,128)(2,1)} %get-tuple-element.54), channel_id=1, source_target_pairs={{0,1},{1,2},{2,3},{3,0},{4,5},{5,6},{6,7},{7,4},{8,9},{9,10},{10,1... | collective-permute-start | bytes 786440 | tf_op jit(solution)/shard_map/ppermute | solution.py:34
  221.5 27.4 %collective-permute-start.46 = (bf16[128,1024]{1,0:T(8,128)(2,1)}, bf16[128,1024]{1,0:T(8,128)(2,1)S(1)}, u32[]{:S(2)}, u32[]{:S(2)}) collective-permute-start(bf16[128,1024]{1,0:T(8,128)(2,1)} %get-tuple-element.55), channel_id=1, source_target_pairs={{0,3},{1,0},{2,1},{3,2},{4,7},{5,4},{6,5},{7,6},{8,11},{9,8},{10,9... | collective-permute-start | bytes 786440 | tf_op jit(solution)/shard_map/ppermute | solution.py:34
  235.7 13.2 %collective-permute-start.48 = (bf16[128,1024]{1,0:T(8,128)(2,1)S(1)}, bf16[128,1024]{1,0:T(8,128)(2,1)S(1)}, u32[]{:S(2)}, u32[]{:S(2)}) collective-permute-start(bf16[128,1024]{1,0:T(8,128)(2,1)S(1)} %add_convert_fusion.2), channel_id=1, source_target_pairs={{0,1},{1,2},{2,3},{3,0},{4,5},{5,6},{6,7},{7,4},{8,9},{9,10},{10,1... | collective-permute-start | bytes 786440 | tf_op jit(solution)/shard_map/ppermute | solution.py:34
  245.5 10.4 %collective-permute-start.61 = (bf16[128,1024]{1,0:T(8,128)(2,1)S(1)}, bf16[128,1024]{1,0:T(8,128)(2,1)S(1)}, u32[]{:S(2)}, u32[]{:S(2)}) collective-permute-start(bf16[128,1024]{1,0:T(8,128)(2,1)S(1)} %copy-done.35), channel_id=1, source_target_pairs={{0,4},{4,8},{8,12},{12,0},{1,5},{5,9},{9,13},{13,1},{2,6},{6,10},{... | collective-permute-start | bytes 786440 | tf_op jit(solution)/shard_map/ppermute | solution.py:34
  245.7 10.2 %collective-permute-start.62 = (bf16[128,1024]{1,0:T(8,128)(2,1)S(1)}, bf16[128,1024]{1,0:T(8,128)(2,1)S(1)}, u32[]{:S(2)}, u32[]{:S(2)}) collective-permute-start(bf16[128,1024]{1,0:T(8,128)(2,1)S(1)} %copy-done.34), channel_id=1, source_target_pairs={{0,12},{4,0},{8,4},{12,8},{1,13},{5,1},{9,5},{13,9},{2,14},{6,2},{... | collective-permute-start | bytes 786440 | tf_op jit(solution)/shard_map/ppermute | solution.py:34
  248.9 9.8 %collective-permute-start.64 = (bf16[128,1024]{1,0:T(8,128)(2,1)S(1)}, bf16[128,1024]{1,0:T(8,128)(2,1)S(1)}, u32[]{:S(2)}, u32[]{:S(2)}) collective-permute-start(bf16[128,1024]{1,0:T(8,128)(2,1)S(1)} %add_convert_fusion), channel_id=1, source_target_pairs={{0,4},{4,8},{8,12},{12,0},{1,5},{5,9},{9,13},{13,1},{2,6},{6,10},{... | collective-permute-start | bytes 786440 | tf_op jit(solution)/shard_map/ppermute | solution.py:34
  249.0 9.8 %collective-permute-start.60 = (bf16[128,1024]{1,0:T(8,128)(2,1)S(1)}, bf16[128,1024]{1,0:T(8,128)(2,1)S(1)}, u32[]{:S(2)}, u32[]{:S(2)}) collective-permute-start(bf16[128,1024]{1,0:T(8,128)(2,1)S(1)} %add_convert_fusion.1), channel_id=1, source_target_pairs={{0,12},{4,0},{8,4},{12,8},{1,13},{5,1},{9,5},{13,9},{2,14},{6,2},{... | collective-permute-start | bytes 786440 | tf_op jit(solution)/shard_map/ppermute | solution.py:34
  (59 other events, 802.8 us)

commit v6 on v5

--- a/solution.py
+++ b/solution.py
@@ -182,12 +182,11 @@
     own, tile = wide // 4, hidden // 2
     return pl.pallas_call(
         grad_v_kernel,
-        out_shape=piece_shapes(own, hidden),
+        out_shape=[jax.ShapeDtypeStruct((own, hidden), t) for t in (F32, BF, BF, BF)],
         grid=(2,),
         in_specs=[pl.BlockSpec((wide, tok), lambda n: (0, 0))]
         + [pl.BlockSpec((half, tile), lambda n: (0, n))] * 8,
-        out_specs=[pl.BlockSpec((own, tile), lambda n: (0, n))]
-        + [pl.BlockSpec((own // 2, tile), lambda n: (0, n))] * 6,
+        out_specs=[pl.BlockSpec((own, tile), lambda n: (0, n))] * 4,
         cost_estimate=pl.CostEstimate(
             flops=2 * tok * wide * hidden, bytes_accessed=8 * tok * wide, transcendentals=0
         ),
@@ -293,29 +292,6 @@
     return sum((part.astype(F32) for part in parts[1:]), parts[0])
 
 
-def finish_kernel(own, low1, low3, high1, high3, out, squares):
-    half = low1.shape[0]
-    low = own[:half, :] + low1[...].astype(F32) + low3[...].astype(F32)
-    high = own[half:, :] + high1[...].astype(F32) + high3[...].astype(F32)
-    out[:half, :] = low
-    out[half:, :] = high
-    squares[0, 0] = jnp.sum(low * low + high * high)
-
-
-def finish(*parts):
-    vmem = pl.BlockSpec(memory_space=pltpu.VMEM)
-    return pl.pallas_call(
-        finish_kernel,
-        out_shape=[
-            jax.ShapeDtypeStruct(parts[0].shape, F32),
-            jax.ShapeDtypeStruct((1, 1), F32),
-        ],
-        in_specs=[vmem] * 5,
-        out_specs=[vmem, pl.BlockSpec(memory_space=pltpu.SMEM)],
-        name="finish",
-    )(*parts)
-
-
 def sum_near(pieces, axis):
     own, low1, high1, low2, high2, low3, high3 = pieces
     low2, high2 = shift(low2, axis, -1), shift(high2, axis, 1)
@@ -323,7 +299,9 @@
     low1 = (low1.astype(F32) + low2.astype(F32)).astype(BF)
     high3 = (high3.astype(F32) + high2.astype(F32)).astype(BF)
     low1, high3 = shift(low1, axis, -1), shift(high3, axis, 1)
-    return finish(own, low1, low3, high1, high3)
+    one = jnp.concatenate([low1, high1]).astype(F32)
+    three = jnp.concatenate([low3, high3]).astype(F32)
+    return own + one + three
 
 
 def on_device(inputs, w_in, w_out, cotangent):
@@ -403,10 +381,11 @@
     pair_own = shift(pairs[0], "c", 1)
     pairs += [pair_own] + [shift(a, "c", 1) for a in pairs[1:]]
 
-    g_v, squares_v = sum_near(grad_v_call(turn(vs), rs), "y")
-    g_u, squares_u = sum_near(grad_u_call(at, turn(us), pairs, w_3s), "z")
-
-    squares = squares_u[0, 0] + squares_v[0, 0]
+    g_v = grad_v_call(turn(vs), rs)
+    g_v = sum_back(g_v, "y")
+    g_u = sum_near(grad_u_call(at, turn(us), pairs, w_3s), "z")
+
+    squares = jnp.sum(g_u * g_u) + jnp.sum(g_v * g_v)
     row = jnp.broadcast_to(squares, (lax.axis_size(AXES), 1, 128))
     squares = a2a(row, AXES)[:, 0, 0].sum()
     grad_norm = jnp.sqrt(squares)

time: 289 us -> 290 us (level)
  waiting for transfers between devices: 92.3 us -> 106 us
  starting transfers between devices: 96.4 us -> 89.4 us
  Pallas kernels: 45.8 us -> 40.3 us
    ppermute x58 -> x55, waiting for transfers between devices: 72.9 us -> 85.8 us  [shift(): lax.ppermute(value, axis, [(i, (i + by) % count) for i in range(count)])]
    ppermute x58 -> x55, starting transfers between devices: 77.4 us -> 70.6 us  [shift(): lax.ppermute(value, axis, [(i, (i + by) % count) for i in range(count)])]
    pallas_call x3 -> x1, Pallas kernels: 11.1 us -> 5.72 us  [grad_v_call(): pl.pallas_call(grad_v_kernel, out_shape=[jax.ShapeDtypeStruct((own, hidde...]
    unnamed x87 -> x81, local copies, waits for them, and re-layouts: 8.03 us -> 6.56 us
  transfers between devices with their start and end apart: 66 -> 63, of which waited for: 21 -> 23; matrix products, arithmetic and copies ran while one was open for 3% -> 4% of each run, Pallas kernels for 15% -> 14%
where the time goes in v6:
time: 290 us; the launch traced here: 289 us
  waiting for transfers between devices  106 us (37%)
  starting transfers between devices  89.4 us (31%)
  Pallas kernels  40.3 us (14%)
  blocking collectives  26.3 us (9%)
  local copies, waits for them, and re-layouts  9.89 us (3%)
  other arithmetic  9.89 us (3%)
  between operations  4.41 us (2%)
  matrix products  2.98 us (1%)
    ppermute x55, waiting for transfers between devices, shift(): lax.ppermute(value, axis, [(i, (i + by) % count) for i in range(count)])  85.8 us
    ppermute x55, starting transfers between devices, shift(): lax.ppermute(value, axis, [(i, (i + by) % count) for i in range(count)])  70.6 us
    all_to_all x2, blocking collectives, a2a(): return lax.all_to_all(value, axes, 0, 0, tiled=True)  26.3 us
    ppermute x1, waiting for transfers between devices, on_device(): w_3 = lax.ppermute(w_u, 'p', [(0, 1), (1, 0)])  11.9 us
    pallas_call x2, Pallas kernels, project(): pl.pallas_call(project_kernel, out_shape=[jax.ShapeDtypeStruct((2 * tok,...  11.5 us
    pallas_call x1, Pallas kernels, grad_u_call(): pl.pallas_call(grad_u_kernel, out_shape=piece_shapes(own, hidden), grid=(...  9.99 us
    ppermute x6, starting transfers between devices, shift_x(): return lax.ppermute(value, ('p', 'h'), pairs)  8.91 us
    all_to_all x1, starting transfers between devices, a2a(): return lax.all_to_all(value, axes, 0, 0, tiled=True)  8.28 us
  transfers between devices with their start and end apart: 63, of which 23 were waited for; matrix products, arithmetic and copies ran while one was open for 4% of the time, Pallas kernels for 14%

profile of v6, /device:TPU:0, one launch (start us, length us, event | category | flops | bytes accessed | tf_op | source)
XLA Modules:
  0.0 288.8 jit_solution(11380126621504569179)
XLA Ops:
  1.9 1.9 bitcast_select_fusion
  5.4 11.9 %collective-permute-done.6.refs_0_ = bf16[256,1024]{1,0:T(8,128)(2,1)S(1)} collective-permute-done((bf16[256,1024]{1,0:T(8,128)(2,1)S(1)}, bf16[256,1024]{1,0:T(8,128)(2,1)S(1)}, u32[]{:S(2)}, u32[]{:S(2)}) %collective-permute-start.6) | collective-permute-done | bytes 524320 | tf_op jit(solution)/shard_map/ppermute | solution.py:320
  18.1 5.0 %cut.1 = (bf16[256,1024]{1,0:T(8,128)(2,1)}, bf16[256,1024]{1,0:T(8,128)(2,1)}, bf16[256,1024]{1,0:T(8,128)(2,1)}, bf16[256,1024]{1,0:T(8,128)(2,1)}, bf16[256,1...) custom-call(s32[5]{0:T(128)} %stack.43.at_ref, ...), custom_call_target="tpu_custom_call" | custom-call | tf_op jit(solution)/shard_map/cut/pallas_call | solution.py:90
  23.1 1.8 collective-permute-start.3
  24.9 2.9 %collective-permute-start.4 = (bf16[256,1024]{1,0:T(8,128)(2,1)}, bf16[256,1024]{1,0:T(8,128)(2,1)S(1)}, u32[]{:S(2)}, u32[]{:S(2)}) collective-permute-start(bf16[256,1024]{1,0:T(8,128)(2,1)} %get-tuple-element.35), channel_id=1, source_target_pairs={{0,2},{1,3},{2,0},{3,1},{4,6},{5,7},{6,4},{7,5},{8,10},{9,11},{10,... | collective-permute-start | bytes 1572872 | tf_op jit(solution)/shard_map/ppermute | solution.py:34
  31.6 8.3 %all-to-all-start = ((bf16[32,8,1024]{2,1,0:T(8,128)(2,1)}), bf16[32,8,1024]{2,1,0:T(8,128)(2,1)S(1)}, u32[]{:S(2)}, u32[]{:S(2)}) async-start(bf16[32,8,1024]{2,1,0:T(8,128)(2,1)} %bitcast.12), calls=%async_computation | async-start | bytes 1048576 | tf_op jit(solution)/shard_map/all_to_all | solution.py:29
  39.9 3.4 %collective-permute-start.10 = (bf16[256,1024]{1,0:T(8,128)(2,1)S(1)}, bf16[256,1024]{1,0:T(8,128)(2,1)}, u32[]{:S(2)}, u32[]{:S(2)}) collective-permute-start(bf16[256,1024]{1,0:T(8,128)(2,1)S(1)} %get-tuple-element.37.refs_4_), channel_id=1, source_target_pairs={{0,8},{4,12},{8,0},{12,4},{1,9},{5,13},{9,1},{13,5},{2,10},{6,14},... | collective-permute-start | bytes 1572872 | tf_op jit(solution)/shard_map/ppermute | solution.py:34
  45.4 9.6 %collective-permute-done.4.refs_2_ = bf16[256,1024]{1,0:T(8,128)(2,1)S(1)} collective-permute-done((bf16[256,1024]{1,0:T(8,128)(2,1)}, bf16[256,1024]{1,0:T(8,128)(2,1)S(1)}, u32[]{:S(2)}, u32[]{:S(2)}) %collective-permute-start.4) | collective-permute-done | bytes 524320 | tf_op jit(solution)/shard_map/ppermute | solution.py:34
  55.0 1.9 collective-permute-start
  56.9 3.6 %collective-permute-start.1 = (bf16[256,1024]{1,0:T(8,128)(2,1)}, bf16[256,1024]{1,0:T(8,128)(2,1)S(1)}, u32[]{:S(2)}, u32[]{:S(2)}) collective-permute-start(bf16[256,1024]{1,0:T(8,128)(2,1)} %get-tuple-element.31), channel_id=1, source_target_pairs={{0,8},{4,12},{8,0},{12,4},{1,9},{5,13},{9,1},{13,5},{2,10},{6,14},... | collective-permute-start | bytes 1572872 | tf_op jit(solution)/shard_map/ppermute | solution.py:34
  60.6 9.5 %all_to_all.16 = bf16[4,8,1024]{2,1,0:T(8,128)(2,1)S(1)} all-to-all(bf16[4,8,1024]{2,1,0:T(8,128)(2,1)S(1)} %broadcast_in_dim.15), channel_id=1, replica_groups=mesh['p'=2,'h'=2,'c'=2,'z'=4,'y'=4] {'p','h'}, dimensions={0} | all-to-all | bytes 131072 | tf_op jit(solution)/shard_map/all_to_all | solution.py:29
  73.1 2.5 collective-permute-start.17
  75.6 1.9 collective-permute-start.18
  77.5 6.8 %collective-permute-done.refs_1_ = bf16[256,1024]{1,0:T(8,128)(2,1)S(1)} collective-permute-done((bf16[256,1024]{1,0:T(8,128)(2,1)}, bf16[256,1024]{1,0:T(8,128)(2,1)S(1)}, u32[]{:S(2)}, u32[]{:S(2)}) %collective-permute-start) | collective-permute-done | bytes 524320 | tf_op jit(solution)/shard_map/ppermute | solution.py:34
  84.8 5.7 %shard_map.68 = (bf16[512,1024]{1,0:T(8,128)(2,1)}, f32[512,1024]{1,0:T(8,128)}) custom-call(bf16[256,1024]{1,0:T(8,128)(2,1)} %get-tuple-element.33.refs_0_, bf16[256,1024]{1,0:T(8,128)(2,1)} %copy-done.12, bf16[256,1024]{1,0:T(8,128)(2,1)} %copy-done.14, bf16[256,1024]{1,0:T(8,128)(2,1)} %collective-permute-done.5.refs_3_, bf16[256,1024]{1,0:T(8,128)(2,1)} %copy-done.1, ...), custom_call_target="tpu_custom_call" | custom-call | flops 2147483648 | bytes 4194304 | tf_op jit(solution)/shard_map/pallas_call | solution.py:121
  90.5 3.4 %collective-permute-done.1.refs_2_ = bf16[256,1024]{1,0:T(8,128)(2,1)S(1)} collective-permute-done((bf16[256,1024]{1,0:T(8,128)(2,1)}, bf16[256,1024]{1,0:T(8,128)(2,1)S(1)}, u32[]{:S(2)}, u32[]{:S(2)}) %collective-permute-start.1) | collective-permute-done | bytes 524320 | tf_op jit(solution)/shard_map/ppermute | solution.py:34
  93.8 4.5 %collective-permute-done.2.refs_3_ = bf16[256,1024]{1,0:T(8,128)(2,1)S(1)} collective-permute-done((bf16[256,1024]{1,0:T(8,128)(2,1)}, bf16[256,1024]{1,0:T(8,128)(2,1)S(1)}, u32[]{:S(2)}, u32[]{:S(2)}) %collective-permute-start.2) | collective-permute-done | bytes 524320 | tf_op jit(solution)/shard_map/ppermute | solution.py:34
  99.9 2.8 collective-permute-start.27
  103.8 5.8 %shard_map.69 = (bf16[512,1024]{1,0:T(8,128)(2,1)}, f32[512,1024]{1,0:T(8,128)}) custom-call(bf16[256,1024]{1,0:T(8,128)(2,1)} %get-tuple-element.29.refs_0_, bf16[256,1024]{1,0:T(8,128)(2,1)} %copy-done.13, bf16[256,1024]{1,0:T(8,128)(2,1)} %copy-done.15, bf16[256,1024]{1,0:T(8,128)(2,1)} %copy-done.16, bf16[256,1024]{1,0:T(8,128)(2,1)} %get-tuple-element.40.refs_4_, ...), custom_call_target="tpu_custom_call" | custom-call | flops 2147483648 | bytes 4194304 | tf_op jit(solution)/shard_map/pallas_call | solution.py:121
  111.4 2.9 %collective-permute-start.30 = (bf16[128,1024]{1,0:T(8,128)(2,1)S(1)}, bf16[128,1024]{1,0:T(8,128)(2,1)S(1)}, u32[]{:S(2)}, u32[]{:S(2)}) collective-permute-start(bf16[128,1024]{1,0:T(8,128)(2,1)S(1)} %constant_dynamic-update-slice_fusion.refs_0_), channel_id=1, source_target_pairs={{0,8},{4,12},{8,0},{12,4},{1,9},{5,13},{9,1},{13,5},{2,10},{6,14},... | collective-permute-start | bytes 786440 | tf_op jit(solution)/shard_map/ppermute | solution.py:34
  115.1 2.8 collective-permute-start.14
  118.5 5.6 %collective-permute-done.13 = bf16[128,1024]{1,0:T(8,128)(2,1)S(1)} collective-permute-done((bf16[128,1024]{1,0:T(8,128)(2,1)S(1)}, bf16[128,1024]{1,0:T(8,128)(2,1)S(1)}, u32[]{:S(2)}, u32[]{:S(2)}) %collective-permute-start.13) | collective-permute-done | bytes 262176 | tf_op jit(solution)/shard_map/ppermute | solution.py:34
  127.3 3.0 %collective-permute-done.15 = bf16[128,1024]{1,0:T(8,128)(2,1)S(1)} collective-permute-done((bf16[128,1024]{1,0:T(8,128)(2,1)S(1)}, bf16[128,1024]{1,0:T(8,128)(2,1)S(1)}, u32[]{:S(2)}, u32[]{:S(2)}) %collective-permute-start.15) | collective-permute-done | bytes 262176 | tf_op jit(solution)/shard_map/ppermute | solution.py:34
  134.4 5.4 %collective-permute-done.22 = bf16[128,1024]{1,0:T(8,128)(2,1)S(1)} collective-permute-done((bf16[128,1024]{1,0:T(8,128)(2,1)S(1)}, bf16[128,1024]{1,0:T(8,128)(2,1)S(1)}, u32[]{:S(2)}, u32[]{:S(2)}) %collective-permute-start.22) | collective-permute-done | bytes 262176 | tf_op jit(solution)/shard_map/ppermute | solution.py:34
  140.7 2.4 collective-permute-start.23
  143.7 2.6 collective-permute-start.25
  147.8 2.2 join.1
  154.4 2.8 collective-permute-start.34
  159.2 7.6 %collective-permute-done.33 = bf16[3,32,1024]{2,1,0:T(8,128)(2,1)S(1)} collective-permute-done((bf16[3,32,1024]{2,1,0:T(8,128)(2,1)S(1)}, bf16[3,32,1024]{2,1,0:T(8,128)(2,1)S(1)}, u32[]{:S(2)}, u32[]{:S(2)}) %collective-permute-start.33) | collective-permute-done | bytes 196640 | tf_op jit(solution)/shard_map/ppermute | solution.py:43
  166.8 1.9 collective-permute-start.48
  168.7 3.9 %collective-permute-start.49 = (bf16[2,128,1024]{2,1,0:T(8,128)(2,1)S(1)}, bf16[2,128,1024]{2,1,0:T(8,128)(2,1)S(1)}, u32[]{:S(2)}, u32[]{:S(2)}) collective-permute-start(bf16[2,128,1024]{2,1,0:T(8,128)(2,1)S(1)} %pad_maximum_fusion.1.refs_4_), channel_id=1, source_target_pairs={{0,1},{1,2},{2,3},{3,0},{4,5},{5,6},{6,7},{7,4},{8,9},{9,10},{10,1... | collective-permute-start | bytes 1572872 | tf_op jit(solution)/shard_map/ppermute | solution.py:34
  172.6 3.6 %collective-permute-start.50 = (bf16[2,128,1024]{2,1,0:T(8,128)(2,1)S(1)}, bf16[2,128,1024]{2,1,0:T(8,128)(2,1)S(1)}, u32[]{:S(2)}, u32[]{:S(2)}) collective-permute-start(bf16[2,128,1024]{2,1,0:T(8,128)(2,1)S(1)} %pad_maximum_fusion.1.refs_4_), channel_id=1, source_target_pairs={{0,2},{1,3},{2,0},{3,1},{4,6},{5,7},{6,4},{7,5},{8,10},{9,11},{10,... | collective-permute-start | bytes 1572872 | tf_op jit(solution)/shard_map/ppermute | solution.py:34
  177.0 6.0 %collective-permute-start.51 = (bf16[2,128,1024]{2,1,0:T(8,128)(2,1)S(1)}, bf16[2,128,1024]{2,1,0:T(8,128)(2,1)}, u32[]{:S(2)}, u32[]{:S(2)}) collective-permute-start(bf16[2,128,1024]{2,1,0:T(8,128)(2,1)S(1)} %pad_maximum_fusion.1.refs_4_), channel_id=1, source_target_pairs={{0,3},{1,0},{2,1},{3,2},{4,7},{5,4},{6,5},{7,6},{8,11},{9,8},{10,9... | collective-permute-start | bytes 1572872 | tf_op jit(solution)/shard_map/ppermute | solution.py:34
  184.3 13.2 %collective-permute-done.36.refs_1_ = bf16[128,1024]{1,0:T(8,128)(2,1)S(1)} collective-permute-done((bf16[128,1024]{1,0:T(8,128)(2,1)S(1)}, bf16[128,1024]{1,0:T(8,128)(2,1)S(1)}, u32[]{:S(2)}, u32[]{:S(2)}) %collective-permute-start.36) | collective-permute-done | bytes 262176 | tf_op jit(solution)/shard_map/ppermute | solution.py:34
  199.5 2.9 %shard_map.70.turned = bf16[1024,1024]{1,0:T(8,128)(2,1)} custom-call(bf16[256,1024]{1,0:T(8,128)(2,1)} %get-tuple-element.33.refs_0_, bf16[256,1024]{1,0:T(8,128)(2,1)} %copy-done.12, bf16[256,1024]{1,0:T(8,128)(2,1)} %copy-done.14, bf16[256,1024]{1,0:T(8,128)(2,1)} %collective-permute-done.5.refs_3_), custom_call_target="tpu_custom_call" | custom-call | flops 536870912 | bytes 4194304 | tf_op jit(solution)/shard_map/pallas_call | solution.py:150
  202.5 5.0 %collective-permute-done.38.refs_3_ = bf16[128,1024]{1,0:T(8,128)(2,1)} collective-permute-done((bf16[128,1024]{1,0:T(8,128)(2,1)S(1)}, bf16[128,1024]{1,0:T(8,128)(2,1)}, u32[]{:S(2)}, u32[]{:S(2)}) %collective-permute-start.38) | collective-permute-done | bytes 262176 | tf_op jit(solution)/shard_map/ppermute | solution.py:34
  208.5 10.0 %grad_u.1 = (f32[256,1024]{1,0:T(8,128)}, bf16[128,1024]{1,0:T(8,128)(2,1)}, bf16[128,1024]{1,0:T(8,128)(2,1)}, bf16[128,1024]{1,0:T(8,128)(2,1)}, bf16[128,1024...) custom-call(s32[5]{0:T(128)} %stack.43.at_ref, bf16[1024,1024]{1,0:T(8,128)(2,1)} %shard_map.70.turned, ...), custom_call_target="tpu_custom_call" | custom-call | flops 4294967296 | bytes 16777216 | tf_op jit(solution)/shard_map/grad_u/pallas_call | solution.py:236
  218.5 1.9 collective-permute-start.56
  220.5 2.9 %shard_map.67.turned = bf16[1024,1024]{1,0:T(8,128)(2,1)} custom-call(bf16[256,1024]{1,0:T(8,128)(2,1)} %get-tuple-element.29.refs_0_, bf16[256,1024]{1,0:T(8,128)(2,1)} %copy-done.13, bf16[256,1024]{1,0:T(8,128)(2,1)} %copy-done.15, bf16[256,1024]{1,0:T(8,128)(2,1)} %copy-done.16), custom_call_target="tpu_custom_call" | custom-call | flops 536870912 | bytes 4194304 | tf_op jit(solution)/shard_map/pallas_call | solution.py:150
  225.1 5.7 %grad_v.1 = (f32[256,1024]{1,0:T(8,128)}, bf16[256,1024]{1,0:T(8,128)(2,1)}, bf16[256,1024]{1,0:T(8,128)(2,1)}, bf16[256,1024]{1,0:T(8,128)(2,1)}) custom-call(bf16[1024,1024]{1,0:T(8,128)(2,1)} %shard_map.67.turned, bf16[128,1024]{1,0:T(8,128)(2,1)} %copy-done.23, bf16[128,1024]{1,0:T(8,128)(2,1)} %copy-done.30, ...), custom_call_target="tpu_custom_call" | custom-call | flops 2147483648 | bytes 8388608 | tf_op jit(solution)/shard_map/grad_v/pallas_call | solution.py:183
  230.8 2.0 collective-permute-start.43
  234.2 3.2 %collective-permute-start.58 = (bf16[128,1024]{1,0:T(8,128)(2,1)S(1)}, bf16[128,1024]{1,0:T(8,128)(2,1)S(1)}, u32[]{:S(2)}, u32[]{:S(2)}) collective-permute-start(bf16[128,1024]{1,0:T(8,128)(2,1)S(1)} %copy-done.32), channel_id=1, source_target_pairs={{0,12},{4,0},{8,4},{12,8},{1,13},{5,1},{9,5},{13,9},{2,14},{6,2},{... | collective-permute-start | bytes 786440 | tf_op jit(solution)/shard_map/ppermute | solution.py:34
  237.5 5.3 %collective-permute-done.60 = bf16[128,1024]{1,0:T(8,128)(2,1)S(1)} collective-permute-done((bf16[128,1024]{1,0:T(8,128)(2,1)S(1)}, bf16[128,1024]{1,0:T(8,128)(2,1)S(1)}, u32[]{:S(2)}, u32[]{:S(2)}) %collective-permute-start.60) | collective-permute-done | bytes 262176 | tf_op jit(solution)/shard_map/ppermute | solution.py:34
  242.9 12.6 %collective-permute-done.43 = bf16[256,1024]{1,0:T(8,128)(2,1)S(1)} collective-permute-done((bf16[256,1024]{1,0:T(8,128)(2,1)}, bf16[256,1024]{1,0:T(8,128)(2,1)S(1)}, u32[]{:S(2)}, u32[]{:S(2)}) %collective-permute-start.43) | collective-permute-done | bytes 524320 | tf_op jit(solution)/shard_map/ppermute | solution.py:34
  255.9 1.7 collective-permute-start.61
  260.0 1.9 collective-permute-done.57
  265.7 16.7 %all_to_all.17 = f32[128,1,128]{2,1,0:T(1,128)S(1)} all-to-all(f32[128,1,128]{2,1,0:T(1,128)S(1)} %broadcast_in_dim.16), channel_id=1, replica_groups=mesh['p'=2,'h'=2,'c'=2,'z'=4,'y'=4] {'p','h','c','z','y'}, dimensions={0} | all-to-all | bytes 131072 | tf_op jit(solution)/shard_map/all_to_all | solution.py:29
  283.9 2.5 multiply_bitcast_fusion
  (204 shorter events, 50.8 us)
Async XLA Ops:
  3.8 13.5 %collective-permute-start.6 = (bf16[256,1024]{1,0:T(8,128)(2,1)S(1)}, bf16[256,1024]{1,0:T(8,128)(2,1)S(1)}, u32[]{:S(2)}, u32[]{:S(2)}) collective-permute-start(bf16[256,1024]{1,0:T(8,128)(2,1)S(1)} %get-tuple-element.37.refs_4_), channel_id=1, source_target_pairs={{0,64},{64,0},{1,65},{65,1},{2,66},{66,2},{3,67},{67,3},{4,68},{68... | collective-permute-start | bytes 1572872 | tf_op jit(solution)/shard_map/ppermute | solution.py:320
  5.4 24.5 %collective-permute-start.7 = (bf16[256,1024]{1,0:T(8,128)(2,1)S(1)}, bf16[256,1024]{1,0:T(8,128)(2,1)S(1)}, u32[]{:S(2)}, u32[]{:S(2)}) collective-permute-start(bf16[256,1024]{1,0:T(8,128)(2,1)S(1)} %get-tuple-element.37.refs_4_), channel_id=1, source_target_pairs={{0,16},{16,0},{1,17},{17,1},{2,18},{18,2},{3,19},{19,3},{4,20},{20... | collective-permute-start | bytes 1572872 | tf_op jit(solution)/shard_map/ppermute | solution.py:34
  17.3 12.6 %collective-permute-start.8 = (bf16[256,1024]{1,0:T(8,128)(2,1)S(1)}, bf16[256,1024]{1,0:T(8,128)(2,1)S(1)}, u32[]{:S(2)}, u32[]{:S(2)}) collective-permute-start(bf16[256,1024]{1,0:T(8,128)(2,1)S(1)} %collective-permute-done.6.refs_0_), channel_id=1, source_target_pairs={{0,16},{16,0},{1,17},{17,1},{2,18},{18,2},{3,19},{19,3},{4,20},{20... | collective-permute-start | bytes 1572872 | tf_op jit(solution)/shard_map/ppermute | solution.py:34
  23.1 21.3 %collective-permute-start.3 = (bf16[256,1024]{1,0:T(8,128)(2,1)}, bf16[256,1024]{1,0:T(8,128)(2,1)S(1)}, u32[]{:S(2)}, u32[]{:S(2)}) collective-permute-start(bf16[256,1024]{1,0:T(8,128)(2,1)} %get-tuple-element.34), channel_id=1, source_target_pairs={{0,1},{1,2},{2,3},{3,0},{4,5},{5,6},{6,7},{7,4},{8,9},{9,10},{10,1... | collective-permute-start | bytes 1572872 | tf_op jit(solution)/shard_map/ppermute | solution.py:34
  24.9 30.0 %collective-permute-start.4 = (bf16[256,1024]{1,0:T(8,128)(2,1)}, bf16[256,1024]{1,0:T(8,128)(2,1)S(1)}, u32[]{:S(2)}, u32[]{:S(2)}) collective-permute-start(bf16[256,1024]{1,0:T(8,128)(2,1)} %get-tuple-element.35), channel_id=1, source_target_pairs={{0,2},{1,3},{2,0},{3,1},{4,6},{5,7},{6,4},{7,5},{8,10},{9,11},{10,... | collective-permute-start | bytes 1572872 | tf_op jit(solution)/shard_map/ppermute | solution.py:34
  27.8 29.0 %collective-permute-start.5 = (bf16[256,1024]{1,0:T(8,128)(2,1)}, bf16[256,1024]{1,0:T(8,128)(2,1)}, u32[]{:S(2)}, u32[]{:S(2)}) collective-permute-start(bf16[256,1024]{1,0:T(8,128)(2,1)} %get-tuple-element.36), channel_id=1, source_target_pairs={{0,3},{1,0},{2,1},{3,2},{4,7},{5,4},{6,5},{7,6},{8,11},{9,8},{10,9... | collective-permute-start | bytes 1572872 | tf_op jit(solution)/shard_map/ppermute | solution.py:34
  31.6 28.9 %all-to-all-start = ((bf16[32,8,1024]{2,1,0:T(8,128)(2,1)}), bf16[32,8,1024]{2,1,0:T(8,128)(2,1)S(1)}, u32[]{:S(2)}, u32[]{:S(2)}) async-start(bf16[32,8,1024]{2,1,0:T(8,128)(2,1)} %bitcast.12), calls=%async_computation | async-start | bytes 1048576 | tf_op jit(solution)/shard_map/all_to_all | solution.py:29
  39.9 30.2 %collective-permute-start.10 = (bf16[256,1024]{1,0:T(8,128)(2,1)S(1)}, bf16[256,1024]{1,0:T(8,128)(2,1)}, u32[]{:S(2)}, u32[]{:S(2)}) collective-permute-start(bf16[256,1024]{1,0:T(8,128)(2,1)S(1)} %get-tuple-element.37.refs_4_), channel_id=1, source_target_pairs={{0,8},{4,12},{8,0},{12,4},{1,9},{5,13},{9,1},{13,5},{2,10},{6,14},... | collective-permute-start | bytes 1572872 | tf_op jit(solution)/shard_map/ppermute | solution.py:34
  43.3 29.8 %collective-permute-start.11 = (bf16[256,1024]{1,0:T(8,128)(2,1)S(1)}, bf16[256,1024]{1,0:T(8,128)(2,1)}, u32[]{:S(2)}, u32[]{:S(2)}) collective-permute-start(bf16[256,1024]{1,0:T(8,128)(2,1)S(1)} %get-tuple-element.37.refs_4_), channel_id=1, source_target_pairs={{0,12},{4,0},{8,4},{12,8},{1,13},{5,1},{9,5},{13,9},{2,14},{6,2},{... | collective-permute-start | bytes 1572872 | tf_op jit(solution)/shard_map/ppermute | solution.py:34
  44.5 31.2 %collective-permute-start.9 = (bf16[256,1024]{1,0:T(8,128)(2,1)S(1)}, bf16[256,1024]{1,0:T(8,128)(2,1)}, u32[]{:S(2)}, u32[]{:S(2)}) collective-permute-start(bf16[256,1024]{1,0:T(8,128)(2,1)S(1)} %get-tuple-element.37.refs_4_), channel_id=1, source_target_pairs={{0,4},{4,8},{8,12},{12,0},{1,5},{5,9},{9,13},{13,1},{2,6},{6,10},{... | collective-permute-start | bytes 1572872 | tf_op jit(solution)/shard_map/ppermute | solution.py:34
  55.0 29.3 %collective-permute-start = (bf16[256,1024]{1,0:T(8,128)(2,1)}, bf16[256,1024]{1,0:T(8,128)(2,1)S(1)}, u32[]{:S(2)}, u32[]{:S(2)}) collective-permute-start(bf16[256,1024]{1,0:T(8,128)(2,1)} %get-tuple-element.30), channel_id=1, source_target_pairs={{0,4},{4,8},{8,12},{12,0},{1,5},{5,9},{9,13},{13,1},{2,6},{6,10},{... | collective-permute-start | bytes 1572872 | tf_op jit(solution)/shard_map/ppermute | solution.py:34
  56.9 36.9 %collective-permute-start.1 = (bf16[256,1024]{1,0:T(8,128)(2,1)}, bf16[256,1024]{1,0:T(8,128)(2,1)S(1)}, u32[]{:S(2)}, u32[]{:S(2)}) collective-permute-start(bf16[256,1024]{1,0:T(8,128)(2,1)} %get-tuple-element.31), channel_id=1, source_target_pairs={{0,8},{4,12},{8,0},{12,4},{1,9},{5,13},{9,1},{13,5},{2,10},{6,14},... | collective-permute-start | bytes 1572872 | tf_op jit(solution)/shard_map/ppermute | solution.py:34
  70.1 29.7 %collective-permute-start.16 = (bf16[256,1024]{1,0:T(8,128)(2,1)}, bf16[256,1024]{1,0:T(8,128)(2,1)S(1)}, u32[]{:S(2)}, u32[]{:S(2)}) collective-permute-start(bf16[256,1024]{1,0:T(8,128)(2,1)} %get-tuple-element.40.refs_4_), channel_id=1, source_target_pairs={{0,1},{1,2},{2,3},{3,0},{4,5},{5,6},{6,7},{7,4},{8,9},{9,10},{10,1... | collective-permute-start | bytes 1572872 | tf_op jit(solution)/shard_map/ppermute | solution.py:34
  73.1 29.5 %collective-permute-start.17 = (bf16[256,1024]{1,0:T(8,128)(2,1)}, bf16[256,1024]{1,0:T(8,128)(2,1)}, u32[]{:S(2)}, u32[]{:S(2)}) collective-permute-start(bf16[256,1024]{1,0:T(8,128)(2,1)} %get-tuple-element.40.refs_4_), channel_id=1, source_target_pairs={{0,2},{1,3},{2,0},{3,1},{4,6},{5,7},{6,4},{7,5},{8,10},{9,11},{10,... | collective-permute-start | bytes 1572872 | tf_op jit(solution)/shard_map/ppermute | solution.py:34
  75.6 28.2 %collective-permute-start.18 = (bf16[256,1024]{1,0:T(8,128)(2,1)}, bf16[256,1024]{1,0:T(8,128)(2,1)}, u32[]{:S(2)}, u32[]{:S(2)}) collective-permute-start(bf16[256,1024]{1,0:T(8,128)(2,1)} %get-tuple-element.40.refs_4_), channel_id=1, source_target_pairs={{0,3},{1,0},{2,1},{3,2},{4,7},{5,4},{6,5},{7,6},{8,11},{9,8},{10,9... | collective-permute-start | bytes 1572872 | tf_op jit(solution)/shard_map/ppermute | solution.py:34
  84.2 14.1 %collective-permute-start.2 = (bf16[256,1024]{1,0:T(8,128)(2,1)}, bf16[256,1024]{1,0:T(8,128)(2,1)S(1)}, u32[]{:S(2)}, u32[]{:S(2)}) collective-permute-start(bf16[256,1024]{1,0:T(8,128)(2,1)} %get-tuple-element.32), channel_id=1, source_target_pairs={{0,12},{4,0},{8,4},{12,8},{1,13},{5,1},{9,5},{13,9},{2,14},{6,2},{... | collective-permute-start | bytes 1572872 | tf_op jit(solution)/shard_map/ppermute | solution.py:34
  93.8 20.5 %collective-permute-start.12 = (bf16[512,1024]{1,0:T(8,128)(2,1)}, bf16[512,1024]{1,0:T(8,128)(2,1)S(1)}, u32[]{:S(2)}, u32[]{:S(2)}) collective-permute-start(bf16[512,1024]{1,0:T(8,128)(2,1)} %get-tuple-element.39), channel_id=1, source_target_pairs={{0,16},{16,0},{1,17},{17,1},{2,18},{18,2},{3,19},{19,3},{4,20},{20... | collective-permute-start | bytes 3145736 | tf_op jit(solution)/shard_map/ppermute | solution.py:34
  98.4 11.3 %collective-permute-start.26 = (bf16[32,1024]{1,0:T(8,128)(2,1)S(1)}, bf16[32,1024]{1,0:T(8,128)(2,1)S(1)}, u32[]{:S(2)}, u32[]{:S(2)}) collective-permute-start(bf16[32,1024]{1,0:T(8,128)(2,1)S(1)} %bitcast.45), channel_id=1, source_target_pairs={{0,1},{1,2},{2,3},{3,0},{4,5},{5,6},{6,7},{7,4},{8,9},{9,10},{10,1... | collective-permute-start | bytes 196616 | tf_op jit(solution)/shard_map/ppermute | solution.py:34
  99.9 9.9 %collective-permute-start.27 = (bf16[32,1024]{1,0:T(8,128)(2,1)S(1)}, bf16[32,1024]{1,0:T(8,128)(2,1)}, u32[]{:S(2)}, u32[]{:S(2)}) collective-permute-start(bf16[32,1024]{1,0:T(8,128)(2,1)S(1)} %bitcast.46), channel_id=1, source_target_pairs={{0,2},{1,3},{2,0},{3,1},{4,6},{5,7},{6,4},{7,5},{8,10},{9,11},{10,... | collective-permute-start | bytes 196616 | tf_op jit(solution)/shard_map/ppermute | solution.py:34
  111.4 32.2 %collective-permute-start.29 = (bf16[128,1024]{1,0:T(8,128)(2,1)S(1)}, bf16[128,1024]{1,0:T(8,128)(2,1)S(1)}, u32[]{:S(2)}, u32[]{:S(2)}) collective-permute-start(bf16[128,1024]{1,0:T(8,128)(2,1)S(1)} %constant_dynamic-update-slice_fusion.refs_0_), channel_id=1, source_target_pairs={{0,4},{4,8},{8,12},{12,0},{1,5},{5,9},{9,13},{13,1},{2,6},{6,10},{... | collective-permute-start | bytes 786440 | tf_op jit(solution)/shard_map/ppermute | solution.py:34
  111.4 34.9 %collective-permute-start.30 = (bf16[128,1024]{1,0:T(8,128)(2,1)S(1)}, bf16[128,1024]{1,0:T(8,128)(2,1)S(1)}, u32[]{:S(2)}, u32[]{:S(2)}) collective-permute-start(bf16[128,1024]{1,0:T(8,128)(2,1)S(1)} %constant_dynamic-update-slice_fusion.refs_0_), channel_id=1, source_target_pairs={{0,8},{4,12},{8,0},{12,4},{1,9},{5,13},{9,1},{13,5},{2,10},{6,14},... | collective-permute-start | bytes 786440 | tf_op jit(solution)/shard_map/ppermute | solution.py:34
  115.1 10.7 %collective-permute-start.14 = (bf16[128,1024]{1,0:T(8,128)(2,1)S(1)}, bf16[128,1024]{1,0:T(8,128)(2,1)S(1)}, u32[]{:S(2)}, u32[]{:S(2)}) collective-permute-start(bf16[128,1024]{1,0:T(8,128)(2,1)S(1)} %get-tuple-element.78), channel_id=1, source_target_pairs={{0,2},{1,3},{2,0},{3,1},{4,6},{5,7},{6,4},{7,5},{8,10},{9,11},{10,... | collective-permute-start | bytes 786440 | tf_op jit(solution)/shard_map/ppermute | solution.py:34
  117.9 12.4 %collective-permute-start.15 = (bf16[128,1024]{1,0:T(8,128)(2,1)S(1)}, bf16[128,1024]{1,0:T(8,128)(2,1)S(1)}, u32[]{:S(2)}, u32[]{:S(2)}) collective-permute-start(bf16[128,1024]{1,0:T(8,128)(2,1)S(1)} %get-tuple-element.77), channel_id=1, source_target_pairs={{0,1},{1,2},{2,3},{3,0},{4,5},{5,6},{6,7},{7,4},{8,9},{9,10},{10,1... | collective-permute-start | bytes 786440 | tf_op jit(solution)/shard_map/ppermute | solution.py:34
  133.2 13.9 %collective-permute-start.31 = (bf16[128,1024]{1,0:T(8,128)(2,1)S(1)}, bf16[128,1024]{1,0:T(8,128)(2,1)S(1)}, u32[]{:S(2)}, u32[]{:S(2)}) collective-permute-start(bf16[128,1024]{1,0:T(8,128)(2,1)S(1)} %constant_dynamic-update-slice_fusion.refs_0_), channel_id=1, source_target_pairs={{0,12},{4,0},{8,4},{12,8},{1,13},{5,1},{9,5},{13,9},{2,14},{6,2},{... | collective-permute-start | bytes 786440 | tf_op jit(solution)/shard_map/ppermute | solution.py:34
  150.0 27.0 %collective-permute-start.46 = (bf16[256,1024]{1,0:T(8,128)(2,1)}, bf16[256,1024]{1,0:T(8,128)(2,1)S(1)}, u32[]{:S(2)}, u32[]{:S(2)}) collective-permute-start(bf16[256,1024]{1,0:T(8,128)(2,1)} %copy-done.3), channel_id=1, source_target_pairs={{0,4},{4,8},{8,12},{12,0},{1,5},{5,9},{9,13},{13,1},{2,6},{6,10},{... | collective-permute-start | bytes 1572872 | tf_op jit(solution)/shard_map/ppermute | solution.py:34
  154.3 12.4 %collective-permute-start.33 = (bf16[3,32,1024]{2,1,0:T(8,128)(2,1)S(1)}, bf16[3,32,1024]{2,1,0:T(8,128)(2,1)S(1)}, u32[]{:S(2)}, u32[]{:S(2)}) collective-permute-start(bf16[3,32,1024]{2,1,0:T(8,128)(2,1)S(1)} %get-tuple-element.88), channel_id=1, source_target_pairs={{0,64},{32,96},{64,32},{96,0},{1,65},{33,97},{65,33},{97,1},{2,66}... | collective-permute-start | bytes 589832 | tf_op jit(solution)/shard_map/ppermute | solution.py:43
  154.4 14.2 %collective-permute-start.34 = (bf16[3,32,1024]{2,1,0:T(8,128)(2,1)S(1)}, bf16[3,32,1024]{2,1,0:T(8,128)(2,1)S(1)}, u32[]{:S(2)}, u32[]{:S(2)}) collective-permute-start(bf16[3,32,1024]{2,1,0:T(8,128)(2,1)S(1)} %get-tuple-element.87), channel_id=1, source_target_pairs={{0,32},{32,0},{64,96},{96,64},{1,33},{33,1},{65,97},{97,65},{2,34}... | collective-permute-start | bytes 589832 | tf_op jit(solution)/shard_map/ppermute | solution.py:43
  157.2 11.4 %collective-permute-start.35 = (bf16[3,32,1024]{2,1,0:T(8,128)(2,1)S(1)}, bf16[3,32,1024]{2,1,0:T(8,128)(2,1)S(1)}, u32[]{:S(2)}, u32[]{:S(2)}) collective-permute-start(bf16[3,32,1024]{2,1,0:T(8,128)(2,1)S(1)} %get-tuple-element.88), channel_id=1, source_target_pairs={{0,96},{32,64},{64,0},{96,32},{1,97},{33,65},{65,1},{97,33},{2,98}... | collective-permute-start | bytes 589832 | tf_op jit(solution)/shard_map/ppermute | solution.py:43
  157.7 25.4 %collective-permute-start.47 = (bf16[256,1024]{1,0:T(8,128)(2,1)S(1)}, bf16[256,1024]{1,0:T(8,128)(2,1)S(1)}, u32[]{:S(2)}, u32[]{:S(2)}) collective-permute-start(bf16[256,1024]{1,0:T(8,128)(2,1)S(1)} %copy-done.4), channel_id=1, source_target_pairs={{0,8},{4,12},{8,0},{12,4},{1,9},{5,13},{9,1},{13,5},{2,10},{6,14},... | collective-permute-start | bytes 1572872 | tf_op jit(solution)/shard_map/ppermute | solution.py:34
  166.8 16.4 %collective-permute-start.48 = (bf16[256,1024]{1,0:T(8,128)(2,1)S(1)}, bf16[256,1024]{1,0:T(8,128)(2,1)S(1)}, u32[]{:S(2)}, u32[]{:S(2)}) collective-permute-start(bf16[256,1024]{1,0:T(8,128)(2,1)S(1)} %copy-done.4), channel_id=1, source_target_pairs={{0,12},{4,0},{8,4},{12,8},{1,13},{5,1},{9,5},{13,9},{2,14},{6,2},{... | collective-permute-start | bytes 1572872 | tf_op jit(solution)/shard_map/ppermute | solution.py:34
  168.7 28.8 %collective-permute-start.49 = (bf16[2,128,1024]{2,1,0:T(8,128)(2,1)S(1)}, bf16[2,128,1024]{2,1,0:T(8,128)(2,1)S(1)}, u32[]{:S(2)}, u32[]{:S(2)}) collective-permute-start(bf16[2,128,1024]{2,1,0:T(8,128)(2,1)S(1)} %pad_maximum_fusion.1.refs_4_), channel_id=1, source_target_pairs={{0,1},{1,2},{2,3},{3,0},{4,5},{5,6},{6,7},{7,4},{8,9},{9,10},{10,1... | collective-permute-start | bytes 1572872 | tf_op jit(solution)/shard_map/ppermute | solution.py:34
  172.6 25.8 %collective-permute-start.50 = (bf16[2,128,1024]{2,1,0:T(8,128)(2,1)S(1)}, bf16[2,128,1024]{2,1,0:T(8,128)(2,1)S(1)}, u32[]{:S(2)}, u32[]{:S(2)}) collective-permute-start(bf16[2,128,1024]{2,1,0:T(8,128)(2,1)S(1)} %pad_maximum_fusion.1.refs_4_), channel_id=1, source_target_pairs={{0,2},{1,3},{2,0},{3,1},{4,6},{5,7},{6,4},{7,5},{8,10},{9,11},{10,... | collective-permute-start | bytes 1572872 | tf_op jit(solution)/shard_map/ppermute | solution.py:34
  177.0 21.3 %collective-permute-start.51 = (bf16[2,128,1024]{2,1,0:T(8,128)(2,1)S(1)}, bf16[2,128,1024]{2,1,0:T(8,128)(2,1)}, u32[]{:S(2)}, u32[]{:S(2)}) collective-permute-start(bf16[2,128,1024]{2,1,0:T(8,128)(2,1)S(1)} %pad_maximum_fusion.1.refs_4_), channel_id=1, source_target_pairs={{0,3},{1,0},{2,1},{3,2},{4,7},{5,4},{6,5},{7,6},{8,11},{9,8},{10,9... | collective-permute-start | bytes 1572872 | tf_op jit(solution)/shard_map/ppermute | solution.py:34
  183.1 14.5 %collective-permute-start.36 = (bf16[128,1024]{1,0:T(8,128)(2,1)S(1)}, bf16[128,1024]{1,0:T(8,128)(2,1)S(1)}, u32[]{:S(2)}, u32[]{:S(2)}) collective-permute-start(bf16[128,1024]{1,0:T(8,128)(2,1)S(1)} %maximum_bitcast_fusion.refs_0_), channel_id=1, source_target_pairs={{0,4},{4,8},{8,12},{12,0},{1,5},{5,9},{9,13},{13,1},{2,6},{6,10},{... | collective-permute-start | bytes 786440 | tf_op jit(solution)/shard_map/ppermute | solution.py:34
  183.2 15.7 %collective-permute-start.37 = (bf16[128,1024]{1,0:T(8,128)(2,1)S(1)}, bf16[128,1024]{1,0:T(8,128)(2,1)}, u32[]{:S(2)}, u32[]{:S(2)}) collective-permute-start(bf16[128,1024]{1,0:T(8,128)(2,1)S(1)} %maximum_bitcast_fusion.refs_0_), channel_id=1, source_target_pairs={{0,8},{4,12},{8,0},{12,4},{1,9},{5,13},{9,1},{13,5},{2,10},{6,14},... | collective-permute-start | bytes 786440 | tf_op jit(solution)/shard_map/ppermute | solution.py:34
  197.5 10.0 %collective-permute-start.52 = (bf16[2,128,1024]{2,1,0:T(8,128)(2,1)S(1)}, bf16[2,128,1024]{2,1,0:T(8,128)(2,1)}, u32[]{:S(2)}, u32[]{:S(2)}) collective-permute-start(bf16[2,128,1024]{2,1,0:T(8,128)(2,1)S(1)} %pad_maximum_fusion.1.refs_4_), channel_id=1, source_target_pairs={{0,16},{16,0},{1,17},{17,1},{2,18},{18,2},{3,19},{19,3},{4,20},{20... | collective-permute-start | bytes 1572872 | tf_op jit(solution)/shard_map/ppermute | solution.py:34
  197.6 10.4 %collective-permute-start.53 = (bf16[2,128,1024]{2,1,0:T(8,128)(2,1)S(1)}, bf16[2,128,1024]{2,1,0:T(8,128)(2,1)}, u32[]{:S(2)}, u32[]{:S(2)}) collective-permute-start(bf16[2,128,1024]{2,1,0:T(8,128)(2,1)S(1)} %collective-permute-done.49.refs_5_), channel_id=1, source_target_pairs={{0,16},{16,0},{1,17},{17,1},{2,18},{18,2},{3,19},{19,3},{4,20},{20... | collective-permute-start | bytes 1572872 | tf_op jit(solution)/shard_map/ppermute | solution.py:34
  198.3 10.2 %collective-permute-start.55 = (bf16[2,128,1024]{2,1,0:T(8,128)(2,1)}, bf16[2,128,1024]{2,1,0:T(8,128)(2,1)}, u32[]{:S(2)}, u32[]{:S(2)}) collective-permute-start(bf16[2,128,1024]{2,1,0:T(8,128)(2,1)} %collective-permute-done.51.refs_7_), channel_id=1, source_target_pairs={{0,16},{16,0},{1,17},{17,1},{2,18},{18,2},{3,19},{19,3},{4,20},{20... | collective-permute-start | bytes 1572872 | tf_op jit(solution)/shard_map/ppermute | solution.py:34
  207.5 15.9 %collective-permute-start.39 = (bf16[128,1024]{1,0:T(8,128)(2,1)S(1)}, bf16[128,1024]{1,0:T(8,128)(2,1)S(1)}, u32[]{:S(2)}, u32[]{:S(2)}) collective-permute-start(bf16[128,1024]{1,0:T(8,128)(2,1)S(1)} %maximum_bitcast_fusion.refs_0_), channel_id=1, source_target_pairs={{0,16},{16,0},{1,17},{17,1},{2,18},{18,2},{3,19},{19,3},{4,20},{20... | collective-permute-start | bytes 786440 | tf_op jit(solution)/shard_map/ppermute | solution.py:34
  207.5 15.9 %collective-permute-start.40 = (bf16[128,1024]{1,0:T(8,128)(2,1)S(1)}, bf16[128,1024]{1,0:T(8,128)(2,1)S(1)}, u32[]{:S(2)}, u32[]{:S(2)}) collective-permute-start(bf16[128,1024]{1,0:T(8,128)(2,1)S(1)} %collective-permute-done.36.refs_1_), channel_id=1, source_target_pairs={{0,16},{16,0},{1,17},{17,1},{2,18},{18,2},{3,19},{19,3},{4,20},{20... | collective-permute-start | bytes 786440 | tf_op jit(solution)/shard_map/ppermute | solution.py:34
  208.0 15.5 %collective-permute-start.41 = (bf16[128,1024]{1,0:T(8,128)(2,1)}, bf16[128,1024]{1,0:T(8,128)(2,1)S(1)}, u32[]{:S(2)}, u32[]{:S(2)}) collective-permute-start(bf16[128,1024]{1,0:T(8,128)(2,1)} %collective-permute-done.37.refs_2_), channel_id=1, source_target_pairs={{0,16},{16,0},{1,17},{17,1},{2,18},{18,2},{3,19},{19,3},{4,20},{20... | collective-permute-start | bytes 786440 | tf_op jit(solution)/shard_map/ppermute | solution.py:34
  208.1 15.4 %collective-permute-start.42 = (bf16[128,1024]{1,0:T(8,128)(2,1)}, bf16[128,1024]{1,0:T(8,128)(2,1)S(1)}, u32[]{:S(2)}, u32[]{:S(2)}) collective-permute-start(bf16[128,1024]{1,0:T(8,128)(2,1)} %collective-permute-done.38.refs_3_), channel_id=1, source_target_pairs={{0,16},{16,0},{1,17},{17,1},{2,18},{18,2},{3,19},{19,3},{4,20},{20... | collective-permute-start | bytes 786440 | tf_op jit(solution)/shard_map/ppermute | solution.py:34
  218.5 15.6 %collective-permute-start.56 = (bf16[128,1024]{1,0:T(8,128)(2,1)}, bf16[128,1024]{1,0:T(8,128)(2,1)S(1)}, u32[]{:S(2)}, u32[]{:S(2)}) collective-permute-start(bf16[128,1024]{1,0:T(8,128)(2,1)} %get-tuple-element.50), channel_id=1, source_target_pairs={{0,12},{4,0},{8,4},{12,8},{1,13},{5,1},{9,5},{13,9},{2,14},{6,2},{... | collective-permute-start | bytes 786440 | tf_op jit(solution)/shard_map/ppermute | solution.py:34
  230.8 24.8 %collective-permute-start.43 = (bf16[256,1024]{1,0:T(8,128)(2,1)}, bf16[256,1024]{1,0:T(8,128)(2,1)S(1)}, u32[]{:S(2)}, u32[]{:S(2)}) collective-permute-start(bf16[256,1024]{1,0:T(8,128)(2,1)} %get-tuple-element.45), channel_id=1, source_target_pairs={{0,3},{1,0},{2,1},{3,2},{4,7},{5,4},{6,5},{7,6},{8,11},{9,8},{10,9... | collective-permute-start | bytes 1572872 | tf_op jit(solution)/shard_map/ppermute | solution.py:34
  232.8 23.0 %collective-permute-start.44 = (bf16[256,1024]{1,0:T(8,128)(2,1)}, bf16[256,1024]{1,0:T(8,128)(2,1)S(1)}, u32[]{:S(2)}, u32[]{:S(2)}) collective-permute-start(bf16[256,1024]{1,0:T(8,128)(2,1)} %get-tuple-element.46), channel_id=1, source_target_pairs={{0,2},{1,3},{2,0},{3,1},{4,6},{5,7},{6,4},{7,5},{8,10},{9,11},{10,... | collective-permute-start | bytes 1572872 | tf_op jit(solution)/shard_map/ppermute | solution.py:34
  234.2 25.0 %collective-permute-start.45 = (bf16[256,1024]{1,0:T(8,128)(2,1)}, bf16[256,1024]{1,0:T(8,128)(2,1)S(1)}, u32[]{:S(2)}, u32[]{:S(2)}) collective-permute-start(bf16[256,1024]{1,0:T(8,128)(2,1)} %get-tuple-element.47), channel_id=1, source_target_pairs={{0,1},{1,2},{2,3},{3,0},{4,5},{5,6},{6,7},{7,4},{8,9},{9,10},{10,1... | collective-permute-start | bytes 1572872 | tf_op jit(solution)/shard_map/ppermute | solution.py:34
  234.2 25.9 %collective-permute-start.58 = (bf16[128,1024]{1,0:T(8,128)(2,1)S(1)}, bf16[128,1024]{1,0:T(8,128)(2,1)S(1)}, u32[]{:S(2)}, u32[]{:S(2)}) collective-permute-start(bf16[128,1024]{1,0:T(8,128)(2,1)S(1)} %copy-done.32), channel_id=1, source_target_pairs={{0,12},{4,0},{8,4},{12,8},{1,13},{5,1},{9,5},{13,9},{2,14},{6,2},{... | collective-permute-start | bytes 786440 | tf_op jit(solution)/shard_map/ppermute | solution.py:34
  242.8 17.2 %collective-permute-start.59 = (bf16[128,1024]{1,0:T(8,128)(2,1)S(1)}, bf16[128,1024]{1,0:T(8,128)(2,1)S(1)}, u32[]{:S(2)}, u32[]{:S(2)}) collective-permute-start(bf16[128,1024]{1,0:T(8,128)(2,1)S(1)} %copy-done.31), channel_id=1, source_target_pairs={{0,4},{4,8},{8,12},{12,0},{1,5},{5,9},{9,13},{13,1},{2,6},{6,10},{... | collective-permute-start | bytes 786440 | tf_op jit(solution)/shard_map/ppermute | solution.py:34
  (53 other events, 584.7 us)

commit v7 on v6

--- a/solution.py
+++ b/solution.py
@@ -375,8 +375,10 @@
     other = jnp.stack([jnp.where(first, act1, slope0), act0, slope1])
     got = [same, shift_x(other, 1), shift_x(same, 2), shift_x(other, 3)]
     back = jnp.concatenate(got, 1)
-    rs = gather(back[0], "z")
-    pairs = gather(back[1:], "y")
+    rs, pairs = [back[0]], [back[1:]]
+    for k in (1, 2, 3):
+        rs.append(shift(rs[0], "z", k))
+        pairs.append(shift(pairs[0], "y", k))
     rs += [shift(a, "c", 1) for a in rs]
     pair_own = shift(pairs[0], "c", 1)
     pairs += [pair_own] + [shift(a, "c", 1) for a in pairs[1:]]

time: 290 us -> 290 us (level)
  no operation moved by 1% of the time
where the time goes in v7:
time: 290 us; the launch traced here: 289 us
  waiting for transfers between devices  106 us (37%)
  starting transfers between devices  89.4 us (31%)
  Pallas kernels  40.3 us (14%)
  blocking collectives  26.3 us (9%)
  local copies, waits for them, and re-layouts  9.89 us (3%)
  other arithmetic  9.89 us (3%)
  between operations  4.41 us (2%)
  matrix products  2.98 us (1%)
    ppermute x55, waiting for transfers between devices, shift(): lax.ppermute(value, axis, [(i, (i + by) % count) for i in range(count)])  85.8 us
    ppermute x55, starting transfers between devices, shift(): lax.ppermute(value, axis, [(i, (i + by) % count) for i in range(count)])  70.6 us
    all_to_all x2, blocking collectives, a2a(): return lax.all_to_all(value, axes, 0, 0, tiled=True)  26.3 us
    ppermute x1, waiting for transfers between devices, on_device(): w_3 = lax.ppermute(w_u, 'p', [(0, 1), (1, 0)])  11.9 us
    pallas_call x2, Pallas kernels, project(): pl.pallas_call(project_kernel, out_shape=[jax.ShapeDtypeStruct((2 * tok,...  11.5 us
    pallas_call x1, Pallas kernels, grad_u_call(): pl.pallas_call(grad_u_kernel, out_shape=piece_shapes(own, hidden), grid=(...  9.99 us
    ppermute x6, starting transfers between devices, shift_x(): return lax.ppermute(value, ('p', 'h'), pairs)  8.91 us
    all_to_all x1, starting transfers between devices, a2a(): return lax.all_to_all(value, axes, 0, 0, tiled=True)  8.28 us
  transfers between devices with their start and end apart: 63, of which 23 were waited for; matrix products, arithmetic and copies ran while one was open for 4% of the time, Pallas kernels for 14%

profile of v7, /device:TPU:0, one launch (start us, length us, event | category | flops | bytes accessed | tf_op | source)
XLA Modules:
  0.0 288.8 jit_solution(11380126621504569179)
XLA Ops:
  1.9 1.9 bitcast_select_fusion
  5.4 11.9 %collective-permute-done.6.refs_0_ = bf16[256,1024]{1,0:T(8,128)(2,1)S(1)} collective-permute-done((bf16[256,1024]{1,0:T(8,128)(2,1)S(1)}, bf16[256,1024]{1,0:T(8,128)(2,1)S(1)}, u32[]{:S(2)}, u32[]{:S(2)}) %collective-permute-start.6) | collective-permute-done | bytes 524320 | tf_op jit(solution)/shard_map/ppermute | solution.py:320
  18.1 5.0 %cut.1 = (bf16[256,1024]{1,0:T(8,128)(2,1)}, bf16[256,1024]{1,0:T(8,128)(2,1)}, bf16[256,1024]{1,0:T(8,128)(2,1)}, bf16[256,1024]{1,0:T(8,128)(2,1)}, bf16[256,1...) custom-call(s32[5]{0:T(128)} %stack.43.at_ref, ...), custom_call_target="tpu_custom_call" | custom-call | tf_op jit(solution)/shard_map/cut/pallas_call | solution.py:90
  23.1 1.8 collective-permute-start.3
  24.9 2.9 %collective-permute-start.4 = (bf16[256,1024]{1,0:T(8,128)(2,1)}, bf16[256,1024]{1,0:T(8,128)(2,1)S(1)}, u32[]{:S(2)}, u32[]{:S(2)}) collective-permute-start(bf16[256,1024]{1,0:T(8,128)(2,1)} %get-tuple-element.35), channel_id=1, source_target_pairs={{0,2},{1,3},{2,0},{3,1},{4,6},{5,7},{6,4},{7,5},{8,10},{9,11},{10,... | collective-permute-start | bytes 1572872 | tf_op jit(solution)/shard_map/ppermute | solution.py:34
  31.6 8.3 %all-to-all-start = ((bf16[32,8,1024]{2,1,0:T(8,128)(2,1)}), bf16[32,8,1024]{2,1,0:T(8,128)(2,1)S(1)}, u32[]{:S(2)}, u32[]{:S(2)}) async-start(bf16[32,8,1024]{2,1,0:T(8,128)(2,1)} %bitcast.12), calls=%async_computation | async-start | bytes 1048576 | tf_op jit(solution)/shard_map/all_to_all | solution.py:29
  39.9 3.4 %collective-permute-start.10 = (bf16[256,1024]{1,0:T(8,128)(2,1)S(1)}, bf16[256,1024]{1,0:T(8,128)(2,1)}, u32[]{:S(2)}, u32[]{:S(2)}) collective-permute-start(bf16[256,1024]{1,0:T(8,128)(2,1)S(1)} %get-tuple-element.37.refs_4_), channel_id=1, source_target_pairs={{0,8},{4,12},{8,0},{12,4},{1,9},{5,13},{9,1},{13,5},{2,10},{6,14},... | collective-permute-start | bytes 1572872 | tf_op jit(solution)/shard_map/ppermute | solution.py:34
  45.4 9.6 %collective-permute-done.4.refs_2_ = bf16[256,1024]{1,0:T(8,128)(2,1)S(1)} collective-permute-done((bf16[256,1024]{1,0:T(8,128)(2,1)}, bf16[256,1024]{1,0:T(8,128)(2,1)S(1)}, u32[]{:S(2)}, u32[]{:S(2)}) %collective-permute-start.4) | collective-permute-done | bytes 524320 | tf_op jit(solution)/shard_map/ppermute | solution.py:34
  55.0 1.9 collective-permute-start
  56.9 3.6 %collective-permute-start.1 = (bf16[256,1024]{1,0:T(8,128)(2,1)}, bf16[256,1024]{1,0:T(8,128)(2,1)S(1)}, u32[]{:S(2)}, u32[]{:S(2)}) collective-permute-start(bf16[256,1024]{1,0:T(8,128)(2,1)} %get-tuple-element.31), channel_id=1, source_target_pairs={{0,8},{4,12},{8,0},{12,4},{1,9},{5,13},{9,1},{13,5},{2,10},{6,14},... | collective-permute-start | bytes 1572872 | tf_op jit(solution)/shard_map/ppermute | solution.py:34
  60.6 9.5 %all_to_all.16 = bf16[4,8,1024]{2,1,0:T(8,128)(2,1)S(1)} all-to-all(bf16[4,8,1024]{2,1,0:T(8,128)(2,1)S(1)} %broadcast_in_dim.15), channel_id=1, replica_groups=mesh['p'=2,'h'=2,'c'=2,'z'=4,'y'=4] {'p','h'}, dimensions={0} | all-to-all | bytes 131072 | tf_op jit(solution)/shard_map/all_to_all | solution.py:29
  73.1 2.5 collective-permute-start.17
  75.6 1.9 collective-permute-start.18
  77.5 6.8 %collective-permute-done.refs_1_ = bf16[256,1024]{1,0:T(8,128)(2,1)S(1)} collective-permute-done((bf16[256,1024]{1,0:T(8,128)(2,1)}, bf16[256,1024]{1,0:T(8,128)(2,1)S(1)}, u32[]{:S(2)}, u32[]{:S(2)}) %collective-permute-start) | collective-permute-done | bytes 524320 | tf_op jit(solution)/shard_map/ppermute | solution.py:34
  84.8 5.7 %shard_map.68 = (bf16[512,1024]{1,0:T(8,128)(2,1)}, f32[512,1024]{1,0:T(8,128)}) custom-call(bf16[256,1024]{1,0:T(8,128)(2,1)} %get-tuple-element.33.refs_0_, bf16[256,1024]{1,0:T(8,128)(2,1)} %copy-done.12, bf16[256,1024]{1,0:T(8,128)(2,1)} %copy-done.14, bf16[256,1024]{1,0:T(8,128)(2,1)} %collective-permute-done.5.refs_3_, bf16[256,1024]{1,0:T(8,128)(2,1)} %copy-done.1, ...), custom_call_target="tpu_custom_call" | custom-call | flops 2147483648 | bytes 4194304 | tf_op jit(solution)/shard_map/pallas_call | solution.py:121
  90.5 3.4 %collective-permute-done.1.refs_2_ = bf16[256,1024]{1,0:T(8,128)(2,1)S(1)} collective-permute-done((bf16[256,1024]{1,0:T(8,128)(2,1)}, bf16[256,1024]{1,0:T(8,128)(2,1)S(1)}, u32[]{:S(2)}, u32[]{:S(2)}) %collective-permute-start.1) | collective-permute-done | bytes 524320 | tf_op jit(solution)/shard_map/ppermute | solution.py:34
  93.8 4.5 %collective-permute-done.2.refs_3_ = bf16[256,1024]{1,0:T(8,128)(2,1)S(1)} collective-permute-done((bf16[256,1024]{1,0:T(8,128)(2,1)}, bf16[256,1024]{1,0:T(8,128)(2,1)S(1)}, u32[]{:S(2)}, u32[]{:S(2)}) %collective-permute-start.2) | collective-permute-done | bytes 524320 | tf_op jit(solution)/shard_map/ppermute | solution.py:34
  99.9 2.8 collective-permute-start.27
  103.8 5.8 %shard_map.69 = (bf16[512,1024]{1,0:T(8,128)(2,1)}, f32[512,1024]{1,0:T(8,128)}) custom-call(bf16[256,1024]{1,0:T(8,128)(2,1)} %get-tuple-element.29.refs_0_, bf16[256,1024]{1,0:T(8,128)(2,1)} %copy-done.13, bf16[256,1024]{1,0:T(8,128)(2,1)} %copy-done.15, bf16[256,1024]{1,0:T(8,128)(2,1)} %copy-done.16, bf16[256,1024]{1,0:T(8,128)(2,1)} %get-tuple-element.40.refs_4_, ...), custom_call_target="tpu_custom_call" | custom-call | flops 2147483648 | bytes 4194304 | tf_op jit(solution)/shard_map/pallas_call | solution.py:121
  111.4 2.9 %collective-permute-start.30 = (bf16[128,1024]{1,0:T(8,128)(2,1)S(1)}, bf16[128,1024]{1,0:T(8,128)(2,1)S(1)}, u32[]{:S(2)}, u32[]{:S(2)}) collective-permute-start(bf16[128,1024]{1,0:T(8,128)(2,1)S(1)} %constant_dynamic-update-slice_fusion.refs_0_), channel_id=1, source_target_pairs={{0,8},{4,12},{8,0},{12,4},{1,9},{5,13},{9,1},{13,5},{2,10},{6,14},... | collective-permute-start | bytes 786440 | tf_op jit(solution)/shard_map/ppermute | solution.py:34
  115.1 2.8 collective-permute-start.14
  118.5 5.6 %collective-permute-done.13 = bf16[128,1024]{1,0:T(8,128)(2,1)S(1)} collective-permute-done((bf16[128,1024]{1,0:T(8,128)(2,1)S(1)}, bf16[128,1024]{1,0:T(8,128)(2,1)S(1)}, u32[]{:S(2)}, u32[]{:S(2)}) %collective-permute-start.13) | collective-permute-done | bytes 262176 | tf_op jit(solution)/shard_map/ppermute | solution.py:34
  127.3 3.0 %collective-permute-done.15 = bf16[128,1024]{1,0:T(8,128)(2,1)S(1)} collective-permute-done((bf16[128,1024]{1,0:T(8,128)(2,1)S(1)}, bf16[128,1024]{1,0:T(8,128)(2,1)S(1)}, u32[]{:S(2)}, u32[]{:S(2)}) %collective-permute-start.15) | collective-permute-done | bytes 262176 | tf_op jit(solution)/shard_map/ppermute | solution.py:34
  134.4 5.4 %collective-permute-done.22 = bf16[128,1024]{1,0:T(8,128)(2,1)S(1)} collective-permute-done((bf16[128,1024]{1,0:T(8,128)(2,1)S(1)}, bf16[128,1024]{1,0:T(8,128)(2,1)S(1)}, u32[]{:S(2)}, u32[]{:S(2)}) %collective-permute-start.22) | collective-permute-done | bytes 262176 | tf_op jit(solution)/shard_map/ppermute | solution.py:34
  140.7 2.4 collective-permute-start.23
  143.7 2.6 collective-permute-start.25
  147.8 2.2 join.1
  154.4 2.8 collective-permute-start.34
  159.2 7.6 %collective-permute-done.33 = bf16[3,32,1024]{2,1,0:T(8,128)(2,1)S(1)} collective-permute-done((bf16[3,32,1024]{2,1,0:T(8,128)(2,1)S(1)}, bf16[3,32,1024]{2,1,0:T(8,128)(2,1)S(1)}, u32[]{:S(2)}, u32[]{:S(2)}) %collective-permute-start.33) | collective-permute-done | bytes 196640 | tf_op jit(solution)/shard_map/ppermute | solution.py:43
  166.8 1.9 collective-permute-start.48
  168.7 3.9 %collective-permute-start.49 = (bf16[2,128,1024]{2,1,0:T(8,128)(2,1)S(1)}, bf16[2,128,1024]{2,1,0:T(8,128)(2,1)S(1)}, u32[]{:S(2)}, u32[]{:S(2)}) collective-permute-start(bf16[2,128,1024]{2,1,0:T(8,128)(2,1)S(1)} %pad_maximum_fusion.1.refs_4_), channel_id=1, source_target_pairs={{0,1},{1,2},{2,3},{3,0},{4,5},{5,6},{6,7},{7,4},{8,9},{9,10},{10,1... | collective-permute-start | bytes 1572872 | tf_op jit(solution)/shard_map/ppermute | solution.py:34
  172.6 3.6 %collective-permute-start.50 = (bf16[2,128,1024]{2,1,0:T(8,128)(2,1)S(1)}, bf16[2,128,1024]{2,1,0:T(8,128)(2,1)S(1)}, u32[]{:S(2)}, u32[]{:S(2)}) collective-permute-start(bf16[2,128,1024]{2,1,0:T(8,128)(2,1)S(1)} %pad_maximum_fusion.1.refs_4_), channel_id=1, source_target_pairs={{0,2},{1,3},{2,0},{3,1},{4,6},{5,7},{6,4},{7,5},{8,10},{9,11},{10,... | collective-permute-start | bytes 1572872 | tf_op jit(solution)/shard_map/ppermute | solution.py:34
  177.0 6.0 %collective-permute-start.51 = (bf16[2,128,1024]{2,1,0:T(8,128)(2,1)S(1)}, bf16[2,128,1024]{2,1,0:T(8,128)(2,1)}, u32[]{:S(2)}, u32[]{:S(2)}) collective-permute-start(bf16[2,128,1024]{2,1,0:T(8,128)(2,1)S(1)} %pad_maximum_fusion.1.refs_4_), channel_id=1, source_target_pairs={{0,3},{1,0},{2,1},{3,2},{4,7},{5,4},{6,5},{7,6},{8,11},{9,8},{10,9... | collective-permute-start | bytes 1572872 | tf_op jit(solution)/shard_map/ppermute | solution.py:34
  184.3 13.2 %collective-permute-done.36.refs_1_ = bf16[128,1024]{1,0:T(8,128)(2,1)S(1)} collective-permute-done((bf16[128,1024]{1,0:T(8,128)(2,1)S(1)}, bf16[128,1024]{1,0:T(8,128)(2,1)S(1)}, u32[]{:S(2)}, u32[]{:S(2)}) %collective-permute-start.36) | collective-permute-done | bytes 262176 | tf_op jit(solution)/shard_map/ppermute | solution.py:34
  199.5 2.9 %shard_map.70.turned = bf16[1024,1024]{1,0:T(8,128)(2,1)} custom-call(bf16[256,1024]{1,0:T(8,128)(2,1)} %get-tuple-element.33.refs_0_, bf16[256,1024]{1,0:T(8,128)(2,1)} %copy-done.12, bf16[256,1024]{1,0:T(8,128)(2,1)} %copy-done.14, bf16[256,1024]{1,0:T(8,128)(2,1)} %collective-permute-done.5.refs_3_), custom_call_target="tpu_custom_call" | custom-call | flops 536870912 | bytes 4194304 | tf_op jit(solution)/shard_map/pallas_call | solution.py:150
  202.5 5.0 %collective-permute-done.38.refs_3_ = bf16[128,1024]{1,0:T(8,128)(2,1)} collective-permute-done((bf16[128,1024]{1,0:T(8,128)(2,1)S(1)}, bf16[128,1024]{1,0:T(8,128)(2,1)}, u32[]{:S(2)}, u32[]{:S(2)}) %collective-permute-start.38) | collective-permute-done | bytes 262176 | tf_op jit(solution)/shard_map/ppermute | solution.py:34
  208.5 10.0 %grad_u.1 = (f32[256,1024]{1,0:T(8,128)}, bf16[128,1024]{1,0:T(8,128)(2,1)}, bf16[128,1024]{1,0:T(8,128)(2,1)}, bf16[128,1024]{1,0:T(8,128)(2,1)}, bf16[128,1024...) custom-call(s32[5]{0:T(128)} %stack.43.at_ref, bf16[1024,1024]{1,0:T(8,128)(2,1)} %shard_map.70.turned, ...), custom_call_target="tpu_custom_call" | custom-call | flops 4294967296 | bytes 16777216 | tf_op jit(solution)/shard_map/grad_u/pallas_call | solution.py:236
  218.5 1.9 collective-permute-start.56
  220.5 2.9 %shard_map.67.turned = bf16[1024,1024]{1,0:T(8,128)(2,1)} custom-call(bf16[256,1024]{1,0:T(8,128)(2,1)} %get-tuple-element.29.refs_0_, bf16[256,1024]{1,0:T(8,128)(2,1)} %copy-done.13, bf16[256,1024]{1,0:T(8,128)(2,1)} %copy-done.15, bf16[256,1024]{1,0:T(8,128)(2,1)} %copy-done.16), custom_call_target="tpu_custom_call" | custom-call | flops 536870912 | bytes 4194304 | tf_op jit(solution)/shard_map/pallas_call | solution.py:150
  225.1 5.7 %grad_v.1 = (f32[256,1024]{1,0:T(8,128)}, bf16[256,1024]{1,0:T(8,128)(2,1)}, bf16[256,1024]{1,0:T(8,128)(2,1)}, bf16[256,1024]{1,0:T(8,128)(2,1)}) custom-call(bf16[1024,1024]{1,0:T(8,128)(2,1)} %shard_map.67.turned, bf16[128,1024]{1,0:T(8,128)(2,1)} %copy-done.23, bf16[128,1024]{1,0:T(8,128)(2,1)} %copy-done.30, ...), custom_call_target="tpu_custom_call" | custom-call | flops 2147483648 | bytes 8388608 | tf_op jit(solution)/shard_map/grad_v/pallas_call | solution.py:183
  230.8 2.0 collective-permute-start.43
  234.2 3.2 %collective-permute-start.58 = (bf16[128,1024]{1,0:T(8,128)(2,1)S(1)}, bf16[128,1024]{1,0:T(8,128)(2,1)S(1)}, u32[]{:S(2)}, u32[]{:S(2)}) collective-permute-start(bf16[128,1024]{1,0:T(8,128)(2,1)S(1)} %copy-done.32), channel_id=1, source_target_pairs={{0,12},{4,0},{8,4},{12,8},{1,13},{5,1},{9,5},{13,9},{2,14},{6,2},{... | collective-permute-start | bytes 786440 | tf_op jit(solution)/shard_map/ppermute | solution.py:34
  237.5 5.3 %collective-permute-done.60 = bf16[128,1024]{1,0:T(8,128)(2,1)S(1)} collective-permute-done((bf16[128,1024]{1,0:T(8,128)(2,1)S(1)}, bf16[128,1024]{1,0:T(8,128)(2,1)S(1)}, u32[]{:S(2)}, u32[]{:S(2)}) %collective-permute-start.60) | collective-permute-done | bytes 262176 | tf_op jit(solution)/shard_map/ppermute | solution.py:34
  242.9 12.6 %collective-permute-done.43 = bf16[256,1024]{1,0:T(8,128)(2,1)S(1)} collective-permute-done((bf16[256,1024]{1,0:T(8,128)(2,1)}, bf16[256,1024]{1,0:T(8,128)(2,1)S(1)}, u32[]{:S(2)}, u32[]{:S(2)}) %collective-permute-start.43) | collective-permute-done | bytes 524320 | tf_op jit(solution)/shard_map/ppermute | solution.py:34
  255.9 1.7 collective-permute-start.61
  260.0 1.9 collective-permute-done.57
  265.7 16.7 %all_to_all.17 = f32[128,1,128]{2,1,0:T(1,128)S(1)} all-to-all(f32[128,1,128]{2,1,0:T(1,128)S(1)} %broadcast_in_dim.16), channel_id=1, replica_groups=mesh['p'=2,'h'=2,'c'=2,'z'=4,'y'=4] {'p','h','c','z','y'}, dimensions={0} | all-to-all | bytes 131072 | tf_op jit(solution)/shard_map/all_to_all | solution.py:29
  283.9 2.5 multiply_bitcast_fusion
  (204 shorter events, 50.8 us)
Async XLA Ops:
  3.8 13.5 %collective-permute-start.6 = (bf16[256,1024]{1,0:T(8,128)(2,1)S(1)}, bf16[256,1024]{1,0:T(8,128)(2,1)S(1)}, u32[]{:S(2)}, u32[]{:S(2)}) collective-permute-start(bf16[256,1024]{1,0:T(8,128)(2,1)S(1)} %get-tuple-element.37.refs_4_), channel_id=1, source_target_pairs={{0,64},{64,0},{1,65},{65,1},{2,66},{66,2},{3,67},{67,3},{4,68},{68... | collective-permute-start | bytes 1572872 | tf_op jit(solution)/shard_map/ppermute | solution.py:320
  5.4 24.5 %collective-permute-start.7 = (bf16[256,1024]{1,0:T(8,128)(2,1)S(1)}, bf16[256,1024]{1,0:T(8,128)(2,1)S(1)}, u32[]{:S(2)}, u32[]{:S(2)}) collective-permute-start(bf16[256,1024]{1,0:T(8,128)(2,1)S(1)} %get-tuple-element.37.refs_4_), channel_id=1, source_target_pairs={{0,16},{16,0},{1,17},{17,1},{2,18},{18,2},{3,19},{19,3},{4,20},{20... | collective-permute-start | bytes 1572872 | tf_op jit(solution)/shard_map/ppermute | solution.py:34
  17.3 12.6 %collective-permute-start.8 = (bf16[256,1024]{1,0:T(8,128)(2,1)S(1)}, bf16[256,1024]{1,0:T(8,128)(2,1)S(1)}, u32[]{:S(2)}, u32[]{:S(2)}) collective-permute-start(bf16[256,1024]{1,0:T(8,128)(2,1)S(1)} %collective-permute-done.6.refs_0_), channel_id=1, source_target_pairs={{0,16},{16,0},{1,17},{17,1},{2,18},{18,2},{3,19},{19,3},{4,20},{20... | collective-permute-start | bytes 1572872 | tf_op jit(solution)/shard_map/ppermute | solution.py:34
  23.1 21.3 %collective-permute-start.3 = (bf16[256,1024]{1,0:T(8,128)(2,1)}, bf16[256,1024]{1,0:T(8,128)(2,1)S(1)}, u32[]{:S(2)}, u32[]{:S(2)}) collective-permute-start(bf16[256,1024]{1,0:T(8,128)(2,1)} %get-tuple-element.34), channel_id=1, source_target_pairs={{0,1},{1,2},{2,3},{3,0},{4,5},{5,6},{6,7},{7,4},{8,9},{9,10},{10,1... | collective-permute-start | bytes 1572872 | tf_op jit(solution)/shard_map/ppermute | solution.py:34
  24.9 30.0 %collective-permute-start.4 = (bf16[256,1024]{1,0:T(8,128)(2,1)}, bf16[256,1024]{1,0:T(8,128)(2,1)S(1)}, u32[]{:S(2)}, u32[]{:S(2)}) collective-permute-start(bf16[256,1024]{1,0:T(8,128)(2,1)} %get-tuple-element.35), channel_id=1, source_target_pairs={{0,2},{1,3},{2,0},{3,1},{4,6},{5,7},{6,4},{7,5},{8,10},{9,11},{10,... | collective-permute-start | bytes 1572872 | tf_op jit(solution)/shard_map/ppermute | solution.py:34
  27.8 29.0 %collective-permute-start.5 = (bf16[256,1024]{1,0:T(8,128)(2,1)}, bf16[256,1024]{1,0:T(8,128)(2,1)}, u32[]{:S(2)}, u32[]{:S(2)}) collective-permute-start(bf16[256,1024]{1,0:T(8,128)(2,1)} %get-tuple-element.36), channel_id=1, source_target_pairs={{0,3},{1,0},{2,1},{3,2},{4,7},{5,4},{6,5},{7,6},{8,11},{9,8},{10,9... | collective-permute-start | bytes 1572872 | tf_op jit(solution)/shard_map/ppermute | solution.py:34
  31.6 28.9 %all-to-all-start = ((bf16[32,8,1024]{2,1,0:T(8,128)(2,1)}), bf16[32,8,1024]{2,1,0:T(8,128)(2,1)S(1)}, u32[]{:S(2)}, u32[]{:S(2)}) async-start(bf16[32,8,1024]{2,1,0:T(8,128)(2,1)} %bitcast.12), calls=%async_computation | async-start | bytes 1048576 | tf_op jit(solution)/shard_map/all_to_all | solution.py:29
  39.9 30.2 %collective-permute-start.10 = (bf16[256,1024]{1,0:T(8,128)(2,1)S(1)}, bf16[256,1024]{1,0:T(8,128)(2,1)}, u32[]{:S(2)}, u32[]{:S(2)}) collective-permute-start(bf16[256,1024]{1,0:T(8,128)(2,1)S(1)} %get-tuple-element.37.refs_4_), channel_id=1, source_target_pairs={{0,8},{4,12},{8,0},{12,4},{1,9},{5,13},{9,1},{13,5},{2,10},{6,14},... | collective-permute-start | bytes 1572872 | tf_op jit(solution)/shard_map/ppermute | solution.py:34
  43.3 29.8 %collective-permute-start.11 = (bf16[256,1024]{1,0:T(8,128)(2,1)S(1)}, bf16[256,1024]{1,0:T(8,128)(2,1)}, u32[]{:S(2)}, u32[]{:S(2)}) collective-permute-start(bf16[256,1024]{1,0:T(8,128)(2,1)S(1)} %get-tuple-element.37.refs_4_), channel_id=1, source_target_pairs={{0,12},{4,0},{8,4},{12,8},{1,13},{5,1},{9,5},{13,9},{2,14},{6,2},{... | collective-permute-start | bytes 1572872 | tf_op jit(solution)/shard_map/ppermute | solution.py:34
  44.5 31.2 %collective-permute-start.9 = (bf16[256,1024]{1,0:T(8,128)(2,1)S(1)}, bf16[256,1024]{1,0:T(8,128)(2,1)}, u32[]{:S(2)}, u32[]{:S(2)}) collective-permute-start(bf16[256,1024]{1,0:T(8,128)(2,1)S(1)} %get-tuple-element.37.refs_4_), channel_id=1, source_target_pairs={{0,4},{4,8},{8,12},{12,0},{1,5},{5,9},{9,13},{13,1},{2,6},{6,10},{... | collective-permute-start | bytes 1572872 | tf_op jit(solution)/shard_map/ppermute | solution.py:34
  55.0 29.3 %collective-permute-start = (bf16[256,1024]{1,0:T(8,128)(2,1)}, bf16[256,1024]{1,0:T(8,128)(2,1)S(1)}, u32[]{:S(2)}, u32[]{:S(2)}) collective-permute-start(bf16[256,1024]{1,0:T(8,128)(2,1)} %get-tuple-element.30), channel_id=1, source_target_pairs={{0,4},{4,8},{8,12},{12,0},{1,5},{5,9},{9,13},{13,1},{2,6},{6,10},{... | collective-permute-start | bytes 1572872 | tf_op jit(solution)/shard_map/ppermute | solution.py:34
  56.9 36.9 %collective-permute-start.1 = (bf16[256,1024]{1,0:T(8,128)(2,1)}, bf16[256,1024]{1,0:T(8,128)(2,1)S(1)}, u32[]{:S(2)}, u32[]{:S(2)}) collective-permute-start(bf16[256,1024]{1,0:T(8,128)(2,1)} %get-tuple-element.31), channel_id=1, source_target_pairs={{0,8},{4,12},{8,0},{12,4},{1,9},{5,13},{9,1},{13,5},{2,10},{6,14},... | collective-permute-start | bytes 1572872 | tf_op jit(solution)/shard_map/ppermute | solution.py:34
  70.1 29.7 %collective-permute-start.16 = (bf16[256,1024]{1,0:T(8,128)(2,1)}, bf16[256,1024]{1,0:T(8,128)(2,1)S(1)}, u32[]{:S(2)}, u32[]{:S(2)}) collective-permute-start(bf16[256,1024]{1,0:T(8,128)(2,1)} %get-tuple-element.40.refs_4_), channel_id=1, source_target_pairs={{0,1},{1,2},{2,3},{3,0},{4,5},{5,6},{6,7},{7,4},{8,9},{9,10},{10,1... | collective-permute-start | bytes 1572872 | tf_op jit(solution)/shard_map/ppermute | solution.py:34
  73.1 29.5 %collective-permute-start.17 = (bf16[256,1024]{1,0:T(8,128)(2,1)}, bf16[256,1024]{1,0:T(8,128)(2,1)}, u32[]{:S(2)}, u32[]{:S(2)}) collective-permute-start(bf16[256,1024]{1,0:T(8,128)(2,1)} %get-tuple-element.40.refs_4_), channel_id=1, source_target_pairs={{0,2},{1,3},{2,0},{3,1},{4,6},{5,7},{6,4},{7,5},{8,10},{9,11},{10,... | collective-permute-start | bytes 1572872 | tf_op jit(solution)/shard_map/ppermute | solution.py:34
  75.6 28.2 %collective-permute-start.18 = (bf16[256,1024]{1,0:T(8,128)(2,1)}, bf16[256,1024]{1,0:T(8,128)(2,1)}, u32[]{:S(2)}, u32[]{:S(2)}) collective-permute-start(bf16[256,1024]{1,0:T(8,128)(2,1)} %get-tuple-element.40.refs_4_), channel_id=1, source_target_pairs={{0,3},{1,0},{2,1},{3,2},{4,7},{5,4},{6,5},{7,6},{8,11},{9,8},{10,9... | collective-permute-start | bytes 1572872 | tf_op jit(solution)/shard_map/ppermute | solution.py:34
  84.2 14.1 %collective-permute-start.2 = (bf16[256,1024]{1,0:T(8,128)(2,1)}, bf16[256,1024]{1,0:T(8,128)(2,1)S(1)}, u32[]{:S(2)}, u32[]{:S(2)}) collective-permute-start(bf16[256,1024]{1,0:T(8,128)(2,1)} %get-tuple-element.32), channel_id=1, source_target_pairs={{0,12},{4,0},{8,4},{12,8},{1,13},{5,1},{9,5},{13,9},{2,14},{6,2},{... | collective-permute-start | bytes 1572872 | tf_op jit(solution)/shard_map/ppermute | solution.py:34
  93.8 20.5 %collective-permute-start.12 = (bf16[512,1024]{1,0:T(8,128)(2,1)}, bf16[512,1024]{1,0:T(8,128)(2,1)S(1)}, u32[]{:S(2)}, u32[]{:S(2)}) collective-permute-start(bf16[512,1024]{1,0:T(8,128)(2,1)} %get-tuple-element.39), channel_id=1, source_target_pairs={{0,16},{16,0},{1,17},{17,1},{2,18},{18,2},{3,19},{19,3},{4,20},{20... | collective-permute-start | bytes 3145736 | tf_op jit(solution)/shard_map/ppermute | solution.py:34
  98.4 11.3 %collective-permute-start.26 = (bf16[32,1024]{1,0:T(8,128)(2,1)S(1)}, bf16[32,1024]{1,0:T(8,128)(2,1)S(1)}, u32[]{:S(2)}, u32[]{:S(2)}) collective-permute-start(bf16[32,1024]{1,0:T(8,128)(2,1)S(1)} %bitcast.45), channel_id=1, source_target_pairs={{0,1},{1,2},{2,3},{3,0},{4,5},{5,6},{6,7},{7,4},{8,9},{9,10},{10,1... | collective-permute-start | bytes 196616 | tf_op jit(solution)/shard_map/ppermute | solution.py:34
  99.9 9.9 %collective-permute-start.27 = (bf16[32,1024]{1,0:T(8,128)(2,1)S(1)}, bf16[32,1024]{1,0:T(8,128)(2,1)}, u32[]{:S(2)}, u32[]{:S(2)}) collective-permute-start(bf16[32,1024]{1,0:T(8,128)(2,1)S(1)} %bitcast.46), channel_id=1, source_target_pairs={{0,2},{1,3},{2,0},{3,1},{4,6},{5,7},{6,4},{7,5},{8,10},{9,11},{10,... | collective-permute-start | bytes 196616 | tf_op jit(solution)/shard_map/ppermute | solution.py:34
  111.4 32.2 %collective-permute-start.29 = (bf16[128,1024]{1,0:T(8,128)(2,1)S(1)}, bf16[128,1024]{1,0:T(8,128)(2,1)S(1)}, u32[]{:S(2)}, u32[]{:S(2)}) collective-permute-start(bf16[128,1024]{1,0:T(8,128)(2,1)S(1)} %constant_dynamic-update-slice_fusion.refs_0_), channel_id=1, source_target_pairs={{0,4},{4,8},{8,12},{12,0},{1,5},{5,9},{9,13},{13,1},{2,6},{6,10},{... | collective-permute-start | bytes 786440 | tf_op jit(solution)/shard_map/ppermute | solution.py:34
  111.4 34.9 %collective-permute-start.30 = (bf16[128,1024]{1,0:T(8,128)(2,1)S(1)}, bf16[128,1024]{1,0:T(8,128)(2,1)S(1)}, u32[]{:S(2)}, u32[]{:S(2)}) collective-permute-start(bf16[128,1024]{1,0:T(8,128)(2,1)S(1)} %constant_dynamic-update-slice_fusion.refs_0_), channel_id=1, source_target_pairs={{0,8},{4,12},{8,0},{12,4},{1,9},{5,13},{9,1},{13,5},{2,10},{6,14},... | collective-permute-start | bytes 786440 | tf_op jit(solution)/shard_map/ppermute | solution.py:34
  115.1 10.7 %collective-permute-start.14 = (bf16[128,1024]{1,0:T(8,128)(2,1)S(1)}, bf16[128,1024]{1,0:T(8,128)(2,1)S(1)}, u32[]{:S(2)}, u32[]{:S(2)}) collective-permute-start(bf16[128,1024]{1,0:T(8,128)(2,1)S(1)} %get-tuple-element.78), channel_id=1, source_target_pairs={{0,2},{1,3},{2,0},{3,1},{4,6},{5,7},{6,4},{7,5},{8,10},{9,11},{10,... | collective-permute-start | bytes 786440 | tf_op jit(solution)/shard_map/ppermute | solution.py:34
  117.9 12.4 %collective-permute-start.15 = (bf16[128,1024]{1,0:T(8,128)(2,1)S(1)}, bf16[128,1024]{1,0:T(8,128)(2,1)S(1)}, u32[]{:S(2)}, u32[]{:S(2)}) collective-permute-start(bf16[128,1024]{1,0:T(8,128)(2,1)S(1)} %get-tuple-element.77), channel_id=1, source_target_pairs={{0,1},{1,2},{2,3},{3,0},{4,5},{5,6},{6,7},{7,4},{8,9},{9,10},{10,1... | collective-permute-start | bytes 786440 | tf_op jit(solution)/shard_map/ppermute | solution.py:34
  133.2 13.9 %collective-permute-start.31 = (bf16[128,1024]{1,0:T(8,128)(2,1)S(1)}, bf16[128,1024]{1,0:T(8,128)(2,1)S(1)}, u32[]{:S(2)}, u32[]{:S(2)}) collective-permute-start(bf16[128,1024]{1,0:T(8,128)(2,1)S(1)} %constant_dynamic-update-slice_fusion.refs_0_), channel_id=1, source_target_pairs={{0,12},{4,0},{8,4},{12,8},{1,13},{5,1},{9,5},{13,9},{2,14},{6,2},{... | collective-permute-start | bytes 786440 | tf_op jit(solution)/shard_map/ppermute | solution.py:34
  150.0 27.0 %collective-permute-start.46 = (bf16[256,1024]{1,0:T(8,128)(2,1)}, bf16[256,1024]{1,0:T(8,128)(2,1)S(1)}, u32[]{:S(2)}, u32[]{:S(2)}) collective-permute-start(bf16[256,1024]{1,0:T(8,128)(2,1)} %copy-done.3), channel_id=1, source_target_pairs={{0,4},{4,8},{8,12},{12,0},{1,5},{5,9},{9,13},{13,1},{2,6},{6,10},{... | collective-permute-start | bytes 1572872 | tf_op jit(solution)/shard_map/ppermute | solution.py:34
  154.3 12.4 %collective-permute-start.33 = (bf16[3,32,1024]{2,1,0:T(8,128)(2,1)S(1)}, bf16[3,32,1024]{2,1,0:T(8,128)(2,1)S(1)}, u32[]{:S(2)}, u32[]{:S(2)}) collective-permute-start(bf16[3,32,1024]{2,1,0:T(8,128)(2,1)S(1)} %get-tuple-element.88), channel_id=1, source_target_pairs={{0,64},{32,96},{64,32},{96,0},{1,65},{33,97},{65,33},{97,1},{2,66}... | collective-permute-start | bytes 589832 | tf_op jit(solution)/shard_map/ppermute | solution.py:43
  154.4 14.2 %collective-permute-start.34 = (bf16[3,32,1024]{2,1,0:T(8,128)(2,1)S(1)}, bf16[3,32,1024]{2,1,0:T(8,128)(2,1)S(1)}, u32[]{:S(2)}, u32[]{:S(2)}) collective-permute-start(bf16[3,32,1024]{2,1,0:T(8,128)(2,1)S(1)} %get-tuple-element.87), channel_id=1, source_target_pairs={{0,32},{32,0},{64,96},{96,64},{1,33},{33,1},{65,97},{97,65},{2,34}... | collective-permute-start | bytes 589832 | tf_op jit(solution)/shard_map/ppermute | solution.py:43
  157.2 11.4 %collective-permute-start.35 = (bf16[3,32,1024]{2,1,0:T(8,128)(2,1)S(1)}, bf16[3,32,1024]{2,1,0:T(8,128)(2,1)S(1)}, u32[]{:S(2)}, u32[]{:S(2)}) collective-permute-start(bf16[3,32,1024]{2,1,0:T(8,128)(2,1)S(1)} %get-tuple-element.88), channel_id=1, source_target_pairs={{0,96},{32,64},{64,0},{96,32},{1,97},{33,65},{65,1},{97,33},{2,98}... | collective-permute-start | bytes 589832 | tf_op jit(solution)/shard_map/ppermute | solution.py:43
  157.7 25.4 %collective-permute-start.47 = (bf16[256,1024]{1,0:T(8,128)(2,1)S(1)}, bf16[256,1024]{1,0:T(8,128)(2,1)S(1)}, u32[]{:S(2)}, u32[]{:S(2)}) collective-permute-start(bf16[256,1024]{1,0:T(8,128)(2,1)S(1)} %copy-done.4), channel_id=1, source_target_pairs={{0,8},{4,12},{8,0},{12,4},{1,9},{5,13},{9,1},{13,5},{2,10},{6,14},... | collective-permute-start | bytes 1572872 | tf_op jit(solution)/shard_map/ppermute | solution.py:34
  166.8 16.4 %collective-permute-start.48 = (bf16[256,1024]{1,0:T(8,128)(2,1)S(1)}, bf16[256,1024]{1,0:T(8,128)(2,1)S(1)}, u32[]{:S(2)}, u32[]{:S(2)}) collective-permute-start(bf16[256,1024]{1,0:T(8,128)(2,1)S(1)} %copy-done.4), channel_id=1, source_target_pairs={{0,12},{4,0},{8,4},{12,8},{1,13},{5,1},{9,5},{13,9},{2,14},{6,2},{... | collective-permute-start | bytes 1572872 | tf_op jit(solution)/shard_map/ppermute | solution.py:34
  168.7 28.8 %collective-permute-start.49 = (bf16[2,128,1024]{2,1,0:T(8,128)(2,1)S(1)}, bf16[2,128,1024]{2,1,0:T(8,128)(2,1)S(1)}, u32[]{:S(2)}, u32[]{:S(2)}) collective-permute-start(bf16[2,128,1024]{2,1,0:T(8,128)(2,1)S(1)} %pad_maximum_fusion.1.refs_4_), channel_id=1, source_target_pairs={{0,1},{1,2},{2,3},{3,0},{4,5},{5,6},{6,7},{7,4},{8,9},{9,10},{10,1... | collective-permute-start | bytes 1572872 | tf_op jit(solution)/shard_map/ppermute | solution.py:34
  172.6 25.8 %collective-permute-start.50 = (bf16[2,128,1024]{2,1,0:T(8,128)(2,1)S(1)}, bf16[2,128,1024]{2,1,0:T(8,128)(2,1)S(1)}, u32[]{:S(2)}, u32[]{:S(2)}) collective-permute-start(bf16[2,128,1024]{2,1,0:T(8,128)(2,1)S(1)} %pad_maximum_fusion.1.refs_4_), channel_id=1, source_target_pairs={{0,2},{1,3},{2,0},{3,1},{4,6},{5,7},{6,4},{7,5},{8,10},{9,11},{10,... | collective-permute-start | bytes 1572872 | tf_op jit(solution)/shard_map/ppermute | solution.py:34
  177.0 21.3 %collective-permute-start.51 = (bf16[2,128,1024]{2,1,0:T(8,128)(2,1)S(1)}, bf16[2,128,1024]{2,1,0:T(8,128)(2,1)}, u32[]{:S(2)}, u32[]{:S(2)}) collective-permute-start(bf16[2,128,1024]{2,1,0:T(8,128)(2,1)S(1)} %pad_maximum_fusion.1.refs_4_), channel_id=1, source_target_pairs={{0,3},{1,0},{2,1},{3,2},{4,7},{5,4},{6,5},{7,6},{8,11},{9,8},{10,9... | collective-permute-start | bytes 1572872 | tf_op jit(solution)/shard_map/ppermute | solution.py:34
  183.1 14.5 %collective-permute-start.36 = (bf16[128,1024]{1,0:T(8,128)(2,1)S(1)}, bf16[128,1024]{1,0:T(8,128)(2,1)S(1)}, u32[]{:S(2)}, u32[]{:S(2)}) collective-permute-start(bf16[128,1024]{1,0:T(8,128)(2,1)S(1)} %maximum_bitcast_fusion.refs_0_), channel_id=1, source_target_pairs={{0,4},{4,8},{8,12},{12,0},{1,5},{5,9},{9,13},{13,1},{2,6},{6,10},{... | collective-permute-start | bytes 786440 | tf_op jit(solution)/shard_map/ppermute | solution.py:34
  183.2 15.7 %collective-permute-start.37 = (bf16[128,1024]{1,0:T(8,128)(2,1)S(1)}, bf16[128,1024]{1,0:T(8,128)(2,1)}, u32[]{:S(2)}, u32[]{:S(2)}) collective-permute-start(bf16[128,1024]{1,0:T(8,128)(2,1)S(1)} %maximum_bitcast_fusion.refs_0_), channel_id=1, source_target_pairs={{0,8},{4,12},{8,0},{12,4},{1,9},{5,13},{9,1},{13,5},{2,10},{6,14},... | collective-permute-start | bytes 786440 | tf_op jit(solution)/shard_map/ppermute | solution.py:34
  197.5 10.0 %collective-permute-start.52 = (bf16[2,128,1024]{2,1,0:T(8,128)(2,1)S(1)}, bf16[2,128,1024]{2,1,0:T(8,128)(2,1)}, u32[]{:S(2)}, u32[]{:S(2)}) collective-permute-start(bf16[2,128,1024]{2,1,0:T(8,128)(2,1)S(1)} %pad_maximum_fusion.1.refs_4_), channel_id=1, source_target_pairs={{0,16},{16,0},{1,17},{17,1},{2,18},{18,2},{3,19},{19,3},{4,20},{20... | collective-permute-start | bytes 1572872 | tf_op jit(solution)/shard_map/ppermute | solution.py:34
  197.6 10.4 %collective-permute-start.53 = (bf16[2,128,1024]{2,1,0:T(8,128)(2,1)S(1)}, bf16[2,128,1024]{2,1,0:T(8,128)(2,1)}, u32[]{:S(2)}, u32[]{:S(2)}) collective-permute-start(bf16[2,128,1024]{2,1,0:T(8,128)(2,1)S(1)} %collective-permute-done.49.refs_5_), channel_id=1, source_target_pairs={{0,16},{16,0},{1,17},{17,1},{2,18},{18,2},{3,19},{19,3},{4,20},{20... | collective-permute-start | bytes 1572872 | tf_op jit(solution)/shard_map/ppermute | solution.py:34
  198.3 10.2 %collective-permute-start.55 = (bf16[2,128,1024]{2,1,0:T(8,128)(2,1)}, bf16[2,128,1024]{2,1,0:T(8,128)(2,1)}, u32[]{:S(2)}, u32[]{:S(2)}) collective-permute-start(bf16[2,128,1024]{2,1,0:T(8,128)(2,1)} %collective-permute-done.51.refs_7_), channel_id=1, source_target_pairs={{0,16},{16,0},{1,17},{17,1},{2,18},{18,2},{3,19},{19,3},{4,20},{20... | collective-permute-start | bytes 1572872 | tf_op jit(solution)/shard_map/ppermute | solution.py:34
  207.5 15.9 %collective-permute-start.39 = (bf16[128,1024]{1,0:T(8,128)(2,1)S(1)}, bf16[128,1024]{1,0:T(8,128)(2,1)S(1)}, u32[]{:S(2)}, u32[]{:S(2)}) collective-permute-start(bf16[128,1024]{1,0:T(8,128)(2,1)S(1)} %maximum_bitcast_fusion.refs_0_), channel_id=1, source_target_pairs={{0,16},{16,0},{1,17},{17,1},{2,18},{18,2},{3,19},{19,3},{4,20},{20... | collective-permute-start | bytes 786440 | tf_op jit(solution)/shard_map/ppermute | solution.py:34
  207.5 15.9 %collective-permute-start.40 = (bf16[128,1024]{1,0:T(8,128)(2,1)S(1)}, bf16[128,1024]{1,0:T(8,128)(2,1)S(1)}, u32[]{:S(2)}, u32[]{:S(2)}) collective-permute-start(bf16[128,1024]{1,0:T(8,128)(2,1)S(1)} %collective-permute-done.36.refs_1_), channel_id=1, source_target_pairs={{0,16},{16,0},{1,17},{17,1},{2,18},{18,2},{3,19},{19,3},{4,20},{20... | collective-permute-start | bytes 786440 | tf_op jit(solution)/shard_map/ppermute | solution.py:34
  208.0 15.5 %collective-permute-start.41 = (bf16[128,1024]{1,0:T(8,128)(2,1)}, bf16[128,1024]{1,0:T(8,128)(2,1)S(1)}, u32[]{:S(2)}, u32[]{:S(2)}) collective-permute-start(bf16[128,1024]{1,0:T(8,128)(2,1)} %collective-permute-done.37.refs_2_), channel_id=1, source_target_pairs={{0,16},{16,0},{1,17},{17,1},{2,18},{18,2},{3,19},{19,3},{4,20},{20... | collective-permute-start | bytes 786440 | tf_op jit(solution)/shard_map/ppermute | solution.py:34
  208.1 15.4 %collective-permute-start.42 = (bf16[128,1024]{1,0:T(8,128)(2,1)}, bf16[128,1024]{1,0:T(8,128)(2,1)S(1)}, u32[]{:S(2)}, u32[]{:S(2)}) collective-permute-start(bf16[128,1024]{1,0:T(8,128)(2,1)} %collective-permute-done.38.refs_3_), channel_id=1, source_target_pairs={{0,16},{16,0},{1,17},{17,1},{2,18},{18,2},{3,19},{19,3},{4,20},{20... | collective-permute-start | bytes 786440 | tf_op jit(solution)/shard_map/ppermute | solution.py:34
  218.5 15.6 %collective-permute-start.56 = (bf16[128,1024]{1,0:T(8,128)(2,1)}, bf16[128,1024]{1,0:T(8,128)(2,1)S(1)}, u32[]{:S(2)}, u32[]{:S(2)}) collective-permute-start(bf16[128,1024]{1,0:T(8,128)(2,1)} %get-tuple-element.50), channel_id=1, source_target_pairs={{0,12},{4,0},{8,4},{12,8},{1,13},{5,1},{9,5},{13,9},{2,14},{6,2},{... | collective-permute-start | bytes 786440 | tf_op jit(solution)/shard_map/ppermute | solution.py:34
  230.8 24.8 %collective-permute-start.43 = (bf16[256,1024]{1,0:T(8,128)(2,1)}, bf16[256,1024]{1,0:T(8,128)(2,1)S(1)}, u32[]{:S(2)}, u32[]{:S(2)}) collective-permute-start(bf16[256,1024]{1,0:T(8,128)(2,1)} %get-tuple-element.45), channel_id=1, source_target_pairs={{0,3},{1,0},{2,1},{3,2},{4,7},{5,4},{6,5},{7,6},{8,11},{9,8},{10,9... | collective-permute-start | bytes 1572872 | tf_op jit(solution)/shard_map/ppermute | solution.py:34
  232.8 23.0 %collective-permute-start.44 = (bf16[256,1024]{1,0:T(8,128)(2,1)}, bf16[256,1024]{1,0:T(8,128)(2,1)S(1)}, u32[]{:S(2)}, u32[]{:S(2)}) collective-permute-start(bf16[256,1024]{1,0:T(8,128)(2,1)} %get-tuple-element.46), channel_id=1, source_target_pairs={{0,2},{1,3},{2,0},{3,1},{4,6},{5,7},{6,4},{7,5},{8,10},{9,11},{10,... | collective-permute-start | bytes 1572872 | tf_op jit(solution)/shard_map/ppermute | solution.py:34
  234.2 25.0 %collective-permute-start.45 = (bf16[256,1024]{1,0:T(8,128)(2,1)}, bf16[256,1024]{1,0:T(8,128)(2,1)S(1)}, u32[]{:S(2)}, u32[]{:S(2)}) collective-permute-start(bf16[256,1024]{1,0:T(8,128)(2,1)} %get-tuple-element.47), channel_id=1, source_target_pairs={{0,1},{1,2},{2,3},{3,0},{4,5},{5,6},{6,7},{7,4},{8,9},{9,10},{10,1... | collective-permute-start | bytes 1572872 | tf_op jit(solution)/shard_map/ppermute | solution.py:34
  234.2 25.9 %collective-permute-start.58 = (bf16[128,1024]{1,0:T(8,128)(2,1)S(1)}, bf16[128,1024]{1,0:T(8,128)(2,1)S(1)}, u32[]{:S(2)}, u32[]{:S(2)}) collective-permute-start(bf16[128,1024]{1,0:T(8,128)(2,1)S(1)} %copy-done.32), channel_id=1, source_target_pairs={{0,12},{4,0},{8,4},{12,8},{1,13},{5,1},{9,5},{13,9},{2,14},{6,2},{... | collective-permute-start | bytes 786440 | tf_op jit(solution)/shard_map/ppermute | solution.py:34
  242.8 17.2 %collective-permute-start.59 = (bf16[128,1024]{1,0:T(8,128)(2,1)S(1)}, bf16[128,1024]{1,0:T(8,128)(2,1)S(1)}, u32[]{:S(2)}, u32[]{:S(2)}) collective-permute-start(bf16[128,1024]{1,0:T(8,128)(2,1)S(1)} %copy-done.31), channel_id=1, source_target_pairs={{0,4},{4,8},{8,12},{12,0},{1,5},{5,9},{9,13},{13,1},{2,6},{6,10},{... | collective-permute-start | bytes 786440 | tf_op jit(solution)/shard_map/ppermute | solution.py:34
  (53 other events, 584.7 us)
